TPU v7x, 32 devices: a whole 2x2x4 slice. The times are simulated.
32 devices in a mesh: dp: 16 (over z, y, x), tensor: 2 (over core).
Axes of the slice: x: 2, y: 2, z: 4, core: 2. Of those that a mesh axis runs over, the one named last changes fastest.
Arguments:
- inputs: bfloat16 [6144, 2560], P('dp'), may hold values from -6 to 6
- segment_ids: int32 [6144], P('dp'), may hold values from 0 to 11, never falling along the last dimension, each value on 1 to 1024 neighbouring positions
- cotangent: bfloat16 [6144, 2560], P('dp'), may hold values from -6 to 6
- branch_weight: bfloat16 [2, 2560, 2560], P(None, 'dp', 'tensor'), may hold values from -0.125 to 0.125
- out_weight: bfloat16 [2560, 2560], P('tensor', 'dp'), may hold values from -0.15625 to 0.15625
- ffw_in: bfloat16 [2, 2560, 7680], P(None, 'dp', 'tensor'), may hold values from -0.125 to 0.125
- ffw_out: bfloat16 [7680, 2560], P('tensor', 'dp'), may hold values from -0.09375 to 0.09375
- norm_scales: float32 [2, 2560], replicated, may hold values from -0.5 to 0.5
- branch_bias: float32 [2, 2560], P(None, 'tensor'), may hold values from -3 to 3
- conv_weight: float32 [4, 2560], P(None, 'tensor'), may hold values from -3 to 3
- conv_bias: float32 [2560], P('tensor'), may hold values from -3 to 3
- gate_weights: bfloat16 [2, 10, 256, 256], P(None, 'tensor'), may hold values from -0.375 to 0.375
- gate_bias: float32 [2, 2560], P(None, 'tensor'), may hold values from -3 to 3
- decay_param: float32 [2560], P('tensor'), may hold values from -10.5 to -5
- out_bias: float32 [2, 2560], replicated, may hold values from -3 to 3
- ffw_bias: float32 [2, 7680], P(None, 'tensor'), may hold values from -3 to 3
Outputs:
- output: float32 [6144, 2560], P('dp')
- input_grad: float32 [6144, 2560], P('dp')
- branch_weight_grad: float32 [2, 2560, 2560], P(None, 'dp', 'tensor')
- out_weight_grad: float32 [2560, 2560], P('tensor', 'dp')
- ffw_in_grad: float32 [2, 2560, 7680], P(None, 'dp', 'tensor')
- ffw_out_grad: float32 [7680, 2560], P('tensor', 'dp')
- norm_scales_grad: float32 [2, 2560], replicated
- branch_bias_grad: float32 [2, 2560], P(None, 'tensor')
- conv_weight_grad: float32 [4, 2560], P(None, 'tensor')
- conv_bias_grad: float32 [2560], P('tensor')
- gate_weights_grad: float32 [2, 10, 256, 256], P(None, 'tensor', 'dp')
- gate_bias_grad: float32 [2, 2560], P(None, 'tensor')
- decay_param_grad: float32 [2560], P('tensor')
- out_bias_grad: float32 [2, 2560], replicated
- ffw_bias_grad: float32 [2, 7680], P(None, 'tensor')
Inputs may be any that keep to these rules, and one draw needn't show every extreme that they name: `segment_ids`: segment numbers never fall along the tokens; each sequence holds 1 to 1024 tokens and one holds exactly 1024.
All inputs are finite; a program needn't handle non-finite values.
Results may differ from a plain program's by a relative error of at most 0.0095.
Values may be sent and summed in bfloat16 or wider, within the bound.
A program may use at most 448 MiB of HBM per device.

v0:
```python
import jax
import jax.numpy as jnp
from jax import lax
from jax.sharding import PartitionSpec as P


def from_behind(value, axis, steps):
    count = lax.axis_size(axis)
    leading, last = (max(0, -steps), min(count, count - steps))
    return lax.ppermute(value, axis, [(source, source + steps) for source in range(leading, last)])


def entering_2(x, axis, combine, identity, reverse):
    length, index = (lax.axis_size(axis), lax.axis_index(axis))
    everything = jax.tree.map(lambda part: lax.all_gather(part, axis), x)
    start = jax.tree.map(
        lambda part, zero: jnp.broadcast_to(jnp.asarray(zero, part.dtype), part.shape), x, identity
    )

    def hop(k, before):
        at = length - 1 - k if reverse else k
        reached = at > index if reverse else at < index
        new = combine(before, jax.tree.map(lambda part: part[at], everything))
        return jax.tree.map(lambda a, b: jnp.where(reached, a, b), new, before)

    return lax.fori_loop(0, length, hop, start)


def rms_norm(values, scaling):
    inverse = lax.rsqrt(jnp.mean(values * values, axis=-1, keepdims=True) + 1e-06)
    return values * inverse * (1.0 + scaling)


def gelu_tanh(values):
    return jax.nn.gelu(values, approximate=True)


def geglu(gate_vals, up_vals):
    return gelu_tanh(gate_vals) * up_vals


def lru_inputs(gate_decay, gate_input, conv_in, decay_in, resets):
    log_decay = -8.0 * jax.nn.sigmoid(gate_decay) * jax.nn.softplus(decay_in)
    decay = jnp.exp(log_decay)
    multiplier = jnp.sqrt(jnp.maximum(-jnp.expm1(2.0 * log_decay), 0.001))
    multiplier = jnp.where(resets, 1.0, multiplier)
    keep_rate = jnp.where(resets, 0.0, decay)
    return (keep_rate, conv_in * jax.nn.sigmoid(gate_input) * multiplier)


def pair_combine(earlier, latter):
    return (earlier[0] * latter[0], latter[0] * earlier[1] + latter[1])


def per_device(
    inputs,
    segment_ids,
    cotangent,
    branch_weight,
    out_weight,
    ffw_in,
    ffw_out,
    norm_scales,
    branch_bias,
    conv_weight,
    conv_bias,
    gate_weights,
    gate_bias,
    decay_param,
    out_bias,
    ffw_bias,
):
    branch_full, out_full, ffw_in_full, ffw_out_full = (
        lax.all_gather(branch_weight, "dp", axis=1, tiled=True),
        lax.all_gather(out_weight, "dp", axis=1, tiled=True),
        lax.all_gather(ffw_in, "dp", axis=1, tiled=True),
        lax.all_gather(ffw_out, "dp", axis=1, tiled=True),
    )
    tok_rows = inputs.shape[0]
    taps_count = conv_weight.shape[0]
    rim_rows = taps_count - 1
    heads_half = gate_weights.shape[1]
    block_size = gate_weights.shape[2]
    width_half = heads_half * block_size
    seg_marks = (segment_ids + 1).astype(jnp.float32)
    source = inputs.astype(jnp.float32)
    normed, norm_one_back = jax.vjp(rms_norm, source, norm_scales[0])
    normed_low = normed.astype(jnp.bfloat16)
    branches = (
        jnp.einsum("td,kdr->ktr", normed_low, branch_full, preferred_element_type=jnp.float32)
        + branch_bias[:, None, :]
    )
    branch_x = branches[0]
    rim_values, rim_marks = from_behind(
        (branch_x[tok_rows - rim_rows :], seg_marks[tok_rows - rim_rows :]), "dp", 1
    )
    padded_branch = jnp.concatenate([rim_values, branch_x], axis=0)
    padded_marks = jnp.concatenate([rim_marks, seg_marks], axis=0)
    resets = (seg_marks != padded_marks[rim_rows - 1 : rim_rows - 1 + tok_rows])[:, None]
    conv_out = jnp.zeros_like(branch_x) + conv_bias
    shifted_rows = []
    for offset in range(taps_count):
        matches = (
            padded_marks[rim_rows - offset : rim_rows - offset + tok_rows] == seg_marks
        ).astype(jnp.float32)[:, None]
        shifted = padded_branch[rim_rows - offset : rim_rows - offset + tok_rows] * matches
        shifted_rows.append(shifted)
        conv_out = conv_out + conv_weight[offset] * shifted
    conv_low = conv_out.astype(jnp.bfloat16)
    conv_float = conv_low.astype(jnp.float32)
    conv_blocks = conv_low.reshape(tok_rows, heads_half, block_size)
    gate_pre = (
        jnp.einsum(
            "thb,ghbc->gthc", conv_blocks, gate_weights, preferred_element_type=jnp.float32
        ).reshape(2, tok_rows, width_half)
        + gate_bias[:, None, :]
    )

    def lru_local(gate_decay, gate_input, conv_in, decay_in):
        return lru_inputs(gate_decay, gate_input, conv_in, decay_in, resets)

    (keep_rate, drive_in), lru_back = jax.vjp(
        lru_local, gate_pre[0], gate_pre[1], conv_float, decay_param
    )
    cumulative, local_state = lax.associative_scan(pair_combine, (keep_rate, drive_in), axis=0)
    entering = entering_2(
        (cumulative[tok_rows - 1], local_state[tok_rows - 1]),
        "dp",
        pair_combine,
        (jnp.ones((width_half,), jnp.float32), jnp.zeros((width_half,), jnp.float32)),
        False,
    )
    carry_in = entering[1]
    states = local_state + cumulative * carry_in
    branch_act, gelu_back = jax.vjp(gelu_tanh, branches[1])
    mixed_in = (states * branch_act).astype(jnp.bfloat16)
    mixed_part = jnp.dot(mixed_in, out_full, preferred_element_type=jnp.float32)
    residual = source + lax.psum(mixed_part, "tensor") + out_bias[0]
    normed_two, norm_two_back = jax.vjp(rms_norm, residual, norm_scales[1])
    normed_two_low = normed_two.astype(jnp.bfloat16)
    gate_up = (
        jnp.einsum("td,kdf->ktf", normed_two_low, ffw_in_full, preferred_element_type=jnp.float32)
        + ffw_bias[:, None, :]
    )
    hidden, hidden_back = jax.vjp(geglu, gate_up[0], gate_up[1])
    hidden_low = hidden.astype(jnp.bfloat16)
    ffw_part = jnp.dot(hidden_low, ffw_out_full, preferred_element_type=jnp.float32)
    result = (
        residual
        + lax.psum(ffw_part.astype(jnp.bfloat16), "tensor").astype(jnp.float32)
        + out_bias[1]
    )
    incoming_grad = cotangent.astype(jnp.float32)
    grad_ffw_out = jnp.einsum(
        "tf,td->fd", hidden_low, cotangent, preferred_element_type=jnp.float32
    )
    delta_hidden = jnp.einsum(
        "td,fd->tf", cotangent, ffw_out_full, preferred_element_type=jnp.float32
    )
    delta_gate, delta_up = hidden_back(delta_hidden)
    delta_gate_up = jnp.stack([delta_gate, delta_up]).astype(jnp.bfloat16)
    grad_ffw_in = jnp.einsum(
        "td,ktf->kdf", normed_two_low, delta_gate_up, preferred_element_type=jnp.float32
    )
    grad_ffw_bias = jnp.sum(delta_gate_up, axis=1, dtype=jnp.float32)
    delta_normed_two = lax.psum(
        jnp.einsum("ktf,kdf->td", delta_gate_up, ffw_in_full, preferred_element_type=jnp.float32),
        "tensor",
    )
    delta_res_norm, grad_scale_two = norm_two_back(delta_normed_two)
    delta_residual = incoming_grad + delta_res_norm
    delta_mixed = delta_residual.astype(jnp.bfloat16)
    grad_out_weight = jnp.einsum(
        "tr,td->rd", mixed_in, delta_mixed, preferred_element_type=jnp.float32
    )
    delta_mixed_in = jnp.einsum(
        "td,rd->tr", delta_mixed, out_full, preferred_element_type=jnp.float32
    )
    delta_states = delta_mixed_in * branch_act
    (delta_branch_y,) = gelu_back(delta_mixed_in * states)
    alpha_next = jnp.concatenate([keep_rate[1:], jnp.ones((1, width_half), jnp.float32)], axis=0)
    suffix, local_adjoint = lax.associative_scan(
        pair_combine, (alpha_next, delta_states), reverse=True, axis=0
    )
    leaving = entering_2(
        (keep_rate[0] * suffix[0], keep_rate[0] * local_adjoint[0]),
        "dp",
        pair_combine,
        (jnp.ones((width_half,), jnp.float32), jnp.zeros((width_half,), jnp.float32)),
        True,
    )
    adjoint = local_adjoint + suffix * leaving[1]
    states_before = jnp.concatenate([carry_in[None, :], states[: tok_rows - 1]], axis=0)
    delta_gate_decay, delta_gate_input, delta_conv_direct, grad_decay = lru_back(
        (adjoint * states_before, adjoint)
    )
    delta_gates = jnp.stack([delta_gate_decay, delta_gate_input]).astype(jnp.bfloat16)
    delta_blocks = delta_gates.reshape(2, tok_rows, heads_half, block_size)
    grad_gate_weights = jnp.einsum(
        "thb,gthc->ghbc", conv_blocks, delta_blocks, preferred_element_type=jnp.float32
    )
    grad_gate_bias = jnp.sum(delta_gates, axis=1, dtype=jnp.float32)
    delta_conv = delta_conv_direct + jnp.einsum(
        "gthc,ghbc->thb", delta_blocks, gate_weights, preferred_element_type=jnp.float32
    ).reshape(tok_rows, width_half)
    rim_delta, rim_next_marks = from_behind((delta_conv[:rim_rows], seg_marks[:rim_rows]), "dp", -1)
    padded_delta = jnp.concatenate([delta_conv, rim_delta], axis=0)
    next_marks = jnp.concatenate([seg_marks, rim_next_marks], axis=0)
    delta_branch_x = jnp.zeros_like(delta_conv)
    conv_weight_rows = []
    for offset in range(taps_count):
        matches = (next_marks[offset : offset + tok_rows] == seg_marks).astype(jnp.float32)[:, None]
        delta_branch_x = (
            delta_branch_x
            + conv_weight[offset] * padded_delta[offset : offset + tok_rows] * matches
        )
        conv_weight_rows.append(jnp.sum(delta_conv * shifted_rows[offset], axis=0))
    grad_conv_weight = jnp.stack(conv_weight_rows)
    grad_conv_bias = jnp.sum(delta_conv, axis=0)
    delta_branches = jnp.stack([delta_branch_x, delta_branch_y]).astype(jnp.bfloat16)
    grad_branch_bias = jnp.sum(delta_branches, axis=1, dtype=jnp.float32)
    grad_branch_weight = jnp.einsum(
        "td,ktr->kdr", normed_low, delta_branches, preferred_element_type=jnp.float32
    )
    delta_normed = lax.psum(
        jnp.einsum(
            "ktr,kdr->td", delta_branches, branch_full, preferred_element_type=jnp.float32
        ).astype(jnp.bfloat16),
        "tensor",
    ).astype(jnp.float32)
    delta_source_norm, grad_scale_one = norm_one_back(delta_normed)
    input_grad = delta_residual + delta_source_norm
    grad_out_bias = jnp.stack(
        [jnp.sum(delta_mixed, axis=0, dtype=jnp.float32), jnp.sum(incoming_grad, axis=0)]
    )
    branch_grad, out_grad, ffw_in_grad, ffw_out_grad, gate_grad = (
        lax.psum_scatter(grad_branch_weight, "dp", scatter_dimension=1, tiled=True),
        lax.psum_scatter(grad_out_weight, "dp", scatter_dimension=1, tiled=True),
        lax.psum_scatter(grad_ffw_in, "dp", scatter_dimension=1, tiled=True),
        lax.psum_scatter(grad_ffw_out, "dp", scatter_dimension=1, tiled=True),
        lax.psum_scatter(grad_gate_weights, "dp", scatter_dimension=2, tiled=True),
    )
    small_sums = lax.psum(
        (
            jnp.stack([grad_scale_one, grad_scale_two]),
            grad_branch_bias,
            grad_conv_weight,
            grad_conv_bias,
            grad_gate_bias,
            grad_decay,
            grad_out_bias,
            grad_ffw_bias,
        ),
        "dp",
    )
    return (
        result,
        input_grad,
        branch_grad,
        out_grad,
        ffw_in_grad,
        ffw_out_grad,
        small_sums[0],
        small_sums[1],
        small_sums[2],
        small_sums[3],
        gate_grad,
        small_sums[4],
        small_sums[5],
        small_sums[6],
        small_sums[7],
    )


def solution(mesh):
    in_specs = (
        P("dp", None),
        P("dp"),
        P("dp", None),
        P(None, "dp", "tensor"),
        P("tensor", "dp"),
        P(None, "dp", "tensor"),
        P("tensor", "dp"),
        P(),
        P(None, "tensor"),
        P(None, "tensor"),
        P("tensor"),
        P(None, "tensor", None, None),
        P(None, "tensor"),
        P("tensor"),
        P(),
        P(None, "tensor"),
    )
    out_specs = (
        P("dp", None),
        P("dp", None),
        P(None, "dp", "tensor"),
        P("tensor", "dp"),
        P(None, "dp", "tensor"),
        P("tensor", "dp"),
        P(),
        P(None, "tensor"),
        P(None, "tensor"),
        P("tensor"),
        P(None, "tensor", "dp", None),
        P(None, "tensor"),
        P("tensor"),
        P(),
        P(None, "tensor"),
    )
    return jax.shard_map(
        per_device, mesh=mesh, in_specs=in_specs, out_specs=out_specs, check_vma=False
    )
```

profile of v0, /device:TPU:0, one launch (start us, length us, event | category | flops | bytes accessed | tf_op | source)
XLA Modules:
  0.0 5467.6 jit_solution(928746770152064234)
XLA Ops:
  10.1 5.5 collective-permute-start.1
  19.3 150.5 %all-gather.9.cloned.1.call-done = bf16[2,2560,1280]{2,1,0:T(8,128)(2,1)} async-done(((bf16[2,160,1280]{2,1,0:T(8,128)(2,1)}), bf16[2,2560,1280]{2,1,0:T(8,128)(2,1)}) %all-gather.9.cloned.1.call-update) | async-done | bytes 13107216 | tf_op jit(solution)/shard_map/all_gather | solution.py:74
  169.8 8.4 add_bitcast_fusion.1
  192.4 5.5 copy.67
  205.1 5.4 slice.632
  210.5 5.4 slice.631
  215.8 5.4 slice.634
  221.2 5.4 slice.630
  299.6 5.4 slice.688
  335.2 5.4 slice.629
  415.7 5.5 pad.229
  423.8 5.5 pad.213
  434.3 5.5 pad.228
  440.6 38.7 all-gather
  481.6 5.6 pad.212
  488.1 35.9 all-gather.1
  525.3 6.4 multiply_convert_fusion.3
  531.8 7.8 fusion.129
  541.5 21.0 all-reduce.79.cloned.1.call-done
  562.5 4.7 multiply_reduce_fusion.2
  567.1 403.8 %all-gather.13.cloned.1.call-done = bf16[2,2560,3840]{2,1,0:T(8,128)(2,1)} async-done(((bf16[2,160,3840]{2,1,0:T(8,128)(2,1)}), bf16[2,2560,3840]{2,1,0:T(8,128)(2,1)}) %all-gather.13.cloned.1.call-update) | async-done | bytes 39321616 | tf_op jit(solution)/shard_map/all_gather | solution.py:76
  971.0 25.0 add_bitcast_fusion
  996.0 194.2 %all-gather.15.cloned.1.call-done = bf16[3840,2560]{0,1:T(8,128)(2,1)} async-done(((bf16[3840,160]{0,1:T(8,128)(2,1)}), bf16[3840,2560]{0,1:T(8,128)(2,1)}) %all-gather.15.cloned.1.call-update) | async-done | bytes 19660816 | tf_op jit(solution)/shard_map/all_gather | solution.py:77
  1190.2 19.5 fusion.17
  1209.6 23.4 convolution_bitcast_fusion.3
  1236.1 5.7 slice.723
  1241.9 5.5 slice.716
  1247.3 5.6 slice.714
  1252.9 10.4 slice.724
  1263.2 10.6 slice.715
  1273.8 10.3 slice.717
  1284.2 5.0 multiply_reduce_fusion
  1293.7 9.0 fusion.71
  1304.6 5.4 slice.778
  1309.9 5.4 slice.720
  1315.3 5.4 slice.718
  1320.7 10.3 slice.719
  1331.0 10.3 slice.721
  1404.6 10.6 slice.779
  1497.0 5.6 pad.244
  1502.6 5.6 pad.260
  1508.2 5.6 pad.261
  1513.8 5.6 pad.245
  1524.3 9.8 rev.8
  1534.1 15.9 rev.9
  1550.0 37.9 all-gather.3
  1588.0 35.9 all-gather.2
  1625.4 8.0 multiply_reduce_fusion.3
  1646.5 5.1 multiply_reduce_fusion.6
  1652.9 13.3 convolution_convert_fusion
  1669.0 10.2 fusion.9
  1683.5 5.7 copy.80
  1689.1 15.3 convolution_bitcast_fusion.1
  1704.4 38.6 copy.75
  1743.1 35.2 convolution_bitcast_fusion
  1778.3 114.3 %copy.77 = f32[2,2560,3840]{2,0,1:T(2,128)} copy(f32[2,2560,3840]{1,2,0:T(8,128)} %convolution_bitcast_fusion) | data formatting | bytes 157286400 | tf_op jit(solution)/shard_map/td,ktf->kdf/transpose | solution.py:162
  1904.6 9.4 fusion.112
  1914.0 20.7 fusion.130
  1937.3 5.4 add_add_fusion.2
  1945.8 538.1 %all-reduce.87.cloned.1.call-done = (f32[2,2560,1280]{2,0,1:T(2,128)}, f32[2,5,256,256]{3,0,1,2:T(2,128)}) async-done(((f32[2,2560,1280]{2,0,1:T(2,128)}, f32[2,5,256,256]{3,0,1,2:T(2,128)}), (f32[2,2560,1280]{2,0,1:T(2,128)}, f32[2,5,256,256]{3,0,1,2:T(2,128)})) %all-reduce.87.cloned.1.call-update) | async-done | bytes 28835856
  2488.8 2001.3 %all-reduce.83.cloned.1.call-done = f32[2,2560,3840]{2,0,1:T(2,128)} async-done(((f32[2,2560,3840]{2,0,1:T(2,128)}), f32[2,2560,3840]{2,0,1:T(2,128)}) %all-reduce.83.cloned.1.call-update) | async-done | bytes 78643216
  4496.8 107.8 %all-reduce.85.cloned.1.call-done = (f32[2,2560]{1,0:T(2,128)}, f32[2,1280]{1,0:T(2,128)}, f32[4,1280]{1,0:T(4,128)}, f32[1280]{0:T(1024)}, f32[2,1280]{1,0:T(2,...) async-done(((f32[2,2560]{1,0:T(2,128)}, f32[2,1280]{1,0:T(2,128)}, f32[4,1280]{1,0:T(4,128)}, f32[1280]{0:T(1024)}, f32[2,1280]{1,0:T(2,128)}, ...) | async-done | bytes 122896 | tf_op jit(solution)/shard_map/psum | solution.py:243
  4604.6 274.7 %reduce-scatter.3.cloned.1.call-done = f32[1280,160]{0,1:T(8,128)} async-done(((f32[1280,2560]{0,1:T(8,128)}), f32[1280,160]{0,1:T(8,128)}) %reduce-scatter.3.cloned.1.call-update) | async-done | bytes 819216 | tf_op jit(solution)/shard_map/reduce_scatter | solution.py:238
  4879.3 570.7 %reduce-scatter.5.cloned.1.call-done = f32[3840,160]{0,1:T(8,128)} async-done(((f32[3840,2560]{0,1:T(8,128)}), f32[3840,160]{0,1:T(8,128)}) %reduce-scatter.5.cloned.1.call-update) | async-done | bytes 2457616 | tf_op jit(solution)/shard_map/reduce_scatter | solution.py:240
  (679 shorter events, 441.9 us)
Async XLA Ops:
  7.2 180.9 %copy-start = (bf16[2,5,256,256]{3,2,1,0:T(8,128)(2,1)S(1)}, bf16[2,5,256,256]{3,2,1,0:T(8,128)(2,1)}, u32[]{:S(2)}) copy-start(bf16[2,5,256,256]{3,2,1,0:T(8,128)(2,1)} %param.31) | copy-start | bytes 3932164
  7.2 11.4 copy-start.122
  7.2 162.6 %copy-start.5 = (bf16[384,2560]{1,0:T(8,128)(2,1)S(1)}, bf16[384,2560]{1,0:T(8,128)(2,1)}, u32[]{:S(2)}) copy-start(bf16[384,2560]{1,0:T(8,128)(2,1)} %param.20) | copy-start | bytes 5898244
  7.2 11.1 copy-start.87
  7.2 11.1 copy-start.106
  7.2 11.1 copy-start.107
  7.3 162.6 %copy-start.129 = (f32[2,1280]{1,0:T(2,128)S(1)}, f32[2,1280]{1,0:T(2,128)}, u32[]{:S(2)}) copy-start(f32[2,1280]{1,0:T(2,128)} %param.28) | copy-start | bytes 30724
  7.3 162.6 %all-gather.9.cloned.1.call-start = ((), (), s32[]{:S(2)}) async-start(), calls=%async_computation.2 | async-start | bytes 13926400 | tf_op jit(solution)/shard_map/all_gather | solution.py:74
  8.0 523.8 %all-gather.11.cloned.1.call-start = ((), (), s32[]{:S(2)}) async-start(), calls=%async_computation.3 | async-start | bytes 6963200 | tf_op jit(solution)/shard_map/all_gather | solution.py:75
  8.8 9.7 collective-permute-start.3
  10.1 8.4 collective-permute-start.1
  15.6 546.8 %all-reduce.79.cloned.1.call-start = ((), (), s32[]{:S(2)}) async-start(), calls=%async_computation.4 | async-start | bytes 7864320 | tf_op jit(solution)/shard_map/psum | solution.py:138
  18.3 160.0 %copy-start.85 = (f32[384]{0:T(512)}, f32[384]{0:T(512)S(1)}, u32[]{:S(2)}) copy-start(f32[384]{0:T(512)S(1)} %fusion.104) | copy-start | bytes 4612
  18.3 182.4 %copy-start.79 = (f32[1280]{0:T(1024)}, f32[1280]{0:T(1024)S(1)}, u32[]{:S(2)}) copy-start(f32[1280]{0:T(1024)S(1)} %broadcast_multiply_fusion) | copy-start | bytes 15364
  18.4 159.9 %copy-start.63 = (f32[2560]{0:T(1024)}, f32[2560]{0:T(1024)S(1)}, u32[]{:S(2)}) copy-start(f32[2560]{0:T(1024)S(1)} %get-tuple-element.336) | copy-start | bytes 30724
  18.5 164.8 %copy-start.71 = (f32[1280]{0:T(1024)}, f32[1280]{0:T(1024)S(1)}, u32[]{:S(2)}) copy-start(f32[1280]{0:T(1024)S(1)} %get-tuple-element.337) | copy-start | bytes 15364
  18.5 164.8 %copy-start.73 = (f32[1280]{0:T(1024)}, f32[1280]{0:T(1024)S(1)}, u32[]{:S(2)}) copy-start(f32[1280]{0:T(1024)S(1)} %get-tuple-element.338) | copy-start | bytes 15364
  18.5 164.8 %copy-start.75 = (f32[1280]{0:T(1024)}, f32[1280]{0:T(1024)S(1)}, u32[]{:S(2)}) copy-start(f32[1280]{0:T(1024)S(1)} %get-tuple-element.339) | copy-start | bytes 15364
  18.5 164.8 %copy-start.77 = (f32[1280]{0:T(1024)}, f32[1280]{0:T(1024)S(1)}, u32[]{:S(2)}) copy-start(f32[1280]{0:T(1024)S(1)} %get-tuple-element.340) | copy-start | bytes 15364
  19.3 164.0 %copy-start.93 = (f32[384]{0:T(512)}, f32[384]{0:T(512)S(1)}, u32[]{:S(2)}) copy-start(f32[384]{0:T(512)S(1)} %get-tuple-element.481) | copy-start | bytes 4612
  19.3 164.0 %copy-start.114 = (f32[384]{0:T(512)}, f32[384]{0:T(512)S(1)}, u32[]{:S(2)}) copy-start(f32[384]{0:T(512)S(1)} %get-tuple-element.482) | copy-start | bytes 4612
  19.3 164.0 %copy-start.116 = (f32[384]{0:T(512)}, f32[384]{0:T(512)S(1)}, u32[]{:S(2)}) copy-start(f32[384]{0:T(512)S(1)} %get-tuple-element.483) | copy-start | bytes 4612
  19.3 164.0 %copy-start.118 = (f32[384]{0:T(512)}, f32[384]{0:T(512)S(1)}, u32[]{:S(2)}) copy-start(f32[384]{0:T(512)S(1)} %get-tuple-element.485) | copy-start | bytes 4612
  19.3 181.4 %copy-start.126 = (pred[384]{0:T(512)(128)(4,1)}, pred[384]{0:T(512)(128)(4,1)S(1)}, u32[]{:S(2)}) copy-start(pred[384]{0:T(512)(128)(4,1)S(1)} %get-tuple-element.484) | copy-start | bytes 1156
  178.3 5.0 collective-permute-start
  323.1 17.5 copy-start.70
  323.1 17.5 copy-start.65
  323.1 17.5 copy-start.66
  323.1 18.9 copy-start.69
  351.3 15.6 copy-start.110
  377.1 7.3 copy-start.104
  381.0 10.1 copy-start.60
  434.3 45.0 copy-start.96
  539.6 431.3 %all-gather.13.cloned.1.call-start = ((), (), s32[]{:S(2)}) async-start(), calls=%async_computation.5 | async-start | bytes 41779200 | tf_op jit(solution)/shard_map/all_gather | solution.py:76
  540.2 649.9 %all-gather.15.cloned.1.call-start = ((), (), s32[]{:S(2)}) async-start(), calls=%async_computation.6 | async-start | bytes 20889600 | tf_op jit(solution)/shard_map/all_gather | solution.py:77
  540.8 743.4 %all-reduce.81.cloned.1.call-start = ((), (), s32[]{:S(2)}) async-start(), calls=%async_computation.7 | async-start | bytes 7864320 | tf_op jit(solution)/shard_map/psum | solution.py:166
  562.5 408.5 %copy-start.128 = (f32[2,3840]{1,0:T(2,128)S(1)}, f32[2,3840]{1,0:T(2,128)}, u32[]{:S(2)}) copy-start(f32[2,3840]{1,0:T(2,128)} %param.35) | copy-start | bytes 92164
  971.0 219.2 %copy-start.33 = (bf16[384,2560]{1,0:T(8,128)(2,1)S(1)}, bf16[384,2560]{1,0:T(8,128)(2,1)}, u32[]{:S(2)}) copy-start(bf16[384,2560]{1,0:T(8,128)(2,1)} %param.22) | copy-start | bytes 5898244
  1233.0 667.6 %all-reduce.89.cloned.1.call-start = ((), (), s32[]{:S(2)}) async-start(), calls=%async_computation.13 | async-start | bytes 7864320 | tf_op jit(solution)/shard_map/psum | solution.py:150
  1293.7 9.0 copy-start.7
  1427.4 15.6 copy-start.109
  1453.3 7.4 copy-start.100
  1457.3 10.2 copy-start.61
  1534.1 91.2 %copy-start.14 = (bf16[384,1280]{1,0:T(8,128)(2,1)S(1)}, bf16[384,1280]{1,0:T(8,128)(2,1)}, u32[]{:S(2)}) copy-start(bf16[384,1280]{1,0:T(8,128)(2,1)} %add_convert_fusion) | copy-start | bytes 2949124
  1534.1 91.2 %copy-start.80 = (f32[1280]{0:T(1024)S(1)}, f32[1280]{0:T(1024)}, u32[]{:S(2)}) copy-start(f32[1280]{0:T(1024)} %copy-done.79) | copy-start | bytes 15364
  1534.1 91.2 %copy-start.111 = (f32[1,1280]{1,0:T(1,128)S(1)}, f32[1,1280]{1,0:T(1,128)}, u32[]{:S(2)}) copy-start(f32[1,1280]{1,0:T(1,128)} %broadcast_in_dim.27) | copy-start | bytes 15364
  1534.1 91.2 %copy-start.127 = (pred[384]{0:T(512)(128)(4,1)S(1)}, pred[384]{0:T(512)(128)(4,1)}, u32[]{:S(2)}) copy-start(pred[384]{0:T(512)(128)(4,1)} %copy-done.126) | copy-start | bytes 1156
  1625.3 8.0 copy-start.88
  1625.3 8.7 copy-start.4
  1651.6 14.7 collective-permute-start.2
  1652.9 13.4 copy-start.72
  1652.9 13.4 copy-start.74
  1652.9 13.4 copy-start.76
  1652.9 13.4 copy-start.78
  1652.9 13.4 copy-start.123
  1652.9 13.4 copy-start.124
  1652.9 13.4 copy-start.125
  1669.0 10.2 copy-start.22
  1679.3 804.6 %all-reduce.87.cloned.1.call-start = ((), (), s32[]{:S(2)}) async-start(), calls=%async_computation.12 | async-start | bytes 57671680
  1743.0 2747.1 %all-reduce.83.cloned.1.call-start = ((), (), s32[]{:S(2)}) async-start(), calls=%async_computation.10 | async-start | bytes 157286400
  1892.7 2711.9 %all-reduce.85.cloned.1.call-start = ((), (), s32[]{:S(2)}) async-start(), calls=%async_computation.11 | async-start | bytes 258048 | tf_op jit(solution)/shard_map/psum | solution.py:243
  1904.5 2974.8 %reduce-scatter.3.cloned.1.call-start = ((), (), s32[]{:S(2)}) async-start(), calls=%async_computation.8 | async-start | bytes 13926400 | tf_op jit(solution)/shard_map/reduce_scatter | solution.py:238
  1914.0 3536.0 %reduce-scatter.5.cloned.1.call-start = ((), (), s32[]{:S(2)}) async-start(), calls=%async_computation.9 | async-start | bytes 41779200 | tf_op jit(solution)/shard_map/reduce_scatter | solution.py:240
  4494.2 966.4 %copy-start.1 = (bf16[2,5,256,256]{3,2,1,0:T(8,128)(2,1)S(1)}, bf16[2,5,256,256]{3,2,1,0:T(8,128)(2,1)}, u32[]{:S(2)}) copy-start(bf16[2,5,256,256]{3,2,1,0:T(8,128)(2,1)} %param.31) | copy-start | bytes 3932164
  (83 other events, 290.3 us)
Sparse Core Ops, SparseCore 0:
  10.8 158.9 all-gather.8
  172.5 94.2 all-gather.10
  539.7 22.6 all-reduce.78
  565.0 405.9 all-gather.12
  973.6 216.4 all-gather.14
  1233.1 23.0 all-reduce.80
  1679.4 24.7 all-reduce.88
  1743.2 740.6 all-reduce.86
  2490.3 1999.7 all-reduce.82
  4497.5 107.0 all-reduce.84
  4607.5 271.7 reduce-scatter.2
  4885.8 564.1 reduce-scatter.4
where the time goes:
time: 5490 us; the launch traced here: 5470 us
  waiting for transfers between devices  4270 us (78%)
  local copies, waits for them, and re-layouts  627 us (11%)
  matrix products  204 us (4%)
  other arithmetic  192 us (3%)
  blocking collectives  148 us (3%)
    unnamed x14, waiting for transfers between devices  2540 us
    reduce_scatter x1, waiting for transfers between devices, per_device(): lax.psum_scatter(grad_ffw_out, 'dp', scatter_dimension=1, tiled=True)  571 us
    all_gather x1, waiting for transfers between devices, per_device(): lax.all_gather(ffw_in, 'dp', axis=1, tiled=True)  404 us
    reduce_scatter x1, waiting for transfers between devices, per_device(): lax.psum_scatter(grad_out_weight, 'dp', scatter_dimension=1, tiled=True)  275 us
    all_gather x1, waiting for transfers between devices, per_device(): lax.all_gather(ffw_out, 'dp', axis=1, tiled=True)  194 us
    all_gather x1, waiting for transfers between devices, per_device(): lax.all_gather(branch_weight, 'dp', axis=1, tiled=True)  151 us
    all_gather x4, blocking collectives, entering_2(): everything = jax.tree.map(lambda part: lax.all_gather(part, axis), x)  148 us
    slice x61, local copies, waits for them, and re-layouts, per_device(): lax.associative_scan(pair_combine, (alpha_next, delta_states), reverse=Tr...  147 us
  transfers between devices with their start and end apart: 16, of which 10 were waited for; matrix products, arithmetic and copies ran while one was open for 12% of the time, Pallas kernels for 0%

commit v1 on v0

v1 whole, which is shorter than its diff:
```python
import functools

import jax
import jax.numpy as jnp
from jax import lax
from jax.experimental import pallas as pl
from jax.experimental.pallas import tpu as pltpu
from jax.sharding import Mesh
from jax.sharding import PartitionSpec as P

INNER = 4
DP = ("o", "i")
EPS = 1e-06
F32 = jnp.float32
BF16 = jnp.bfloat16


def swap(value):
    return lax.ppermute(value, "tensor", [(0, 1), (1, 0)])


def ring(value):
    count = lax.axis_size("o")
    return lax.ppermute(value, "o", [(k, (k + 1) % count) for k in range(count)])


def from_behind(value, steps):
    count = lax.axis_size(DP)
    first, last = max(0, -steps), min(count, count - steps)
    return lax.ppermute(value, DP, [(k, k + steps) for k in range(first, last)])


def sum_over_all(value):
    count, bit = lax.axis_size(DP), 1
    while bit < count:
        value = value + lax.ppermute(value, DP, [(k, k ^ bit) for k in range(count)])
        bit *= 2
    return value


def half_of(value, which):
    rows = value.shape[0] // 2
    return lax.dynamic_slice_in_dim(value, which * rows, rows, 0)


def join_halves(own, other, core):
    first = jnp.where(core == 0, own, other)
    second = jnp.where(core == 0, other, own)
    return jnp.concatenate([first, second], axis=0)


def scan_kernel(reverse, keep_ref, drive_ref, cum_ref, state_ref):
    rows, width = keep_ref.shape
    groups = rows // 8
    place = lax.broadcasted_iota(jnp.int32, (8, width), 0)

    def step(k, carried):
        before_a, before_b = carried
        group = groups - 1 - k if reverse else k
        at = pl.ds(pl.multiple_of(group * 8, 8), 8)
        a, b = keep_ref[at, :], drive_ref[at, :]
        for d in (1, 2, 4):
            far_a = pltpu.roll(a, 8 - d if reverse else d, 0)
            far_b = pltpu.roll(b, 8 - d if reverse else d, 0)
            inside = place < 8 - d if reverse else place >= d
            b = jnp.where(inside, a * far_b + b, b)
            a = jnp.where(inside, a * far_a, a)
        b = a * before_b + b
        a = a * before_a
        cum_ref[at, :] = a
        state_ref[at, :] = b
        edge = slice(0, 1) if reverse else slice(7, 8)
        return (a[edge], b[edge])

    lax.fori_loop(
        0, groups, step, (jnp.ones((1, width), F32), jnp.zeros((1, width), F32))
    )


def local_scan(keep, drive, reverse):
    rows, width = keep.shape
    block = 256
    spec = pl.BlockSpec((rows, block), lambda j: (0, j))
    shape = jax.ShapeDtypeStruct((rows, width), F32)
    return pl.pallas_call(
        functools.partial(scan_kernel, reverse),
        grid=(width // block,),
        in_specs=[spec, spec],
        out_specs=[spec, spec],
        out_shape=[shape, shape],
        cost_estimate=pl.CostEstimate(
            flops=20 * rows * width, bytes_accessed=16 * rows * width, transcendentals=0
        ),
    )(keep, drive)


def entering(decay, state, reverse):
    count, index = lax.axis_size(DP), lax.axis_index(DP)
    every = lax.all_gather(jnp.stack([decay, state]), DP)
    carried = jnp.zeros_like(state)
    for k in range(count):
        at = count - 1 - k if reverse else k
        reached = at > index if reverse else at < index
        carried = jnp.where(reached, every[at, 0] * carried + every[at, 1], carried)
    return carried


def gelu_tanh(values):
    return jax.nn.gelu(values, approximate=True)


def geglu(gate_vals, up_vals):
    return gelu_tanh(gate_vals) * up_vals


def lru_inputs(gate_decay, gate_input, conv_in, decay_in, resets):
    log_decay = -8.0 * jax.nn.sigmoid(gate_decay) * jax.nn.softplus(decay_in)
    decay = jnp.exp(log_decay)
    multiplier = jnp.sqrt(jnp.maximum(-jnp.expm1(2.0 * log_decay), 0.001))
    multiplier = jnp.where(resets, 1.0, multiplier)
    keep_rate = jnp.where(resets, 0.0, decay)
    return (keep_rate, conv_in * jax.nn.sigmoid(gate_input) * multiplier)


def norm_back(values, scaling, delta):
    inverse = lax.rsqrt(jnp.mean(values * values, axis=-1, keepdims=True) + EPS)
    unit = values * inverse
    scaled = delta * (1.0 + scaling)
    moved = inverse * (scaled - unit * jnp.mean(scaled * unit, axis=-1, keepdims=True))
    return moved, jnp.sum(delta * unit, axis=0)


def rms_norm(values, scaling):
    inverse = lax.rsqrt(jnp.mean(values * values, axis=-1, keepdims=True) + EPS)
    return values * inverse * (1.0 + scaling)


def dot(a, b, contract):
    return lax.dot_general(a, b, ((contract[0], contract[1]), ((), ())), preferred_element_type=F32)


def mm(a, b):
    return dot(a, b, ((1,), (0,)))


def mm_nt(a, b):
    return dot(a, b, ((1,), (1,)))


def mm_tn(a, b):
    return dot(a, b, ((0,), (0,)))


def gather_slots(half):
    slots = []
    for k in range(lax.axis_size("o")):
        half = ring(half) if k else half
        slots.append(jnp.concatenate([half, swap(half)], axis=0))
    return slots


def reduce_slots(parts):
    count = len(parts)
    rows = parts[0].shape[0] // 2

    def both(part):
        return part[:rows] + swap(part[rows:].astype(BF16)).astype(F32)

    if count == 1:
        return both(parts[0])
    total = both(parts[1])
    for k in range(1, count):
        total = both(parts[(k + 1) % count]) + ring(total.astype(BF16)).astype(F32)
    return total


def spread(value, axis):
    return lax.all_to_all(value, "o", axis, axis, tiled=True)


def per_device(
    inputs,
    segment_ids,
    cotangent,
    branch_weight,
    out_weight,
    ffw_in,
    ffw_out,
    norm_scales,
    branch_bias,
    conv_weight,
    conv_bias,
    gate_weights,
    gate_bias,
    decay_param,
    out_bias,
    ffw_bias,
):
    outer, inner = lax.axis_size("o"), lax.axis_size("i")
    count = outer * inner
    core, along = lax.axis_index("tensor"), lax.axis_index("o")
    tok_rows, width = inputs.shape
    part_width = width // count
    hidden_half = ffw_out.shape[0]
    hidden_part = hidden_half // outer
    taps_count = conv_weight.shape[0]
    rim_rows = taps_count - 1
    heads_half, block_size = gate_weights.shape[1], gate_weights.shape[2]
    width_half = heads_half * block_size

    branch_x_full = lax.all_gather(branch_weight[0], DP, axis=0, tiled=True)
    branch_y_full = lax.all_gather(branch_weight[1], DP, axis=0, tiled=True)
    out_full_t = lax.all_gather(out_weight.T, DP, axis=0, tiled=True)
    in_parts = (
        ffw_in.reshape(2, part_width, outer, hidden_part)
        .transpose(2, 1, 0, 3)
        .reshape(outer, part_width, 2 * hidden_part)
    )
    out_parts = ffw_out.reshape(outer, hidden_part, part_width).transpose(0, 2, 1)
    ffw_in_full = lax.all_gather(spread(in_parts, 0), "i", axis=1, tiled=True).reshape(
        width, 2 * hidden_part
    )
    ffw_out_full_t = lax.all_gather(spread(out_parts, 0), "i", axis=1, tiled=True).reshape(
        width, hidden_part
    )
    cot_slots = gather_slots(half_of(cotangent, core))

    seg_marks = (segment_ids + 1).astype(F32)
    source_half = half_of(inputs, core).astype(F32)
    normed_low = rms_norm(inputs.astype(F32), norm_scales[0]).astype(BF16)
    branch_x = mm(normed_low, branch_x_full) + branch_bias[0]
    branch_y = mm(normed_low, branch_y_full) + branch_bias[1]
    rim_values, rim_marks = from_behind(
        (branch_x[tok_rows - rim_rows :], seg_marks[tok_rows - rim_rows :]), 1
    )
    padded_branch = jnp.concatenate([rim_values, branch_x], axis=0)
    padded_marks = jnp.concatenate([rim_marks, seg_marks], axis=0)
    resets = (seg_marks != padded_marks[rim_rows - 1 : rim_rows - 1 + tok_rows])[:, None]
    conv_out = jnp.zeros_like(branch_x) + conv_bias
    shifted_rows = []
    for offset in range(taps_count):
        matches = (
            padded_marks[rim_rows - offset : rim_rows - offset + tok_rows] == seg_marks
        ).astype(F32)[:, None]
        shifted = padded_branch[rim_rows - offset : rim_rows - offset + tok_rows] * matches
        shifted_rows.append(shifted)
        conv_out = conv_out + conv_weight[offset] * shifted
    conv_low = conv_out.astype(BF16)
    conv_float = conv_low.astype(F32)
    conv_blocks = conv_low.reshape(tok_rows, heads_half, block_size)
    gate_pre = (
        jnp.einsum(
            "thb,ghbc->gthc", conv_blocks, gate_weights, preferred_element_type=F32
        ).reshape(2, tok_rows, width_half)
        + gate_bias[:, None, :]
    )

    def lru_local(gate_decay, gate_input, conv_in, decay_in):
        return lru_inputs(gate_decay, gate_input, conv_in, decay_in, resets)

    (keep_rate, drive_in), lru_back = jax.vjp(
        lru_local, gate_pre[0], gate_pre[1], conv_float, decay_param
    )
    cumulative, local_state = local_scan(keep_rate, drive_in, False)
    carry_in = entering(cumulative[tok_rows - 1], local_state[tok_rows - 1], False)
    states = local_state + cumulative * carry_in
    branch_act, gelu_back = jax.vjp(gelu_tanh, branch_y)
    mixed_in = (states * branch_act).astype(BF16)
    mixed_part = mm_nt(mixed_in, out_full_t)
    residual = (
        source_half
        + half_of(mixed_part, core)
        + swap(half_of(mixed_part, 1 - core))
        + out_bias[0]
    )

    normed_slots = gather_slots(rms_norm(residual, norm_scales[1]).astype(BF16))
    bias_part = lax.dynamic_slice_in_dim(ffw_bias, along * hidden_part, hidden_part, 1)
    bias_row = bias_part.reshape(2 * hidden_part)
    hidden_slots, delta_slots, result_parts, delta_parts = [], [], [], []
    for normed_two, cot in zip(normed_slots, cot_slots):
        gate_up = mm(normed_two, ffw_in_full) + bias_row
        hidden, hidden_back = jax.vjp(geglu, gate_up[:, :hidden_part], gate_up[:, hidden_part:])
        hidden_low = hidden.astype(BF16)
        delta_gate_up = jnp.concatenate(hidden_back(mm(cot, ffw_out_full_t)), axis=1).astype(BF16)
        hidden_slots.append(hidden_low)
        delta_slots.append(delta_gate_up)
        delta_parts.append(mm_nt(delta_gate_up, ffw_in_full))
    delta_normed_two = reduce_slots(delta_parts)
    for hidden_low in hidden_slots:
        result_parts.append(mm_nt(hidden_low, ffw_out_full_t))
    normed_all, cot_all = jnp.concatenate(normed_slots), jnp.concatenate(cot_slots)
    hidden_all, delta_all = jnp.concatenate(hidden_slots), jnp.concatenate(delta_slots)

    def sum_inner(grad):
        rows = grad.reshape(outer, inner, part_width, -1).transpose(1, 0, 2, 3)
        own = lax.psum_scatter(
            rows.reshape(width, -1).astype(BF16), "i", scatter_dimension=0, tiled=True
        )
        return spread(own.reshape(outer, part_width, -1), 0)

    grad_ffw_out_t = sum_inner(mm_tn(cot_all, hidden_all))
    ffw_out_grad = (
        grad_ffw_out_t.transpose(0, 2, 1).reshape(hidden_half, part_width).astype(F32)
    )
    grad_ffw_in = sum_inner(mm_tn(normed_all, delta_all)).reshape(
        outer, part_width, 2, hidden_part
    )
    ffw_in_grad = (
        grad_ffw_in.transpose(2, 1, 0, 3).reshape(2, part_width, hidden_half).astype(F32)
    )
    bias_sum = jnp.sum(delta_all, axis=0, dtype=F32).reshape(2, hidden_part)
    grad_ffw_bias = lax.dynamic_update_slice_in_dim(
        jnp.zeros((2, hidden_half), F32), bias_sum, along * hidden_part, 1
    )
    result_half = residual + reduce_slots(result_parts) + out_bias[1]
    result = join_halves(result_half, swap(result_half), core)

    cot_half = half_of(cotangent, core).astype(F32)
    delta_res_norm, grad_scale_two = norm_back(residual, norm_scales[1], delta_normed_two)
    delta_residual = cot_half + delta_res_norm
    delta_half = delta_residual.astype(BF16)
    delta_mixed = join_halves(delta_half, swap(delta_half), core)
    delta_mixed_in = mm(delta_mixed, out_full_t)
    grad_out_t = lax.psum_scatter(
        mm_tn(delta_mixed, mixed_in).astype(BF16), DP, scatter_dimension=0, tiled=True
    )
    delta_states = delta_mixed_in * branch_act
    (delta_branch_y,) = gelu_back(delta_mixed_in * states)
    delta_y_low = delta_branch_y.astype(BF16)
    grad_branch_y = lax.psum_scatter(
        mm_tn(normed_low, delta_y_low).astype(BF16), DP, scatter_dimension=0, tiled=True
    )
    alpha_next = jnp.concatenate([keep_rate[1:], jnp.ones((1, width_half), F32)], axis=0)
    suffix, local_adjoint = local_scan(alpha_next, delta_states, True)
    leaving = entering(keep_rate[0] * suffix[0], keep_rate[0] * local_adjoint[0], True)
    adjoint = local_adjoint + suffix * leaving
    states_before = jnp.concatenate([carry_in[None, :], states[: tok_rows - 1]], axis=0)
    delta_gate_decay, delta_gate_input, delta_conv_direct, grad_decay = lru_back(
        (adjoint * states_before, adjoint)
    )
    delta_gates = jnp.stack([delta_gate_decay, delta_gate_input]).astype(BF16)
    delta_blocks = delta_gates.reshape(2, tok_rows, heads_half, block_size)
    grad_gate_weights = jnp.einsum(
        "thb,gthc->ghbc", conv_blocks, delta_blocks, preferred_element_type=F32
    )
    gate_rows = (
        grad_gate_weights.reshape(2, heads_half, count, block_size // count, block_size)
        .transpose(2, 0, 1, 3, 4)
        .reshape(2 * heads_half * block_size, block_size)
        .astype(BF16)
    )
    gate_grad = lax.psum_scatter(gate_rows, DP, scatter_dimension=0, tiled=True)
    gate_grad = gate_grad.reshape(2, heads_half, block_size // count, block_size).astype(F32)
    grad_gate_bias = jnp.sum(delta_gates, axis=1, dtype=F32)
    delta_conv = delta_conv_direct + jnp.einsum(
        "gthc,ghbc->thb", delta_blocks, gate_weights, preferred_element_type=F32
    ).reshape(tok_rows, width_half)
    rim_delta, rim_next_marks = from_behind((delta_conv[:rim_rows], seg_marks[:rim_rows]), -1)
    padded_delta = jnp.concatenate([delta_conv, rim_delta], axis=0)
    next_marks = jnp.concatenate([seg_marks, rim_next_marks], axis=0)
    delta_branch_x = jnp.zeros_like(delta_conv)
    conv_weight_rows = []
    for offset in range(taps_count):
        matches = (next_marks[offset : offset + tok_rows] == seg_marks).astype(F32)[:, None]
        delta_branch_x = (
            delta_branch_x
            + conv_weight[offset] * padded_delta[offset : offset + tok_rows] * matches
        )
        conv_weight_rows.append(jnp.sum(delta_conv * shifted_rows[offset], axis=0))
    grad_conv_bias = jnp.sum(delta_conv, axis=0)
    delta_x_low = delta_branch_x.astype(BF16)
    grad_branch_x = lax.psum_scatter(
        mm_tn(normed_low, delta_x_low).astype(BF16), DP, scatter_dimension=0, tiled=True
    )
    delta_part = mm_nt(delta_x_low, branch_x_full) + mm_nt(delta_y_low, branch_y_full)
    delta_normed = half_of(delta_part, core) + swap(
        half_of(delta_part, 1 - core).astype(BF16)
    ).astype(F32)
    delta_source_norm, grad_scale_one = norm_back(source_half, norm_scales[0], delta_normed)
    grad_half = delta_residual + delta_source_norm
    input_grad = join_halves(grad_half, swap(grad_half), core)

    halves = jnp.stack(
        [
            grad_scale_one,
            grad_scale_two,
            jnp.sum(delta_half, axis=0, dtype=F32),
            jnp.sum(cot_half, axis=0),
        ]
    )
    halves = halves + swap(halves)
    flat = [
        halves.reshape(-1),
        jnp.sum(delta_x_low, axis=0, dtype=F32),
        jnp.sum(delta_y_low, axis=0, dtype=F32),
        *conv_weight_rows,
        grad_conv_bias,
        grad_gate_bias.reshape(-1),
        grad_decay,
        grad_ffw_bias.reshape(-1),
    ]
    small = sum_over_all(jnp.concatenate(flat).reshape(-1, 128)).reshape(-1)
    at = 0
    taken = []
    for shape in (
        (2, width),
        (2, width),
        (2, width_half),
        (taps_count, width_half),
        (width_half,),
        (2, width_half),
        (width_half,),
        (2, hidden_half),
    ):
        size = 1
        for n in shape:
            size *= n
        taken.append(small[at : at + size].reshape(shape))
        at += size
    scales, out_bias_grad, branch_bias_grad, taps_grad, conv_bias_grad, gate_bias_grad, decay_grad, ffw_bias_grad = taken
    return (
        result,
        input_grad,
        jnp.stack([grad_branch_x, grad_branch_y]).astype(F32),
        grad_out_t.T.astype(F32),
        ffw_in_grad,
        ffw_out_grad,
        scales,
        branch_bias_grad,
        taps_grad,
        conv_bias_grad,
        gate_grad,
        gate_bias_grad,
        decay_grad,
        out_bias_grad,
        ffw_bias_grad,
    )


def solution(mesh):
    count = mesh.shape["dp"]
    grid = Mesh(
        mesh.devices.reshape(count // INNER, INNER, mesh.shape["tensor"]), ("o", "i", "tensor")
    )
    in_specs = (
        P(DP, None),
        P(DP),
        P(DP, None),
        P(None, DP, "tensor"),
        P("tensor", DP),
        P(None, DP, "tensor"),
        P("tensor", DP),
        P(),
        P(None, "tensor"),
        P(None, "tensor"),
        P("tensor"),
        P(None, "tensor", None, None),
        P(None, "tensor"),
        P("tensor"),
        P(),
        P(None, "tensor"),
    )
    out_specs = (
        P(DP, None),
        P(DP, None),
        P(None, DP, "tensor"),
        P("tensor", DP),
        P(None, DP, "tensor"),
        P("tensor", DP),
        P(),
        P(None, "tensor"),
        P(None, "tensor"),
        P("tensor"),
        P(None, "tensor", DP, None),
        P(None, "tensor"),
        P("tensor"),
        P(),
        P(None, "tensor"),
    )
    return jax.shard_map(
        per_device, mesh=grid, in_specs=in_specs, out_specs=out_specs, check_vma=False
    )
```

time: 5490 us -> 1490 us (0.27)
  waiting for transfers between devices: 4270 us -> 804 us
  local copies, waits for them, and re-layouts: 627 us -> 183 us
  other arithmetic: 192 us -> 77.3 us
    unnamed x14 -> x11, waiting for transfers between devices: 2540 us -> 1.52 us
    all_gather x4 -> x5, waiting for transfers between devices: 749 us -> 80.4 us  [the longest x1 80.4 us: per_device(): out_full_t = lax.all_gather(out_weight.T, DP, axis=0, tiled=True)]
    reduce_scatter x2 -> x6, waiting for transfers between devices: 845 us -> 298 us  [the longest x1 153 us: per_device(): lax.psum_scatter(mm_tn(normed_low, delta_y_low).astype(BF16), DP, scatter...]
    ppermute x4 -> x42, waiting for transfers between devices: 1.14 us -> 318 us  [the longest x12 225 us: ring(): lax.ppermute(value, 'o', [(k, (k + 1) % count) for k in range(count)])]
    slice x118 -> x19, local copies, waits for them, and re-layouts: 260 us -> 7.24 us  [the longest x1 2.15 us: per_device(): branch_x_full = lax.all_gather(branch_weight[0], DP, axis=0, tiled=True)]
    transpose x3 -> x1, local copies, waits for them, and re-layouts: 159 us -> 0.39 us  [per_device(): ffw_out.reshape(outer, hidden_part, part_width).transpose(0, 2, 1)]
    psum x4 -> x0, waiting for transfers between devices: 129 us -> none  [the longest x1 108 us: per_device(): lax.psum((jnp.stack([grad_scale_one, grad_scale_two]), grad_branch_bias,...]
    pad x60 -> x0, local copies, waits for them, and re-layouts: 126 us -> none  [the longest x30 64.7 us: per_device(): lax.associative_scan(pair_combine, (keep_rate, drive_in), axis=0)]
  transfers between devices with their start and end apart: 16 -> 56, of which waited for: 10 -> 25; matrix products, arithmetic and copies ran while one was open for 12% -> 25% of each run, Pallas kernels for 0% -> 1%
where the time goes in v1:
time: 1490 us; the launch traced here: 1480 us
  waiting for transfers between devices  804 us (54%)
  matrix products  191 us (13%)
  local copies, waits for them, and re-layouts  183 us (12%)
  blocking collectives  140 us (9%)
  other arithmetic  77.3 us (5%)
  starting transfers between devices  53.8 us (4%)
  between operations  16 us (1%)
    ppermute x12, waiting for transfers between devices, ring(): lax.ppermute(value, 'o', [(k, (k + 1) % count) for k in range(count)])  225 us
    dot_general x27, matrix products, dot(): lax.dot_general(a, b, ((contract[0], contract[1]), ((), ())), preferred_e...  185 us
    reduce_scatter x1, waiting for transfers between devices, per_device(): lax.psum_scatter(mm_tn(normed_low, delta_y_low).astype(BF16), DP, scatter...  153 us
    reduce_scatter x1, waiting for transfers between devices, per_device(): lax.psum_scatter(mm_tn(normed_low, delta_x_low).astype(BF16), DP, scatter...  145 us
    all_to_all x3, waiting for transfers between devices, spread(): return lax.all_to_all(value, 'o', axis, axis, tiled=True)  106 us
    ppermute x4, waiting for transfers between devices, sum_over_all(): lax.ppermute(value, DP, [(k, k ^ bit) for k in range(count)])  85.6 us
    all_gather x2, blocking collectives, entering(): every = lax.all_gather(jnp.stack([decay, state]), DP)  80.8 us
    all_gather x1, waiting for transfers between devices, per_device(): out_full_t = lax.all_gather(out_weight.T, DP, axis=0, tiled=True)  80.4 us
  transfers between devices with their start and end apart: 56, of which 25 were waited for; matrix products, arithmetic and copies ran while one was open for 25% of the time, Pallas kernels for 1%

profile of v1, /device:TPU:0, one launch (start us, length us, event | category | flops | bytes accessed | tf_op | source)
XLA Modules:
  0.0 1479.4 jit_solution(6619146317876733268)
XLA Ops:
  15.1 58.7 %all_to_all.20 = bf16[4,160,960]{2,1,0:T(8,128)(2,1)S(1)} all-to-all(bf16[4,160,960]{2,1,0:T(8,128)(2,1)S(1)} %copy.133), channel_id=1, replica_groups=mesh['o'=4,'i'=4,'tensor'=2] {'o'}, dimensions={0} | all-to-all | bytes 2457600 | tf_op jit(solution)/shard_map/all_to_all | solution.py:178
  75.8 7.2 reshape.794
  83.0 6.6 copy.173
  89.6 7.0 reshape.795
  96.7 4.8 all-to-all-start
  102.8 4.5 collective-permute-start
  108.2 75.4 %all-to-all-done = bf16[4,160,1920]{2,1,0:T(8,128)(2,1)} async-done(((bf16[4,160,1920]{2,1,0:T(8,128)(2,1)}), bf16[4,160,1920]{2,1,0:T(8,128)(2,1)}, u32[]{:S(2)}, u32[]{:S(2)}) %all-to-all-start) | async-done | bytes 2457632 | tf_op jit(solution)/shard_map/all_to_all | solution.py:178
  184.7 5.6 fusion.21
  201.8 5.5 copy.131
  214.0 7.3 shard_map.271
  222.9 42.6 %all-gather.4 = f32[16,2,1280]{2,1,0:T(2,128)S(1)} all-gather(f32[1,2,1280]{2,1,0:T(2,128)S(1)} %maximum_bitcast_fusion), channel_id=3, replica_groups=mesh['o'=4,'i'=4,'tensor'=2] {'o','i'}, dimensions={0}, use_global_device_ids=true | all-gather | bytes 174080 | tf_op jit(solution)/shard_map/all_gather | solution.py:99
  266.5 8.8 multiply_convert_fusion.1
  275.3 80.4 %all-gather.12.cloned.1.call-done = bf16[2560,1280]{1,0:T(8,128)(2,1)} async-done(((bf16[160,1280]{1,0:T(8,128)(2,1)}), bf16[2560,1280]{1,0:T(8,128)(2,1)}) %all-gather.12.cloned.1.call-update) | async-done | bytes 6553616 | tf_op jit(solution)/shard_map/all_gather | solution.py:213
  355.7 5.2 fusion.194
  374.5 18.8 %collective-permute-done.20 = bf16[192,2560]{1,0:T(8,128)(2,1)} collective-permute-done((bf16[192,2560]{1,0:T(8,128)(2,1)}, bf16[192,2560]{1,0:T(8,128)(2,1)}, u32[]{:S(2)}, u32[]{:S(2)}) %collective-permute-start.20) | collective-permute-done | bytes 983072 | tf_op jit(solution)/shard_map/ppermute | solution.py:24
  393.3 21.0 %collective-permute-done.5 = bf16[192,2560]{1,0:T(8,128)(2,1)S(1)} collective-permute-done((bf16[192,2560]{1,0:T(8,128)(2,1)S(1)}, bf16[192,2560]{1,0:T(8,128)(2,1)S(1)}, u32[]{:S(2)}, u32[]{:S(2)}) %collective-permute-start.5) | collective-permute-done | bytes 983072 | tf_op jit(solution)/shard_map/ppermute | solution.py:24
  417.4 18.1 %collective-permute-done.21 = bf16[192,2560]{1,0:T(8,128)(2,1)} collective-permute-done((bf16[192,2560]{1,0:T(8,128)(2,1)}, bf16[192,2560]{1,0:T(8,128)(2,1)}, u32[]{:S(2)}, u32[]{:S(2)}) %collective-permute-start.21) | collective-permute-done | bytes 983072 | tf_op jit(solution)/shard_map/ppermute | solution.py:24
  437.7 18.8 %collective-permute-done.6 = bf16[192,2560]{1,0:T(8,128)(2,1)} collective-permute-done((bf16[192,2560]{1,0:T(8,128)(2,1)S(1)}, bf16[192,2560]{1,0:T(8,128)(2,1)}, u32[]{:S(2)}, u32[]{:S(2)}) %collective-permute-start.6) | collective-permute-done | bytes 983072 | tf_op jit(solution)/shard_map/ppermute | solution.py:24
  456.5 8.4 collective-permute-start.7
  468.5 9.0 collective-permute-done.22
  480.1 18.0 %collective-permute-done.7 = bf16[192,2560]{1,0:T(8,128)(2,1)} collective-permute-done((bf16[192,2560]{1,0:T(8,128)(2,1)}, bf16[192,2560]{1,0:T(8,128)(2,1)}, u32[]{:S(2)}, u32[]{:S(2)}) %collective-permute-start.7) | collective-permute-done | bytes 983072 | tf_op jit(solution)/shard_map/ppermute | solution.py:24
  502.4 12.4 copy.135
  514.8 5.4 copy.167
  521.2 10.4 convolution_add_fusion.2
  531.6 6.0 convolution_add_fusion.1
  537.6 5.7 convolution_add_fusion
  543.3 6.7 fusion.133
  550.0 5.7 fusion.140
  555.7 5.7 fusion.147
  561.5 5.8 convolution_add_fusion.3
  567.3 5.7 fusion.126
  573.9 12.2 convolution_convert_fusion.4
  586.1 7.9 copy.152
  594.0 5.6 copy.153
  619.8 22.2 %convolution_convert_fusion = bf16[2560,1920]{1,0:T(8,128)(2,1)} fusion(bf16[1536,2560]{1,0:T(8,128)(2,1)} %constant_dynamic-update-slice_fusion, bf16[384,1920]{1,0:T(8,128)(2,1)S(1)} %pad_maximum_fusion.8, bf16[384,1920]{1,0:T(8,128)(2,1)S(1)} %pad_maximum_fusion.9, bf16[384,1920]{1,0:T(8,128)(2,1)S(1)} %pad_maximum_fusion.10, ...), kind=kOutput, calls=%fused_computation.1 | convolution fusion | flops 15128002560 | bytes 23592960 | tf_op jit(solution)/shard_map/dot_general | solution.py:139
  642.0 8.5 copy.150
  650.6 7.7 fusion.202
  660.6 7.0 fusion.199
  667.7 7.7 fusion.201
  675.4 7.1 fusion.200
  695.1 22.3 %collective-permute-done.29 = bf16[192,2560]{1,0:T(8,128)(2,1)S(1)} collective-permute-done((bf16[192,2560]{1,0:T(8,128)(2,1)S(1)}, bf16[192,2560]{1,0:T(8,128)(2,1)S(1)}, u32[]{:S(2)}, u32[]{:S(2)}) %collective-permute-start.29) | collective-permute-done | bytes 983072 | tf_op jit(solution)/shard_map/ppermute | solution.py:24
  718.1 20.4 %collective-permute-done.14 = bf16[192,2560]{1,0:T(8,128)(2,1)S(1)} collective-permute-done((bf16[192,2560]{1,0:T(8,128)(2,1)S(1)}, bf16[192,2560]{1,0:T(8,128)(2,1)S(1)}, u32[]{:S(2)}, u32[]{:S(2)}) %collective-permute-start.14) | collective-permute-done | bytes 983072 | tf_op jit(solution)/shard_map/ppermute | solution.py:24
  742.0 17.6 %collective-permute-done.30 = bf16[192,2560]{1,0:T(8,128)(2,1)S(1)} collective-permute-done((bf16[192,2560]{1,0:T(8,128)(2,1)S(1)}, bf16[192,2560]{1,0:T(8,128)(2,1)S(1)}, u32[]{:S(2)}, u32[]{:S(2)}) %collective-permute-start.30) | collective-permute-done | bytes 983072 | tf_op jit(solution)/shard_map/ppermute | solution.py:24
  760.0 20.6 %collective-permute-done.15 = bf16[192,2560]{1,0:T(8,128)(2,1)S(1)} collective-permute-done((bf16[192,2560]{1,0:T(8,128)(2,1)S(1)}, bf16[192,2560]{1,0:T(8,128)(2,1)S(1)}, u32[]{:S(2)}, u32[]{:S(2)}) %collective-permute-start.15) | collective-permute-done | bytes 983072 | tf_op jit(solution)/shard_map/ppermute | solution.py:24
  781.0 20.6 %collective-permute-done.31 = bf16[192,2560]{1,0:T(8,128)(2,1)S(1)} collective-permute-done((bf16[192,2560]{1,0:T(8,128)(2,1)S(1)}, bf16[192,2560]{1,0:T(8,128)(2,1)S(1)}, u32[]{:S(2)}, u32[]{:S(2)}) %collective-permute-start.31) | collective-permute-done | bytes 983072 | tf_op jit(solution)/shard_map/ppermute | solution.py:24
  802.5 19.5 %collective-permute-done.16 = bf16[192,2560]{1,0:T(8,128)(2,1)S(1)} collective-permute-done((bf16[192,2560]{1,0:T(8,128)(2,1)S(1)}, bf16[192,2560]{1,0:T(8,128)(2,1)S(1)}, u32[]{:S(2)}, u32[]{:S(2)}) %collective-permute-start.16) | collective-permute-done | bytes 983072 | tf_op jit(solution)/shard_map/ppermute | solution.py:24
  831.1 9.6 convert_reduce_fusion.3
  840.7 7.1 shard_map.272
  848.7 38.3 %all-gather.5 = f32[16,2,1280]{2,1,0:T(2,128)S(1)} all-gather(f32[1,2,1280]{2,1,0:T(2,128)S(1)} %maximum_bitcast_fusion.1), channel_id=5, replica_groups=mesh['o'=4,'i'=4,'tensor'=2] {'o','i'}, dimensions={0}, use_global_device_ids=true | all-gather | bytes 174080 | tf_op jit(solution)/shard_map/all_gather | solution.py:99
  887.5 8.0 multiply_reduce_fusion
  907.6 6.7 convolution_convert_fusion.1
  915.8 7.0 convolution_convert_fusion.2
  929.5 7.3 multiply_reduce_fusion.1
  946.7 5.8 convolution_convert_fusion.3
  952.5 5.3 fusion
  957.9 5.1 fusion.8
  997.1 30.6 %all-to-all-done.3 = bf16[4,160,960]{2,1,0:T(8,128)(2,1)} async-done(((bf16[4,160,960]{2,1,0:T(8,128)(2,1)}), bf16[4,160,960]{2,1,0:T(8,128)(2,1)}, u32[]{:S(2)}, u32[]{:S(2)}) %all-to-all-start.3) | async-done | bytes 1228832 | tf_op jit(solution)/shard_map/all_to_all | solution.py:178
  1027.6 10.9 all-to-all-start.2
  1045.6 81.1 %collective-permute-done.41 = f32[240,128]{1,0:T(8,128)S(1)} collective-permute-done((f32[240,128]{1,0:T(8,128)S(1)}, f32[240,128]{1,0:T(8,128)S(1)}, u32[]{:S(2)}, u32[]{:S(2)}) %collective-permute-start.41) | collective-permute-done | bytes 122912 | tf_op jit(solution)/shard_map/ppermute | solution.py:36
  1148.3 153.1 %reduce-scatter.9.cloned.1.call-done = bf16[160,1280]{1,0:T(8,128)(2,1)} async-done(((bf16[2560,1280]{1,0:T(8,128)(2,1)}), bf16[160,1280]{1,0:T(8,128)(2,1)}) %reduce-scatter.9.cloned.1.call-update) | async-done | bytes 409616 | tf_op jit(solution)/shard_map/reduce_scatter | solution.py:331
  1301.4 145.1 %reduce-scatter.7.cloned.1.call-done = bf16[160,1280]{1,0:T(8,128)(2,1)} async-done(((bf16[2560,1280]{1,0:T(8,128)(2,1)}), bf16[160,1280]{1,0:T(8,128)(2,1)}) %reduce-scatter.7.cloned.1.call-update) | async-done | bytes 409616 | tf_op jit(solution)/shard_map/reduce_scatter | solution.py:373
  1448.9 8.2 reshape.816
  1457.1 8.2 copy.151
  1465.3 7.4 reshape.813
  (486 shorter events, 210.7 us)
Async XLA Ops:
  7.2 191.4 %copy-start = (bf16[2,5,256,256]{3,2,1,0:T(8,128)(2,1)S(1)}, bf16[2,5,256,256]{3,2,1,0:T(8,128)(2,1)}, u32[]{:S(2)}) copy-start(bf16[2,5,256,256]{3,2,1,0:T(8,128)(2,1)} %param.27) | copy-start | bytes 3932164
  7.2 177.5 %all-gather.18.cloned.1.call-start = ((), (), s32[]{:S(2)}) async-start(), calls=%async_computation.19 | async-start | bytes 6963200 | tf_op jit(solution)/shard_map/all_gather | solution.py:211
  9.4 257.0 %all-gather.20.cloned.1.call-start = ((), (), s32[]{:S(2)}) async-start(), calls=%async_computation.20 | async-start | bytes 6963200 | tf_op jit(solution)/shard_map/all_gather | solution.py:212
  10.2 345.5 %all-gather.12.cloned.1.call-start = ((), (), s32[]{:S(2)}) async-start(), calls=%async_computation.10 | async-start | bytes 6963200 | tf_op jit(solution)/shard_map/all_gather | solution.py:213
  10.9 491.5 %all-gather.16.cloned.1.call-start = ((), (), s32[]{:S(2)}) async-start(), calls=%async_computation.12 | async-start | bytes 6553600 | tf_op jit(solution)/shard_map/all_gather | solution.py:223
  96.7 87.0 %all-to-all-start = ((bf16[4,160,1920]{2,1,0:T(8,128)(2,1)}), bf16[4,160,1920]{2,1,0:T(8,128)(2,1)}, u32[]{:S(2)}, u32[]{:S(2)}) async-start(bf16[4,160,1920]{2,1,0:T(8,128)(2,1)} %reshape.795), calls=%async_computation | async-start | bytes 4915200 | tf_op jit(solution)/shard_map/all_to_all | solution.py:178
  101.4 419.8 %all-gather.14.cloned.1.call-start = ((), (), s32[]{:S(2)}) async-start(), calls=%async_computation.11 | async-start | bytes 12288000 | tf_op jit(solution)/shard_map/all_gather | solution.py:220
  101.6 83.1 %collective-permute-start.34 = (f32[3]{0:T(128)S(1)}, f32[3]{0:T(128)S(1)}, u32[]{:S(2)}, u32[]{:S(2)}) collective-permute-start(f32[3]{0:T(128)S(1)} %get-tuple-element.176), channel_id=1, source_target_pairs={{2,0},{4,2},{6,4},{8,6},{10,8},{12,10},{14,12},{16,14},{18,16},{20... | collective-permute-start | bytes 44 | tf_op jit(solution)/shard_map/ppermute | solution.py:30
  102.8 81.8 %collective-permute-start = (f32[3]{0:T(128)S(1)}, f32[3]{0:T(128)S(1)}, u32[]{:S(2)}, u32[]{:S(2)}) collective-permute-start(f32[3]{0:T(128)S(1)} %get-tuple-element.177), channel_id=1, source_target_pairs={{0,2},{2,4},{4,6},{6,8},{8,10},{10,12},{12,14},{14,16},{16,18},{18... | collective-permute-start | bytes 44 | tf_op jit(solution)/shard_map/ppermute | solution.py:30
  107.5 158.9 %copy-start.60 = (f32[2560]{0:T(1024)}, f32[2560]{0:T(1024)S(1)}, u32[]{:S(2)}) copy-start(f32[2560]{0:T(1024)S(1)} %get-tuple-element.97) | copy-start | bytes 30724
  107.5 264.1 %copy-start.58 = (f32[2560]{0:T(1024)}, f32[2560]{0:T(1024)S(1)}, u32[]{:S(2)}) copy-start(f32[2560]{0:T(1024)S(1)} %get-tuple-element.96) | copy-start | bytes 30724
  107.6 88.0 %copy-start.64 = (f32[1280]{0:T(1024)}, f32[1280]{0:T(1024)S(1)}, u32[]{:S(2)}) copy-start(f32[1280]{0:T(1024)S(1)} %get-tuple-element.98) | copy-start | bytes 15364
  107.6 88.0 %copy-start.66 = (f32[1280]{0:T(1024)}, f32[1280]{0:T(1024)S(1)}, u32[]{:S(2)}) copy-start(f32[1280]{0:T(1024)S(1)} %get-tuple-element.99) | copy-start | bytes 15364
  107.7 88.0 %copy-start.68 = (f32[1280]{0:T(1024)}, f32[1280]{0:T(1024)S(1)}, u32[]{:S(2)}) copy-start(f32[1280]{0:T(1024)S(1)} %get-tuple-element.100) | copy-start | bytes 15364
  107.7 88.0 %copy-start.70 = (f32[1280]{0:T(1024)}, f32[1280]{0:T(1024)S(1)}, u32[]{:S(2)}) copy-start(f32[1280]{0:T(1024)S(1)} %get-tuple-element.101) | copy-start | bytes 15364
  108.2 158.3 %copy-start.102 = (f32[384]{0:T(512)}, f32[384]{0:T(512)S(1)}, u32[]{:S(2)}) copy-start(f32[384]{0:T(512)S(1)} %add_rsqrt_fusion) | copy-start | bytes 4612
  183.6 794.1 %reduce-scatter.15.cloned.1.call-start = ((), (), s32[]{:S(2)}) async-start(), calls=%async_computation.17 | async-start | bytes 6553600 | tf_op jit(solution)/shard_map/reduce_scatter | solution.py:297
  190.4 5.2 collective-permute-start.1
  363.4 4.9 collective-permute-start.2
  366.6 26.7 %collective-permute-start.20 = (bf16[192,2560]{1,0:T(8,128)(2,1)}, bf16[192,2560]{1,0:T(8,128)(2,1)}, u32[]{:S(2)}, u32[]{:S(2)}) collective-permute-start(bf16[192,2560]{1,0:T(8,128)(2,1)} %get-tuple-element.115), channel_id=1, source_target_pairs={{0,8},{8,16},{16,24},{24,0},{1,9},{9,17},{17,25},{25,1},{2,10},{10... | collective-permute-start | bytes 2949128 | tf_op jit(solution)/shard_map/ppermute | solution.py:24
  373.3 41.0 %collective-permute-start.5 = (bf16[192,2560]{1,0:T(8,128)(2,1)S(1)}, bf16[192,2560]{1,0:T(8,128)(2,1)S(1)}, u32[]{:S(2)}, u32[]{:S(2)}) collective-permute-start(bf16[192,2560]{1,0:T(8,128)(2,1)S(1)} %get-tuple-element.117), channel_id=1, source_target_pairs={{0,8},{8,16},{16,24},{24,0},{1,9},{9,17},{17,25},{25,1},{2,10},{10... | collective-permute-start | bytes 2949128 | tf_op jit(solution)/shard_map/ppermute | solution.py:24
  393.3 42.1 %collective-permute-start.21 = (bf16[192,2560]{1,0:T(8,128)(2,1)}, bf16[192,2560]{1,0:T(8,128)(2,1)}, u32[]{:S(2)}, u32[]{:S(2)}) collective-permute-start(bf16[192,2560]{1,0:T(8,128)(2,1)} %collective-permute-done.20), channel_id=1, source_target_pairs={{0,8},{8,16},{16,24},{24,0},{1,9},{9,17},{17,25},{25,1},{2,10},{10... | collective-permute-start | bytes 2949128 | tf_op jit(solution)/shard_map/ppermute | solution.py:24
  393.3 42.1 %collective-permute-start.18 = (bf16[192,2560]{1,0:T(8,128)(2,1)}, bf16[192,2560]{1,0:T(8,128)(2,1)}, u32[]{:S(2)}, u32[]{:S(2)}) collective-permute-start(bf16[192,2560]{1,0:T(8,128)(2,1)} %get-tuple-element.115), channel_id=1, source_target_pairs={{0,1},{1,0},{2,3},{3,2},{4,5},{5,4},{6,7},{7,6},{8,9},{9,8},{10,11... | collective-permute-start | bytes 2949128 | tf_op jit(solution)/shard_map/ppermute | solution.py:19
  414.3 42.2 %collective-permute-start.6 = (bf16[192,2560]{1,0:T(8,128)(2,1)S(1)}, bf16[192,2560]{1,0:T(8,128)(2,1)}, u32[]{:S(2)}, u32[]{:S(2)}) collective-permute-start(bf16[192,2560]{1,0:T(8,128)(2,1)S(1)} %collective-permute-done.5), channel_id=1, source_target_pairs={{0,8},{8,16},{16,24},{24,0},{1,9},{9,17},{17,25},{25,1},{2,10},{10... | collective-permute-start | bytes 2949128 | tf_op jit(solution)/shard_map/ppermute | solution.py:24
  415.1 52.3 %collective-permute-start.27 = (bf16[192,2560]{1,0:T(8,128)(2,1)}, bf16[192,2560]{1,0:T(8,128)(2,1)S(1)}, u32[]{:S(2)}, u32[]{:S(2)}) collective-permute-start(bf16[192,2560]{1,0:T(8,128)(2,1)} %collective-permute-done.20), channel_id=1, source_target_pairs={{0,1},{1,0},{2,3},{3,2},{4,5},{5,4},{6,7},{7,6},{8,9},{9,8},{10,11... | collective-permute-start | bytes 2949128 | tf_op jit(solution)/shard_map/ppermute | solution.py:19
  435.5 42.0 %collective-permute-start.22 = (bf16[192,2560]{1,0:T(8,128)(2,1)}, bf16[192,2560]{1,0:T(8,128)(2,1)S(1)}, u32[]{:S(2)}, u32[]{:S(2)}) collective-permute-start(bf16[192,2560]{1,0:T(8,128)(2,1)} %collective-permute-done.21), channel_id=1, source_target_pairs={{0,8},{8,16},{16,24},{24,0},{1,9},{9,17},{17,25},{25,1},{2,10},{10... | collective-permute-start | bytes 2949128 | tf_op jit(solution)/shard_map/ppermute | solution.py:24
  437.7 60.5 %collective-permute-start.25 = (bf16[192,2560]{1,0:T(8,128)(2,1)}, bf16[192,2560]{1,0:T(8,128)(2,1)S(1)}, u32[]{:S(2)}, u32[]{:S(2)}) collective-permute-start(bf16[192,2560]{1,0:T(8,128)(2,1)} %collective-permute-done.21), channel_id=1, source_target_pairs={{0,1},{1,0},{2,3},{3,2},{4,5},{5,4},{6,7},{7,6},{8,9},{9,8},{10,11... | collective-permute-start | bytes 2949128 | tf_op jit(solution)/shard_map/ppermute | solution.py:19
  456.5 41.6 %collective-permute-start.7 = (bf16[192,2560]{1,0:T(8,128)(2,1)}, bf16[192,2560]{1,0:T(8,128)(2,1)}, u32[]{:S(2)}, u32[]{:S(2)}) collective-permute-start(bf16[192,2560]{1,0:T(8,128)(2,1)} %collective-permute-done.6), channel_id=1, source_target_pairs={{0,8},{8,16},{16,24},{24,0},{1,9},{9,17},{17,25},{25,1},{2,10},{10... | collective-permute-start | bytes 2949128 | tf_op jit(solution)/shard_map/ppermute | solution.py:24
  477.5 22.9 %collective-permute-start.23 = (bf16[192,2560]{1,0:T(8,128)(2,1)S(1)}, bf16[192,2560]{1,0:T(8,128)(2,1)S(1)}, u32[]{:S(2)}, u32[]{:S(2)}) collective-permute-start(bf16[192,2560]{1,0:T(8,128)(2,1)S(1)} %collective-permute-done.22), channel_id=1, source_target_pairs={{0,1},{1,0},{2,3},{3,2},{4,5},{5,4},{6,7},{7,6},{8,9},{9,8},{10,11... | collective-permute-start | bytes 2949128 | tf_op jit(solution)/shard_map/ppermute | solution.py:19
  498.2 23.0 %collective-permute-start.8 = (bf16[192,2560]{1,0:T(8,128)(2,1)}, bf16[192,2560]{1,0:T(8,128)(2,1)}, u32[]{:S(2)}, u32[]{:S(2)}) collective-permute-start(bf16[192,2560]{1,0:T(8,128)(2,1)} %collective-permute-done.7), channel_id=1, source_target_pairs={{0,1},{1,0},{2,3},{3,2},{4,5},{5,4},{6,7},{7,6},{8,9},{9,8},{10,11... | collective-permute-start | bytes 2949128 | tf_op jit(solution)/shard_map/ppermute | solution.py:19
  520.2 41.3 %collective-permute-start.3 = (bf16[192,2560]{1,0:T(8,128)(2,1)S(1)}, bf16[192,2560]{1,0:T(8,128)(2,1)}, u32[]{:S(2)}, u32[]{:S(2)}) collective-permute-start(bf16[192,2560]{1,0:T(8,128)(2,1)S(1)} %get-tuple-element.117), channel_id=1, source_target_pairs={{0,1},{1,0},{2,3},{3,2},{4,5},{5,4},{6,7},{7,6},{8,9},{9,8},{10,11... | collective-permute-start | bytes 2949128 | tf_op jit(solution)/shard_map/ppermute | solution.py:19
  520.7 16.9 %collective-permute-start.12 = (bf16[192,2560]{1,0:T(8,128)(2,1)S(1)}, bf16[192,2560]{1,0:T(8,128)(2,1)}, u32[]{:S(2)}, u32[]{:S(2)}) collective-permute-start(bf16[192,2560]{1,0:T(8,128)(2,1)S(1)} %collective-permute-done.5), channel_id=1, source_target_pairs={{0,1},{1,0},{2,3},{3,2},{4,5},{5,4},{6,7},{7,6},{8,9},{9,8},{10,11... | collective-permute-start | bytes 2949128 | tf_op jit(solution)/shard_map/ppermute | solution.py:19
  520.7 10.9 collective-permute-start.10
  599.6 428.1 %reduce-scatter.13.cloned.1.call-start = ((), (), s32[]{:S(2)}) async-start(), calls=%async_computation.16 | async-start | bytes 12288000 | tf_op jit(solution)/shard_map/reduce_scatter | solution.py:297
  650.6 480.5 %reduce-scatter.17.cloned.1.call-start = ((), (), s32[]{:S(2)}) async-start(), calls=%async_computation.18 | async-start | bytes 1392640 | tf_op jit(solution)/shard_map/reduce_scatter | solution.py:353
  660.6 28.9 %collective-permute-start.28 = (bf16[192,2560]{1,0:T(8,128)(2,1)}, bf16[192,2560]{1,0:T(8,128)(2,1)}, u32[]{:S(2)}, u32[]{:S(2)}) collective-permute-start(bf16[192,2560]{1,0:T(8,128)(2,1)} %slice.1010), channel_id=1, source_target_pairs={{0,1},{1,0},{2,3},{3,2},{4,5},{5,4},{6,7},{7,6},{8,9},{9,8},{10,11... | collective-permute-start | bytes 2949128 | tf_op jit(solution)/shard_map/ppermute | solution.py:19
  686.1 4.9 collective-permute-start.13
  688.7 6.1 collective-permute-start.26
  689.1 28.9 %collective-permute-start.11 = (bf16[192,2560]{1,0:T(8,128)(2,1)S(1)}, bf16[192,2560]{1,0:T(8,128)(2,1)S(1)}, u32[]{:S(2)}, u32[]{:S(2)}) collective-permute-start(bf16[192,2560]{1,0:T(8,128)(2,1)S(1)} %slice.1015), channel_id=1, source_target_pairs={{0,1},{1,0},{2,3},{3,2},{4,5},{5,4},{6,7},{7,6},{8,9},{9,8},{10,11... | collective-permute-start | bytes 2949128 | tf_op jit(solution)/shard_map/ppermute | solution.py:19
  690.9 26.5 %collective-permute-start.29 = (bf16[192,2560]{1,0:T(8,128)(2,1)S(1)}, bf16[192,2560]{1,0:T(8,128)(2,1)S(1)}, u32[]{:S(2)}, u32[]{:S(2)}) collective-permute-start(bf16[192,2560]{1,0:T(8,128)(2,1)S(1)} %fusion.65), channel_id=1, source_target_pairs={{0,8},{8,16},{16,24},{24,0},{1,9},{9,17},{17,25},{25,1},{2,10},{10... | collective-permute-start | bytes 2949128 | tf_op jit(solution)/shard_map/ppermute | solution.py:24
  691.2 47.3 %collective-permute-start.14 = (bf16[192,2560]{1,0:T(8,128)(2,1)S(1)}, bf16[192,2560]{1,0:T(8,128)(2,1)S(1)}, u32[]{:S(2)}, u32[]{:S(2)}) collective-permute-start(bf16[192,2560]{1,0:T(8,128)(2,1)S(1)} %fusion.71), channel_id=1, source_target_pairs={{0,8},{8,16},{16,24},{24,0},{1,9},{9,17},{17,25},{25,1},{2,10},{10... | collective-permute-start | bytes 2949128 | tf_op jit(solution)/shard_map/ppermute | solution.py:24
  694.4 47.0 %collective-permute-start.24 = (bf16[192,2560]{1,0:T(8,128)(2,1)S(1)}, bf16[192,2560]{1,0:T(8,128)(2,1)S(1)}, u32[]{:S(2)}, u32[]{:S(2)}) collective-permute-start(bf16[192,2560]{1,0:T(8,128)(2,1)S(1)} %slice.1012), channel_id=1, source_target_pairs={{0,1},{1,0},{2,3},{3,2},{4,5},{5,4},{6,7},{7,6},{8,9},{9,8},{10,11... | collective-permute-start | bytes 2949128 | tf_op jit(solution)/shard_map/ppermute | solution.py:19
  694.9 65.1 %collective-permute-start.9 = (bf16[192,2560]{1,0:T(8,128)(2,1)S(1)}, bf16[192,2560]{1,0:T(8,128)(2,1)S(1)}, u32[]{:S(2)}, u32[]{:S(2)}) collective-permute-start(bf16[192,2560]{1,0:T(8,128)(2,1)S(1)} %slice.1016), channel_id=1, source_target_pairs={{0,1},{1,0},{2,3},{3,2},{4,5},{5,4},{6,7},{7,6},{8,9},{9,8},{10,11... | collective-permute-start | bytes 2949128 | tf_op jit(solution)/shard_map/ppermute | solution.py:19
  717.8 41.8 %collective-permute-start.30 = (bf16[192,2560]{1,0:T(8,128)(2,1)S(1)}, bf16[192,2560]{1,0:T(8,128)(2,1)S(1)}, u32[]{:S(2)}, u32[]{:S(2)}) collective-permute-start(bf16[192,2560]{1,0:T(8,128)(2,1)S(1)} %fusion.67), channel_id=1, source_target_pairs={{0,8},{8,16},{16,24},{24,0},{1,9},{9,17},{17,25},{25,1},{2,10},{10... | collective-permute-start | bytes 2949128 | tf_op jit(solution)/shard_map/ppermute | solution.py:24
  738.8 41.8 %collective-permute-start.15 = (bf16[192,2560]{1,0:T(8,128)(2,1)S(1)}, bf16[192,2560]{1,0:T(8,128)(2,1)S(1)}, u32[]{:S(2)}, u32[]{:S(2)}) collective-permute-start(bf16[192,2560]{1,0:T(8,128)(2,1)S(1)} %fusion.73), channel_id=1, source_target_pairs={{0,8},{8,16},{16,24},{24,0},{1,9},{9,17},{17,25},{25,1},{2,10},{10... | collective-permute-start | bytes 2949128 | tf_op jit(solution)/shard_map/ppermute | solution.py:24
  741.2 39.8 %collective-permute-start.19 = (bf16[192,2560]{1,0:T(8,128)(2,1)S(1)}, bf16[192,2560]{1,0:T(8,128)(2,1)S(1)}, u32[]{:S(2)}, u32[]{:S(2)}) collective-permute-start(bf16[192,2560]{1,0:T(8,128)(2,1)S(1)} %slice.1013), channel_id=1, source_target_pairs={{0,1},{1,0},{2,3},{3,2},{4,5},{5,4},{6,7},{7,6},{8,9},{9,8},{10,11... | collective-permute-start | bytes 2949128 | tf_op jit(solution)/shard_map/ppermute | solution.py:19
  741.4 61.1 %collective-permute-start.4 = (bf16[192,2560]{1,0:T(8,128)(2,1)S(1)}, bf16[192,2560]{1,0:T(8,128)(2,1)S(1)}, u32[]{:S(2)}, u32[]{:S(2)}) collective-permute-start(bf16[192,2560]{1,0:T(8,128)(2,1)S(1)} %slice.1017), channel_id=1, source_target_pairs={{0,1},{1,0},{2,3},{3,2},{4,5},{5,4},{6,7},{7,6},{8,9},{9,8},{10,11... | collective-permute-start | bytes 2949128 | tf_op jit(solution)/shard_map/ppermute | solution.py:19
  759.9 41.8 %collective-permute-start.31 = (bf16[192,2560]{1,0:T(8,128)(2,1)S(1)}, bf16[192,2560]{1,0:T(8,128)(2,1)S(1)}, u32[]{:S(2)}, u32[]{:S(2)}) collective-permute-start(bf16[192,2560]{1,0:T(8,128)(2,1)S(1)} %fusion.69), channel_id=1, source_target_pairs={{0,8},{8,16},{16,24},{24,0},{1,9},{9,17},{17,25},{25,1},{2,10},{10... | collective-permute-start | bytes 2949128 | tf_op jit(solution)/shard_map/ppermute | solution.py:24
  781.0 41.0 %collective-permute-start.16 = (bf16[192,2560]{1,0:T(8,128)(2,1)S(1)}, bf16[192,2560]{1,0:T(8,128)(2,1)S(1)}, u32[]{:S(2)}, u32[]{:S(2)}) collective-permute-start(bf16[192,2560]{1,0:T(8,128)(2,1)S(1)} %fusion.75), channel_id=1, source_target_pairs={{0,8},{8,16},{16,24},{24,0},{1,9},{9,17},{17,25},{25,1},{2,10},{10... | collective-permute-start | bytes 2949128 | tf_op jit(solution)/shard_map/ppermute | solution.py:24
  826.5 2.9 collective-permute-start.32
  906.8 239.5 %reduce-scatter.11.cloned.1.call-start = ((), (), s32[]{:S(2)}) async-start(), calls=%async_computation.15 | async-start | bytes 6963200 | tf_op jit(solution)/shard_map/reduce_scatter | solution.py:325
  914.3 387.1 %reduce-scatter.9.cloned.1.call-start = ((), (), s32[]{:S(2)}) async-start(), calls=%async_computation.14 | async-start | bytes 6963200 | tf_op jit(solution)/shard_map/reduce_scatter | solution.py:331
  922.8 523.7 %reduce-scatter.7.cloned.1.call-start = ((), (), s32[]{:S(2)}) async-start(), calls=%async_computation.13 | async-start | bytes 6963200 | tf_op jit(solution)/shard_map/reduce_scatter | solution.py:373
  936.8 5.9 collective-permute-start.33
  966.0 2.9 collective-permute-start.35
  968.3 70.3 %collective-permute-start.17 = (f32[192,2560]{1,0:T(8,128)}, f32[192,2560]{1,0:T(8,128)}, u32[]{:S(2)}, u32[]{:S(2)}) collective-permute-start(f32[192,2560]{1,0:T(8,128)} %get-tuple-element.150), channel_id=1, source_target_pairs={{0,1},{1,0},{2,3},{3,2},{4,5},{5,4},{6,7},{7,6},{8,9},{9,8},{10,11... | collective-permute-start | bytes 5898248 | tf_op jit(solution)/shard_map/ppermute | solution.py:19
  972.1 1.3 collective-permute-start.37
  977.8 49.9 %all-to-all-start.3 = ((bf16[4,160,960]{2,1,0:T(8,128)(2,1)}), bf16[4,160,960]{2,1,0:T(8,128)(2,1)}, u32[]{:S(2)}, u32[]{:S(2)}) async-start(bf16[4,160,960]{2,1,0:T(8,128)(2,1)} %bitcast.397), calls=%async_computation.8 | async-start | bytes 2621440 | tf_op jit(solution)/shard_map/all_to_all | solution.py:178
  982.8 5.5 collective-permute-start.38
  988.3 5.5 collective-permute-start.39
  992.8 139.9 %collective-permute-start.36 = (f32[192,2560]{1,0:T(8,128)}, f32[192,2560]{1,0:T(8,128)}, u32[]{:S(2)}, u32[]{:S(2)}) collective-permute-start(f32[192,2560]{1,0:T(8,128)} %fusion.35), channel_id=1, source_target_pairs={{0,1},{1,0},{2,3},{3,2},{4,5},{5,4},{6,7},{7,6},{8,9},{9,8},{10,11... | collective-permute-start | bytes 5898248 | tf_op jit(solution)/shard_map/ppermute | solution.py:19
  993.8 46.6 %collective-permute-start.40 = (f32[240,128]{1,0:T(8,128)S(1)}, f32[240,128]{1,0:T(8,128)S(1)}, u32[]{:S(2)}, u32[]{:S(2)}) collective-permute-start(f32[240,128]{1,0:T(8,128)S(1)} %fusion.239), channel_id=1, source_target_pairs={{0,8},{2,10},{4,12},{6,14},{8,0},{10,2},{12,4},{14,6},{16,24},{18,... | collective-permute-start | bytes 368648 | tf_op jit(solution)/shard_map/ppermute | solution.py:36
  1027.6 421.3 %all-to-all-start.2 = ((bf16[4,160,1920]{2,1,0:T(8,128)(2,1)}), bf16[4,160,1920]{2,1,0:T(8,128)(2,1)}, u32[]{:S(2)}, u32[]{:S(2)}) async-start(bf16[4,160,1920]{2,1,0:T(8,128)(2,1)} %bitcast.394), calls=%async_computation.6 | async-start | bytes 4915200 | tf_op jit(solution)/shard_map/all_to_all | solution.py:178
  1040.5 86.2 %collective-permute-start.41 = (f32[240,128]{1,0:T(8,128)S(1)}, f32[240,128]{1,0:T(8,128)S(1)}, u32[]{:S(2)}, u32[]{:S(2)}) collective-permute-start(f32[240,128]{1,0:T(8,128)S(1)} %add.761), channel_id=1, source_target_pairs={{0,16},{2,18},{4,20},{6,22},{8,24},{10,26},{12,28},{14,30},{16,0},... | collective-permute-start | bytes 368648 | tf_op jit(solution)/shard_map/ppermute | solution.py:36
  (109 other events, 1196.8 us)
Sparse Core Ops, SparseCore 0:
  11.3 135.1 all-gather.17
  149.1 109.5 all-gather.19
  261.4 94.2 all-gather.11
  358.0 59.7 all-gather.15
  419.5 99.4 all-gather.13
  599.7 59.1 reduce-scatter.14
  662.0 98.0 reduce-scatter.12
  907.0 75.8 reduce-scatter.16
  985.1 146.3 reduce-scatter.10
  1133.7 167.6 reduce-scatter.8
  1303.7 142.7 reduce-scatter.6

commit v2 on v1

--- a/solution.py
+++ b/solution.py
@@ -7,6 +7,7 @@
 from jax.experimental.pallas import tpu as pltpu
 from jax.sharding import Mesh
 from jax.sharding import PartitionSpec as P
+
 
 INNER = 4
 DP = ("o", "i")
@@ -94,15 +95,302 @@
     )(keep, drive)
 
 
-def entering(decay, state, reverse):
-    count, index = lax.axis_size(DP), lax.axis_index(DP)
-    every = lax.all_gather(jnp.stack([decay, state]), DP)
-    carried = jnp.zeros_like(state)
+MESH_ID = pl.DeviceIdType.MESH
+VMEM = pl.BlockSpec(memory_space=pltpu.VMEM)
+ANY = pl.BlockSpec(memory_space=pl.ANY)
+
+
+def enter_kernel(outer, inner, reverse, ends_ref, carry_ref, every, send_sem, recv_sem):
+    count = outer * inner
+    core = lax.axis_index("tensor")
+    me = lax.axis_index("o") * inner + lax.axis_index("i")
+    barrier = pltpu.get_barrier_semaphore()
+    for k in range(1, count):
+        peer = lax.rem(me + k, count)
+        to = (peer // inner, lax.rem(peer, inner), core)
+        pl.semaphore_signal(barrier, inc=1, device_id=to, device_id_type=MESH_ID)
+    pl.semaphore_wait(barrier, count - 1)
+
+    def copy(k, mine):
+        peer = lax.rem(me + k, count)
+        return pltpu.make_async_remote_copy(
+            src_ref=ends_ref,
+            dst_ref=every.at[me if mine else peer],
+            send_sem=send_sem.at[k],
+            recv_sem=recv_sem.at[me if mine else peer],
+            device_id=(peer // inner, lax.rem(peer, inner), core),
+            device_id_type=MESH_ID,
+        )
+
+    for k in range(1, count):
+        copy(k, True).start()
+    for k in range(1, count):
+        copy(k, False).wait_recv()
+    carried = jnp.zeros((1, ends_ref.shape[1]), F32)
     for k in range(count):
         at = count - 1 - k if reverse else k
-        reached = at > index if reverse else at < index
-        carried = jnp.where(reached, every[at, 0] * carried + every[at, 1], carried)
-    return carried
+        reached = at > me if reverse else at < me
+        block = every[at]
+        carried = jnp.where(reached, block[0:1] * carried + block[1:2], carried)
+    carry_ref[...] = carried
+    for k in range(1, count):
+        copy(k, True).wait_send()
+
+
+def entering(decay, state, reverse):
+    outer, inner = lax.axis_size("o"), lax.axis_size("i")
+    count, width = outer * inner, state.shape[0]
+    carried = pl.pallas_call(
+        functools.partial(enter_kernel, outer, inner, reverse),
+        in_specs=[VMEM],
+        out_specs=VMEM,
+        out_shape=jax.ShapeDtypeStruct((1, width), F32),
+        scratch_shapes=[
+            pltpu.VMEM((count, 2, width), F32),
+            pltpu.SemaphoreType.DMA((count,)),
+            pltpu.SemaphoreType.DMA((count,)),
+        ],
+        compiler_params=pltpu.CompilerParams(
+            collective_id=2 if reverse else 1, has_side_effects=True
+        ),
+    )(jnp.stack([decay, state]))
+    return carried[0]
+
+
+def gather_kernel(outer, groups, parts, *refs):
+    own, send = refs[:groups], refs[groups : groups + parts]
+    refs = refs[groups + parts :]
+    full, got = refs[:groups], refs[groups : groups + parts]
+    line_send, line_recv, side_send, side_recv, half_send, half_recv, part_send, part_recv, local = refs[
+        groups + parts :
+    ]
+    o, i, core = lax.axis_index("o"), lax.axis_index("i"), lax.axis_index("tensor")
+    sides = (i + 1 - 2 * lax.rem(i, 2), lax.rem(i + 2, 4))
+    far = lax.rem(sides[0] + 2, 4)
+    lanes = own[0].shape[1] // 2
+
+    barrier = pltpu.get_barrier_semaphore()
+    for k in range(1, outer):
+        pl.semaphore_signal(
+            barrier, inc=1, device_id=(lax.rem(o + k, outer), i, core), device_id_type=MESH_ID
+        )
+    for side in sides:
+        pl.semaphore_signal(barrier, inc=1, device_id=(o, side, core), device_id_type=MESH_ID)
+    pl.semaphore_wait(barrier, outer + 1)
+
+    def remote(src, dst, send_sem, recv_sem, to):
+        return pltpu.make_async_remote_copy(
+            src_ref=src,
+            dst_ref=dst,
+            send_sem=send_sem,
+            recv_sem=recv_sem,
+            device_id=to,
+            device_id_type=MESH_ID,
+        )
+
+    def block(g, k, j):
+        return full[g].at[k, j]
+
+    def along_line(g, k, mine, step):
+        return remote(
+            own[g] if mine else block(g, k, i),
+            block(g, k, i),
+            line_send.at[g, k, step],
+            line_recv.at[g, k],
+            (o + 2 * step - 1, i, core),
+        )
+
+    def to_side(g, k, mine, side):
+        return remote(
+            own[g] if mine else block(g, k, i),
+            block(g, k, i),
+            side_send.at[g, k, side],
+            side_recv.at[g, k, side],
+            (o, sides[side], core),
+        )
+
+    def from_side(g, k, side):
+        return remote(
+            block(g, k, sides[side]),
+            block(g, k, sides[side]),
+            side_send.at[g, k, side],
+            side_recv.at[g, k, side],
+            (o, sides[side], core),
+        )
+
+    def half(g, k, side, to):
+        part = full[g].at[k, side, :, pl.ds(lanes * to, lanes)]
+        return remote(
+            part, part, half_send.at[g, k, to], half_recv.at[g, k, to], (o, sides[to], core)
+        )
+
+    def visit(first, then):
+        first(o)
+        for d in range(1, outer):
+            pl.when(o - d >= 0)(functools.partial(then, o - d, True))
+            pl.when(o + d < outer)(functools.partial(then, o + d, False))
+
+    for g in range(groups):
+        pltpu.make_async_copy(own[g], block(g, o, i), local.at[g]).start()
+        pl.when(o + 1 < outer)(lambda g=g: along_line(g, o, True, 1).start())
+        pl.when(o > 0)(lambda g=g: along_line(g, o, True, 0).start())
+        for side in range(2):
+            to_side(g, o, True, side).start()
+
+    def pass_on(k, from_left):
+        for g in range(groups):
+            along_line(g, k, False, 0).wait_recv()
+            if from_left:
+                pl.when(o + 1 < outer)(lambda g=g: along_line(g, k, False, 1).start())
+            else:
+                pl.when(o > 0)(lambda g=g: along_line(g, k, False, 0).start())
+            for side in range(2):
+                to_side(g, k, False, side).start()
+
+    visit(lambda k: None, pass_on)
+
+    def part(p, k, mine):
+        peer = lax.rem(o + k, outer)
+        return remote(
+            send[p].at[peer],
+            got[p].at[o if mine else peer],
+            part_send.at[p, k],
+            part_recv.at[p, o if mine else peer],
+            (peer, i, core),
+        )
+
+    for p in range(parts):
+        pltpu.make_async_copy(send[p].at[o], got[p].at[o], local.at[groups + p]).start()
+        for k in range(1, outer):
+            part(p, k, True).start()
+
+    def turn(k, _=None):
+        for g in range(groups):
+            for side in range(2):
+                from_side(g, k, side).wait_recv()
+                half(g, k, sides[side], 1 - side).start()
+
+    visit(turn, turn)
+
+    def finish(k, _=None):
+        for g in range(groups):
+            for side in range(2):
+                half(g, k, far, side).wait_recv()
+
+    visit(finish, finish)
+    for p in range(parts):
+        for k in range(1, outer):
+            part(p, k, False).wait_recv()
+
+    def sent(k, from_left):
+        for g in range(groups):
+            if from_left is None or from_left:
+                pl.when(o + 1 < outer)(lambda g=g: along_line(g, k, False, 1).wait_send())
+            if not from_left:
+                pl.when(o > 0)(lambda g=g: along_line(g, k, False, 0).wait_send())
+            for side in range(2):
+                to_side(g, k, False, side).wait_send()
+                half(g, k, sides[side], 1 - side).wait_send()
+
+    visit(functools.partial(sent, from_left=None), sent)
+    for p in range(parts):
+        for k in range(1, outer):
+            part(p, k, True).wait_send()
+    for g in range(groups):
+        pltpu.make_async_copy(own[g], block(g, o, i), local.at[g]).wait()
+    for p in range(parts):
+        pltpu.make_async_copy(send[p].at[o], got[p].at[o], local.at[groups + p]).wait()
+
+
+def gather_weights(own, send):
+    outer, inner = lax.axis_size("o"), lax.axis_size("i")
+    groups, parts = len(own), len(send)
+    dma = pltpu.SemaphoreType.DMA
+    out_shape = [jax.ShapeDtypeStruct((outer, inner, *w.shape), w.dtype) for w in own] + [
+        jax.ShapeDtypeStruct(w.shape, w.dtype) for w in send
+    ]
+    result = pl.pallas_call(
+        functools.partial(gather_kernel, outer, groups, parts),
+        in_specs=[VMEM] * (groups + parts),
+        out_specs=[ANY] * (groups + parts),
+        out_shape=out_shape,
+        scratch_shapes=[
+            dma((groups, outer, 2)),
+            dma((groups, outer)),
+            dma((groups, outer, 2)),
+            dma((groups, outer, 2)),
+            dma((groups, outer, 2)),
+            dma((groups, outer, 2)),
+            dma((parts, outer)),
+            dma((parts, outer)),
+            dma((groups + parts,)),
+        ],
+        compiler_params=pltpu.CompilerParams(collective_id=0, has_side_effects=True),
+    )(*own, *send)
+    full = [w.reshape(-1, w.shape[-1]) for w in result[:groups]]
+    return full, result[groups:]
+
+
+def grads_kernel(plan, added, *refs):
+    out_ref = refs[-1]
+    inner, _, rows, _ = out_ref.shape
+    take = rows - added
+    if added:
+        out_ref[:, 0, take:, :] = refs[-2][0]
+    refs = iter(refs)
+    at = 0
+    for terms in plan:
+        total = None
+        for pieces in terms:
+            a = [next(refs)[...] for _ in range(pieces)]
+            term = mm_tn(jnp.concatenate(a) if pieces > 1 else a[0], next(refs)[...])
+            total = term if total is None else total + term
+        size = total.shape[1]
+        out_ref[:, 0, :take, at : at + size] = total.astype(BF16).reshape(inner, take, size)
+        at += size
+
+
+def grads_rows(columns, extra=None):
+    outer, inner = lax.axis_size("o"), lax.axis_size("i")
+    width = columns[0][0][0][0].shape[1]
+    block = width // outer
+    rows = block // inner
+    size = sum(terms[0][1].shape[1] for terms in columns)
+    tokens = sum(b.shape[0] for _, b in columns[0])
+    added = 0 if extra is None else extra.shape[2]
+    if block % 128:
+        whole = [
+            sum(mm_tn(jnp.concatenate(a), b) for a, b in terms).astype(BF16) for terms in columns
+        ]
+        whole = jnp.concatenate(whole, axis=1).reshape(outer, inner, rows, size)
+        if added:
+            whole = jnp.concatenate([whole, extra], axis=2)
+        return whole.transpose(1, 0, 2, 3).reshape(inner, -1, size)
+    specs, given = [], []
+    for terms in columns:
+        for a, b in terms:
+            for piece in a:
+                specs.append(pl.BlockSpec((piece.shape[0], block), lambda k: (0, k)))
+                given.append(piece)
+            specs.append(pl.BlockSpec(b.shape, lambda k: (0, 0)))
+            given.append(b)
+    if added:
+        specs.append(pl.BlockSpec((1, inner, added, size), lambda k: (k, 0, 0, 0)))
+        given.append(extra)
+    plan = tuple(tuple(len(a) for a, _ in terms) for terms in columns)
+    result = pl.pallas_call(
+        functools.partial(grads_kernel, plan, added),
+        grid=(outer,),
+        in_specs=specs,
+        out_specs=pl.BlockSpec((inner, 1, rows + added, size), lambda k: (0, k, 0, 0)),
+        out_shape=jax.ShapeDtypeStruct((inner, outer, rows + added, size), BF16),
+        cost_estimate=pl.CostEstimate(
+            flops=2 * tokens * width * size,
+            bytes_accessed=2 * (tokens * (width + size) + width * size),
+            transcendentals=0,
+        ),
+    )(*given)
+    return result.reshape(inner, -1, size)
 
 
 def gelu_tanh(values):
@@ -154,28 +442,68 @@
 def gather_slots(half):
     slots = []
     for k in range(lax.axis_size("o")):
-        half = ring(half) if k else half
-        slots.append(jnp.concatenate([half, swap(half)], axis=0))
+        if k:
+            half = ring(half)
+        slots.append([half, swap(half)])
     return slots
 
 
-def reduce_slots(parts):
-    count = len(parts)
-    rows = parts[0].shape[0] // 2
-
-    def both(part):
-        return part[:rows] + swap(part[rows:].astype(BF16)).astype(F32)
-
-    if count == 1:
-        return both(parts[0])
-    total = both(parts[1])
+def shift_outer(value, k):
+    count = lax.axis_size("o")
+    return lax.ppermute(value, "o", [(j, (j + k) % count) for j in range(count)])
+
+
+def both_cores(part):
+    rows = part.shape[0] // 2
+    return part[:rows] + swap(part[rows:].astype(BF16)).astype(F32)
+
+
+def reduce_slots(sums):
+    total = sums[0]
+    for part in sums[1:]:
+        low = total.astype(BF16)
+        moved = ring(low)
+        total = part + moved.astype(F32)
+    return total
+
+
+def reduce_direct(halves):
+    count = len(halves)
+    total = halves[0].astype(F32)
     for k in range(1, count):
-        total = both(parts[(k + 1) % count]) + ring(total.astype(BF16)).astype(F32)
+        moved = lax.ppermute(halves[k], "o", [(j, (j - k) % count) for j in range(count)])
+        total = total + moved.astype(F32)
     return total
 
 
-def spread(value, axis):
-    return lax.all_to_all(value, "o", axis, axis, tiled=True)
+def spread(value):
+    return lax.all_to_all(value, "o", 0, 0, tiled=True)
+
+
+def gather_inner(whole):
+    return lax.all_gather(whole, "i", axis=1, tiled=True).reshape(-1, whole.shape[-1])
+
+
+def sum_inner(rows):
+    own = lax.psum_scatter(
+        rows.reshape(-1, rows.shape[-1]), "i", scatter_dimension=0, tiled=True
+    )
+    return own.reshape(lax.axis_size("o"), -1, rows.shape[-1])
+
+
+def sum_outer(parts):
+    count, at = lax.axis_size("o"), lax.axis_index("o")
+    total = lax.dynamic_index_in_dim(parts, at, 0, False).astype(F32)
+    for k in range(1, count):
+        part = lax.dynamic_index_in_dim(parts, lax.rem(at + k, count), 0, False)
+        moved = lax.ppermute(part, "o", [(j, (j + k) % count) for j in range(count)])
+        total = total + moved.astype(F32)
+    return total
+
+
+def cuts_of(size):
+    first = size // 2 // 128 * 128 + 128 if size > 512 else size
+    return ((0, first), (first, size - first)) if size > first else ((0, size),)
 
 
 def per_device(
@@ -208,22 +536,34 @@
     heads_half, block_size = gate_weights.shape[1], gate_weights.shape[2]
     width_half = heads_half * block_size
 
-    branch_x_full = lax.all_gather(branch_weight[0], DP, axis=0, tiled=True)
-    branch_y_full = lax.all_gather(branch_weight[1], DP, axis=0, tiled=True)
-    out_full_t = lax.all_gather(out_weight.T, DP, axis=0, tiled=True)
-    in_parts = (
-        ffw_in.reshape(2, part_width, outer, hidden_part)
-        .transpose(2, 1, 0, 3)
-        .reshape(outer, part_width, 2 * hidden_part)
-    )
-    out_parts = ffw_out.reshape(outer, hidden_part, part_width).transpose(0, 2, 1)
-    ffw_in_full = lax.all_gather(spread(in_parts, 0), "i", axis=1, tiled=True).reshape(
-        width, 2 * hidden_part
-    )
-    ffw_out_full_t = lax.all_gather(spread(out_parts, 0), "i", axis=1, tiled=True).reshape(
-        width, hidden_part
-    )
-    cot_slots = gather_slots(half_of(cotangent, core))
+    cuts = cuts_of(hidden_part)
+    ffw_out_t = ffw_out.T
+    packed = [
+        jnp.stack(
+            [
+                jnp.concatenate(
+                    [
+                        w[:, k * hidden_part + start : k * hidden_part + start + size]
+                        for w in (ffw_in[0], ffw_in[1], ffw_out_t)
+                    ],
+                    axis=1,
+                )
+                for k in range(outer)
+            ]
+        )
+        for start, size in cuts
+    ]
+    (branch_x_full, branch_y_full, out_full_t), parts = gather_weights(
+        [branch_weight[0], branch_weight[1], out_weight.T], packed
+    )
+    ffw_parts = []
+    for k, (_, size) in enumerate(cuts):
+        whole = gather_inner(parts[k])
+        ffw_parts.append((whole[:, : 2 * size], whole[:, 2 * size :]))
+    cot_own, branch_x_full = lax.optimization_barrier((half_of(cotangent, core), branch_x_full))
+    near = [k for k in range(1, outer) if k in (1, outer - 1)]
+    far = [k for k in range(1, outer) if k not in near]
+    cot_near = [shift_outer(cot_own, k) for k in near]
 
     seg_marks = (segment_ids + 1).astype(F32)
     source_half = half_of(inputs, core).astype(F32)
@@ -262,7 +602,11 @@
         lru_local, gate_pre[0], gate_pre[1], conv_float, decay_param
     )
     cumulative, local_state = local_scan(keep_rate, drive_in, False)
-    carry_in = entering(cumulative[tok_rows - 1], local_state[tok_rows - 1], False)
+    ends = (cumulative[tok_rows - 1], local_state[tok_rows - 1])
+    ends, cot_near = lax.optimization_barrier((ends, cot_near))
+    carry_in = entering(*ends, False)
+    carry_in, cot_own = lax.optimization_barrier((carry_in, cot_own))
+    cot_far = [shift_outer(cot_own, k) for k in far]
     states = local_state + cumulative * carry_in
     branch_act, gelu_back = jax.vjp(gelu_tanh, branch_y)
     mixed_in = (states * branch_act).astype(BF16)
@@ -274,47 +618,61 @@
         + out_bias[0]
     )
 
+    residual, cot_far = lax.optimization_barrier((residual, cot_far))
+    cot_halves = dict(zip([0, *near, *far], [cot_own, *cot_near, *cot_far]))
+    cot_slots = [[cot_halves[k], swap(cot_halves[k])] for k in range(outer)]
     normed_slots = gather_slots(rms_norm(residual, norm_scales[1]).astype(BF16))
+    normed_joined = [jnp.concatenate(slot) for slot in normed_slots]
+    cot_joined = [jnp.concatenate(slot) for slot in cot_slots]
     bias_part = lax.dynamic_slice_in_dim(ffw_bias, along * hidden_part, hidden_part, 1)
-    bias_row = bias_part.reshape(2 * hidden_part)
-    hidden_slots, delta_slots, result_parts, delta_parts = [], [], [], []
-    for normed_two, cot in zip(normed_slots, cot_slots):
-        gate_up = mm(normed_two, ffw_in_full) + bias_row
-        hidden, hidden_back = jax.vjp(geglu, gate_up[:, :hidden_part], gate_up[:, hidden_part:])
-        hidden_low = hidden.astype(BF16)
-        delta_gate_up = jnp.concatenate(hidden_back(mm(cot, ffw_out_full_t)), axis=1).astype(BF16)
-        hidden_slots.append(hidden_low)
-        delta_slots.append(delta_gate_up)
-        delta_parts.append(mm_nt(delta_gate_up, ffw_in_full))
-    delta_normed_two = reduce_slots(delta_parts)
-    for hidden_low in hidden_slots:
-        result_parts.append(mm_nt(hidden_low, ffw_out_full_t))
-    normed_all, cot_all = jnp.concatenate(normed_slots), jnp.concatenate(cot_slots)
-    hidden_all, delta_all = jnp.concatenate(hidden_slots), jnp.concatenate(delta_slots)
-
-    def sum_inner(grad):
-        rows = grad.reshape(outer, inner, part_width, -1).transpose(1, 0, 2, 3)
-        own = lax.psum_scatter(
-            rows.reshape(width, -1).astype(BF16), "i", scatter_dimension=0, tiled=True
-        )
-        return spread(own.reshape(outer, part_width, -1), 0)
-
-    grad_ffw_out_t = sum_inner(mm_tn(cot_all, hidden_all))
-    ffw_out_grad = (
-        grad_ffw_out_t.transpose(0, 2, 1).reshape(hidden_half, part_width).astype(F32)
-    )
-    grad_ffw_in = sum_inner(mm_tn(normed_all, delta_all)).reshape(
-        outer, part_width, 2, hidden_part
-    )
-    ffw_in_grad = (
-        grad_ffw_in.transpose(2, 1, 0, 3).reshape(2, part_width, hidden_half).astype(F32)
-    )
-    bias_sum = jnp.sum(delta_all, axis=0, dtype=F32).reshape(2, hidden_part)
+    slots = range(outer)
+    hidden_of, delta_of, inner_sums, bias_sums, rows = [], [], [], [], None
+    for p, (start, size) in enumerate(cuts):
+        if rows is not None:
+            rows, normed_joined, cot_joined = lax.optimization_barrier(
+                (rows, normed_joined, cot_joined)
+            )
+            inner_sums.append(sum_inner(rows))
+        in_full, out_full = ffw_parts[p]
+        bias_row = bias_part[:, start : start + size].reshape(2 * size)
+        hiddens, deltas = [], []
+        for k in slots:
+            gate_up = mm(normed_joined[k], in_full) + bias_row
+            hidden, hidden_back = jax.vjp(geglu, gate_up[:, :size], gate_up[:, size:])
+            hiddens.append(hidden.astype(BF16))
+            deltas.append(
+                jnp.concatenate(hidden_back(mm(cot_joined[k], out_full)), axis=1).astype(BF16)
+            )
+        if p == len(cuts) - 1:
+            delta_parts = [
+                sum(mm_nt(d[k], w[0]) for d, w in zip(delta_of + [deltas], ffw_parts))
+                for k in slots
+            ]
+            sums = [both_cores(part) for part in delta_parts[1:] + delta_parts[:1]]
+            _, hiddens, deltas = lax.optimization_barrier((sums[0], hiddens, deltas))
+        hidden_of.append(hiddens)
+        delta_of.append(deltas)
+        bias_sums.append(
+            sum(jnp.sum(d, axis=0, dtype=F32) for d in deltas).reshape(2, size)
+        )
+        rows = grads_rows([list(zip(normed_slots, deltas)), list(zip(cot_slots, hiddens))])
+    inner_sums.append(sum_inner(rows))
+    delta_normed_two = reduce_slots(sums)
+    result_parts = [
+        sum(mm_nt(hidden_of[p][k], ffw_parts[p][1]) for p in range(len(cuts))) for k in slots
+    ]
+    result_parts = [both_cores(part) for part in result_parts]
+    result_parts = [result_parts[0]] + [part.astype(BF16) for part in result_parts[1:]]
+    delta_normed_two, result_parts, inner_sums[0] = lax.optimization_barrier(
+        (delta_normed_two, result_parts, inner_sums[0])
+    )
+    grads = [spread(inner_sums[0])]
     grad_ffw_bias = lax.dynamic_update_slice_in_dim(
-        jnp.zeros((2, hidden_half), F32), bias_sum, along * hidden_part, 1
-    )
-    result_half = residual + reduce_slots(result_parts) + out_bias[1]
-    result = join_halves(result_half, swap(result_half), core)
+        jnp.zeros((2, hidden_half), F32),
+        jnp.concatenate(bias_sums, axis=1),
+        along * hidden_part,
+        1,
+    )
 
     cot_half = half_of(cotangent, core).astype(F32)
     delta_res_norm, grad_scale_two = norm_back(residual, norm_scales[1], delta_normed_two)
@@ -322,15 +680,11 @@
     delta_half = delta_residual.astype(BF16)
     delta_mixed = join_halves(delta_half, swap(delta_half), core)
     delta_mixed_in = mm(delta_mixed, out_full_t)
-    grad_out_t = lax.psum_scatter(
-        mm_tn(delta_mixed, mixed_in).astype(BF16), DP, scatter_dimension=0, tiled=True
-    )
     delta_states = delta_mixed_in * branch_act
     (delta_branch_y,) = gelu_back(delta_mixed_in * states)
     delta_y_low = delta_branch_y.astype(BF16)
-    grad_branch_y = lax.psum_scatter(
-        mm_tn(normed_low, delta_y_low).astype(BF16), DP, scatter_dimension=0, tiled=True
-    )
+    oy_rows = grads_rows([[([delta_mixed], mixed_in)], [([normed_low], delta_y_low)]])
+    grad_oy_inner = sum_inner(oy_rows)
     alpha_next = jnp.concatenate([keep_rate[1:], jnp.ones((1, width_half), F32)], axis=0)
     suffix, local_adjoint = local_scan(alpha_next, delta_states, True)
     leaving = entering(keep_rate[0] * suffix[0], keep_rate[0] * local_adjoint[0], True)
@@ -347,16 +701,35 @@
     gate_rows = (
         grad_gate_weights.reshape(2, heads_half, count, block_size // count, block_size)
         .transpose(2, 0, 1, 3, 4)
-        .reshape(2 * heads_half * block_size, block_size)
+        .reshape(outer, inner, -1, width_half)
         .astype(BF16)
     )
-    gate_grad = lax.psum_scatter(gate_rows, DP, scatter_dimension=0, tiled=True)
-    gate_grad = gate_grad.reshape(2, heads_half, block_size // count, block_size).astype(F32)
     grad_gate_bias = jnp.sum(delta_gates, axis=1, dtype=F32)
     delta_conv = delta_conv_direct + jnp.einsum(
         "gthc,ghbc->thb", delta_blocks, gate_weights, preferred_element_type=F32
     ).reshape(tok_rows, width_half)
     rim_delta, rim_next_marks = from_behind((delta_conv[:rim_rows], seg_marks[:rim_rows]), -1)
+    rim_delta, inner_sums, result_parts = lax.optimization_barrier(
+        (rim_delta, inner_sums[1:], result_parts)
+    )
+    for k in range(1, len(cuts)):
+        grads.append(spread(inner_sums[k - 1]))
+    result_half = residual + reduce_direct(result_parts) + out_bias[1]
+    result = join_halves(result_half, swap(result_half), core)
+    ffw_in_grad = jnp.concatenate(
+        [
+            grad[:, :, : 2 * size].reshape(outer, part_width, 2, size)
+            for grad, (_, size) in zip(grads, cuts)
+        ],
+        axis=3,
+    )
+    ffw_in_grad = (
+        ffw_in_grad.transpose(2, 1, 0, 3).reshape(2, part_width, hidden_half).astype(F32)
+    )
+    ffw_out_grad = jnp.concatenate(
+        [grad[:, :, 2 * size :] for grad, (_, size) in zip(grads, cuts)], axis=2
+    )
+    ffw_out_grad = ffw_out_grad.transpose(0, 2, 1).reshape(hidden_half, part_width).astype(F32)
     padded_delta = jnp.concatenate([delta_conv, rim_delta], axis=0)
     next_marks = jnp.concatenate([seg_marks, rim_next_marks], axis=0)
     delta_branch_x = jnp.zeros_like(delta_conv)
@@ -370,9 +743,9 @@
         conv_weight_rows.append(jnp.sum(delta_conv * shifted_rows[offset], axis=0))
     grad_conv_bias = jnp.sum(delta_conv, axis=0)
     delta_x_low = delta_branch_x.astype(BF16)
-    grad_branch_x = lax.psum_scatter(
-        mm_tn(normed_low, delta_x_low).astype(BF16), DP, scatter_dimension=0, tiled=True
-    )
+    x_rows = grads_rows([[([normed_low], delta_x_low)]], gate_rows)
+    grad_x_inner = sum_inner(x_rows)
+    grad_oy = sum_outer(grad_oy_inner)
     delta_part = mm_nt(delta_x_low, branch_x_full) + mm_nt(delta_y_low, branch_y_full)
     delta_normed = half_of(delta_part, core) + swap(
         half_of(delta_part, 1 - core).astype(BF16)
@@ -400,7 +773,16 @@
         grad_decay,
         grad_ffw_bias.reshape(-1),
     ]
-    small = sum_over_all(jnp.concatenate(flat).reshape(-1, 128)).reshape(-1)
+    flat = jnp.concatenate(flat).reshape(-1, 128)
+    grad_x_inner, flat, input_grad, result, ffw_in_grad, ffw_out_grad, grad_oy = (
+        lax.optimization_barrier(
+            (grad_x_inner, flat, input_grad, result, ffw_in_grad, ffw_out_grad, grad_oy)
+        )
+    )
+    grad_x_gate = sum_outer(grad_x_inner)
+    grad_branch_x = grad_x_gate[:part_width]
+    gate_grad = grad_x_gate[part_width:].reshape(2, heads_half, block_size // count, block_size)
+    small = sum_over_all(flat).reshape(-1)
     at = 0
     taken = []
     for shape in (
@@ -422,8 +804,8 @@
     return (
         result,
         input_grad,
-        jnp.stack([grad_branch_x, grad_branch_y]).astype(F32),
-        grad_out_t.T.astype(F32),
+        jnp.stack([grad_branch_x, grad_oy[:, width_half:]]),
+        grad_oy[:, :width_half].T,
         ffw_in_grad,
         ffw_out_grad,
         scales,
@@ -478,6 +860,7 @@
         P(),
         P(None, "tensor"),
     )
+
     return jax.shard_map(
         per_device, mesh=grid, in_specs=in_specs, out_specs=out_specs, check_vma=False
     )

time: 1490 us -> 1160 us (0.78)
  waiting for transfers between devices: 804 us -> 348 us
  Pallas kernels: 14.4 us -> 289 us
  blocking collectives: 140 us -> 0 us
  starting transfers between devices: 53.8 us -> 108 us
  local copies, waits for them, and re-layouts: 183 us -> 129 us
  matrix products: 191 us -> 141 us
  other arithmetic: 77.3 us -> 121 us
    reduce_scatter x6 -> x4, waiting for transfers between devices: 298 us -> 0.03 us  [sum_inner(): lax.psum_scatter(rows.reshape(-1, rows.shape[-1]), 'i', scatter_dimension...]
    pallas_call x0 -> x7, Pallas kernels: none -> 274 us  [the longest x1 173 us: gather_weights(): pl.pallas_call(functools.partial(gather_kernel, outer, groups, parts), in...]
    ppermute x0 -> x12, waiting for transfers between devices: none -> 142 us  [the longest x3 57.4 us: reduce_direct(): lax.ppermute(halves[k], 'o', [(j, (j - k) % count) for j in range(count)])]
    ppermute x12 -> x6, waiting for transfers between devices: 225 us -> 128 us  [ring(): lax.ppermute(value, 'o', [(k, (k + 1) % count) for k in range(count)])]
    all_to_all x3 -> x2, waiting for transfers between devices: 106 us -> 22.1 us  [spread(): return lax.all_to_all(value, 'o', 0, 0, tiled=True)]
    all_gather x2 -> x0, blocking collectives: 80.8 us -> none  [entering(): every = lax.all_gather(jnp.stack([decay, state]), DP)]
    all_gather x5 -> x2, waiting for transfers between devices: 80.4 us -> 0.01 us  [gather_inner(): lax.all_gather(whole, 'i', axis=1, tiled=True).reshape(-1, whole.shape[-1])]
    all_to_all x1 -> x0, blocking collectives: 58.7 us -> none  [spread(): return lax.all_to_all(value, 'o', axis, axis, tiled=True)]
  transfers between devices with their start and end apart: 56 -> 56, of which waited for: 25 -> 18; matrix products, arithmetic and copies ran while one was open for 25% -> 31% of each run, Pallas kernels for 1% -> 10%
where the time goes in v2:
time: 1160 us; the launch traced here: 1150 us
  waiting for transfers between devices  348 us (30%)
  Pallas kernels  289 us (25%)
  matrix products  141 us (12%)
  local copies, waits for them, and re-layouts  129 us (11%)
  other arithmetic  121 us (10%)
  starting transfers between devices  108 us (9%)
  between operations  16.8 us (1%)
    pallas_call x1, Pallas kernels, gather_weights(): pl.pallas_call(functools.partial(gather_kernel, outer, groups, parts), in...  173 us
    dot_general x38, matrix products, dot(): lax.dot_general(a, b, ((contract[0], contract[1]), ((), ())), preferred_e...  134 us
    ppermute x6, waiting for transfers between devices, ring(): lax.ppermute(value, 'o', [(k, (k + 1) % count) for k in range(count)])  128 us
    pallas_call x4, Pallas kernels, grads_rows(): pl.pallas_call(functools.partial(grads_kernel, plan, added), grid=(outer,...  63.1 us
    ppermute x3, waiting for transfers between devices, reduce_direct(): lax.ppermute(halves[k], 'o', [(j, (j - k) % count) for j in range(count)])  57.4 us
    all_to_all x2, starting transfers between devices, spread(): return lax.all_to_all(value, 'o', 0, 0, tiled=True)  52.9 us
    ppermute x4, waiting for transfers between devices, sum_over_all(): lax.ppermute(value, DP, [(k, k ^ bit) for k in range(count)])  48.1 us
    ppermute x6, waiting for transfers between devices, sum_outer(): lax.ppermute(part, 'o', [(j, (j + k) % count) for j in range(count)])  46.7 us
  transfers between devices with their start and end apart: 56, of which 18 were waited for; matrix products, arithmetic and copies ran while one was open for 31% of the time, Pallas kernels for 10%

profile of v2, /device:TPU:0, one launch (start us, length us, event | category | flops | bytes accessed | tf_op | source)
XLA Modules:
  0.0 1151.1 jit_solution(9110428137351623619)
XLA Ops:
  23.8 173.5 %shard_map.271 = (bf16[4,4,160,1280]{3,2,1,0:T(8,128)(2,1)}, bf16[4,4,160,1280]{3,2,1,0:T(8,128)(2,1)}, bf16[4,4,160,1280]{3,2,1,0:T(8,128)(2,1)}, bf16[4,160,1536]{2,1,0:T(8,128)(2,1)}, bf16[4,160,1344]{2,1,0:T(8,128)(2,1)}) custom-call(bf16[160,1280]{1,0:T(8,128)(2,1)} %get-tuple-element.235.refs_0_, bf16[160,1280]{1,0:T(8,128)(2,1)} %get-tuple-element.234.refs_1_, ...), custom_call_target="tpu_custom_call" | custom-call | tf_op jit(solution)/shard_map/pallas_call | solution.py:312
  200.5 3.8 collective-permute-start.3
  209.6 3.4 collective-permute-start.1
  218.6 3.4 collective-permute-done.30
  223.3 6.1 add_convert_fusion
  236.6 5.6 copy.76
  244.7 4.3 fusion.64
  249.1 7.1 shard_map.272
  258.4 28.5 %shard_map.273 = f32[1,1280]{1,0:T(1,128)} custom-call(f32[2,1280]{1,0:T(2,128)} %pad_maximum_fusion.21.ends_ref), custom_call_target="tpu_custom_call" | custom-call | tf_op jit(solution)/shard_map/pallas_call | solution.py:143
  287.6 9.6 multiply_convert_fusion.1
  297.2 5.3 fusion.204
  315.2 37.8 %collective-permute-done.5.refs_18_ = bf16[192,2560]{1,0:T(8,128)(2,1)S(1)} collective-permute-done((bf16[192,2560]{1,0:T(8,128)(2,1)}, bf16[192,2560]{1,0:T(8,128)(2,1)S(1)}, u32[]{:S(2)}, u32[]{:S(2)}) %collective-permute-start.5) | collective-permute-done | bytes 983072 | tf_op jit(solution)/shard_map/ppermute | solution.py:453
  356.5 22.5 %collective-permute-done.8.refs_3_ = bf16[192,2560]{1,0:T(8,128)(2,1)S(1)} collective-permute-done((bf16[192,2560]{1,0:T(8,128)(2,1)S(1)}, bf16[192,2560]{1,0:T(8,128)(2,1)S(1)}, u32[]{:S(2)}, u32[]{:S(2)}) %collective-permute-start.8) | collective-permute-done | bytes 983072 | tf_op jit(solution)/shard_map/ppermute | solution.py:25
  381.8 21.5 %collective-permute-done.11.refs_6_ = bf16[192,2560]{1,0:T(8,128)(2,1)S(1)} collective-permute-done((bf16[192,2560]{1,0:T(8,128)(2,1)S(1)}, bf16[192,2560]{1,0:T(8,128)(2,1)S(1)}, u32[]{:S(2)}, u32[]{:S(2)}) %collective-permute-start.11) | collective-permute-done | bytes 983072 | tf_op jit(solution)/shard_map/ppermute | solution.py:25
  406.2 20.5 %collective-permute-done.14.refs_9_ = bf16[192,2560]{1,0:T(8,128)(2,1)S(1)} collective-permute-done((bf16[192,2560]{1,0:T(8,128)(2,1)S(1)}, bf16[192,2560]{1,0:T(8,128)(2,1)S(1)}, u32[]{:S(2)}, u32[]{:S(2)}) %collective-permute-start.14) | collective-permute-done | bytes 983072 | tf_op jit(solution)/shard_map/ppermute | solution.py:25
  431.9 5.4 convolution_add_fusion.11
  443.5 4.1 fusion.104
  458.1 4.0 fusion.90
  463.9 22.2 %shard_map.274 = bf16[4,4,160,1536]{3,2,1,0:T(8,128)(2,1)} custom-call(bf16[192,2560]{1,0:T(8,128)(2,1)} %copy-done.21, bf16[192,2560]{1,0:T(8,128)(2,1)} %copy-done.70, bf16[384,1024]{1,0:T(8,128)(2,1)} %pad_maximum_fusion.12.refs_2_, bf16[192,2560]{1,0:T(8,128)(2,1)} %copy-done.60, bf16[192,2560]{1,0:T(8,128)(2,1)} %copy-done.64, ...), custom_call_target="tpu_custom_call" | custom-call | flops 12079595520 | bytes 20447232 | tf_op jit(solution)/shard_map/pallas_call | solution.py:381
  487.3 5.9 convolution_add_fusion.15
  493.5 4.2 fusion.139
  505.2 4.0 fusion.132
  509.4 4.2 fusion.74
  513.6 5.1 convolution_add_fusion.6
  519.9 4.4 convolution_add_fusion.17
  527.0 4.1 fusion.76
  531.1 4.5 convolution_add_fusion.7
  537.4 4.4 fusion.81
  544.0 4.0 fusion.118
  553.6 21.6 %shard_map.277 = bf16[4,4,160,1344]{3,2,1,0:T(8,128)(2,1)} custom-call(bf16[192,2560]{1,0:T(8,128)(2,1)} %copy-done.21, bf16[192,2560]{1,0:T(8,128)(2,1)} %copy-done.70, bf16[384,896]{1,0:T(8,128)(2,1)} %copy-done.29, bf16[192,2560]{1,0:T(8,128)(2,1)} %copy-done.60, bf16[192,2560]{1,0:T(8,128)(2,1)} %copy-done.64, bf16[384,896]{1,0:T(8,128)(2,1)} %copy-done.23, ...), custom_call_target="tpu_custom_call" | custom-call | flops 10569646080 | bytes 18874368 | tf_op jit(solution)/shard_map/pallas_call | solution.py:381
  593.0 18.1 %collective-permute-done.21 = bf16[192,2560]{1,0:T(8,128)(2,1)S(1)} collective-permute-done((bf16[192,2560]{1,0:T(8,128)(2,1)S(1)}, bf16[192,2560]{1,0:T(8,128)(2,1)S(1)}, u32[]{:S(2)}, u32[]{:S(2)}) %collective-permute-start.21) | collective-permute-done | bytes 983072 | tf_op jit(solution)/shard_map/ppermute | solution.py:25
  615.5 23.1 %collective-permute-done.22 = bf16[192,2560]{1,0:T(8,128)(2,1)S(1)} collective-permute-done((bf16[192,2560]{1,0:T(8,128)(2,1)S(1)}, bf16[192,2560]{1,0:T(8,128)(2,1)S(1)}, u32[]{:S(2)}, u32[]{:S(2)}) %collective-permute-start.22) | collective-permute-done | bytes 983072 | tf_op jit(solution)/shard_map/ppermute | solution.py:25
  641.9 22.4 %collective-permute-done.23 = bf16[192,2560]{1,0:T(8,128)(2,1)S(1)} collective-permute-done((bf16[192,2560]{1,0:T(8,128)(2,1)S(1)}, bf16[192,2560]{1,0:T(8,128)(2,1)S(1)}, u32[]{:S(2)}, u32[]{:S(2)}) %collective-permute-start.23) | collective-permute-done | bytes 983072 | tf_op jit(solution)/shard_map/ppermute | solution.py:25
  679.7 8.9 convert_reduce_fusion.2
  688.6 11.2 shard_map.279
  703.4 7.4 shard_map.275
  712.3 9.2 shard_map.276
  722.2 8.6 multiply_reduce_fusion
  741.3 3.6 fusion.65
  748.0 7.5 multiply_reduce_fusion.1
  758.9 3.5 convert_element_type.308.refs_2_
  762.5 7.6 convert_reduce_fusion.3
  770.2 8.1 shard_map.278
  783.1 6.7 all-to-all-start
  789.8 5.3 fusion.205
  795.1 5.0 convolution_add_fusion.4
  804.0 3.8 collective-permute-start.34
  814.2 21.2 %all-to-all-done = bf16[4,160,1536]{2,1,0:T(8,128)(2,1)} async-done(((bf16[4,160,1536]{2,1,0:T(8,128)(2,1)}), bf16[4,160,1536]{2,1,0:T(8,128)(2,1)}, u32[]{:S(2)}, u32[]{:S(2)}) %all-to-all-start) | async-done | bytes 1966112 | tf_op jit(solution)/shard_map/all_to_all | solution.py:480
  835.4 46.2 %all-to-all-start.1 = ((bf16[4,160,1344]{2,1,0:T(8,128)(2,1)}), bf16[4,160,1344]{2,1,0:T(8,128)(2,1)}, u32[]{:S(2)}, u32[]{:S(2)}) async-start(bf16[4,160,1344]{2,1,0:T(8,128)(2,1)} %bitcast.233), calls=%async_computation.4 | async-start | bytes 3604480 | tf_op jit(solution)/shard_map/all_to_all | solution.py:480
  881.6 57.4 %collective-permute-done.35 = bf16[192,2560]{1,0:T(8,128)(2,1)} collective-permute-done((bf16[192,2560]{1,0:T(8,128)(2,1)}, bf16[192,2560]{1,0:T(8,128)(2,1)}, u32[]{:S(2)}, u32[]{:S(2)}) %collective-permute-start.35) | collective-permute-done | bytes 983072 | tf_op jit(solution)/shard_map/ppermute | solution.py:474
  939.0 8.2 add_add_fusion
  962.0 4.2 reshape.252
  968.7 5.0 reshape.242
  973.7 3.7 convert_bitcast_fusion
  977.3 5.6 copy.92
  983.0 7.4 reshape.251
  990.4 3.7 broadcast_select_fusion.1
  994.1 4.4 broadcast_select_fusion.3
  1010.2 13.3 %collective-permute-done.38 = bf16[160,2560]{1,0:T(8,128)(2,1)S(1)} collective-permute-done((bf16[160,2560]{1,0:T(8,128)(2,1)S(1)}, bf16[160,2560]{1,0:T(8,128)(2,1)S(1)}, u32[]{:S(2)}, u32[]{:S(2)}) %collective-permute-start.38) | collective-permute-done | bytes 819232 | tf_op jit(solution)/shard_map/ppermute | solution.py:499
  1023.5 33.4 %collective-permute-done.39 = bf16[160,2560]{1,0:T(8,128)(2,1)S(1)} collective-permute-done((bf16[160,2560]{1,0:T(8,128)(2,1)S(1)}, bf16[160,2560]{1,0:T(8,128)(2,1)S(1)}, u32[]{:S(2)}, u32[]{:S(2)}) %collective-permute-start.39) | collective-permute-done | bytes 819232 | tf_op jit(solution)/shard_map/ppermute | solution.py:499
  1059.2 4.1 collective-permute-done.44
  1064.9 3.4 collective-permute-done.45
  1068.4 17.3 %collective-permute-start.46 = (f32[240,128]{1,0:T(8,128)S(1)}, f32[240,128]{1,0:T(8,128)S(1)}, u32[]{:S(2)}, u32[]{:S(2)}) collective-permute-start(f32[240,128]{1,0:T(8,128)S(1)} %add.588), channel_id=1, source_target_pairs={{0,8},{2,10},{4,12},{6,14},{8,0},{10,2},{12,4},{14,6},{16,24},{18,... | collective-permute-start | bytes 368648 | tf_op jit(solution)/shard_map/ppermute | solution.py:37
  1095.3 40.6 %collective-permute-done.47 = f32[240,128]{1,0:T(8,128)S(1)} collective-permute-done((f32[240,128]{1,0:T(8,128)S(1)}, f32[240,128]{1,0:T(8,128)S(1)}, u32[]{:S(2)}, u32[]{:S(2)}) %collective-permute-start.47) | collective-permute-done | bytes 122912 | tf_op jit(solution)/shard_map/ppermute | solution.py:37
  (603 shorter events, 240.4 us)
Async XLA Ops:
  7.2 224.5 %copy-start = (bf16[2,5,256,256]{3,2,1,0:T(8,128)(2,1)S(1)}, bf16[2,5,256,256]{3,2,1,0:T(8,128)(2,1)}, u32[]{:S(2)}) copy-start(bf16[2,5,256,256]{3,2,1,0:T(8,128)(2,1)} %param.27) | copy-start | bytes 3932164
  7.2 424.7 %all-gather.3.cloned.1.call-start = ((), (), s32[]{:S(2)}) async-start(), calls=%async_computation.6 | async-start | bytes 9830400 | tf_op jit(solution)/shard_map/all_gather | solution.py:484
  197.4 289.9 %all-gather.5.cloned.1.call-start = ((), (), s32[]{:S(2)}) async-start(), calls=%async_computation.7 | async-start | bytes 9011200 | tf_op jit(solution)/shard_map/all_gather | solution.py:484
  200.5 57.2 %collective-permute-start.2 = (bf16[192,2560]{1,0:T(8,128)(2,1)}, bf16[192,2560]{1,0:T(8,128)(2,1)}, u32[]{:S(2)}, u32[]{:S(2)}) collective-permute-start(bf16[192,2560]{1,0:T(8,128)(2,1)} %get-tuple-element.80.refs_12_), channel_id=1, source_target_pairs={{0,8},{8,16},{16,24},{24,0},{1,9},{9,17},{17,25},{25,1},{2,10},{10... | collective-permute-start | bytes 2949128 | tf_op jit(solution)/shard_map/ppermute | solution.py:453
  200.5 57.2 %collective-permute-start.3 = (bf16[192,2560]{1,0:T(8,128)(2,1)}, bf16[192,2560]{1,0:T(8,128)(2,1)}, u32[]{:S(2)}, u32[]{:S(2)}) collective-permute-start(bf16[192,2560]{1,0:T(8,128)(2,1)} %get-tuple-element.80.refs_12_), channel_id=1, source_target_pairs={{0,24},{8,0},{16,8},{24,16},{1,25},{9,1},{17,9},{25,17},{2,26},{10... | collective-permute-start | bytes 2949128 | tf_op jit(solution)/shard_map/ppermute | solution.py:453
  204.5 148.7 %copy-start.98 = (f32[2560]{0:T(1024)}, f32[2560]{0:T(1024)S(1)}, u32[]{:S(2)}) copy-start(f32[2560]{0:T(1024)S(1)} %get-tuple-element.136) | copy-start | bytes 30724
  209.6 13.2 %collective-permute-start.1 = (f32[3,1280]{1,0:T(4,128)S(1)}, f32[3,1280]{1,0:T(4,128)S(1)}, u32[]{:S(2)}, u32[]{:S(2)}) collective-permute-start(f32[3,1280]{1,0:T(4,128)S(1)} %slice.536), channel_id=1, source_target_pairs={{0,2},{2,4},{4,6},{6,8},{8,10},{10,12},{12,14},{14,16},{16,18},{18... | collective-permute-start | bytes 46088 | tf_op jit(solution)/shard_map/ppermute | solution.py:31
  213.0 5.6 collective-permute-start
  216.4 5.6 collective-permute-start.30
  305.1 6.8 collective-permute-start.4
  305.1 362.0 %reduce-scatter.5.cloned.1.call-start = ((), (), s32[]{:S(2)}) async-start(), calls=%async_computation.8 | async-start | bytes 9830400 | tf_op jit(solution)/shard_map/reduce_scatter | solution.py:488
  306.6 46.3 %collective-permute-start.5 = (bf16[192,2560]{1,0:T(8,128)(2,1)}, bf16[192,2560]{1,0:T(8,128)(2,1)S(1)}, u32[]{:S(2)}, u32[]{:S(2)}) collective-permute-start(bf16[192,2560]{1,0:T(8,128)(2,1)} %get-tuple-element.80.refs_12_), channel_id=1, source_target_pairs={{0,16},{8,24},{16,0},{24,8},{1,17},{9,25},{17,1},{25,9},{2,18},{10... | collective-permute-start | bytes 2949128 | tf_op jit(solution)/shard_map/ppermute | solution.py:453
  308.5 70.5 %collective-permute-start.6 = (bf16[192,2560]{1,0:T(8,128)(2,1)}, bf16[192,2560]{1,0:T(8,128)(2,1)S(1)}, u32[]{:S(2)}, u32[]{:S(2)}) collective-permute-start(bf16[192,2560]{1,0:T(8,128)(2,1)} %get-tuple-element.80.refs_12_), channel_id=1, source_target_pairs={{0,1},{1,0},{2,3},{3,2},{4,5},{5,4},{6,7},{7,6},{8,9},{9,8},{10,11... | collective-permute-start | bytes 2949128 | tf_op jit(solution)/shard_map/ppermute | solution.py:20
  308.8 47.5 %collective-permute-start.16 = (bf16[192,2560]{1,0:T(8,128)(2,1)}, bf16[192,2560]{1,0:T(8,128)(2,1)S(1)}, u32[]{:S(2)}, u32[]{:S(2)}) collective-permute-start(bf16[192,2560]{1,0:T(8,128)(2,1)} %collective-permute-done.3.refs_21_), channel_id=1, source_target_pairs={{0,1},{1,0},{2,3},{3,2},{4,5},{5,4},{6,7},{7,6},{8,9},{9,8},{10,11... | collective-permute-start | bytes 2949128 | tf_op jit(solution)/shard_map/ppermute | solution.py:20
  309.0 47.3 %collective-permute-start.10 = (bf16[192,2560]{1,0:T(8,128)(2,1)}, bf16[192,2560]{1,0:T(8,128)(2,1)S(1)}, u32[]{:S(2)}, u32[]{:S(2)}) collective-permute-start(bf16[192,2560]{1,0:T(8,128)(2,1)} %collective-permute-done.2.refs_15_), channel_id=1, source_target_pairs={{0,1},{1,0},{2,3},{3,2},{4,5},{5,4},{6,7},{7,6},{8,9},{9,8},{10,11... | collective-permute-start | bytes 2949128 | tf_op jit(solution)/shard_map/ppermute | solution.py:20
  315.2 38.2 %copy-start.1 = (f32[192,2560]{1,0:T(8,128)}, f32[192,2560]{1,0:T(8,128)S(1)}, u32[]{:S(2)}) copy-start(f32[192,2560]{1,0:T(8,128)S(1)} %get-tuple-element.81) | copy-start | bytes 5898244
  353.4 102.5 %copy-start.21 = (bf16[192,2560]{1,0:T(8,128)(2,1)}, bf16[192,2560]{1,0:T(8,128)(2,1)S(1)}, u32[]{:S(2)}) copy-start(bf16[192,2560]{1,0:T(8,128)(2,1)S(1)} %multiply_convert_fusion.refs_0_) | copy-start | bytes 2949124
  353.5 25.6 %collective-permute-start.8 = (bf16[192,2560]{1,0:T(8,128)(2,1)S(1)}, bf16[192,2560]{1,0:T(8,128)(2,1)S(1)}, u32[]{:S(2)}, u32[]{:S(2)}) collective-permute-start(bf16[192,2560]{1,0:T(8,128)(2,1)S(1)} %multiply_convert_fusion.refs_0_), channel_id=1, source_target_pairs={{0,8},{8,16},{16,24},{24,0},{1,9},{9,17},{17,25},{25,1},{2,10},{10... | collective-permute-start | bytes 2949128 | tf_op jit(solution)/shard_map/ppermute | solution.py:25
  356.5 46.8 %collective-permute-start.13 = (bf16[192,2560]{1,0:T(8,128)(2,1)S(1)}, bf16[192,2560]{1,0:T(8,128)(2,1)S(1)}, u32[]{:S(2)}, u32[]{:S(2)}) collective-permute-start(bf16[192,2560]{1,0:T(8,128)(2,1)S(1)} %collective-permute-done.5.refs_18_), channel_id=1, source_target_pairs={{0,1},{1,0},{2,3},{3,2},{4,5},{5,4},{6,7},{7,6},{8,9},{9,8},{10,11... | collective-permute-start | bytes 2949128 | tf_op jit(solution)/shard_map/ppermute | solution.py:20
  379.0 24.3 %collective-permute-start.11 = (bf16[192,2560]{1,0:T(8,128)(2,1)S(1)}, bf16[192,2560]{1,0:T(8,128)(2,1)S(1)}, u32[]{:S(2)}, u32[]{:S(2)}) collective-permute-start(bf16[192,2560]{1,0:T(8,128)(2,1)S(1)} %collective-permute-done.8.refs_3_), channel_id=1, source_target_pairs={{0,8},{8,16},{16,24},{24,0},{1,9},{9,17},{17,25},{25,1},{2,10},{10... | collective-permute-start | bytes 2949128 | tf_op jit(solution)/shard_map/ppermute | solution.py:25
  380.1 24.3 %collective-permute-start.7 = (bf16[192,2560]{1,0:T(8,128)(2,1)S(1)}, bf16[192,2560]{1,0:T(8,128)(2,1)S(1)}, u32[]{:S(2)}, u32[]{:S(2)}) collective-permute-start(bf16[192,2560]{1,0:T(8,128)(2,1)S(1)} %multiply_convert_fusion.refs_0_), channel_id=1, source_target_pairs={{0,1},{1,0},{2,3},{3,2},{4,5},{5,4},{6,7},{7,6},{8,9},{9,8},{10,11... | collective-permute-start | bytes 2949128 | tf_op jit(solution)/shard_map/ppermute | solution.py:20
  381.2 45.5 %collective-permute-start.9 = (bf16[192,2560]{1,0:T(8,128)(2,1)S(1)}, bf16[192,2560]{1,0:T(8,128)(2,1)S(1)}, u32[]{:S(2)}, u32[]{:S(2)}) collective-permute-start(bf16[192,2560]{1,0:T(8,128)(2,1)S(1)} %collective-permute-done.8.refs_3_), channel_id=1, source_target_pairs={{0,1},{1,0},{2,3},{3,2},{4,5},{5,4},{6,7},{7,6},{8,9},{9,8},{10,11... | collective-permute-start | bytes 2949128 | tf_op jit(solution)/shard_map/ppermute | solution.py:20
  403.3 23.4 %collective-permute-start.14 = (bf16[192,2560]{1,0:T(8,128)(2,1)S(1)}, bf16[192,2560]{1,0:T(8,128)(2,1)S(1)}, u32[]{:S(2)}, u32[]{:S(2)}) collective-permute-start(bf16[192,2560]{1,0:T(8,128)(2,1)S(1)} %collective-permute-done.11.refs_6_), channel_id=1, source_target_pairs={{0,8},{8,16},{16,24},{24,0},{1,9},{9,17},{17,25},{25,1},{2,10},{10... | collective-permute-start | bytes 2949128 | tf_op jit(solution)/shard_map/ppermute | solution.py:25
  406.1 21.8 %collective-permute-start.12 = (bf16[192,2560]{1,0:T(8,128)(2,1)S(1)}, bf16[192,2560]{1,0:T(8,128)(2,1)S(1)}, u32[]{:S(2)}, u32[]{:S(2)}) collective-permute-start(bf16[192,2560]{1,0:T(8,128)(2,1)S(1)} %collective-permute-done.11.refs_6_), channel_id=1, source_target_pairs={{0,1},{1,0},{2,3},{3,2},{4,5},{5,4},{6,7},{7,6},{8,9},{9,8},{10,11... | collective-permute-start | bytes 2949128 | tf_op jit(solution)/shard_map/ppermute | solution.py:20
  426.7 2.6 collective-permute-start.15
  440.2 86.8 %copy-start.39 = (bf16[384,512]{1,0:T(8,128)(2,1)}, bf16[384,512]{1,0:T(8,128)(2,1)S(1)}, u32[]{:S(2)}) copy-start(bf16[384,512]{1,0:T(8,128)(2,1)S(1)} %get-tuple-element.173) | copy-start | bytes 1179652
  440.2 86.8 %copy-start.40 = (bf16[384,512]{1,0:T(8,128)(2,1)}, bf16[384,512]{1,0:T(8,128)(2,1)S(1)}, u32[]{:S(2)}) copy-start(bf16[384,512]{1,0:T(8,128)(2,1)S(1)} %get-tuple-element.174) | copy-start | bytes 1179652
  447.6 61.8 %copy-start.41 = (bf16[384,512]{1,0:T(8,128)(2,1)}, bf16[384,512]{1,0:T(8,128)(2,1)S(1)}, u32[]{:S(2)}) copy-start(bf16[384,512]{1,0:T(8,128)(2,1)S(1)} %get-tuple-element.175) | copy-start | bytes 1179652
  486.2 276.3 %reduce-scatter.7.cloned.1.call-start = ((), (), s32[]{:S(2)}) async-start(), calls=%async_computation.9 | async-start | bytes 9011200 | tf_op jit(solution)/shard_map/reduce_scatter | solution.py:488
  502.7 49.5 %collective-permute-start.20 = (bf16[192,2560]{1,0:T(8,128)(2,1)S(1)}, bf16[192,2560]{1,0:T(8,128)(2,1)S(1)}, u32[]{:S(2)}, u32[]{:S(2)}) collective-permute-start(bf16[192,2560]{1,0:T(8,128)(2,1)S(1)} %slice.939), channel_id=1, source_target_pairs={{0,1},{1,0},{2,3},{3,2},{4,5},{5,4},{6,7},{7,6},{8,9},{9,8},{10,11... | collective-permute-start | bytes 2949128 | tf_op jit(solution)/shard_map/ppermute | solution.py:20
  519.9 72.8 %collective-permute-start.19 = (bf16[192,2560]{1,0:T(8,128)(2,1)}, bf16[192,2560]{1,0:T(8,128)(2,1)}, u32[]{:S(2)}, u32[]{:S(2)}) collective-permute-start(bf16[192,2560]{1,0:T(8,128)(2,1)} %slice.940), channel_id=1, source_target_pairs={{0,1},{1,0},{2,3},{3,2},{4,5},{5,4},{6,7},{7,6},{8,9},{9,8},{10,11... | collective-permute-start | bytes 2949128 | tf_op jit(solution)/shard_map/ppermute | solution.py:20
  536.9 78.6 %collective-permute-start.18 = (bf16[192,2560]{1,0:T(8,128)(2,1)}, bf16[192,2560]{1,0:T(8,128)(2,1)S(1)}, u32[]{:S(2)}, u32[]{:S(2)}) collective-permute-start(bf16[192,2560]{1,0:T(8,128)(2,1)} %slice.941), channel_id=1, source_target_pairs={{0,1},{1,0},{2,3},{3,2},{4,5},{5,4},{6,7},{7,6},{8,9},{9,8},{10,11... | collective-permute-start | bytes 2949128 | tf_op jit(solution)/shard_map/ppermute | solution.py:20
  552.2 89.7 %collective-permute-start.17 = (bf16[192,2560]{1,0:T(8,128)(2,1)}, bf16[192,2560]{1,0:T(8,128)(2,1)}, u32[]{:S(2)}, u32[]{:S(2)}) collective-permute-start(bf16[192,2560]{1,0:T(8,128)(2,1)} %slice.942), channel_id=1, source_target_pairs={{0,1},{1,0},{2,3},{3,2},{4,5},{5,4},{6,7},{7,6},{8,9},{9,8},{10,11... | collective-permute-start | bytes 2949128 | tf_op jit(solution)/shard_map/ppermute | solution.py:20
  575.3 423.2 %reduce-scatter.11.cloned.1.call-start = ((), (), s32[]{:S(2)}) async-start(), calls=%async_computation.11 | async-start | bytes 16384000 | tf_op jit(solution)/shard_map/reduce_scatter | solution.py:488
  585.2 25.8 %collective-permute-start.21 = (bf16[192,2560]{1,0:T(8,128)(2,1)S(1)}, bf16[192,2560]{1,0:T(8,128)(2,1)S(1)}, u32[]{:S(2)}, u32[]{:S(2)}) collective-permute-start(bf16[192,2560]{1,0:T(8,128)(2,1)S(1)} %copy-done.72), channel_id=1, source_target_pairs={{0,8},{8,16},{16,24},{24,0},{1,9},{9,17},{17,25},{25,1},{2,10},{10... | collective-permute-start | bytes 2949128 | tf_op jit(solution)/shard_map/ppermute | solution.py:25
  587.8 24.9 %collective-permute-start.27 = (bf16[192,2560]{1,0:T(8,128)(2,1)S(1)}, bf16[192,2560]{1,0:T(8,128)(2,1)S(1)}, u32[]{:S(2)}, u32[]{:S(2)}) collective-permute-start(bf16[192,2560]{1,0:T(8,128)(2,1)S(1)} %slice.935), channel_id=1, source_target_pairs={{0,1},{1,0},{2,3},{3,2},{4,5},{5,4},{6,7},{7,6},{8,9},{9,8},{10,11... | collective-permute-start | bytes 2949128 | tf_op jit(solution)/shard_map/ppermute | solution.py:20
  592.7 21.2 %collective-permute-start.26 = (bf16[192,2560]{1,0:T(8,128)(2,1)S(1)}, bf16[192,2560]{1,0:T(8,128)(2,1)S(1)}, u32[]{:S(2)}, u32[]{:S(2)}) collective-permute-start(bf16[192,2560]{1,0:T(8,128)(2,1)S(1)} %slice.936), channel_id=1, source_target_pairs={{0,1},{1,0},{2,3},{3,2},{4,5},{5,4},{6,7},{7,6},{8,9},{9,8},{10,11... | collective-permute-start | bytes 2949128 | tf_op jit(solution)/shard_map/ppermute | solution.py:20
  611.0 28.2 %collective-permute-start.25 = (bf16[192,2560]{1,0:T(8,128)(2,1)S(1)}, bf16[192,2560]{1,0:T(8,128)(2,1)S(1)}, u32[]{:S(2)}, u32[]{:S(2)}) collective-permute-start(bf16[192,2560]{1,0:T(8,128)(2,1)S(1)} %slice.937), channel_id=1, source_target_pairs={{0,1},{1,0},{2,3},{3,2},{4,5},{5,4},{6,7},{7,6},{8,9},{9,8},{10,11... | collective-permute-start | bytes 2949128 | tf_op jit(solution)/shard_map/ppermute | solution.py:20
  612.6 26.0 %collective-permute-start.22 = (bf16[192,2560]{1,0:T(8,128)(2,1)S(1)}, bf16[192,2560]{1,0:T(8,128)(2,1)S(1)}, u32[]{:S(2)}, u32[]{:S(2)}) collective-permute-start(bf16[192,2560]{1,0:T(8,128)(2,1)S(1)} %fusion.45), channel_id=1, source_target_pairs={{0,8},{8,16},{16,24},{24,0},{1,9},{9,17},{17,25},{25,1},{2,10},{10... | collective-permute-start | bytes 2949128 | tf_op jit(solution)/shard_map/ppermute | solution.py:25
  613.9 26.5 %collective-permute-start.24 = (bf16[192,2560]{1,0:T(8,128)(2,1)S(1)}, bf16[192,2560]{1,0:T(8,128)(2,1)S(1)}, u32[]{:S(2)}, u32[]{:S(2)}) collective-permute-start(bf16[192,2560]{1,0:T(8,128)(2,1)S(1)} %slice.938), channel_id=1, source_target_pairs={{0,1},{1,0},{2,3},{3,2},{4,5},{5,4},{6,7},{7,6},{8,9},{9,8},{10,11... | collective-permute-start | bytes 2949128 | tf_op jit(solution)/shard_map/ppermute | solution.py:20
  639.0 25.3 %collective-permute-start.23 = (bf16[192,2560]{1,0:T(8,128)(2,1)S(1)}, bf16[192,2560]{1,0:T(8,128)(2,1)S(1)}, u32[]{:S(2)}, u32[]{:S(2)}) collective-permute-start(bf16[192,2560]{1,0:T(8,128)(2,1)S(1)} %fusion.47), channel_id=1, source_target_pairs={{0,8},{8,16},{16,24},{24,0},{1,9},{9,17},{17,25},{25,1},{2,10},{10... | collective-permute-start | bytes 2949128 | tf_op jit(solution)/shard_map/ppermute | solution.py:25
  672.3 2.9 collective-permute-start.28
  699.8 358.6 %reduce-scatter.9.cloned.1.call-start = ((), (), s32[]{:S(2)}) async-start(), calls=%async_computation.10 | async-start | bytes 9830400 | tf_op jit(solution)/shard_map/reduce_scatter | solution.py:488
  755.5 6.9 collective-permute-start.29
  783.1 52.3 %all-to-all-start = ((bf16[4,160,1536]{2,1,0:T(8,128)(2,1)}), bf16[4,160,1536]{2,1,0:T(8,128)(2,1)}, u32[]{:S(2)}, u32[]{:S(2)}) async-start(bf16[4,160,1536]{2,1,0:T(8,128)(2,1)} %bitcast.226), calls=%async_computation.3 | async-start | bytes 3932160 | tf_op jit(solution)/shard_map/all_to_all | solution.py:480
  801.2 9.9 collective-permute-start.31
  804.0 77.6 %collective-permute-start.34 = (bf16[192,2560]{1,0:T(8,128)(2,1)}, bf16[192,2560]{1,0:T(8,128)(2,1)}, u32[]{:S(2)}, u32[]{:S(2)}) collective-permute-start(bf16[192,2560]{1,0:T(8,128)(2,1)} %fusion.43), channel_id=1, source_target_pairs={{0,24},{8,0},{16,8},{24,16},{1,25},{9,1},{17,9},{25,17},{2,26},{10... | collective-permute-start | bytes 2949128 | tf_op jit(solution)/shard_map/ppermute | solution.py:474
  807.8 131.2 %collective-permute-start.35 = (bf16[192,2560]{1,0:T(8,128)(2,1)}, bf16[192,2560]{1,0:T(8,128)(2,1)}, u32[]{:S(2)}, u32[]{:S(2)}) collective-permute-start(bf16[192,2560]{1,0:T(8,128)(2,1)} %fusion.42), channel_id=1, source_target_pairs={{0,16},{8,24},{16,0},{24,8},{1,17},{9,25},{17,1},{25,9},{2,18},{10... | collective-permute-start | bytes 2949128 | tf_op jit(solution)/shard_map/ppermute | solution.py:474
  807.8 131.2 %collective-permute-start.36 = (bf16[192,2560]{1,0:T(8,128)(2,1)}, bf16[192,2560]{1,0:T(8,128)(2,1)}, u32[]{:S(2)}, u32[]{:S(2)}) collective-permute-start(bf16[192,2560]{1,0:T(8,128)(2,1)} %fusion.41), channel_id=1, source_target_pairs={{0,8},{8,16},{16,24},{24,0},{1,9},{9,17},{17,25},{25,1},{2,10},{10... | collective-permute-start | bytes 2949128 | tf_op jit(solution)/shard_map/ppermute | solution.py:474
  814.0 124.9 %copy-start.115 = (f32[2560]{0:T(1024)S(1)}, f32[2560]{0:T(1024)}, u32[]{:S(2)}) copy-start(f32[2560]{0:T(1024)} %get-tuple-element.134) | copy-start | bytes 30724
  814.1 133.6 %collective-permute-start.32 = (f32[4,2560]{1,0:T(4,128)S(1)}, f32[4,2560]{1,0:T(4,128)S(1)}, u32[]{:S(2)}, u32[]{:S(2)}) collective-permute-start(f32[4,2560]{1,0:T(4,128)S(1)} %pad_maximum_fusion.20), channel_id=1, source_target_pairs={{0,1},{1,0},{2,3},{3,2},{4,5},{5,4},{6,7},{7,6},{8,9},{9,8},{10,11... | collective-permute-start | bytes 122888 | tf_op jit(solution)/shard_map/ppermute | solution.py:20
  835.4 122.0 %all-to-all-start.1 = ((bf16[4,160,1344]{2,1,0:T(8,128)(2,1)}), bf16[4,160,1344]{2,1,0:T(8,128)(2,1)}, u32[]{:S(2)}, u32[]{:S(2)}) async-start(bf16[4,160,1344]{2,1,0:T(8,128)(2,1)} %bitcast.233), calls=%async_computation.4 | async-start | bytes 3604480 | tf_op jit(solution)/shard_map/all_to_all | solution.py:480
  947.2 43.2 %collective-permute-start.37 = (f32[192,2560]{1,0:T(8,128)}, f32[192,2560]{1,0:T(8,128)}, u32[]{:S(2)}, u32[]{:S(2)}) collective-permute-start(f32[192,2560]{1,0:T(8,128)} %get-tuple-element.192), channel_id=1, source_target_pairs={{0,1},{1,0},{2,3},{3,2},{4,5},{5,4},{6,7},{7,6},{8,9},{9,8},{10,11... | collective-permute-start | bytes 5898248 | tf_op jit(solution)/shard_map/ppermute | solution.py:20
  947.2 46.9 %collective-permute-start.33 = (f32[192,2560]{1,0:T(8,128)}, f32[192,2560]{1,0:T(8,128)}, u32[]{:S(2)}, u32[]{:S(2)}) collective-permute-start(f32[192,2560]{1,0:T(8,128)} %get-tuple-element.193), channel_id=1, source_target_pairs={{0,1},{1,0},{2,3},{3,2},{4,5},{5,4},{6,7},{7,6},{8,9},{9,8},{10,11... | collective-permute-start | bytes 5898248 | tf_op jit(solution)/shard_map/ppermute | solution.py:20
  1000.5 23.1 %collective-permute-start.38 = (bf16[160,2560]{1,0:T(8,128)(2,1)S(1)}, bf16[160,2560]{1,0:T(8,128)(2,1)S(1)}, u32[]{:S(2)}, u32[]{:S(2)}) collective-permute-start(bf16[160,2560]{1,0:T(8,128)(2,1)S(1)} %get-tuple-element.168), channel_id=1, source_target_pairs={{0,8},{8,16},{16,24},{24,0},{1,9},{9,17},{17,25},{25,1},{2,10},{10... | collective-permute-start | bytes 2457608 | tf_op jit(solution)/shard_map/ppermute | solution.py:499
  1000.5 56.4 %collective-permute-start.39 = (bf16[160,2560]{1,0:T(8,128)(2,1)S(1)}, bf16[160,2560]{1,0:T(8,128)(2,1)S(1)}, u32[]{:S(2)}, u32[]{:S(2)}) collective-permute-start(bf16[160,2560]{1,0:T(8,128)(2,1)S(1)} %get-tuple-element.170), channel_id=1, source_target_pairs={{0,16},{8,24},{16,0},{24,8},{1,17},{9,25},{17,1},{25,9},{2,18},{10... | collective-permute-start | bytes 2457608 | tf_op jit(solution)/shard_map/ppermute | solution.py:499
  1002.7 54.1 %collective-permute-start.40 = (bf16[160,2560]{1,0:T(8,128)(2,1)S(1)}, bf16[160,2560]{1,0:T(8,128)(2,1)S(1)}, u32[]{:S(2)}, u32[]{:S(2)}) collective-permute-start(bf16[160,2560]{1,0:T(8,128)(2,1)S(1)} %get-tuple-element.169), channel_id=1, source_target_pairs={{0,24},{8,0},{16,8},{24,16},{1,25},{9,1},{17,9},{25,17},{2,26},{10... | collective-permute-start | bytes 2457608 | tf_op jit(solution)/shard_map/ppermute | solution.py:499
  1058.4 4.9 collective-permute-start.44
  1063.4 4.9 collective-permute-start.45
  1068.4 24.4 %collective-permute-start.46 = (f32[240,128]{1,0:T(8,128)S(1)}, f32[240,128]{1,0:T(8,128)S(1)}, u32[]{:S(2)}, u32[]{:S(2)}) collective-permute-start(f32[240,128]{1,0:T(8,128)S(1)} %add.588), channel_id=1, source_target_pairs={{0,8},{2,10},{4,12},{6,14},{8,0},{10,2},{12,4},{14,6},{16,24},{18,... | collective-permute-start | bytes 368648 | tf_op jit(solution)/shard_map/ppermute | solution.py:37
  1088.1 52.2 %collective-permute-start.41 = (bf16[192,1280]{1,0:T(8,128)(2,1)}, bf16[192,1280]{1,0:T(8,128)(2,1)S(1)}, u32[]{:S(2)}, u32[]{:S(2)}) collective-permute-start(bf16[192,1280]{1,0:T(8,128)(2,1)} %get-tuple-element.189), channel_id=1, source_target_pairs={{0,8},{8,16},{16,24},{24,0},{1,9},{9,17},{17,25},{25,1},{2,10},{10... | collective-permute-start | bytes 1474568 | tf_op jit(solution)/shard_map/ppermute | solution.py:499
  1088.1 52.1 %collective-permute-start.42 = (bf16[192,1280]{1,0:T(8,128)(2,1)}, bf16[192,1280]{1,0:T(8,128)(2,1)}, u32[]{:S(2)}, u32[]{:S(2)}) collective-permute-start(bf16[192,1280]{1,0:T(8,128)(2,1)} %get-tuple-element.191), channel_id=1, source_target_pairs={{0,16},{8,24},{16,0},{24,8},{1,17},{9,25},{17,1},{25,9},{2,18},{10... | collective-permute-start | bytes 1474568 | tf_op jit(solution)/shard_map/ppermute | solution.py:499
  1089.9 50.4 %collective-permute-start.43 = (bf16[192,1280]{1,0:T(8,128)(2,1)}, bf16[192,1280]{1,0:T(8,128)(2,1)}, u32[]{:S(2)}, u32[]{:S(2)}) collective-permute-start(bf16[192,1280]{1,0:T(8,128)(2,1)} %get-tuple-element.190), channel_id=1, source_target_pairs={{0,24},{8,0},{16,8},{24,16},{1,25},{9,1},{17,9},{25,17},{2,26},{10... | collective-permute-start | bytes 1474568 | tf_op jit(solution)/shard_map/ppermute | solution.py:499
  1092.8 43.1 %collective-permute-start.47 = (f32[240,128]{1,0:T(8,128)S(1)}, f32[240,128]{1,0:T(8,128)S(1)}, u32[]{:S(2)}, u32[]{:S(2)}) collective-permute-start(f32[240,128]{1,0:T(8,128)S(1)} %add.589), channel_id=1, source_target_pairs={{0,16},{2,18},{4,20},{6,22},{8,24},{10,26},{12,28},{14,30},{16,0},... | collective-permute-start | bytes 368648 | tf_op jit(solution)/shard_map/ppermute | solution.py:37
  (144 other events, 879.3 us)
Sparse Core Ops, SparseCore 0:
  197.5 81.9 all-gather.2
  305.3 77.2 all-gather.4
  486.3 79.8 reduce-scatter.4
  575.4 74.1 reduce-scatter.6
  700.0 124.5 reduce-scatter.10
  827.4 83.0 reduce-scatter.8

commit v3 on v2

--- a/solution.py
+++ b/solution.py
@@ -448,11 +448,6 @@
     return slots
 
 
-def shift_outer(value, k):
-    count = lax.axis_size("o")
-    return lax.ppermute(value, "o", [(j, (j + k) % count) for j in range(count)])
-
-
 def both_cores(part):
     rows = part.shape[0] // 2
     return part[:rows] + swap(part[rows:].astype(BF16)).astype(F32)
@@ -467,13 +462,12 @@
     return total
 
 
-def reduce_direct(halves):
+def send_direct(halves):
     count = len(halves)
-    total = halves[0].astype(F32)
-    for k in range(1, count):
-        moved = lax.ppermute(halves[k], "o", [(j, (j - k) % count) for j in range(count)])
-        total = total + moved.astype(F32)
-    return total
+    return [halves[0]] + [
+        lax.ppermute(halves[k], "o", [(j, (j - k) % count) for j in range(count)])
+        for k in range(1, count)
+    ]
 
 
 def spread(value):
@@ -561,9 +555,7 @@
         whole = gather_inner(parts[k])
         ffw_parts.append((whole[:, : 2 * size], whole[:, 2 * size :]))
     cot_own, branch_x_full = lax.optimization_barrier((half_of(cotangent, core), branch_x_full))
-    near = [k for k in range(1, outer) if k in (1, outer - 1)]
-    far = [k for k in range(1, outer) if k not in near]
-    cot_near = [shift_outer(cot_own, k) for k in near]
+    cot_whole = lax.all_gather(cot_own, "o")
 
     seg_marks = (segment_ids + 1).astype(F32)
     source_half = half_of(inputs, core).astype(F32)
@@ -602,11 +594,7 @@
         lru_local, gate_pre[0], gate_pre[1], conv_float, decay_param
     )
     cumulative, local_state = local_scan(keep_rate, drive_in, False)
-    ends = (cumulative[tok_rows - 1], local_state[tok_rows - 1])
-    ends, cot_near = lax.optimization_barrier((ends, cot_near))
-    carry_in = entering(*ends, False)
-    carry_in, cot_own = lax.optimization_barrier((carry_in, cot_own))
-    cot_far = [shift_outer(cot_own, k) for k in far]
+    carry_in = entering(cumulative[tok_rows - 1], local_state[tok_rows - 1], False)
     states = local_state + cumulative * carry_in
     branch_act, gelu_back = jax.vjp(gelu_tanh, branch_y)
     mixed_in = (states * branch_act).astype(BF16)
@@ -618,10 +606,12 @@
         + out_bias[0]
     )
 
-    residual, cot_far = lax.optimization_barrier((residual, cot_far))
-    cot_halves = dict(zip([0, *near, *far], [cot_own, *cot_near, *cot_far]))
-    cot_slots = [[cot_halves[k], swap(cot_halves[k])] for k in range(outer)]
     normed_slots = gather_slots(rms_norm(residual, norm_scales[1]).astype(BF16))
+    cot_other = swap(cot_whole)
+    sources = [lax.rem(along - k + outer, outer) for k in range(outer)]
+    cot_slots = [
+        [lax.dynamic_index_in_dim(w, k, 0, False) for w in (cot_whole, cot_other)] for k in sources
+    ]
     normed_joined = [jnp.concatenate(slot) for slot in normed_slots]
     cot_joined = [jnp.concatenate(slot) for slot in cot_slots]
     bias_part = lax.dynamic_slice_in_dim(ffw_bias, along * hidden_part, hidden_part, 1)
@@ -688,6 +678,9 @@
     alpha_next = jnp.concatenate([keep_rate[1:], jnp.ones((1, width_half), F32)], axis=0)
     suffix, local_adjoint = local_scan(alpha_next, delta_states, True)
     leaving = entering(keep_rate[0] * suffix[0], keep_rate[0] * local_adjoint[0], True)
+    leaving, inner_sums[1:] = lax.optimization_barrier((leaving, inner_sums[1:]))
+    for k in range(1, len(cuts)):
+        grads.append(spread(inner_sums[k]))
     adjoint = local_adjoint + suffix * leaving
     states_before = jnp.concatenate([carry_in[None, :], states[: tok_rows - 1]], axis=0)
     delta_gate_decay, delta_gate_input, delta_conv_direct, grad_decay = lru_back(
@@ -709,13 +702,8 @@
         "gthc,ghbc->thb", delta_blocks, gate_weights, preferred_element_type=F32
     ).reshape(tok_rows, width_half)
     rim_delta, rim_next_marks = from_behind((delta_conv[:rim_rows], seg_marks[:rim_rows]), -1)
-    rim_delta, inner_sums, result_parts = lax.optimization_barrier(
-        (rim_delta, inner_sums[1:], result_parts)
-    )
-    for k in range(1, len(cuts)):
-        grads.append(spread(inner_sums[k - 1]))
-    result_half = residual + reduce_direct(result_parts) + out_bias[1]
-    result = join_halves(result_half, swap(result_half), core)
+    rim_delta, result_parts = lax.optimization_barrier((rim_delta, result_parts))
+    result_moved = send_direct(result_parts)
     ffw_in_grad = jnp.concatenate(
         [
             grad[:, :, : 2 * size].reshape(outer, part_width, 2, size)
@@ -745,7 +733,6 @@
     delta_x_low = delta_branch_x.astype(BF16)
     x_rows = grads_rows([[([normed_low], delta_x_low)]], gate_rows)
     grad_x_inner = sum_inner(x_rows)
-    grad_oy = sum_outer(grad_oy_inner)
     delta_part = mm_nt(delta_x_low, branch_x_full) + mm_nt(delta_y_low, branch_y_full)
     delta_normed = half_of(delta_part, core) + swap(
         half_of(delta_part, 1 - core).astype(BF16)
@@ -773,16 +760,18 @@
         grad_decay,
         grad_ffw_bias.reshape(-1),
     ]
-    flat = jnp.concatenate(flat).reshape(-1, 128)
-    grad_x_inner, flat, input_grad, result, ffw_in_grad, ffw_out_grad, grad_oy = (
-        lax.optimization_barrier(
-            (grad_x_inner, flat, input_grad, result, ffw_in_grad, ffw_out_grad, grad_oy)
-        )
+    small = sum_over_all(jnp.concatenate(flat).reshape(-1, 128))
+    small, grad_oy_inner = lax.optimization_barrier((small, grad_oy_inner))
+    grad_oy = sum_outer(grad_oy_inner)
+    result_half = residual + sum(part.astype(F32) for part in result_moved) + out_bias[1]
+    result = join_halves(result_half, swap(result_half), core)
+    grad_x_inner, input_grad, result, ffw_in_grad, ffw_out_grad = lax.optimization_barrier(
+        (grad_x_inner, input_grad, result, ffw_in_grad, ffw_out_grad)
     )
     grad_x_gate = sum_outer(grad_x_inner)
     grad_branch_x = grad_x_gate[:part_width]
     gate_grad = grad_x_gate[part_width:].reshape(2, heads_half, block_size // count, block_size)
-    small = sum_over_all(flat).reshape(-1)
+    small = small.reshape(-1)
     at = 0
     taken = []
     for shape in (

time: 1160 us -> 1100 us (0.948)
  the two profiles are of different devices: /device:TPU:0 before, /device:TPU:12 now
where the time goes in v3:
time: 1100 us; the launch traced here: 1090 us
  waiting for transfers between devices  363 us (33%)
  Pallas kernels  275 us (25%)
  matrix products  141 us (13%)
  other arithmetic  125 us (11%)
  local copies, waits for them, and re-layouts  122 us (11%)
  starting transfers between devices  52.6 us (5%)
  between operations  16.8 us (2%)
    pallas_call x1, Pallas kernels, gather_weights(): pl.pallas_call(functools.partial(gather_kernel, outer, groups, parts), in...  167 us
    dot_general x38, matrix products, dot(): lax.dot_general(a, b, ((contract[0], contract[1]), ((), ())), preferred_e...  135 us
    ppermute x6, waiting for transfers between devices, ring(): lax.ppermute(value, 'o', [(k, (k + 1) % count) for k in range(count)])  121 us
    ppermute x6, waiting for transfers between devices, sum_outer(): lax.ppermute(part, 'o', [(j, (j + k) % count) for j in range(count)])  65.1 us
    pallas_call x4, Pallas kernels, grads_rows(): pl.pallas_call(functools.partial(grads_kernel, plan, added), grid=(outer,...  63.7 us
    all_to_all x2, waiting for transfers between devices, spread(): return lax.all_to_all(value, 'o', 0, 0, tiled=True)  59.7 us
    ppermute x3, waiting for transfers between devices, send_direct(): lax.ppermute(halves[k], 'o', [(j, (j - k) % count) for j in range(count)])  55.2 us
    ppermute x4, waiting for transfers between devices, sum_over_all(): lax.ppermute(value, DP, [(k, k ^ bit) for k in range(count)])  48.3 us
  transfers between devices with their start and end apart: 51, of which 19 were waited for; matrix products, arithmetic and copies ran while one was open for 28% of the time, Pallas kernels for 9%

profile of v3, /device:TPU:12, one launch (start us, length us, event | category | flops | bytes accessed | tf_op | source)
XLA Modules:
  0.0 1095.0 jit_solution(117463408840992335)
XLA Ops:
  26.7 166.6 %shard_map.271 = (bf16[4,4,160,1280]{3,2,1,0:T(8,128)(2,1)}, bf16[4,4,160,1280]{3,2,1,0:T(8,128)(2,1)}, bf16[4,4,160,1280]{3,2,1,0:T(8,128)(2,1)}, bf16[4,160,1536]{2,1,0:T(8,128)(2,1)}, bf16[4,160,1344]{2,1,0:T(8,128)(2,1)}) custom-call(bf16[160,1280]{1,0:T(8,128)(2,1)} %get-tuple-element.230.refs_0_, bf16[160,1280]{1,0:T(8,128)(2,1)} %get-tuple-element.229.refs_1_, ...), custom_call_target="tpu_custom_call" | custom-call | tf_op jit(solution)/shard_map/pallas_call | solution.py:312
  196.0 6.3 convolution_add_fusion.10
  206.1 5.6 collective-permute-start
  218.5 6.1 add_convert_fusion
  231.2 5.5 copy.76
  239.1 4.3 fusion.64
  243.5 7.2 shard_map.272
  252.8 16.8 %shard_map.273 = f32[1,1280]{1,0:T(1,128)} custom-call(f32[2,1280]{1,0:T(2,128)} %pad_maximum_fusion.25.ends_ref), custom_call_target="tpu_custom_call" | custom-call | tf_op jit(solution)/shard_map/pallas_call | solution.py:143
  270.4 9.5 multiply_convert_fusion.1
  279.9 5.3 fusion.206
  292.8 23.2 %collective-permute-done.5.refs_3_ = bf16[192,2560]{1,0:T(8,128)(2,1)S(1)} collective-permute-done((bf16[192,2560]{1,0:T(8,128)(2,1)S(1)}, bf16[192,2560]{1,0:T(8,128)(2,1)S(1)}, u32[]{:S(2)}, u32[]{:S(2)}) %collective-permute-start.5) | collective-permute-done | bytes 983072 | tf_op jit(solution)/shard_map/ppermute | solution.py:25
  320.1 19.4 %collective-permute-done.7.refs_6_ = bf16[192,2560]{1,0:T(8,128)(2,1)} collective-permute-done((bf16[192,2560]{1,0:T(8,128)(2,1)S(1)}, bf16[192,2560]{1,0:T(8,128)(2,1)}, u32[]{:S(2)}, u32[]{:S(2)}) %collective-permute-start.7) | collective-permute-done | bytes 983072 | tf_op jit(solution)/shard_map/ppermute | solution.py:25
  342.4 21.9 %collective-permute-done.9.refs_9_ = bf16[192,2560]{1,0:T(8,128)(2,1)S(1)} collective-permute-done((bf16[192,2560]{1,0:T(8,128)(2,1)}, bf16[192,2560]{1,0:T(8,128)(2,1)S(1)}, u32[]{:S(2)}, u32[]{:S(2)}) %collective-permute-start.9) | collective-permute-done | bytes 983072 | tf_op jit(solution)/shard_map/ppermute | solution.py:25
  367.0 4.8 dynamic-slice_bitcast_fusion
  377.9 5.4 convolution_add_fusion.11
  387.6 3.8 convolution_add_fusion.12
  402.4 3.5 convolution_add_fusion.14
  410.2 22.3 %shard_map.274 = bf16[4,4,160,1536]{3,2,1,0:T(8,128)(2,1)} custom-call(bf16[192,2560]{1,0:T(8,128)(2,1)} %copy-done.33, bf16[192,2560]{1,0:T(8,128)(2,1)} %collective-permute-done.4.refs_1_, bf16[384,1024]{1,0:T(8,128)(2,1)} %pad_maximum_fusion.16.refs_2_, bf16[192,2560]{1,0:T(8,128)(2,1)} %copy-done.75, bf16[192,2560]{1,0:T(8,128)(2,1)} %copy-done.76, ...), custom_call_target="tpu_custom_call" | custom-call | flops 12079595520 | bytes 20447232 | tf_op jit(solution)/shard_map/pallas_call | solution.py:381
  433.7 6.9 all-gather.7.cloned.1.call-done
  440.6 5.2 convolution_add_fusion.15
  453.4 3.9 convolution_add_fusion.16
  459.9 4.2 fusion.74
  464.1 5.0 convolution_add_fusion.6
  475.5 4.2 fusion.76
  479.7 4.7 convolution_add_fusion.7
  491.4 4.2 fusion.81
  496.8 21.8 %shard_map.277 = bf16[4,4,160,1344]{3,2,1,0:T(8,128)(2,1)} custom-call(bf16[192,2560]{1,0:T(8,128)(2,1)} %copy-done.33, bf16[192,2560]{1,0:T(8,128)(2,1)} %collective-permute-done.4.refs_1_, bf16[384,896]{1,0:T(8,128)(2,1)} %pad_maximum_fusion.20.refs_2_, bf16[192,2560]{1,0:T(8,128)(2,1)} %copy-done.75, bf16[192,2560]{1,0:T(8,128)(2,1)} %copy-done.76, ...), custom_call_target="tpu_custom_call" | custom-call | flops 10569646080 | bytes 18874368 | tf_op jit(solution)/shard_map/pallas_call | solution.py:381
  519.7 5.9 convolution_add_fusion.8
  544.1 15.8 %collective-permute-done.15 = bf16[192,2560]{1,0:T(8,128)(2,1)S(1)} collective-permute-done((bf16[192,2560]{1,0:T(8,128)(2,1)S(1)}, bf16[192,2560]{1,0:T(8,128)(2,1)S(1)}, u32[]{:S(2)}, u32[]{:S(2)}) %collective-permute-start.15) | collective-permute-done | bytes 983072 | tf_op jit(solution)/shard_map/ppermute | solution.py:25
  566.7 19.5 %collective-permute-done.16 = bf16[192,2560]{1,0:T(8,128)(2,1)S(1)} collective-permute-done((bf16[192,2560]{1,0:T(8,128)(2,1)S(1)}, bf16[192,2560]{1,0:T(8,128)(2,1)S(1)}, u32[]{:S(2)}, u32[]{:S(2)}) %collective-permute-start.16) | collective-permute-done | bytes 983072 | tf_op jit(solution)/shard_map/ppermute | solution.py:25
  590.3 21.5 %collective-permute-done.17 = bf16[192,2560]{1,0:T(8,128)(2,1)S(1)} collective-permute-done((bf16[192,2560]{1,0:T(8,128)(2,1)S(1)}, bf16[192,2560]{1,0:T(8,128)(2,1)S(1)}, u32[]{:S(2)}, u32[]{:S(2)}) %collective-permute-start.17) | collective-permute-done | bytes 983072 | tf_op jit(solution)/shard_map/ppermute | solution.py:25
  624.5 8.9 convert_reduce_fusion.2
  633.4 7.3 shard_map.275
  642.2 12.9 %shard_map.276 = f32[1,1280]{1,0:T(1,128)} custom-call(f32[2,1280]{1,0:T(2,128)} %pad_maximum_fusion.26.ends_ref), custom_call_target="tpu_custom_call" | custom-call | tf_op jit(solution)/shard_map/pallas_call | solution.py:143
  655.9 8.3 multiply_reduce_fusion
  674.8 3.7 fusion.65
  681.5 6.8 multiply_reduce_fusion.1
  688.3 3.3 collective-permute-start.23
  693.7 3.5 convert_element_type.308.refs_2_
  697.3 7.0 convert_reduce_fusion.3
  704.3 8.1 shard_map.278
  715.3 11.6 %shard_map.279 = bf16[4,4,160,2560]{3,2,1,0:T(8,128)(2,1)} custom-call(bf16[384,2560]{1,0:T(8,128)(2,1)} %pad_maximum_fusion.10.refs_0_, bf16[384,1280]{1,0:T(8,128)(2,1)} %copy-done.74, bf16[384,2560]{1,0:T(8,128)(2,1)} %copy-done.7, bf16[384,1280]{1,0:T(8,128)(2,1)} %get-tuple-element.134.refs_3_), custom_call_target="tpu_custom_call" | custom-call | flops 5033164800 | bytes 17039360 | tf_op jit(solution)/shard_map/pallas_call | solution.py:381
  731.7 4.6 all-to-all-start
  736.3 5.6 fusion.207
  741.9 5.3 convolution_add_fusion.4
  762.3 59.7 %all-to-all-done = bf16[4,160,1536]{2,1,0:T(8,128)(2,1)} async-done(((bf16[4,160,1536]{2,1,0:T(8,128)(2,1)}), bf16[4,160,1536]{2,1,0:T(8,128)(2,1)}, u32[]{:S(2)}, u32[]{:S(2)}) %all-to-all-start) | async-done | bytes 1966112 | tf_op jit(solution)/shard_map/all_to_all | solution.py:474
  822.0 6.3 all-to-all-start.1
  828.3 35.1 %collective-permute-done.27 = bf16[192,2560]{1,0:T(8,128)(2,1)} collective-permute-done((bf16[192,2560]{1,0:T(8,128)(2,1)}, bf16[192,2560]{1,0:T(8,128)(2,1)}, u32[]{:S(2)}, u32[]{:S(2)}) %collective-permute-start.27) | collective-permute-done | bytes 983072 | tf_op jit(solution)/shard_map/ppermute | solution.py:468
  863.4 20.0 %collective-permute-done.29 = bf16[192,2560]{1,0:T(8,128)(2,1)} collective-permute-done((bf16[192,2560]{1,0:T(8,128)(2,1)}, bf16[192,2560]{1,0:T(8,128)(2,1)}, u32[]{:S(2)}, u32[]{:S(2)}) %collective-permute-start.29) | collective-permute-done | bytes 983072 | tf_op jit(solution)/shard_map/ppermute | solution.py:468
  883.5 9.3 add_add_fusion
  895.1 7.4 collective-permute-done.35
  909.6 3.2 copy.93
  912.8 4.3 reshape.252
  919.6 5.0 reshape.238
  924.6 3.7 convert_bitcast_fusion
  928.3 5.7 copy.92
  934.0 7.4 reshape.251
  959.9 29.5 %collective-permute-done.37 = f32[240,128]{1,0:T(8,128)S(1)} collective-permute-done((f32[240,128]{1,0:T(8,128)S(1)}, f32[240,128]{1,0:T(8,128)S(1)}, u32[]{:S(2)}, u32[]{:S(2)}) %collective-permute-start.37) | collective-permute-done | bytes 122912 | tf_op jit(solution)/shard_map/ppermute | solution.py:37
  990.2 11.4 %collective-permute-done.38 = f32[240,128]{1,0:T(8,128)S(1)} collective-permute-done((f32[240,128]{1,0:T(8,128)S(1)}, f32[240,128]{1,0:T(8,128)S(1)}, u32[]{:S(2)}, u32[]{:S(2)}) %collective-permute-start.38) | collective-permute-done | bytes 122912 | tf_op jit(solution)/shard_map/ppermute | solution.py:37
  1004.0 3.1 dynamic-slice_bitcast_fusion.10
  1008.8 4.3 collective-permute-start.40
  1018.2 11.9 %collective-permute-done.39 = bf16[160,2560]{1,0:T(8,128)(2,1)} collective-permute-done((bf16[160,2560]{1,0:T(8,128)(2,1)}, bf16[160,2560]{1,0:T(8,128)(2,1)}, u32[]{:S(2)}, u32[]{:S(2)}) %collective-permute-start.39) | collective-permute-done | bytes 819232 | tf_op jit(solution)/shard_map/ppermute | solution.py:493
  1030.1 49.3 %collective-permute-done.40 = bf16[160,2560]{1,0:T(8,128)(2,1)} collective-permute-done((bf16[160,2560]{1,0:T(8,128)(2,1)}, bf16[160,2560]{1,0:T(8,128)(2,1)}, u32[]{:S(2)}, u32[]{:S(2)}) %collective-permute-start.40) | collective-permute-done | bytes 819232 | tf_op jit(solution)/shard_map/ppermute | solution.py:493
  1079.5 3.9 collective-permute-done.41
  (600 shorter events, 240.6 us)
Async XLA Ops:
  7.2 219.7 %copy-start = (bf16[2,5,256,256]{3,2,1,0:T(8,128)(2,1)S(1)}, bf16[2,5,256,256]{3,2,1,0:T(8,128)(2,1)}, u32[]{:S(2)}) copy-start(bf16[2,5,256,256]{3,2,1,0:T(8,128)(2,1)} %param.27) | copy-start | bytes 3932164
  7.2 285.2 %all-gather.9.cloned.1.call-start = ((), (), s32[]{:S(2)}) async-start(), calls=%async_computation.12 | async-start | bytes 4915200 | tf_op jit(solution)/shard_map/all_gather | solution.py:558
  193.3 184.6 %all-gather.5.cloned.1.call-start = ((), (), s32[]{:S(2)}) async-start(), calls=%async_computation.6 | async-start | bytes 9830400 | tf_op jit(solution)/shard_map/all_gather | solution.py:478
  194.1 246.5 %all-gather.7.cloned.1.call-start = ((), (), s32[]{:S(2)}) async-start(), calls=%async_computation.7 | async-start | bytes 9011200 | tf_op jit(solution)/shard_map/all_gather | solution.py:478
  194.9 95.7 %copy-start.104 = (f32[2560]{0:T(1024)}, f32[2560]{0:T(1024)S(1)}, u32[]{:S(2)}) copy-start(f32[2560]{0:T(1024)S(1)} %get-tuple-element.122) | copy-start | bytes 30724
  203.6 14.3 %collective-permute-start.1 = (f32[3,1280]{1,0:T(4,128)S(1)}, f32[3,1280]{1,0:T(4,128)S(1)}, u32[]{:S(2)}, u32[]{:S(2)}) collective-permute-start(f32[3,1280]{1,0:T(4,128)S(1)} %slice.536), channel_id=1, source_target_pairs={{0,2},{2,4},{4,6},{6,8},{8,10},{10,12},{12,14},{14,16},{16,18},{18... | collective-permute-start | bytes 46088 | tf_op jit(solution)/shard_map/ppermute | solution.py:31
  206.1 8.4 collective-permute-start
  211.7 5.5 collective-permute-start.24
  214.5 24.6 %copy-start.118 = (f32[1280]{0:T(1024)}, f32[1280]{0:T(1024)S(1)}, u32[]{:S(2)}) copy-start(f32[1280]{0:T(1024)S(1)} %get-tuple-element.239) | copy-start | bytes 15364
  285.3 4.0 collective-permute-start.2
  292.1 28.0 %copy-start.33 = (bf16[192,2560]{1,0:T(8,128)(2,1)}, bf16[192,2560]{1,0:T(8,128)(2,1)S(1)}, u32[]{:S(2)}) copy-start(bf16[192,2560]{1,0:T(8,128)(2,1)S(1)} %multiply_convert_fusion.refs_0_) | copy-start | bytes 2949124
  292.1 23.8 %collective-permute-start.5 = (bf16[192,2560]{1,0:T(8,128)(2,1)S(1)}, bf16[192,2560]{1,0:T(8,128)(2,1)S(1)}, u32[]{:S(2)}, u32[]{:S(2)}) collective-permute-start(bf16[192,2560]{1,0:T(8,128)(2,1)S(1)} %multiply_convert_fusion.refs_0_), channel_id=1, source_target_pairs={{0,8},{8,16},{16,24},{24,0},{1,9},{9,17},{17,25},{25,1},{2,10},{10... | collective-permute-start | bytes 2949128 | tf_op jit(solution)/shard_map/ppermute | solution.py:25
  292.2 25.0 %collective-permute-start.4 = (bf16[192,2560]{1,0:T(8,128)(2,1)S(1)}, bf16[192,2560]{1,0:T(8,128)(2,1)}, u32[]{:S(2)}, u32[]{:S(2)}) collective-permute-start(bf16[192,2560]{1,0:T(8,128)(2,1)S(1)} %multiply_convert_fusion.refs_0_), channel_id=1, source_target_pairs={{0,1},{1,0},{2,3},{3,2},{4,5},{5,4},{6,7},{7,6},{8,9},{9,8},{10,11... | collective-permute-start | bytes 2949128 | tf_op jit(solution)/shard_map/ppermute | solution.py:20
  292.4 74.6 %collective-permute-start.3 = (bf16[4,192,2560]{2,1,0:T(8,128)(2,1)}, bf16[4,192,2560]{2,1,0:T(8,128)(2,1)}, u32[]{:S(2)}, u32[]{:S(2)}) collective-permute-start(bf16[4,192,2560]{2,1,0:T(8,128)(2,1)} %bitcast.234), channel_id=1, source_target_pairs={{0,1},{1,0},{2,3},{3,2},{4,5},{5,4},{6,7},{7,6},{8,9},{9,8},{10,11... | collective-permute-start | bytes 11796488 | tf_op jit(solution)/shard_map/ppermute | solution.py:20
  316.0 24.0 %copy-start.75 = (bf16[192,2560]{1,0:T(8,128)(2,1)}, bf16[192,2560]{1,0:T(8,128)(2,1)S(1)}, u32[]{:S(2)}) copy-start(bf16[192,2560]{1,0:T(8,128)(2,1)S(1)} %collective-permute-done.5.refs_3_) | copy-start | bytes 2949124
  316.0 23.6 %collective-permute-start.7 = (bf16[192,2560]{1,0:T(8,128)(2,1)S(1)}, bf16[192,2560]{1,0:T(8,128)(2,1)}, u32[]{:S(2)}, u32[]{:S(2)}) collective-permute-start(bf16[192,2560]{1,0:T(8,128)(2,1)S(1)} %collective-permute-done.5.refs_3_), channel_id=1, source_target_pairs={{0,8},{8,16},{16,24},{24,0},{1,9},{9,17},{17,25},{25,1},{2,10},{10... | collective-permute-start | bytes 2949128 | tf_op jit(solution)/shard_map/ppermute | solution.py:25
  316.3 298.3 %reduce-scatter.5.cloned.1.call-start = ((), (), s32[]{:S(2)}) async-start(), calls=%async_computation.8 | async-start | bytes 9830400 | tf_op jit(solution)/shard_map/reduce_scatter | solution.py:482
  317.2 25.1 %collective-permute-start.6 = (bf16[192,2560]{1,0:T(8,128)(2,1)S(1)}, bf16[192,2560]{1,0:T(8,128)(2,1)S(1)}, u32[]{:S(2)}, u32[]{:S(2)}) collective-permute-start(bf16[192,2560]{1,0:T(8,128)(2,1)S(1)} %collective-permute-done.5.refs_3_), channel_id=1, source_target_pairs={{0,1},{1,0},{2,3},{3,2},{4,5},{5,4},{6,7},{7,6},{8,9},{9,8},{10,11... | collective-permute-start | bytes 2949128 | tf_op jit(solution)/shard_map/ppermute | solution.py:20
  339.5 24.8 %collective-permute-start.9 = (bf16[192,2560]{1,0:T(8,128)(2,1)}, bf16[192,2560]{1,0:T(8,128)(2,1)S(1)}, u32[]{:S(2)}, u32[]{:S(2)}) collective-permute-start(bf16[192,2560]{1,0:T(8,128)(2,1)} %collective-permute-done.7.refs_6_), channel_id=1, source_target_pairs={{0,8},{8,16},{16,24},{24,0},{1,9},{9,17},{17,25},{25,1},{2,10},{10... | collective-permute-start | bytes 2949128 | tf_op jit(solution)/shard_map/ppermute | solution.py:25
  340.0 24.3 %collective-permute-start.8 = (bf16[192,2560]{1,0:T(8,128)(2,1)}, bf16[192,2560]{1,0:T(8,128)(2,1)S(1)}, u32[]{:S(2)}, u32[]{:S(2)}) collective-permute-start(bf16[192,2560]{1,0:T(8,128)(2,1)} %collective-permute-done.7.refs_6_), channel_id=1, source_target_pairs={{0,1},{1,0},{2,3},{3,2},{4,5},{5,4},{6,7},{7,6},{8,9},{9,8},{10,11... | collective-permute-start | bytes 2949128 | tf_op jit(solution)/shard_map/ppermute | solution.py:20
  342.3 24.1 %copy-start.17 = (bf16[768,2560]{1,0:T(8,128)(2,1)S(1)}, bf16[768,2560]{1,0:T(8,128)(2,1)}, u32[]{:S(2)}) copy-start(bf16[768,2560]{1,0:T(8,128)(2,1)} %all-gather.9.cloned.1.call-done) | copy-start | bytes 11796484
  364.3 2.6 collective-permute-start.10
  366.7 24.7 %copy-start.20 = (bf16[192,2560]{1,0:T(8,128)(2,1)}, bf16[192,2560]{1,0:T(8,128)(2,1)S(1)}, u32[]{:S(2)}) copy-start(bf16[192,2560]{1,0:T(8,128)(2,1)S(1)} %get-tuple-element.157.refs_18_) | copy-start | bytes 2949124
  432.5 223.4 %reduce-scatter.7.cloned.1.call-start = ((), (), s32[]{:S(2)}) async-start(), calls=%async_computation.9 | async-start | bytes 9011200 | tf_op jit(solution)/shard_map/reduce_scatter | solution.py:482
  453.3 42.3 %collective-permute-start.14 = (bf16[192,2560]{1,0:T(8,128)(2,1)S(1)}, bf16[192,2560]{1,0:T(8,128)(2,1)S(1)}, u32[]{:S(2)}, u32[]{:S(2)}) collective-permute-start(bf16[192,2560]{1,0:T(8,128)(2,1)S(1)} %slice.931), channel_id=1, source_target_pairs={{0,1},{1,0},{2,3},{3,2},{4,5},{5,4},{6,7},{7,6},{8,9},{9,8},{10,11... | collective-permute-start | bytes 2949128 | tf_op jit(solution)/shard_map/ppermute | solution.py:20
  470.3 73.5 %collective-permute-start.13 = (bf16[192,2560]{1,0:T(8,128)(2,1)}, bf16[192,2560]{1,0:T(8,128)(2,1)}, u32[]{:S(2)}, u32[]{:S(2)}) collective-permute-start(bf16[192,2560]{1,0:T(8,128)(2,1)} %slice.932), channel_id=1, source_target_pairs={{0,1},{1,0},{2,3},{3,2},{4,5},{5,4},{6,7},{7,6},{8,9},{9,8},{10,11... | collective-permute-start | bytes 2949128 | tf_op jit(solution)/shard_map/ppermute | solution.py:20
  485.5 81.2 %collective-permute-start.12 = (bf16[192,2560]{1,0:T(8,128)(2,1)}, bf16[192,2560]{1,0:T(8,128)(2,1)S(1)}, u32[]{:S(2)}, u32[]{:S(2)}) collective-permute-start(bf16[192,2560]{1,0:T(8,128)(2,1)} %slice.933), channel_id=1, source_target_pairs={{0,1},{1,0},{2,3},{3,2},{4,5},{5,4},{6,7},{7,6},{8,9},{9,8},{10,11... | collective-permute-start | bytes 2949128 | tf_op jit(solution)/shard_map/ppermute | solution.py:20
  518.6 431.6 %reduce-scatter.9.cloned.1.call-start = ((), (), s32[]{:S(2)}) async-start(), calls=%async_computation.10 | async-start | bytes 9830400 | tf_op jit(solution)/shard_map/reduce_scatter | solution.py:482
  526.7 63.6 %collective-permute-start.11 = (bf16[192,2560]{1,0:T(8,128)(2,1)}, bf16[192,2560]{1,0:T(8,128)(2,1)}, u32[]{:S(2)}, u32[]{:S(2)}) collective-permute-start(bf16[192,2560]{1,0:T(8,128)(2,1)} %slice.934), channel_id=1, source_target_pairs={{0,1},{1,0},{2,3},{3,2},{4,5},{5,4},{6,7},{7,6},{8,9},{9,8},{10,11... | collective-permute-start | bytes 2949128 | tf_op jit(solution)/shard_map/ppermute | solution.py:20
  535.8 24.0 %collective-permute-start.15 = (bf16[192,2560]{1,0:T(8,128)(2,1)S(1)}, bf16[192,2560]{1,0:T(8,128)(2,1)S(1)}, u32[]{:S(2)}, u32[]{:S(2)}) collective-permute-start(bf16[192,2560]{1,0:T(8,128)(2,1)S(1)} %copy-done.83), channel_id=1, source_target_pairs={{0,8},{8,16},{16,24},{24,0},{1,9},{9,17},{17,25},{25,1},{2,10},{10... | collective-permute-start | bytes 2949128 | tf_op jit(solution)/shard_map/ppermute | solution.py:25
  538.8 22.6 %collective-permute-start.21 = (bf16[192,2560]{1,0:T(8,128)(2,1)S(1)}, bf16[192,2560]{1,0:T(8,128)(2,1)}, u32[]{:S(2)}, u32[]{:S(2)}) collective-permute-start(bf16[192,2560]{1,0:T(8,128)(2,1)S(1)} %slice.927), channel_id=1, source_target_pairs={{0,1},{1,0},{2,3},{3,2},{4,5},{5,4},{6,7},{7,6},{8,9},{9,8},{10,11... | collective-permute-start | bytes 2949128 | tf_op jit(solution)/shard_map/ppermute | solution.py:20
  543.8 21.5 %collective-permute-start.20 = (bf16[192,2560]{1,0:T(8,128)(2,1)S(1)}, bf16[192,2560]{1,0:T(8,128)(2,1)S(1)}, u32[]{:S(2)}, u32[]{:S(2)}) collective-permute-start(bf16[192,2560]{1,0:T(8,128)(2,1)S(1)} %slice.928), channel_id=1, source_target_pairs={{0,1},{1,0},{2,3},{3,2},{4,5},{5,4},{6,7},{7,6},{8,9},{9,8},{10,11... | collective-permute-start | bytes 2949128 | tf_op jit(solution)/shard_map/ppermute | solution.py:20
  559.9 27.7 %collective-permute-start.19 = (bf16[192,2560]{1,0:T(8,128)(2,1)S(1)}, bf16[192,2560]{1,0:T(8,128)(2,1)S(1)}, u32[]{:S(2)}, u32[]{:S(2)}) collective-permute-start(bf16[192,2560]{1,0:T(8,128)(2,1)S(1)} %slice.929), channel_id=1, source_target_pairs={{0,1},{1,0},{2,3},{3,2},{4,5},{5,4},{6,7},{7,6},{8,9},{9,8},{10,11... | collective-permute-start | bytes 2949128 | tf_op jit(solution)/shard_map/ppermute | solution.py:20
  561.4 24.8 %collective-permute-start.16 = (bf16[192,2560]{1,0:T(8,128)(2,1)S(1)}, bf16[192,2560]{1,0:T(8,128)(2,1)S(1)}, u32[]{:S(2)}, u32[]{:S(2)}) collective-permute-start(bf16[192,2560]{1,0:T(8,128)(2,1)S(1)} %fusion.45), channel_id=1, source_target_pairs={{0,8},{8,16},{16,24},{24,0},{1,9},{9,17},{17,25},{25,1},{2,10},{10... | collective-permute-start | bytes 2949128 | tf_op jit(solution)/shard_map/ppermute | solution.py:25
  565.3 23.5 %collective-permute-start.18 = (bf16[192,2560]{1,0:T(8,128)(2,1)S(1)}, bf16[192,2560]{1,0:T(8,128)(2,1)S(1)}, u32[]{:S(2)}, u32[]{:S(2)}) collective-permute-start(bf16[192,2560]{1,0:T(8,128)(2,1)S(1)} %slice.930), channel_id=1, source_target_pairs={{0,1},{1,0},{2,3},{3,2},{4,5},{5,4},{6,7},{7,6},{8,9},{9,8},{10,11... | collective-permute-start | bytes 2949128 | tf_op jit(solution)/shard_map/ppermute | solution.py:20
  586.6 25.2 %collective-permute-start.17 = (bf16[192,2560]{1,0:T(8,128)(2,1)S(1)}, bf16[192,2560]{1,0:T(8,128)(2,1)S(1)}, u32[]{:S(2)}, u32[]{:S(2)}) collective-permute-start(bf16[192,2560]{1,0:T(8,128)(2,1)S(1)} %fusion.47), channel_id=1, source_target_pairs={{0,8},{8,16},{16,24},{24,0},{1,9},{9,17},{17,25},{25,1},{2,10},{10... | collective-permute-start | bytes 2949128 | tf_op jit(solution)/shard_map/ppermute | solution.py:25
  590.2 24.4 %copy-start.4 = (f32[192,2560]{1,0:T(8,128)S(1)}, f32[192,2560]{1,0:T(8,128)}, u32[]{:S(2)}) copy-start(f32[192,2560]{1,0:T(8,128)} %copy-done.3) | copy-start | bytes 5898244
  590.2 24.4 %copy-start.105 = (f32[2560]{0:T(1024)S(1)}, f32[2560]{0:T(1024)}, u32[]{:S(2)}) copy-start(f32[2560]{0:T(1024)} %copy-done.104) | copy-start | bytes 30724
  590.2 24.4 %copy-start.129 = (f32[192]{0:T(256)S(1)}, f32[192]{0:T(256)}, u32[]{:S(2)}) copy-start(f32[192]{0:T(256)} %copy-done.128) | copy-start | bytes 2308
  618.7 3.1 collective-permute-start.22
  633.4 22.5 %copy-start.149 = (pred[384]{0:T(512)(128)(4,1)S(1)}, pred[384]{0:T(512)(128)(4,1)}, u32[]{:S(2)}) copy-start(pred[384]{0:T(512)(128)(4,1)} %copy-done.148) | copy-start | bytes 1156
  688.3 8.9 collective-permute-start.23
  712.4 291.6 %reduce-scatter.11.cloned.1.call-start = ((), (), s32[]{:S(2)}) async-start(), calls=%async_computation.11 | async-start | bytes 16384000 | tf_op jit(solution)/shard_map/reduce_scatter | solution.py:482
  727.7 30.8 %copy-start.142 = (f32[192]{0:T(256)}, f32[192]{0:T(256)S(1)}, u32[]{:S(2)}) copy-start(f32[192]{0:T(256)S(1)} %add_rsqrt_fusion.1) | copy-start | bytes 2308
  731.7 90.3 %all-to-all-start = ((bf16[4,160,1536]{2,1,0:T(8,128)(2,1)}), bf16[4,160,1536]{2,1,0:T(8,128)(2,1)}, u32[]{:S(2)}, u32[]{:S(2)}) async-start(bf16[4,160,1536]{2,1,0:T(8,128)(2,1)} %bitcast.245), calls=%async_computation.3 | async-start | bytes 3932160 | tf_op jit(solution)/shard_map/all_to_all | solution.py:474
  748.3 10.2 collective-permute-start.25
  750.9 112.5 %collective-permute-start.27 = (bf16[192,2560]{1,0:T(8,128)(2,1)}, bf16[192,2560]{1,0:T(8,128)(2,1)}, u32[]{:S(2)}, u32[]{:S(2)}) collective-permute-start(bf16[192,2560]{1,0:T(8,128)(2,1)} %fusion.43), channel_id=1, source_target_pairs={{0,24},{8,0},{16,8},{24,16},{1,25},{9,1},{17,9},{25,17},{2,26},{10... | collective-permute-start | bytes 2949128 | tf_op jit(solution)/shard_map/ppermute | solution.py:468
  750.9 112.5 %collective-permute-start.28 = (bf16[192,2560]{1,0:T(8,128)(2,1)}, bf16[192,2560]{1,0:T(8,128)(2,1)}, u32[]{:S(2)}, u32[]{:S(2)}) collective-permute-start(bf16[192,2560]{1,0:T(8,128)(2,1)} %fusion.42), channel_id=1, source_target_pairs={{0,16},{8,24},{16,0},{24,8},{1,17},{9,25},{17,1},{25,9},{2,18},{10... | collective-permute-start | bytes 2949128 | tf_op jit(solution)/shard_map/ppermute | solution.py:468
  753.8 129.7 %collective-permute-start.29 = (bf16[192,2560]{1,0:T(8,128)(2,1)}, bf16[192,2560]{1,0:T(8,128)(2,1)}, u32[]{:S(2)}, u32[]{:S(2)}) collective-permute-start(bf16[192,2560]{1,0:T(8,128)(2,1)} %fusion.41), channel_id=1, source_target_pairs={{0,8},{8,16},{16,24},{24,0},{1,9},{9,17},{17,25},{25,1},{2,10},{10... | collective-permute-start | bytes 2949128 | tf_op jit(solution)/shard_map/ppermute | solution.py:468
  761.5 121.9 %copy-start.121 = (f32[2560]{0:T(1024)S(1)}, f32[2560]{0:T(1024)}, u32[]{:S(2)}) copy-start(f32[2560]{0:T(1024)} %get-tuple-element.120) | copy-start | bytes 30724
  761.6 131.1 %collective-permute-start.34 = (f32[4,2560]{1,0:T(4,128)S(1)}, f32[4,2560]{1,0:T(4,128)S(1)}, u32[]{:S(2)}, u32[]{:S(2)}) collective-permute-start(f32[4,2560]{1,0:T(4,128)S(1)} %pad_maximum_fusion.24), channel_id=1, source_target_pairs={{0,1},{1,0},{2,3},{3,2},{4,5},{5,4},{6,7},{7,6},{8,9},{9,8},{10,11... | collective-permute-start | bytes 122888 | tf_op jit(solution)/shard_map/ppermute | solution.py:20
  822.0 86.1 %all-to-all-start.1 = ((bf16[4,160,1344]{2,1,0:T(8,128)(2,1)}), bf16[4,160,1344]{2,1,0:T(8,128)(2,1)}, u32[]{:S(2)}, u32[]{:S(2)}) async-start(bf16[4,160,1344]{2,1,0:T(8,128)(2,1)} %bitcast.251), calls=%async_computation.4 | async-start | bytes 3604480 | tf_op jit(solution)/shard_map/all_to_all | solution.py:474
  892.7 48.6 %collective-permute-start.30 = (f32[192,2560]{1,0:T(8,128)}, f32[192,2560]{1,0:T(8,128)}, u32[]{:S(2)}, u32[]{:S(2)}) collective-permute-start(f32[192,2560]{1,0:T(8,128)} %get-tuple-element.188), channel_id=1, source_target_pairs={{0,1},{1,0},{2,3},{3,2},{4,5},{5,4},{6,7},{7,6},{8,9},{9,8},{10,11... | collective-permute-start | bytes 5898248 | tf_op jit(solution)/shard_map/ppermute | solution.py:20
  893.7 8.8 collective-permute-start.35
  894.9 51.1 %collective-permute-start.26 = (f32[192,2560]{1,0:T(8,128)}, f32[192,2560]{1,0:T(8,128)}, u32[]{:S(2)}, u32[]{:S(2)}) collective-permute-start(f32[192,2560]{1,0:T(8,128)} %get-tuple-element.189), channel_id=1, source_target_pairs={{0,1},{1,0},{2,3},{3,2},{4,5},{5,4},{6,7},{7,6},{8,9},{9,8},{10,11... | collective-permute-start | bytes 5898248 | tf_op jit(solution)/shard_map/ppermute | solution.py:20
  902.5 53.5 %collective-permute-start.36 = (f32[240,128]{1,0:T(8,128)S(1)}, f32[240,128]{1,0:T(8,128)}, u32[]{:S(2)}, u32[]{:S(2)}) collective-permute-start(f32[240,128]{1,0:T(8,128)S(1)} %bitcast_add_fusion), channel_id=1, source_target_pairs={{0,4},{2,6},{4,0},{6,2},{8,12},{10,14},{12,8},{14,10},{16,20},{18,... | collective-permute-start | bytes 368648 | tf_op jit(solution)/shard_map/ppermute | solution.py:37
  952.6 49.0 %collective-permute-start.31 = (bf16[192,1280]{1,0:T(8,128)(2,1)}, bf16[192,1280]{1,0:T(8,128)(2,1)S(1)}, u32[]{:S(2)}, u32[]{:S(2)}) collective-permute-start(bf16[192,1280]{1,0:T(8,128)(2,1)} %get-tuple-element.185), channel_id=1, source_target_pairs={{0,8},{8,16},{16,24},{24,0},{1,9},{9,17},{17,25},{25,1},{2,10},{10... | collective-permute-start | bytes 1474568 | tf_op jit(solution)/shard_map/ppermute | solution.py:493
  954.5 47.1 %collective-permute-start.32 = (bf16[192,1280]{1,0:T(8,128)(2,1)}, bf16[192,1280]{1,0:T(8,128)(2,1)S(1)}, u32[]{:S(2)}, u32[]{:S(2)}) collective-permute-start(bf16[192,1280]{1,0:T(8,128)(2,1)} %get-tuple-element.187), channel_id=1, source_target_pairs={{0,16},{8,24},{16,0},{24,8},{1,17},{9,25},{17,1},{25,9},{2,18},{10... | collective-permute-start | bytes 1474568 | tf_op jit(solution)/shard_map/ppermute | solution.py:493
  956.0 46.4 %collective-permute-start.33 = (bf16[192,1280]{1,0:T(8,128)(2,1)S(1)}, bf16[192,1280]{1,0:T(8,128)(2,1)}, u32[]{:S(2)}, u32[]{:S(2)}) collective-permute-start(bf16[192,1280]{1,0:T(8,128)(2,1)S(1)} %get-tuple-element.186), channel_id=1, source_target_pairs={{0,24},{8,0},{16,8},{24,16},{1,25},{9,1},{17,9},{25,17},{2,26},{10... | collective-permute-start | bytes 1474568 | tf_op jit(solution)/shard_map/ppermute | solution.py:493
  956.9 32.5 %collective-permute-start.37 = (f32[240,128]{1,0:T(8,128)S(1)}, f32[240,128]{1,0:T(8,128)S(1)}, u32[]{:S(2)}, u32[]{:S(2)}) collective-permute-start(f32[240,128]{1,0:T(8,128)S(1)} %fusion.244), channel_id=1, source_target_pairs={{0,8},{2,10},{4,12},{6,14},{8,0},{10,2},{12,4},{14,6},{16,24},{18,... | collective-permute-start | bytes 368648 | tf_op jit(solution)/shard_map/ppermute | solution.py:37
  989.5 12.2 %collective-permute-start.38 = (f32[240,128]{1,0:T(8,128)S(1)}, f32[240,128]{1,0:T(8,128)S(1)}, u32[]{:S(2)}, u32[]{:S(2)}) collective-permute-start(f32[240,128]{1,0:T(8,128)S(1)} %add.611), channel_id=1, source_target_pairs={{0,16},{2,18},{4,20},{6,22},{8,24},{10,26},{12,28},{14,30},{16,0},... | collective-permute-start | bytes 368648 | tf_op jit(solution)/shard_map/ppermute | solution.py:37
  1007.2 23.0 %collective-permute-start.39 = (bf16[160,2560]{1,0:T(8,128)(2,1)}, bf16[160,2560]{1,0:T(8,128)(2,1)}, u32[]{:S(2)}, u32[]{:S(2)}) collective-permute-start(bf16[160,2560]{1,0:T(8,128)(2,1)} %get-tuple-element.164), channel_id=1, source_target_pairs={{0,8},{8,16},{16,24},{24,0},{1,9},{9,17},{17,25},{25,1},{2,10},{10... | collective-permute-start | bytes 2457608 | tf_op jit(solution)/shard_map/ppermute | solution.py:493
  1008.8 70.7 %collective-permute-start.40 = (bf16[160,2560]{1,0:T(8,128)(2,1)}, bf16[160,2560]{1,0:T(8,128)(2,1)}, u32[]{:S(2)}, u32[]{:S(2)}) collective-permute-start(bf16[160,2560]{1,0:T(8,128)(2,1)} %get-tuple-element.166), channel_id=1, source_target_pairs={{0,16},{8,24},{16,0},{24,8},{1,17},{9,25},{17,1},{25,9},{2,18},{10... | collective-permute-start | bytes 2457608 | tf_op jit(solution)/shard_map/ppermute | solution.py:493
  1013.1 70.3 %collective-permute-start.41 = (bf16[160,2560]{1,0:T(8,128)(2,1)}, bf16[160,2560]{1,0:T(8,128)(2,1)}, u32[]{:S(2)}, u32[]{:S(2)}) collective-permute-start(bf16[160,2560]{1,0:T(8,128)(2,1)} %get-tuple-element.165), channel_id=1, source_target_pairs={{0,24},{8,0},{16,8},{24,16},{1,25},{9,1},{17,9},{25,17},{2,26},{10... | collective-permute-start | bytes 2457608 | tf_op jit(solution)/shard_map/ppermute | solution.py:493
  (145 other events, 722.7 us)
Sparse Core Ops, SparseCore 0:
  193.5 80.6 all-gather.8
  276.0 84.9 all-gather.4
  362.9 77.6 all-gather.6
  443.4 83.0 reduce-scatter.4
  529.5 77.6 reduce-scatter.6
  712.5 82.2 reduce-scatter.8
  797.9 128.3 reduce-scatter.10

commit v4 on v3

--- a/solution.py
+++ b/solution.py
@@ -50,7 +50,7 @@
     return jnp.concatenate([first, second], axis=0)
 
 
-def scan_kernel(reverse, keep_ref, drive_ref, cum_ref, state_ref):
+def run_scan(reverse, keep_ref, drive_ref, cum_ref, state_ref):
     rows, width = keep_ref.shape
     groups = rows // 8
     place = lax.broadcasted_iota(jnp.int32, (8, width), 0)
@@ -73,9 +73,13 @@
         edge = slice(0, 1) if reverse else slice(7, 8)
         return (a[edge], b[edge])
 
-    lax.fori_loop(
+    return lax.fori_loop(
         0, groups, step, (jnp.ones((1, width), F32), jnp.zeros((1, width), F32))
     )
+
+
+def scan_kernel(reverse, keep_ref, drive_ref, cum_ref, state_ref):
+    run_scan(reverse, keep_ref, drive_ref, cum_ref, state_ref)
 
 
 def local_scan(keep, drive, reverse):
@@ -95,6 +99,63 @@
     )(keep, drive)
 
 
+HALO = 8
+
+
+def mix_kernel(branch_ref, mask_ref, taps_ref, rows_ref, gate_ref, *refs):
+    conv_ref, decay_gate_ref, input_gate_ref, cum_ref, state_ref, ends_ref, keep, drive = refs
+    rows = conv_ref.shape[0]
+    conv = rows_ref[0:1, :] + taps_ref[0:1, :] * branch_ref[HALO : HALO + rows, :]
+    for k in range(1, taps_ref.shape[0]):
+        shifted = branch_ref[HALO - k : HALO - k + rows, :] * mask_ref[:, k : k + 1]
+        conv = conv + taps_ref[k : k + 1, :] * shifted
+    low = conv.astype(BF16)
+    conv_ref[...] = low
+    decay_gate = jax.nn.sigmoid(mm(low, gate_ref[0, 0]) + rows_ref[1:2, :])
+    input_gate = jax.nn.sigmoid(mm(low, gate_ref[1, 0]) + rows_ref[2:3, :])
+    decay_gate_ref[...] = decay_gate
+    input_gate_ref[...] = input_gate
+    reset = mask_ref[:, 0:1]
+    log_decay = -8.0 * decay_gate * rows_ref[3:4, :]
+    multiplier = jnp.sqrt(jnp.maximum(1.0 - jnp.exp(2.0 * log_decay), 0.001))
+    keep[...] = jnp.exp(log_decay) * (1.0 - reset)
+    drive[...] = low.astype(F32) * input_gate * (multiplier * (1.0 - reset) + reset)
+    ends_ref[0:1, :], ends_ref[1:2, :] = run_scan(False, keep, drive, cum_ref, state_ref)
+
+
+def mix(branch, masks, taps, row_params, gate_weights):
+    rows, width = branch.shape[0] - HALO, branch.shape[1]
+    block = gate_weights.shape[2]
+    over = lambda n: pl.BlockSpec((n, block), lambda h: (0, h))
+    full = jax.ShapeDtypeStruct((rows, width), F32)
+    return pl.pallas_call(
+        mix_kernel,
+        grid=(width // block,),
+        in_specs=[
+            over(rows + HALO),
+            pl.BlockSpec(masks.shape, lambda h: (0, 0)),
+            over(taps.shape[0]),
+            over(row_params.shape[0]),
+            pl.BlockSpec((2, 1, block, block), lambda h: (0, h, 0, 0)),
+        ],
+        out_specs=[over(rows)] * 5 + [over(2)],
+        out_shape=[
+            jax.ShapeDtypeStruct((rows, width), BF16),
+            full,
+            full,
+            full,
+            full,
+            jax.ShapeDtypeStruct((2, width), F32),
+        ],
+        scratch_shapes=[pltpu.VMEM((rows, block), F32)] * 2,
+        cost_estimate=pl.CostEstimate(
+            flops=4 * rows * width * block,
+            bytes_accessed=22 * rows * width,
+            transcendentals=8 * rows * width,
+        ),
+    )(branch, masks, taps, row_params, gate_weights)
+
+
 MESH_ID = pl.DeviceIdType.MESH
 VMEM = pl.BlockSpec(memory_space=pltpu.VMEM)
 ANY = pl.BlockSpec(memory_space=pl.ANY)
@@ -137,9 +198,9 @@
         copy(k, True).wait_send()
 
 
-def entering(decay, state, reverse):
+def entering(ends, reverse):
     outer, inner = lax.axis_size("o"), lax.axis_size("i")
-    count, width = outer * inner, state.shape[0]
+    count, width = outer * inner, ends.shape[1]
     carried = pl.pallas_call(
         functools.partial(enter_kernel, outer, inner, reverse),
         in_specs=[VMEM],
@@ -153,7 +214,7 @@
         compiler_params=pltpu.CompilerParams(
             collective_id=2 if reverse else 1, has_side_effects=True
         ),
-    )(jnp.stack([decay, state]))
+    )(ends)
     return carried[0]
 
 
@@ -401,15 +462,6 @@
     return gelu_tanh(gate_vals) * up_vals
 
 
-def lru_inputs(gate_decay, gate_input, conv_in, decay_in, resets):
-    log_decay = -8.0 * jax.nn.sigmoid(gate_decay) * jax.nn.softplus(decay_in)
-    decay = jnp.exp(log_decay)
-    multiplier = jnp.sqrt(jnp.maximum(-jnp.expm1(2.0 * log_decay), 0.001))
-    multiplier = jnp.where(resets, 1.0, multiplier)
-    keep_rate = jnp.where(resets, 0.0, decay)
-    return (keep_rate, conv_in * jax.nn.sigmoid(gate_input) * multiplier)
-
-
 def norm_back(values, scaling, delta):
     inverse = lax.rsqrt(jnp.mean(values * values, axis=-1, keepdims=True) + EPS)
     unit = values * inverse
@@ -485,14 +537,13 @@
     return own.reshape(lax.axis_size("o"), -1, rows.shape[-1])
 
 
-def sum_outer(parts):
+def send_parts(parts):
     count, at = lax.axis_size("o"), lax.axis_index("o")
-    total = lax.dynamic_index_in_dim(parts, at, 0, False).astype(F32)
+    moved = [lax.dynamic_index_in_dim(parts, at, 0, False)]
     for k in range(1, count):
         part = lax.dynamic_index_in_dim(parts, lax.rem(at + k, count), 0, False)
-        moved = lax.ppermute(part, "o", [(j, (j + k) % count) for j in range(count)])
-        total = total + moved.astype(F32)
-    return total
+        moved.append(lax.ppermute(part, "o", [(j, (j + k) % count) for j in range(count)]))
+    return moved
 
 
 def cuts_of(size):
@@ -555,46 +606,45 @@
         whole = gather_inner(parts[k])
         ffw_parts.append((whole[:, : 2 * size], whole[:, 2 * size :]))
     cot_own, branch_x_full = lax.optimization_barrier((half_of(cotangent, core), branch_x_full))
-    cot_whole = lax.all_gather(cot_own, "o")
-
+    cot_moved = ring(cot_own)
+
+    source_half = half_of(inputs, core).astype(F32)
     seg_marks = (segment_ids + 1).astype(F32)
-    source_half = half_of(inputs, core).astype(F32)
-    normed_low = rms_norm(inputs.astype(F32), norm_scales[0]).astype(BF16)
-    branch_x = mm(normed_low, branch_x_full) + branch_bias[0]
+    halo = from_behind(
+        jnp.concatenate(
+            [
+                inputs[tok_rows - HALO :].astype(F32),
+                jnp.broadcast_to(seg_marks[tok_rows - HALO :, None], (HALO, 128)),
+            ],
+            axis=1,
+        ),
+        1,
+    )
+    marks_after = from_behind(seg_marks[:rim_rows], -1)
+    normed_ext = rms_norm(
+        jnp.concatenate([halo[:, :width], inputs.astype(F32)], axis=0), norm_scales[0]
+    ).astype(BF16)
+    normed_low = normed_ext[HALO:]
+    marks_ext = jnp.concatenate([halo[:, width], seg_marks])
+    same = [
+        (marks_ext[HALO - k : HALO - k + tok_rows] == seg_marks).astype(F32)
+        for k in range(taps_count)
+    ]
+    masks = jnp.stack([1.0 - same[1], *same[1:], *[same[0]] * (8 - taps_count)], axis=1)
+    branch_ext = mm(normed_ext, branch_x_full) + branch_bias[0]
     branch_y = mm(normed_low, branch_y_full) + branch_bias[1]
-    rim_values, rim_marks = from_behind(
-        (branch_x[tok_rows - rim_rows :], seg_marks[tok_rows - rim_rows :]), 1
-    )
-    padded_branch = jnp.concatenate([rim_values, branch_x], axis=0)
-    padded_marks = jnp.concatenate([rim_marks, seg_marks], axis=0)
-    resets = (seg_marks != padded_marks[rim_rows - 1 : rim_rows - 1 + tok_rows])[:, None]
-    conv_out = jnp.zeros_like(branch_x) + conv_bias
-    shifted_rows = []
-    for offset in range(taps_count):
-        matches = (
-            padded_marks[rim_rows - offset : rim_rows - offset + tok_rows] == seg_marks
-        ).astype(F32)[:, None]
-        shifted = padded_branch[rim_rows - offset : rim_rows - offset + tok_rows] * matches
-        shifted_rows.append(shifted)
-        conv_out = conv_out + conv_weight[offset] * shifted
-    conv_low = conv_out.astype(BF16)
-    conv_float = conv_low.astype(F32)
+    rate = jax.nn.softplus(decay_param)
+    row_params = jnp.stack([conv_bias, gate_bias[0], gate_bias[1], rate] + [rate] * 4)
+    conv_low, decay_gate, input_gate, cumulative, local_state, ends = mix(
+        branch_ext, masks, conv_weight, row_params, gate_weights
+    )
     conv_blocks = conv_low.reshape(tok_rows, heads_half, block_size)
-    gate_pre = (
-        jnp.einsum(
-            "thb,ghbc->gthc", conv_blocks, gate_weights, preferred_element_type=F32
-        ).reshape(2, tok_rows, width_half)
-        + gate_bias[:, None, :]
-    )
-
-    def lru_local(gate_decay, gate_input, conv_in, decay_in):
-        return lru_inputs(gate_decay, gate_input, conv_in, decay_in, resets)
-
-    (keep_rate, drive_in), lru_back = jax.vjp(
-        lru_local, gate_pre[0], gate_pre[1], conv_float, decay_param
-    )
-    cumulative, local_state = local_scan(keep_rate, drive_in, False)
-    carry_in = entering(cumulative[tok_rows - 1], local_state[tok_rows - 1], False)
+    ends, cot_moved = lax.optimization_barrier((ends, cot_moved))
+    carry_in = entering(ends, False)
+    carry_in, cot_moved = lax.optimization_barrier((carry_in, cot_moved))
+    cot_halves = [cot_own, cot_moved]
+    for _ in range(2, outer):
+        cot_halves.append(ring(cot_halves[-1]))
     states = local_state + cumulative * carry_in
     branch_act, gelu_back = jax.vjp(gelu_tanh, branch_y)
     mixed_in = (states * branch_act).astype(BF16)
@@ -607,11 +657,7 @@
     )
 
     normed_slots = gather_slots(rms_norm(residual, norm_scales[1]).astype(BF16))
-    cot_other = swap(cot_whole)
-    sources = [lax.rem(along - k + outer, outer) for k in range(outer)]
-    cot_slots = [
-        [lax.dynamic_index_in_dim(w, k, 0, False) for w in (cot_whole, cot_other)] for k in sources
-    ]
+    cot_slots = [[half, swap(half)] for half in cot_halves[:outer]]
     normed_joined = [jnp.concatenate(slot) for slot in normed_slots]
     cot_joined = [jnp.concatenate(slot) for slot in cot_slots]
     bias_part = lax.dynamic_slice_in_dim(ffw_bias, along * hidden_part, hidden_part, 1)
@@ -675,18 +721,37 @@
     delta_y_low = delta_branch_y.astype(BF16)
     oy_rows = grads_rows([[([delta_mixed], mixed_in)], [([normed_low], delta_y_low)]])
     grad_oy_inner = sum_inner(oy_rows)
+    reset = masks[:, :1]
+    log_decay = -8.0 * decay_gate * rate
+    decay = jnp.exp(log_decay)
+    keep_rate = decay * (1.0 - reset)
     alpha_next = jnp.concatenate([keep_rate[1:], jnp.ones((1, width_half), F32)], axis=0)
     suffix, local_adjoint = local_scan(alpha_next, delta_states, True)
-    leaving = entering(keep_rate[0] * suffix[0], keep_rate[0] * local_adjoint[0], True)
+    leaving = entering(
+        jnp.stack([keep_rate[0] * suffix[0], keep_rate[0] * local_adjoint[0]]), True
+    )
     leaving, inner_sums[1:] = lax.optimization_barrier((leaving, inner_sums[1:]))
     for k in range(1, len(cuts)):
         grads.append(spread(inner_sums[k]))
     adjoint = local_adjoint + suffix * leaving
     states_before = jnp.concatenate([carry_in[None, :], states[: tok_rows - 1]], axis=0)
-    delta_gate_decay, delta_gate_input, delta_conv_direct, grad_decay = lru_back(
-        (adjoint * states_before, adjoint)
-    )
-    delta_gates = jnp.stack([delta_gate_decay, delta_gate_input]).astype(BF16)
+    conv_float = conv_low.astype(F32)
+    room = -jnp.expm1(2.0 * log_decay)
+    multiplier = jnp.sqrt(jnp.maximum(room, 0.001)) * (1.0 - reset) + reset
+    drawn = adjoint * input_gate
+    delta_log = keep_rate * (
+        adjoint * states_before
+        - jnp.where(room > 0.001, drawn * conv_float * decay / multiplier, 0.0)
+    )
+    decay_sum = jnp.sum(delta_log * decay_gate, axis=0)
+    delta_conv_direct = drawn * multiplier
+    delta_gates = jnp.stack(
+        [
+            delta_log * (-8.0 * rate) * decay_gate * (1.0 - decay_gate),
+            delta_conv_direct * conv_float * (1.0 - input_gate),
+        ]
+    ).astype(BF16)
+    grad_decay = -8.0 * decay_sum * jax.nn.sigmoid(decay_param)
     delta_blocks = delta_gates.reshape(2, tok_rows, heads_half, block_size)
     grad_gate_weights = jnp.einsum(
         "thb,gthc->ghbc", conv_blocks, delta_blocks, preferred_element_type=F32
@@ -701,7 +766,7 @@
     delta_conv = delta_conv_direct + jnp.einsum(
         "gthc,ghbc->thb", delta_blocks, gate_weights, preferred_element_type=F32
     ).reshape(tok_rows, width_half)
-    rim_delta, rim_next_marks = from_behind((delta_conv[:rim_rows], seg_marks[:rim_rows]), -1)
+    rim_delta = from_behind(delta_conv[:rim_rows], -1)
     rim_delta, result_parts = lax.optimization_barrier((rim_delta, result_parts))
     result_moved = send_direct(result_parts)
     ffw_in_grad = jnp.concatenate(
@@ -719,7 +784,7 @@
     )
     ffw_out_grad = ffw_out_grad.transpose(0, 2, 1).reshape(hidden_half, part_width).astype(F32)
     padded_delta = jnp.concatenate([delta_conv, rim_delta], axis=0)
-    next_marks = jnp.concatenate([seg_marks, rim_next_marks], axis=0)
+    next_marks = jnp.concatenate([seg_marks, marks_after], axis=0)
     delta_branch_x = jnp.zeros_like(delta_conv)
     conv_weight_rows = []
     for offset in range(taps_count):
@@ -728,7 +793,8 @@
             delta_branch_x
             + conv_weight[offset] * padded_delta[offset : offset + tok_rows] * matches
         )
-        conv_weight_rows.append(jnp.sum(delta_conv * shifted_rows[offset], axis=0))
+        shifted = branch_ext[HALO - offset : HALO - offset + tok_rows] * same[offset][:, None]
+        conv_weight_rows.append(jnp.sum(delta_conv * shifted, axis=0))
     grad_conv_bias = jnp.sum(delta_conv, axis=0)
     delta_x_low = delta_branch_x.astype(BF16)
     x_rows = grads_rows([[([normed_low], delta_x_low)]], gate_rows)
@@ -760,15 +826,16 @@
         grad_decay,
         grad_ffw_bias.reshape(-1),
     ]
+    oy_moved = send_parts(grad_oy_inner)
     small = sum_over_all(jnp.concatenate(flat).reshape(-1, 128))
-    small, grad_oy_inner = lax.optimization_barrier((small, grad_oy_inner))
-    grad_oy = sum_outer(grad_oy_inner)
     result_half = residual + sum(part.astype(F32) for part in result_moved) + out_bias[1]
     result = join_halves(result_half, swap(result_half), core)
     grad_x_inner, input_grad, result, ffw_in_grad, ffw_out_grad = lax.optimization_barrier(
         (grad_x_inner, input_grad, result, ffw_in_grad, ffw_out_grad)
     )
-    grad_x_gate = sum_outer(grad_x_inner)
+    x_moved = send_parts(grad_x_inner)
+    grad_oy = sum(part.astype(F32) for part in oy_moved)
+    grad_x_gate = sum(part.astype(F32) for part in x_moved)
     grad_branch_x = grad_x_gate[:part_width]
     gate_grad = grad_x_gate[part_width:].reshape(2, heads_half, block_size // count, block_size)
     small = small.reshape(-1)

time: 1100 us -> 1110 us (level)
  the two profiles are of different devices: /device:TPU:12 before, /device:TPU:0 now
where the time goes in v4:
time: 1110 us; the launch traced here: 1090 us
  waiting for transfers between devices  362 us (33%)
  Pallas kernels  275 us (25%)
  matrix products  130 us (12%)
  local copies, waits for them, and re-layouts  119 us (11%)
  other arithmetic  106 us (10%)
  starting transfers between devices  80.5 us (7%)
  between operations  16.6 us (1%)
    pallas_call x1, Pallas kernels, gather_weights(): pl.pallas_call(functools.partial(gather_kernel, outer, groups, parts), in...  174 us
    ppermute x9, waiting for transfers between devices, ring(): lax.ppermute(value, 'o', [(k, (k + 1) % count) for k in range(count)])  167 us
    dot_general x38, matrix products, dot(): lax.dot_general(a, b, ((contract[0], contract[1]), ((), ())), preferred_e...  125 us
    ppermute x6, waiting for transfers between devices, send_parts(): lax.ppermute(part, 'o', [(j, (j + k) % count) for j in range(count)])  80.8 us
    pallas_call x4, Pallas kernels, grads_rows(): pl.pallas_call(functools.partial(grads_kernel, plan, added), grid=(outer,...  63.7 us
    ppermute x3, waiting for transfers between devices, send_direct(): lax.ppermute(halves[k], 'o', [(j, (j - k) % count) for j in range(count)])  57.3 us
    all_to_all x2, starting transfers between devices, spread(): return lax.all_to_all(value, 'o', 0, 0, tiled=True)  53.7 us
    all_to_all x2, waiting for transfers between devices, spread(): return lax.all_to_all(value, 'o', 0, 0, tiled=True)  34.2 us
  transfers between devices with their start and end apart: 55, of which 19 were waited for; matrix products, arithmetic and copies ran while one was open for 26% of the time, Pallas kernels for 8%

profile of v4, /device:TPU:0, one launch (start us, length us, event | category | flops | bytes accessed | tf_op | source)
XLA Modules:
  0.0 1089.8 jit_solution(3828093048750071091)
XLA Ops:
  18.6 174.3 %shard_map.271 = (bf16[4,4,160,1280]{3,2,1,0:T(8,128)(2,1)}, bf16[4,4,160,1280]{3,2,1,0:T(8,128)(2,1)}, bf16[4,4,160,1280]{3,2,1,0:T(8,128)(2,1)}, bf16[4,160,1536]{2,1,0:T(8,128)(2,1)}, bf16[4,160,1344]{2,1,0:T(8,128)(2,1)}) custom-call(bf16[160,1280]{1,0:T(8,128)(2,1)} %get-tuple-element.234.refs_0_, bf16[160,1280]{1,0:T(8,128)(2,1)} %get-tuple-element.233.refs_1_, ...), custom_call_target="tpu_custom_call" | custom-call | tf_op jit(solution)/shard_map/pallas_call | solution.py:373
  200.7 3.5 collective-permute-start.1
  213.4 7.6 convolution_add_fusion.9.branch_ref
  222.5 10.5 shard_map.272
  233.0 7.5 convolution_add_fusion.10
  240.5 9.9 shard_map.273
  251.1 4.8 multiply_convert_fusion.3
  255.9 5.3 fusion.192
  268.2 21.8 %collective-permute-done.10.refs_18_ = bf16[192,2560]{1,0:T(8,128)(2,1)} collective-permute-done((bf16[192,2560]{1,0:T(8,128)(2,1)}, bf16[192,2560]{1,0:T(8,128)(2,1)}, u32[]{:S(2)}, u32[]{:S(2)}) %collective-permute-start.10) | collective-permute-done | bytes 983072 | tf_op jit(solution)/shard_map/ppermute | solution.py:25
  290.0 2.8 multiply_reduce_fusion.4
  298.3 18.3 %collective-permute-done.14.refs_21_ = bf16[192,2560]{1,0:T(8,128)(2,1)S(1)} collective-permute-done((bf16[192,2560]{1,0:T(8,128)(2,1)}, bf16[192,2560]{1,0:T(8,128)(2,1)S(1)}, u32[]{:S(2)}, u32[]{:S(2)}) %collective-permute-start.14) | collective-permute-done | bytes 983072 | tf_op jit(solution)/shard_map/ppermute | solution.py:25
  316.6 19.7 %collective-permute-done.5.refs_3_ = bf16[192,2560]{1,0:T(8,128)(2,1)S(1)} collective-permute-done((bf16[192,2560]{1,0:T(8,128)(2,1)S(1)}, bf16[192,2560]{1,0:T(8,128)(2,1)S(1)}, u32[]{:S(2)}, u32[]{:S(2)}) %collective-permute-start.5) | collective-permute-done | bytes 983072 | tf_op jit(solution)/shard_map/ppermute | solution.py:25
  337.4 23.3 %collective-permute-done.8.refs_6_ = bf16[192,2560]{1,0:T(8,128)(2,1)S(1)} collective-permute-done((bf16[192,2560]{1,0:T(8,128)(2,1)S(1)}, bf16[192,2560]{1,0:T(8,128)(2,1)S(1)}, u32[]{:S(2)}, u32[]{:S(2)}) %collective-permute-start.8) | collective-permute-done | bytes 983072 | tf_op jit(solution)/shard_map/ppermute | solution.py:25
  363.6 20.6 %collective-permute-done.12.refs_9_ = bf16[192,2560]{1,0:T(8,128)(2,1)S(1)} collective-permute-done((bf16[192,2560]{1,0:T(8,128)(2,1)S(1)}, bf16[192,2560]{1,0:T(8,128)(2,1)S(1)}, u32[]{:S(2)}, u32[]{:S(2)}) %collective-permute-start.12) | collective-permute-done | bytes 983072 | tf_op jit(solution)/shard_map/ppermute | solution.py:25
  389.3 5.4 convolution_add_fusion.11
  408.3 4.1 fusion.86
  420.7 22.2 %shard_map.274 = bf16[4,4,160,1536]{3,2,1,0:T(8,128)(2,1)} custom-call(bf16[192,2560]{1,0:T(8,128)(2,1)} %copy-done.23, bf16[192,2560]{1,0:T(8,128)(2,1)} %copy-done.70, bf16[384,1024]{1,0:T(8,128)(2,1)} %pad_maximum_fusion.12.refs_2_, bf16[192,2560]{1,0:T(8,128)(2,1)} %copy-done.58, bf16[192,2560]{1,0:T(8,128)(2,1)} %copy-done.62, ...), custom_call_target="tpu_custom_call" | custom-call | flops 12079595520 | bytes 20447232 | tf_op jit(solution)/shard_map/pallas_call | solution.py:442
  443.6 5.2 convolution_add_fusion.15
  449.8 4.1 fusion.128
  471.4 4.7 convolution_add_fusion.17
  490.7 4.2 fusion.70
  495.0 22.1 %shard_map.277 = bf16[4,4,160,1344]{3,2,1,0:T(8,128)(2,1)} custom-call(bf16[192,2560]{1,0:T(8,128)(2,1)} %copy-done.23, bf16[192,2560]{1,0:T(8,128)(2,1)} %copy-done.70, bf16[384,896]{1,0:T(8,128)(2,1)} %pad_maximum_fusion.16.refs_2_, bf16[192,2560]{1,0:T(8,128)(2,1)} %copy-done.58, bf16[192,2560]{1,0:T(8,128)(2,1)} %copy-done.62, ...), custom_call_target="tpu_custom_call" | custom-call | flops 10569646080 | bytes 18874368 | tf_op jit(solution)/shard_map/pallas_call | solution.py:442
  518.2 5.8 convolution_add_fusion.8
  525.1 3.1 fusion.149
  528.2 3.1 fusion.151
  542.7 17.5 %collective-permute-done.20 = bf16[192,2560]{1,0:T(8,128)(2,1)S(1)} collective-permute-done((bf16[192,2560]{1,0:T(8,128)(2,1)S(1)}, bf16[192,2560]{1,0:T(8,128)(2,1)S(1)}, u32[]{:S(2)}, u32[]{:S(2)}) %collective-permute-start.20) | collective-permute-done | bytes 983072 | tf_op jit(solution)/shard_map/ppermute | solution.py:25
  564.7 23.1 %collective-permute-done.21 = bf16[192,2560]{1,0:T(8,128)(2,1)S(1)} collective-permute-done((bf16[192,2560]{1,0:T(8,128)(2,1)S(1)}, bf16[192,2560]{1,0:T(8,128)(2,1)S(1)}, u32[]{:S(2)}, u32[]{:S(2)}) %collective-permute-start.21) | collective-permute-done | bytes 983072 | tf_op jit(solution)/shard_map/ppermute | solution.py:25
  592.0 22.5 %collective-permute-done.22 = bf16[192,2560]{1,0:T(8,128)(2,1)S(1)} collective-permute-done((bf16[192,2560]{1,0:T(8,128)(2,1)S(1)}, bf16[192,2560]{1,0:T(8,128)(2,1)S(1)}, u32[]{:S(2)}, u32[]{:S(2)}) %collective-permute-start.22) | collective-permute-done | bytes 983072 | tf_op jit(solution)/shard_map/ppermute | solution.py:25
  614.5 2.8 fusion.52
  621.6 3.1 slice.511.refs_0_.refs_2_
  629.3 3.0 concatenate.135.keep_ref
  635.0 8.3 convert_reduce_fusion.2
  643.3 7.1 shard_map.275
  651.8 9.1 shard_map.276
  661.8 7.2 multiply_reduce_fusion.1
  679.2 4.0 fusion.56
  683.2 2.9 copy.113
  686.2 6.2 fusion.36
  695.8 3.7 convert_element_type.308.refs_2_
  699.5 7.1 convert_reduce_fusion.3
  706.6 8.1 shard_map.278
  714.7 2.9 pad_maximum_fusion.6.refs_0_
  717.6 11.3 %shard_map.279 = bf16[4,4,160,2560]{3,2,1,0:T(8,128)(2,1)} custom-call(bf16[384,2560]{1,0:T(8,128)(2,1)} %pad_maximum_fusion.6.refs_0_, bf16[384,1280]{1,0:T(8,128)(2,1)} %copy-done.22, bf16[384,2560]{1,0:T(8,128)(2,1)} %slice.511.refs_0_.refs_2_, bf16[384,1280]{1,0:T(8,128)(2,1)} %get-tuple-element.146.refs_3_), custom_call_target="tpu_custom_call" | custom-call | flops 5033164800 | bytes 17039360 | tf_op jit(solution)/shard_map/pallas_call | solution.py:442
  733.7 5.3 fusion.193
  738.9 5.0 convolution_add_fusion.4
  747.6 7.5 all-to-all-start
  757.4 4.0 collective-permute-start.32
  762.6 3.0 fusion.14
  767.2 34.2 %all-to-all-done = bf16[4,160,1536]{2,1,0:T(8,128)(2,1)} async-done(((bf16[4,160,1536]{2,1,0:T(8,128)(2,1)}), bf16[4,160,1536]{2,1,0:T(8,128)(2,1)}, u32[]{:S(2)}, u32[]{:S(2)}) %all-to-all-start) | async-done | bytes 1966112 | tf_op jit(solution)/shard_map/all_to_all | solution.py:526
  801.4 46.1 %all-to-all-start.1 = ((bf16[4,160,1344]{2,1,0:T(8,128)(2,1)}), bf16[4,160,1344]{2,1,0:T(8,128)(2,1)}, u32[]{:S(2)}, u32[]{:S(2)}) async-start(bf16[4,160,1344]{2,1,0:T(8,128)(2,1)} %bitcast.197), calls=%async_computation.4 | async-start | bytes 3604480 | tf_op jit(solution)/shard_map/all_to_all | solution.py:526
  847.7 57.3 %collective-permute-done.33 = bf16[192,2560]{1,0:T(8,128)(2,1)} collective-permute-done((bf16[192,2560]{1,0:T(8,128)(2,1)}, bf16[192,2560]{1,0:T(8,128)(2,1)}, u32[]{:S(2)}, u32[]{:S(2)}) %collective-permute-start.33) | collective-permute-done | bytes 983072 | tf_op jit(solution)/shard_map/ppermute | solution.py:520
  905.0 8.4 add_add_fusion
  913.5 8.7 collective-permute-done.44
  922.3 5.1 collective-permute-done.45
  928.6 6.8 collective-permute-done.46
  942.9 3.4 reshape.236
  948.8 4.3 reshape.222
  955.5 5.7 copy.116
  961.2 7.4 reshape.235
  987.9 3.1 dynamic-slice_bitcast_fusion.2
  993.1 2.7 collective-permute-done.36
  996.0 20.9 %collective-permute-done.37 = bf16[192,1280]{1,0:T(8,128)(2,1)S(1)} collective-permute-done((bf16[192,1280]{1,0:T(8,128)(2,1)}, bf16[192,1280]{1,0:T(8,128)(2,1)S(1)}, u32[]{:S(2)}, u32[]{:S(2)}) %collective-permute-start.37) | collective-permute-done | bytes 491552 | tf_op jit(solution)/shard_map/ppermute | solution.py:545
  1021.7 12.7 %collective-permute-done.39 = bf16[160,2560]{1,0:T(8,128)(2,1)S(1)} collective-permute-done((bf16[160,2560]{1,0:T(8,128)(2,1)}, bf16[160,2560]{1,0:T(8,128)(2,1)S(1)}, u32[]{:S(2)}, u32[]{:S(2)}) %collective-permute-start.39) | collective-permute-done | bytes 819232 | tf_op jit(solution)/shard_map/ppermute | solution.py:545
  1034.4 44.6 %collective-permute-done.40 = bf16[160,2560]{1,0:T(8,128)(2,1)S(1)} collective-permute-done((bf16[160,2560]{1,0:T(8,128)(2,1)}, bf16[160,2560]{1,0:T(8,128)(2,1)S(1)}, u32[]{:S(2)}, u32[]{:S(2)}) %collective-permute-start.40) | collective-permute-done | bytes 819232 | tf_op jit(solution)/shard_map/ppermute | solution.py:545
  (587 shorter events, 213.3 us)
Async XLA Ops:
  7.2 257.4 %copy-start = (f32[2,3840]{1,0:T(2,128)S(1)}, f32[2,3840]{1,0:T(2,128)}, u32[]{:S(2)}) copy-start(f32[2,3840]{1,0:T(2,128)} %param.31) | copy-start | bytes 92164
  7.2 382.1 %all-gather.3.cloned.1.call-start = ((), (), s32[]{:S(2)}) async-start(), calls=%async_computation.6 | async-start | bytes 9830400 | tf_op jit(solution)/shard_map/all_gather | solution.py:530
  193.1 250.5 %all-gather.5.cloned.1.call-start = ((), (), s32[]{:S(2)}) async-start(), calls=%async_computation.7 | async-start | bytes 9011200 | tf_op jit(solution)/shard_map/all_gather | solution.py:530
  194.7 13.4 %collective-permute-start = (f32[8,2688]{1,0:T(8,128)S(1)}, f32[8,2688]{1,0:T(8,128)S(1)}, u32[]{:S(2)}, u32[]{:S(2)}) collective-permute-start(f32[8,2688]{1,0:T(8,128)S(1)} %pad_maximum_fusion.20), channel_id=1, source_target_pairs={{0,2},{2,4},{4,6},{6,8},{8,10},{10,12},{12,14},{14,16},{16,18},{18... | collective-permute-start | bytes 258056 | tf_op jit(solution)/shard_map/ppermute | solution.py:31
  197.2 10.9 collective-permute-start.29
  200.7 64.6 %copy-start.8 = (bf16[192,2560]{1,0:T(8,128)(2,1)}, bf16[192,2560]{1,0:T(8,128)(2,1)S(1)}, u32[]{:S(2)}) copy-start(bf16[192,2560]{1,0:T(8,128)(2,1)S(1)} %get-tuple-element.75.refs_12_) | copy-start | bytes 2949124
  200.7 39.7 %collective-permute-start.1 = (bf16[192,2560]{1,0:T(8,128)(2,1)S(1)}, bf16[192,2560]{1,0:T(8,128)(2,1)}, u32[]{:S(2)}, u32[]{:S(2)}) collective-permute-start(bf16[192,2560]{1,0:T(8,128)(2,1)S(1)} %get-tuple-element.75.refs_12_), channel_id=1, source_target_pairs={{0,8},{8,16},{16,24},{24,0},{1,9},{9,17},{17,25},{25,1},{2,10},{10... | collective-permute-start | bytes 2949128 | tf_op jit(solution)/shard_map/ppermute | solution.py:25
  208.0 84.8 %copy-start.99 = (f32[2560]{0:T(1024)}, f32[2560]{0:T(1024)S(1)}, u32[]{:S(2)}) copy-start(f32[2560]{0:T(1024)S(1)} %get-tuple-element.138) | copy-start | bytes 30724
  263.7 26.3 %collective-permute-start.2 = (f32[192,2560]{1,0:T(8,128)}, f32[192,2560]{1,0:T(8,128)}, u32[]{:S(2)}, u32[]{:S(2)}) collective-permute-start(f32[192,2560]{1,0:T(8,128)} %constant_dynamic-slice_fusion.1), channel_id=1, source_target_pairs={{0,1},{1,0},{2,3},{3,2},{4,5},{5,4},{6,7},{7,6},{8,9},{9,8},{10,11... | collective-permute-start | bytes 5898248 | tf_op jit(solution)/shard_map/ppermute | solution.py:20
  263.7 26.3 %collective-permute-start.10 = (bf16[192,2560]{1,0:T(8,128)(2,1)}, bf16[192,2560]{1,0:T(8,128)(2,1)}, u32[]{:S(2)}, u32[]{:S(2)}) collective-permute-start(bf16[192,2560]{1,0:T(8,128)(2,1)} %collective-permute-done.1.refs_15_), channel_id=1, source_target_pairs={{0,8},{8,16},{16,24},{24,0},{1,9},{9,17},{17,25},{25,1},{2,10},{10... | collective-permute-start | bytes 2949128 | tf_op jit(solution)/shard_map/ppermute | solution.py:25
  264.3 29.3 %collective-permute-start.3 = (bf16[192,2560]{1,0:T(8,128)(2,1)S(1)}, bf16[192,2560]{1,0:T(8,128)(2,1)}, u32[]{:S(2)}, u32[]{:S(2)}) collective-permute-start(bf16[192,2560]{1,0:T(8,128)(2,1)S(1)} %get-tuple-element.75.refs_12_), channel_id=1, source_target_pairs={{0,1},{1,0},{2,3},{3,2},{4,5},{5,4},{6,7},{7,6},{8,9},{9,8},{10,11... | collective-permute-start | bytes 2949128 | tf_op jit(solution)/shard_map/ppermute | solution.py:20
  264.5 352.8 %reduce-scatter.5.cloned.1.call-start = ((), (), s32[]{:S(2)}) async-start(), calls=%async_computation.8 | async-start | bytes 9830400 | tf_op jit(solution)/shard_map/reduce_scatter | solution.py:534
  265.4 31.7 %collective-permute-start.7 = (bf16[192,2560]{1,0:T(8,128)(2,1)}, bf16[192,2560]{1,0:T(8,128)(2,1)S(1)}, u32[]{:S(2)}, u32[]{:S(2)}) collective-permute-start(bf16[192,2560]{1,0:T(8,128)(2,1)} %collective-permute-done.1.refs_15_), channel_id=1, source_target_pairs={{0,1},{1,0},{2,3},{3,2},{4,5},{5,4},{6,7},{7,6},{8,9},{9,8},{10,11... | collective-permute-start | bytes 2949128 | tf_op jit(solution)/shard_map/ppermute | solution.py:20
  290.0 26.6 %collective-permute-start.14 = (bf16[192,2560]{1,0:T(8,128)(2,1)}, bf16[192,2560]{1,0:T(8,128)(2,1)S(1)}, u32[]{:S(2)}, u32[]{:S(2)}) collective-permute-start(bf16[192,2560]{1,0:T(8,128)(2,1)} %collective-permute-done.10.refs_18_), channel_id=1, source_target_pairs={{0,8},{8,16},{16,24},{24,0},{1,9},{9,17},{17,25},{25,1},{2,10},{10... | collective-permute-start | bytes 2949128 | tf_op jit(solution)/shard_map/ppermute | solution.py:25
  293.1 121.2 %copy-start.23 = (bf16[192,2560]{1,0:T(8,128)(2,1)}, bf16[192,2560]{1,0:T(8,128)(2,1)S(1)}, u32[]{:S(2)}) copy-start(bf16[192,2560]{1,0:T(8,128)(2,1)S(1)} %multiply_convert_fusion.2.refs_0_) | copy-start | bytes 2949124
  293.1 43.3 %collective-permute-start.5 = (bf16[192,2560]{1,0:T(8,128)(2,1)S(1)}, bf16[192,2560]{1,0:T(8,128)(2,1)S(1)}, u32[]{:S(2)}, u32[]{:S(2)}) collective-permute-start(bf16[192,2560]{1,0:T(8,128)(2,1)S(1)} %multiply_convert_fusion.2.refs_0_), channel_id=1, source_target_pairs={{0,8},{8,16},{16,24},{24,0},{1,9},{9,17},{17,25},{25,1},{2,10},{10... | collective-permute-start | bytes 2949128 | tf_op jit(solution)/shard_map/ppermute | solution.py:25
  295.1 41.3 %collective-permute-start.11 = (bf16[192,2560]{1,0:T(8,128)(2,1)}, bf16[192,2560]{1,0:T(8,128)(2,1)S(1)}, u32[]{:S(2)}, u32[]{:S(2)}) collective-permute-start(bf16[192,2560]{1,0:T(8,128)(2,1)} %collective-permute-done.10.refs_18_), channel_id=1, source_target_pairs={{0,1},{1,0},{2,3},{3,2},{4,5},{5,4},{6,7},{7,6},{8,9},{9,8},{10,11... | collective-permute-start | bytes 2949128 | tf_op jit(solution)/shard_map/ppermute | solution.py:20
  297.1 39.4 %copy-start.56 = (bf16[192,2560]{1,0:T(8,128)(2,1)}, bf16[192,2560]{1,0:T(8,128)(2,1)S(1)}, u32[]{:S(2)}) copy-start(bf16[192,2560]{1,0:T(8,128)(2,1)S(1)} %collective-permute-done.7.refs_16_) | copy-start | bytes 2949124
  298.3 64.3 %collective-permute-start.4 = (bf16[192,2560]{1,0:T(8,128)(2,1)S(1)}, bf16[192,2560]{1,0:T(8,128)(2,1)S(1)}, u32[]{:S(2)}, u32[]{:S(2)}) collective-permute-start(bf16[192,2560]{1,0:T(8,128)(2,1)S(1)} %multiply_convert_fusion.2.refs_0_), channel_id=1, source_target_pairs={{0,1},{1,0},{2,3},{3,2},{4,5},{5,4},{6,7},{7,6},{8,9},{9,8},{10,11... | collective-permute-start | bytes 2949128 | tf_op jit(solution)/shard_map/ppermute | solution.py:20
  316.6 44.2 %collective-permute-start.15 = (bf16[192,2560]{1,0:T(8,128)(2,1)S(1)}, bf16[192,2560]{1,0:T(8,128)(2,1)S(1)}, u32[]{:S(2)}, u32[]{:S(2)}) collective-permute-start(bf16[192,2560]{1,0:T(8,128)(2,1)S(1)} %collective-permute-done.14.refs_21_), channel_id=1, source_target_pairs={{0,1},{1,0},{2,3},{3,2},{4,5},{5,4},{6,7},{7,6},{8,9},{9,8},{10,11... | collective-permute-start | bytes 2949128 | tf_op jit(solution)/shard_map/ppermute | solution.py:20
  336.4 24.3 %collective-permute-start.8 = (bf16[192,2560]{1,0:T(8,128)(2,1)S(1)}, bf16[192,2560]{1,0:T(8,128)(2,1)S(1)}, u32[]{:S(2)}, u32[]{:S(2)}) collective-permute-start(bf16[192,2560]{1,0:T(8,128)(2,1)S(1)} %collective-permute-done.5.refs_3_), channel_id=1, source_target_pairs={{0,8},{8,16},{16,24},{24,0},{1,9},{9,17},{17,25},{25,1},{2,10},{10... | collective-permute-start | bytes 2949128 | tf_op jit(solution)/shard_map/ppermute | solution.py:25
  336.6 47.6 %collective-permute-start.6 = (bf16[192,2560]{1,0:T(8,128)(2,1)S(1)}, bf16[192,2560]{1,0:T(8,128)(2,1)S(1)}, u32[]{:S(2)}, u32[]{:S(2)}) collective-permute-start(bf16[192,2560]{1,0:T(8,128)(2,1)S(1)} %collective-permute-done.5.refs_3_), channel_id=1, source_target_pairs={{0,1},{1,0},{2,3},{3,2},{4,5},{5,4},{6,7},{7,6},{8,9},{9,8},{10,11... | collective-permute-start | bytes 2949128 | tf_op jit(solution)/shard_map/ppermute | solution.py:20
  360.6 23.6 %collective-permute-start.12 = (bf16[192,2560]{1,0:T(8,128)(2,1)S(1)}, bf16[192,2560]{1,0:T(8,128)(2,1)S(1)}, u32[]{:S(2)}, u32[]{:S(2)}) collective-permute-start(bf16[192,2560]{1,0:T(8,128)(2,1)S(1)} %collective-permute-done.8.refs_6_), channel_id=1, source_target_pairs={{0,8},{8,16},{16,24},{24,0},{1,9},{9,17},{17,25},{25,1},{2,10},{10... | collective-permute-start | bytes 2949128 | tf_op jit(solution)/shard_map/ppermute | solution.py:25
  363.5 21.9 %collective-permute-start.9 = (bf16[192,2560]{1,0:T(8,128)(2,1)S(1)}, bf16[192,2560]{1,0:T(8,128)(2,1)S(1)}, u32[]{:S(2)}, u32[]{:S(2)}) collective-permute-start(bf16[192,2560]{1,0:T(8,128)(2,1)S(1)} %collective-permute-done.8.refs_6_), channel_id=1, source_target_pairs={{0,1},{1,0},{2,3},{3,2},{4,5},{5,4},{6,7},{7,6},{8,9},{9,8},{10,11... | collective-permute-start | bytes 2949128 | tf_op jit(solution)/shard_map/ppermute | solution.py:20
  384.2 2.6 collective-permute-start.13
  442.9 218.8 %reduce-scatter.7.cloned.1.call-start = ((), (), s32[]{:S(2)}) async-start(), calls=%async_computation.9 | async-start | bytes 9011200 | tf_op jit(solution)/shard_map/reduce_scatter | solution.py:534
  458.9 35.9 %collective-permute-start.19 = (bf16[192,2560]{1,0:T(8,128)(2,1)S(1)}, bf16[192,2560]{1,0:T(8,128)(2,1)S(1)}, u32[]{:S(2)}, u32[]{:S(2)}) collective-permute-start(bf16[192,2560]{1,0:T(8,128)(2,1)S(1)} %slice.896), channel_id=1, source_target_pairs={{0,1},{1,0},{2,3},{3,2},{4,5},{5,4},{6,7},{7,6},{8,9},{9,8},{10,11... | collective-permute-start | bytes 2949128 | tf_op jit(solution)/shard_map/ppermute | solution.py:20
  471.2 71.0 %collective-permute-start.18 = (bf16[192,2560]{1,0:T(8,128)(2,1)}, bf16[192,2560]{1,0:T(8,128)(2,1)}, u32[]{:S(2)}, u32[]{:S(2)}) collective-permute-start(bf16[192,2560]{1,0:T(8,128)(2,1)} %slice.897), channel_id=1, source_target_pairs={{0,1},{1,0},{2,3},{3,2},{4,5},{5,4},{6,7},{7,6},{8,9},{9,8},{10,11... | collective-permute-start | bytes 2949128 | tf_op jit(solution)/shard_map/ppermute | solution.py:20
  484.6 80.1 %collective-permute-start.17 = (bf16[192,2560]{1,0:T(8,128)(2,1)}, bf16[192,2560]{1,0:T(8,128)(2,1)}, u32[]{:S(2)}, u32[]{:S(2)}) collective-permute-start(bf16[192,2560]{1,0:T(8,128)(2,1)} %slice.898), channel_id=1, source_target_pairs={{0,1},{1,0},{2,3},{3,2},{4,5},{5,4},{6,7},{7,6},{8,9},{9,8},{10,11... | collective-permute-start | bytes 2949128 | tf_op jit(solution)/shard_map/ppermute | solution.py:20
  517.1 460.3 %reduce-scatter.9.cloned.1.call-start = ((), (), s32[]{:S(2)}) async-start(), calls=%async_computation.10 | async-start | bytes 9830400 | tf_op jit(solution)/shard_map/reduce_scatter | solution.py:534
  525.0 67.0 %collective-permute-start.16 = (bf16[192,2560]{1,0:T(8,128)(2,1)}, bf16[192,2560]{1,0:T(8,128)(2,1)}, u32[]{:S(2)}, u32[]{:S(2)}) collective-permute-start(bf16[192,2560]{1,0:T(8,128)(2,1)} %slice.899), channel_id=1, source_target_pairs={{0,1},{1,0},{2,3},{3,2},{4,5},{5,4},{6,7},{7,6},{8,9},{9,8},{10,11... | collective-permute-start | bytes 2949128 | tf_op jit(solution)/shard_map/ppermute | solution.py:20
  533.8 26.4 %collective-permute-start.20 = (bf16[192,2560]{1,0:T(8,128)(2,1)S(1)}, bf16[192,2560]{1,0:T(8,128)(2,1)S(1)}, u32[]{:S(2)}, u32[]{:S(2)}) collective-permute-start(bf16[192,2560]{1,0:T(8,128)(2,1)S(1)} %slice_add_fusion.4), channel_id=1, source_target_pairs={{0,8},{8,16},{16,24},{24,0},{1,9},{9,17},{17,25},{25,1},{2,10},{10... | collective-permute-start | bytes 2949128 | tf_op jit(solution)/shard_map/ppermute | solution.py:25
  537.3 24.5 %collective-permute-start.26 = (bf16[192,2560]{1,0:T(8,128)(2,1)S(1)}, bf16[192,2560]{1,0:T(8,128)(2,1)S(1)}, u32[]{:S(2)}, u32[]{:S(2)}) collective-permute-start(bf16[192,2560]{1,0:T(8,128)(2,1)S(1)} %slice.892), channel_id=1, source_target_pairs={{0,1},{1,0},{2,3},{3,2},{4,5},{5,4},{6,7},{7,6},{8,9},{9,8},{10,11... | collective-permute-start | bytes 2949128 | tf_op jit(solution)/shard_map/ppermute | solution.py:20
  542.2 20.8 %collective-permute-start.25 = (bf16[192,2560]{1,0:T(8,128)(2,1)S(1)}, bf16[192,2560]{1,0:T(8,128)(2,1)S(1)}, u32[]{:S(2)}, u32[]{:S(2)}) collective-permute-start(bf16[192,2560]{1,0:T(8,128)(2,1)S(1)} %slice.893), channel_id=1, source_target_pairs={{0,1},{1,0},{2,3},{3,2},{4,5},{5,4},{6,7},{7,6},{8,9},{9,8},{10,11... | collective-permute-start | bytes 2949128 | tf_op jit(solution)/shard_map/ppermute | solution.py:20
  560.2 29.2 %collective-permute-start.24 = (bf16[192,2560]{1,0:T(8,128)(2,1)S(1)}, bf16[192,2560]{1,0:T(8,128)(2,1)S(1)}, u32[]{:S(2)}, u32[]{:S(2)}) collective-permute-start(bf16[192,2560]{1,0:T(8,128)(2,1)S(1)} %slice.894), channel_id=1, source_target_pairs={{0,1},{1,0},{2,3},{3,2},{4,5},{5,4},{6,7},{7,6},{8,9},{9,8},{10,11... | collective-permute-start | bytes 2949128 | tf_op jit(solution)/shard_map/ppermute | solution.py:20
  561.8 26.0 %collective-permute-start.21 = (bf16[192,2560]{1,0:T(8,128)(2,1)S(1)}, bf16[192,2560]{1,0:T(8,128)(2,1)S(1)}, u32[]{:S(2)}, u32[]{:S(2)}) collective-permute-start(bf16[192,2560]{1,0:T(8,128)(2,1)S(1)} %fusion.49), channel_id=1, source_target_pairs={{0,8},{8,16},{16,24},{24,0},{1,9},{9,17},{17,25},{25,1},{2,10},{10... | collective-permute-start | bytes 2949128 | tf_op jit(solution)/shard_map/ppermute | solution.py:25
  563.0 27.6 %collective-permute-start.23 = (bf16[192,2560]{1,0:T(8,128)(2,1)S(1)}, bf16[192,2560]{1,0:T(8,128)(2,1)S(1)}, u32[]{:S(2)}, u32[]{:S(2)}) collective-permute-start(bf16[192,2560]{1,0:T(8,128)(2,1)S(1)} %slice.895), channel_id=1, source_target_pairs={{0,1},{1,0},{2,3},{3,2},{4,5},{5,4},{6,7},{7,6},{8,9},{9,8},{10,11... | collective-permute-start | bytes 2949128 | tf_op jit(solution)/shard_map/ppermute | solution.py:20
  589.4 25.1 %collective-permute-start.22 = (bf16[192,2560]{1,0:T(8,128)(2,1)S(1)}, bf16[192,2560]{1,0:T(8,128)(2,1)S(1)}, u32[]{:S(2)}, u32[]{:S(2)}) collective-permute-start(bf16[192,2560]{1,0:T(8,128)(2,1)S(1)} %fusion.51), channel_id=1, source_target_pairs={{0,8},{8,16},{16,24},{24,0},{1,9},{9,17},{17,25},{25,1},{2,10},{10... | collective-permute-start | bytes 2949128 | tf_op jit(solution)/shard_map/ppermute | solution.py:25
  592.0 25.3 %copy-start.3 = (f32[192,2560]{1,0:T(8,128)S(1)}, f32[192,2560]{1,0:T(8,128)}, u32[]{:S(2)}) copy-start(f32[192,2560]{1,0:T(8,128)} %copy-done.2) | copy-start | bytes 5898244
  592.0 25.3 %copy-start.100 = (f32[2560]{0:T(1024)S(1)}, f32[2560]{0:T(1024)}, u32[]{:S(2)}) copy-start(f32[2560]{0:T(1024)} %copy-done.99) | copy-start | bytes 30724
  592.0 25.3 %copy-start.115 = (f32[192]{0:T(256)S(1)}, f32[192]{0:T(256)}, u32[]{:S(2)}) copy-start(f32[192]{0:T(256)} %copy-done.114) | copy-start | bytes 2308
  621.5 10.8 collective-permute-start.27
  692.4 7.1 collective-permute-start.28
  714.7 273.2 %reduce-scatter.11.cloned.1.call-start = ((), (), s32[]{:S(2)}) async-start(), calls=%async_computation.11 | async-start | bytes 16384000 | tf_op jit(solution)/shard_map/reduce_scatter | solution.py:534
  745.0 17.6 %collective-permute-start.30 = (bf16[192,2560]{1,0:T(8,128)(2,1)}, bf16[192,2560]{1,0:T(8,128)(2,1)}, u32[]{:S(2)}, u32[]{:S(2)}) collective-permute-start(bf16[192,2560]{1,0:T(8,128)(2,1)} %dynamic-slice_convert_fusion), channel_id=1, source_target_pairs={{0,1},{1,0},{2,3},{3,2},{4,5},{5,4},{6,7},{7,6},{8,9},{9,8},{10,11... | collective-permute-start | bytes 2949128 | tf_op jit(solution)/shard_map/ppermute | solution.py:20
  747.6 53.8 %all-to-all-start = ((bf16[4,160,1536]{2,1,0:T(8,128)(2,1)}), bf16[4,160,1536]{2,1,0:T(8,128)(2,1)}, u32[]{:S(2)}, u32[]{:S(2)}) async-start(bf16[4,160,1536]{2,1,0:T(8,128)(2,1)} %bitcast.191), calls=%async_computation.3 | async-start | bytes 3932160 | tf_op jit(solution)/shard_map/all_to_all | solution.py:526
  757.4 90.3 %collective-permute-start.32 = (bf16[192,2560]{1,0:T(8,128)(2,1)}, bf16[192,2560]{1,0:T(8,128)(2,1)}, u32[]{:S(2)}, u32[]{:S(2)}) collective-permute-start(bf16[192,2560]{1,0:T(8,128)(2,1)} %fusion.47), channel_id=1, source_target_pairs={{0,24},{8,0},{16,8},{24,16},{1,25},{9,1},{17,9},{25,17},{2,26},{10... | collective-permute-start | bytes 2949128 | tf_op jit(solution)/shard_map/ppermute | solution.py:520
  761.4 143.6 %collective-permute-start.33 = (bf16[192,2560]{1,0:T(8,128)(2,1)}, bf16[192,2560]{1,0:T(8,128)(2,1)}, u32[]{:S(2)}, u32[]{:S(2)}) collective-permute-start(bf16[192,2560]{1,0:T(8,128)(2,1)} %fusion.46), channel_id=1, source_target_pairs={{0,16},{8,24},{16,0},{24,8},{1,17},{9,25},{17,1},{25,9},{2,18},{10... | collective-permute-start | bytes 2949128 | tf_op jit(solution)/shard_map/ppermute | solution.py:520
  761.4 143.6 %collective-permute-start.34 = (bf16[192,2560]{1,0:T(8,128)(2,1)}, bf16[192,2560]{1,0:T(8,128)(2,1)}, u32[]{:S(2)}, u32[]{:S(2)}) collective-permute-start(bf16[192,2560]{1,0:T(8,128)(2,1)} %fusion.45), channel_id=1, source_target_pairs={{0,8},{8,16},{16,24},{24,0},{1,9},{9,17},{17,25},{25,1},{2,10},{10... | collective-permute-start | bytes 2949128 | tf_op jit(solution)/shard_map/ppermute | solution.py:520
  765.7 1.3 collective-permute-start.42
  767.0 138.0 %copy-start.106 = (f32[2560]{0:T(1024)S(1)}, f32[2560]{0:T(1024)}, u32[]{:S(2)}) copy-start(f32[2560]{0:T(1024)} %get-tuple-element.132) | copy-start | bytes 30724
  801.4 138.3 %all-to-all-start.1 = ((bf16[4,160,1344]{2,1,0:T(8,128)(2,1)}), bf16[4,160,1344]{2,1,0:T(8,128)(2,1)}, u32[]{:S(2)}, u32[]{:S(2)}) async-start(bf16[4,160,1344]{2,1,0:T(8,128)(2,1)} %bitcast.197), calls=%async_computation.4 | async-start | bytes 3604480 | tf_op jit(solution)/shard_map/all_to_all | solution.py:526
  847.6 65.8 %collective-permute-start.43 = (f32[240,128]{1,0:T(8,128)S(1)}, f32[240,128]{1,0:T(8,128)S(1)}, u32[]{:S(2)}, u32[]{:S(2)}) collective-permute-start(f32[240,128]{1,0:T(8,128)S(1)} %bitcast.202), channel_id=1, source_target_pairs={{0,2},{2,0},{4,6},{6,4},{8,10},{10,8},{12,14},{14,12},{16,18},{18,... | collective-permute-start | bytes 368648 | tf_op jit(solution)/shard_map/ppermute | solution.py:37
  913.4 55.2 %collective-permute-start.35 = (f32[192,2560]{1,0:T(8,128)}, f32[192,2560]{1,0:T(8,128)}, u32[]{:S(2)}, u32[]{:S(2)}) collective-permute-start(f32[192,2560]{1,0:T(8,128)} %get-tuple-element.192), channel_id=1, source_target_pairs={{0,1},{1,0},{2,3},{3,2},{4,5},{5,4},{6,7},{7,6},{8,9},{9,8},{10,11... | collective-permute-start | bytes 5898248 | tf_op jit(solution)/shard_map/ppermute | solution.py:20
  913.4 8.8 collective-permute-start.44
  922.2 5.2 collective-permute-start.45
  927.4 7.9 collective-permute-start.46
  928.5 44.6 %collective-permute-start.31 = (f32[192,2560]{1,0:T(8,128)}, f32[192,2560]{1,0:T(8,128)}, u32[]{:S(2)}, u32[]{:S(2)}) collective-permute-start(f32[192,2560]{1,0:T(8,128)} %get-tuple-element.193), channel_id=1, source_target_pairs={{0,1},{1,0},{2,3},{3,2},{4,5},{5,4},{6,7},{7,6},{8,9},{9,8},{10,11... | collective-permute-start | bytes 5898248 | tf_op jit(solution)/shard_map/ppermute | solution.py:20
  979.7 16.0 %collective-permute-start.36 = (bf16[192,1280]{1,0:T(8,128)(2,1)S(1)}, bf16[192,1280]{1,0:T(8,128)(2,1)S(1)}, u32[]{:S(2)}, u32[]{:S(2)}) collective-permute-start(bf16[192,1280]{1,0:T(8,128)(2,1)S(1)} %get-tuple-element.189), channel_id=1, source_target_pairs={{0,8},{8,16},{16,24},{24,0},{1,9},{9,17},{17,25},{25,1},{2,10},{10... | collective-permute-start | bytes 1474568 | tf_op jit(solution)/shard_map/ppermute | solution.py:545
  979.7 37.1 %collective-permute-start.37 = (bf16[192,1280]{1,0:T(8,128)(2,1)}, bf16[192,1280]{1,0:T(8,128)(2,1)S(1)}, u32[]{:S(2)}, u32[]{:S(2)}) collective-permute-start(bf16[192,1280]{1,0:T(8,128)(2,1)} %get-tuple-element.191), channel_id=1, source_target_pairs={{0,16},{8,24},{16,0},{24,8},{1,17},{9,25},{17,1},{25,9},{2,18},{10... | collective-permute-start | bytes 1474568 | tf_op jit(solution)/shard_map/ppermute | solution.py:545
  981.4 36.2 %collective-permute-start.38 = (bf16[192,1280]{1,0:T(8,128)(2,1)}, bf16[192,1280]{1,0:T(8,128)(2,1)}, u32[]{:S(2)}, u32[]{:S(2)}) collective-permute-start(bf16[192,1280]{1,0:T(8,128)(2,1)} %get-tuple-element.190), channel_id=1, source_target_pairs={{0,24},{8,0},{16,8},{24,16},{1,25},{9,1},{17,9},{25,17},{2,26},{10... | collective-permute-start | bytes 1474568 | tf_op jit(solution)/shard_map/ppermute | solution.py:545
  991.0 43.4 %collective-permute-start.39 = (bf16[160,2560]{1,0:T(8,128)(2,1)}, bf16[160,2560]{1,0:T(8,128)(2,1)S(1)}, u32[]{:S(2)}, u32[]{:S(2)}) collective-permute-start(bf16[160,2560]{1,0:T(8,128)(2,1)} %get-tuple-element.168), channel_id=1, source_target_pairs={{0,8},{8,16},{16,24},{24,0},{1,9},{9,17},{17,25},{25,1},{2,10},{10... | collective-permute-start | bytes 2457608 | tf_op jit(solution)/shard_map/ppermute | solution.py:545
  991.6 87.4 %collective-permute-start.40 = (bf16[160,2560]{1,0:T(8,128)(2,1)}, bf16[160,2560]{1,0:T(8,128)(2,1)S(1)}, u32[]{:S(2)}, u32[]{:S(2)}) collective-permute-start(bf16[160,2560]{1,0:T(8,128)(2,1)} %get-tuple-element.170), channel_id=1, source_target_pairs={{0,16},{8,24},{16,0},{24,8},{1,17},{9,25},{17,1},{25,9},{2,18},{10... | collective-permute-start | bytes 2457608 | tf_op jit(solution)/shard_map/ppermute | solution.py:545
  995.7 83.2 %collective-permute-start.41 = (bf16[160,2560]{1,0:T(8,128)(2,1)}, bf16[160,2560]{1,0:T(8,128)(2,1)S(1)}, u32[]{:S(2)}, u32[]{:S(2)}) collective-permute-start(bf16[160,2560]{1,0:T(8,128)(2,1)} %get-tuple-element.169), channel_id=1, source_target_pairs={{0,24},{8,0},{16,8},{24,16},{1,25},{9,1},{17,9},{25,17},{2,26},{10... | collective-permute-start | bytes 2457608 | tf_op jit(solution)/shard_map/ppermute | solution.py:545
  (131 other events, 594.9 us)
Sparse Core Ops, SparseCore 0:
  193.2 82.8 all-gather.2
  277.9 77.6 all-gather.4
  443.1 80.5 reduce-scatter.4
  526.6 77.6 reduce-scatter.6
  714.8 84.5 reduce-scatter.8
  802.5 130.1 reduce-scatter.10

commit v5 on v4

--- a/solution.py
+++ b/solution.py
@@ -99,7 +99,7 @@
     )(keep, drive)
 
 
-HALO = 8
+HALO = 16
 
 
 def mix_kernel(branch_ref, mask_ref, taps_ref, rows_ref, gate_ref, *refs):
@@ -218,13 +218,16 @@
     return carried[0]
 
 
-def gather_kernel(outer, groups, parts, *refs):
-    own, send = refs[:groups], refs[groups : groups + parts]
-    refs = refs[groups + parts :]
-    full, got = refs[:groups], refs[groups : groups + parts]
-    line_send, line_recv, side_send, side_recv, half_send, half_recv, part_send, part_recv, local = refs[
-        groups + parts :
-    ]
+def gather_kernel(outer, inner, groups, cuts, *refs):
+    parts = len(cuts)
+    own, refs = refs[:groups], refs[groups:]
+    in_ref, out_ref, source_ref, scale_ref, edge_ref, first_ref = refs[:6]
+    refs = refs[6:]
+    full, got, refs = refs[:groups], refs[groups : groups + parts], refs[groups + parts :]
+    normed_ref, before_ref, after_ref = refs[:3]
+    send, refs = refs[3 : 3 + parts], refs[3 + parts :]
+    line_send, line_recv, side_send, side_recv, half_send, half_recv, part_send, part_recv = refs[:8]
+    edge_send, edge_recv, local = refs[8:]
     o, i, core = lax.axis_index("o"), lax.axis_index("i"), lax.axis_index("tensor")
     sides = (i + 1 - 2 * lax.rem(i, 2), lax.rem(i + 2, 4))
     far = lax.rem(sides[0] + 2, 4)
@@ -237,7 +240,14 @@
         )
     for side in sides:
         pl.semaphore_signal(barrier, inc=1, device_id=(o, side, core), device_id_type=MESH_ID)
-    pl.semaphore_wait(barrier, outer + 1)
+    count = outer * inner
+    me = o * inner + i
+    beside = []
+    for step in (1, count - 1):
+        at = lax.rem(me + step, count)
+        beside.append((at // inner, lax.rem(at, inner), core))
+        pl.semaphore_signal(barrier, inc=1, device_id=beside[-1], device_id_type=MESH_ID)
+    pl.semaphore_wait(barrier, outer + 3)
 
     def remote(src, dst, send_sem, recv_sem, to):
         return pltpu.make_async_remote_copy(
@@ -249,6 +259,13 @@
             device_id_type=MESH_ID,
         )
 
+    edges = [
+        remote(edge_ref, before_ref, edge_send.at[0], edge_recv.at[0], beside[0]),
+        remote(first_ref, after_ref, edge_send.at[1], edge_recv.at[1], beside[1]),
+    ]
+    for edge in edges:
+        edge.start()
+
     def block(g, k, j):
         return full[g].at[k, j]
 
@@ -297,6 +314,30 @@
         pl.when(o > 0)(lambda g=g: along_line(g, o, True, 0).start())
         for side in range(2):
             to_side(g, o, True, side).start()
+
+    hidden = in_ref.shape[2] // outer
+    for p, (start, size) in enumerate(cuts):
+        for k in range(outer):
+            at = slice(k * hidden + start, k * hidden + start + size)
+            send[p][k, :, :size] = in_ref[0, :, at]
+            send[p][k, :, size : 2 * size] = in_ref[1, :, at]
+            send[p][k, :, 2 * size :] = out_ref[:, at]
+    tokens, width = source_ref.shape
+
+    def normed(values):
+        inverse = lax.rsqrt(jnp.mean(values * values, axis=-1, keepdims=True) + EPS)
+        return (values * inverse * scale_ref[...]).astype(BF16)
+
+    def norm_rows(k, _):
+        at = pl.multiple_of(k * HALO, HALO)
+        rows = source_ref[pl.ds(at, HALO), :].astype(F32)
+        normed_ref[pl.ds(at + HALO, HALO), :] = normed(rows)
+        return _
+
+    lax.fori_loop(0, tokens // HALO, norm_rows, 0)
+    for edge in edges:
+        edge.wait()
+    normed_ref[:HALO, :] = normed(before_ref[:, :width])
 
     def pass_on(k, from_left):
         for g in range(groups):
@@ -363,19 +404,26 @@
         pltpu.make_async_copy(send[p].at[o], got[p].at[o], local.at[groups + p]).wait()
 
 
-def gather_weights(own, send):
+def gather_weights(own, ffw_in, ffw_out_t, source, scale, edge, first, cuts):
     outer, inner = lax.axis_size("o"), lax.axis_size("i")
-    groups, parts = len(own), len(send)
+    groups, parts = len(own), len(cuts)
     dma = pltpu.SemaphoreType.DMA
-    out_shape = [jax.ShapeDtypeStruct((outer, inner, *w.shape), w.dtype) for w in own] + [
-        jax.ShapeDtypeStruct(w.shape, w.dtype) for w in send
+    blocks = [(outer, own[0].shape[0], 3 * size) for _, size in cuts]
+    shape = jax.ShapeDtypeStruct
+    out_shape = [shape((outer, inner, *w.shape), BF16) for w in own]
+    out_shape += [shape(block, BF16) for block in blocks]
+    out_shape += [
+        shape((HALO + source.shape[0], source.shape[1]), BF16),
+        shape(edge.shape, F32),
+        shape(first.shape, F32),
     ]
     result = pl.pallas_call(
-        functools.partial(gather_kernel, outer, groups, parts),
-        in_specs=[VMEM] * (groups + parts),
-        out_specs=[ANY] * (groups + parts),
+        functools.partial(gather_kernel, outer, inner, groups, cuts),
+        in_specs=[VMEM] * (groups + 6),
+        out_specs=[ANY] * (groups + parts) + [VMEM] * 3,
         out_shape=out_shape,
-        scratch_shapes=[
+        scratch_shapes=[pltpu.VMEM(block, BF16) for block in blocks]
+        + [
             dma((groups, outer, 2)),
             dma((groups, outer)),
             dma((groups, outer, 2)),
@@ -384,12 +432,14 @@
             dma((groups, outer, 2)),
             dma((parts, outer)),
             dma((parts, outer)),
+            dma((2,)),
+            dma((2,)),
             dma((groups + parts,)),
         ],
         compiler_params=pltpu.CompilerParams(collective_id=0, has_side_effects=True),
-    )(*own, *send)
+    )(*own, ffw_in, ffw_out_t, source, scale, edge, first)
     full = [w.reshape(-1, w.shape[-1]) for w in result[:groups]]
-    return full, result[groups:]
+    return full, result[groups : groups + parts], result[groups + parts :]
 
 
 def grads_kernel(plan, added, *refs):
@@ -582,50 +632,33 @@
     width_half = heads_half * block_size
 
     cuts = cuts_of(hidden_part)
-    ffw_out_t = ffw_out.T
-    packed = [
-        jnp.stack(
-            [
-                jnp.concatenate(
-                    [
-                        w[:, k * hidden_part + start : k * hidden_part + start + size]
-                        for w in (ffw_in[0], ffw_in[1], ffw_out_t)
-                    ],
-                    axis=1,
-                )
-                for k in range(outer)
-            ]
-        )
-        for start, size in cuts
-    ]
-    (branch_x_full, branch_y_full, out_full_t), parts = gather_weights(
-        [branch_weight[0], branch_weight[1], out_weight.T], packed
+    seg_marks = (segment_ids + 1).astype(F32)
+    lanes = jnp.broadcast_to(seg_marks[:, None], (tok_rows, 128))
+    (branch_x_full, branch_y_full, out_full_t), parts, (normed_ext, before, after) = (
+        gather_weights(
+            [branch_weight[0], branch_weight[1], out_weight.T],
+            ffw_in,
+            ffw_out.T,
+            inputs,
+            1.0 + norm_scales[:1],
+            jnp.concatenate([inputs[tok_rows - HALO :].astype(F32), lanes[-HALO:]], axis=1),
+            lanes[:HALO],
+            cuts,
+        )
     )
     ffw_parts = []
     for k, (_, size) in enumerate(cuts):
         whole = gather_inner(parts[k])
         ffw_parts.append((whole[:, : 2 * size], whole[:, 2 * size :]))
     cot_own, branch_x_full = lax.optimization_barrier((half_of(cotangent, core), branch_x_full))
-    cot_moved = ring(cot_own)
+    cot_halves = [cot_own, ring(cot_own)]
 
     source_half = half_of(inputs, core).astype(F32)
-    seg_marks = (segment_ids + 1).astype(F32)
-    halo = from_behind(
-        jnp.concatenate(
-            [
-                inputs[tok_rows - HALO :].astype(F32),
-                jnp.broadcast_to(seg_marks[tok_rows - HALO :, None], (HALO, 128)),
-            ],
-            axis=1,
-        ),
-        1,
-    )
-    marks_after = from_behind(seg_marks[:rim_rows], -1)
-    normed_ext = rms_norm(
-        jnp.concatenate([halo[:, :width], inputs.astype(F32)], axis=0), norm_scales[0]
-    ).astype(BF16)
+    place = lax.axis_index(DP)
+    marks_before = jnp.where(place == 0, 0.0, before[:, width])
+    marks_after = jnp.where(place == count - 1, 0.0, after[:rim_rows, 0])
     normed_low = normed_ext[HALO:]
-    marks_ext = jnp.concatenate([halo[:, width], seg_marks])
+    marks_ext = jnp.concatenate([marks_before, seg_marks])
     same = [
         (marks_ext[HALO - k : HALO - k + tok_rows] == seg_marks).astype(F32)
         for k in range(taps_count)
@@ -639,11 +672,9 @@
         branch_ext, masks, conv_weight, row_params, gate_weights
     )
     conv_blocks = conv_low.reshape(tok_rows, heads_half, block_size)
-    ends, cot_moved = lax.optimization_barrier((ends, cot_moved))
     carry_in = entering(ends, False)
-    carry_in, cot_moved = lax.optimization_barrier((carry_in, cot_moved))
-    cot_halves = [cot_own, cot_moved]
-    for _ in range(2, outer):
+    carry_in, cot_halves[-1] = lax.optimization_barrier((carry_in, cot_halves[-1]))
+    for k in range(2, outer):
         cot_halves.append(ring(cot_halves[-1]))
     states = local_state + cumulative * carry_in
     branch_act, gelu_back = jax.vjp(gelu_tanh, branch_y)

time: 1110 us -> 1110 us (level)
  the two profiles are of different devices: /device:TPU:0 before, /device:TPU:8 now
where the time goes in v5:
time: 1110 us; the launch traced here: 1100 us
  waiting for transfers between devices  401 us (36%)
  Pallas kernels  281 us (25%)
  matrix products  141 us (13%)
  local copies, waits for them, and re-layouts  110 us (10%)
  other arithmetic  100 us (9%)
  starting transfers between devices  48.2 us (4%)
  between operations  16.4 us (1%)
    pallas_call x1, Pallas kernels, gather_weights(): pl.pallas_call(functools.partial(gather_kernel, outer, inner, groups, cut...  172 us
    ppermute x9, waiting for transfers between devices, ring(): lax.ppermute(value, 'o', [(k, (k + 1) % count) for k in range(count)])  161 us
    dot_general x38, matrix products, dot(): lax.dot_general(a, b, ((contract[0], contract[1]), ((), ())), preferred_e...  136 us
    ppermute x6, waiting for transfers between devices, send_parts(): lax.ppermute(part, 'o', [(j, (j + k) % count) for j in range(count)])  93.7 us
    all_to_all x2, waiting for transfers between devices, spread(): return lax.all_to_all(value, 'o', 0, 0, tiled=True)  73.6 us
    pallas_call x4, Pallas kernels, grads_rows(): pl.pallas_call(functools.partial(grads_kernel, plan, added), grid=(outer,...  63.3 us
    ppermute x3, waiting for transfers between devices, send_direct(): lax.ppermute(halves[k], 'o', [(j, (j - k) % count) for j in range(count)])  54.7 us
    pallas_call x2, Pallas kernels, entering(): pl.pallas_call(functools.partial(enter_kernel, outer, inner, reverse), in...  28 us
  transfers between devices with their start and end apart: 53, of which 21 were waited for; matrix products, arithmetic and copies ran while one was open for 26% of the time, Pallas kernels for 9%

profile of v5, /device:TPU:8, one launch (start us, length us, event | category | flops | bytes accessed | tf_op | source)
XLA Modules:
  0.0 1097.9 jit_solution(15315256933194489596)
XLA Ops:
  14.4 172.4 %shard_map.271 = (bf16[4,4,160,1280]{3,2,1,0:T(8,128)(2,1)}, bf16[4,4,160,1280]{3,2,1,0:T(8,128)(2,1)}, bf16[4,4,160,1280]{3,2,1,0:T(8,128)(2,1)}, bf16[4,160,15...) custom-call(bf16[160,1280]{1,0:T(8,128)(2,1)} %get-tuple-element.210, ...), custom_call_target="tpu_custom_call" | custom-call | tf_op jit(solution)/shard_map/pallas_call | solution.py:420
  195.6 7.2 convolution_add_fusion.9.branch_ref
  202.8 10.5 shard_map.272
  213.3 15.1 %shard_map.273 = f32[1,1280]{1,0:T(1,128)} custom-call(f32[2,1280]{1,0:T(2,128)} %get-tuple-element.77.ends_ref), custom_call_target="tpu_custom_call" | custom-call | tf_op jit(solution)/shard_map/pallas_call | solution.py:204
  229.2 8.9 multiply_convert_fusion.2
  238.1 5.3 fusion.188
  251.3 19.1 %collective-permute-done.9.refs_18_ = bf16[192,2560]{1,0:T(8,128)(2,1)} collective-permute-done((bf16[192,2560]{1,0:T(8,128)(2,1)}, bf16[192,2560]{1,0:T(8,128)(2,1)}, u32[]{:S(2)}, u32[]{:S(2)}) %collective-permute-start.9) | collective-permute-done | bytes 983072 | tf_op jit(solution)/shard_map/ppermute | solution.py:25
  281.8 14.7 %collective-permute-done.13.refs_21_ = bf16[192,2560]{1,0:T(8,128)(2,1)S(1)} collective-permute-done((bf16[192,2560]{1,0:T(8,128)(2,1)}, bf16[192,2560]{1,0:T(8,128)(2,1)S(1)}, u32[]{:S(2)}, u32[]{:S(2)}) %collective-permute-start.13) | collective-permute-done | bytes 983072 | tf_op jit(solution)/shard_map/ppermute | solution.py:25
  296.6 20.0 %collective-permute-done.4.refs_3_ = bf16[192,2560]{1,0:T(8,128)(2,1)S(1)} collective-permute-done((bf16[192,2560]{1,0:T(8,128)(2,1)S(1)}, bf16[192,2560]{1,0:T(8,128)(2,1)S(1)}, u32[]{:S(2)}, u32[]{:S(2)}) %collective-permute-start.4) | collective-permute-done | bytes 983072 | tf_op jit(solution)/shard_map/ppermute | solution.py:25
  317.6 23.3 %collective-permute-done.7.refs_6_ = bf16[192,2560]{1,0:T(8,128)(2,1)S(1)} collective-permute-done((bf16[192,2560]{1,0:T(8,128)(2,1)S(1)}, bf16[192,2560]{1,0:T(8,128)(2,1)S(1)}, u32[]{:S(2)}, u32[]{:S(2)}) %collective-permute-start.7) | collective-permute-done | bytes 983072 | tf_op jit(solution)/shard_map/ppermute | solution.py:25
  344.5 19.9 %collective-permute-done.11.refs_9_ = bf16[192,2560]{1,0:T(8,128)(2,1)S(1)} collective-permute-done((bf16[192,2560]{1,0:T(8,128)(2,1)S(1)}, bf16[192,2560]{1,0:T(8,128)(2,1)S(1)}, u32[]{:S(2)}, u32[]{:S(2)}) %collective-permute-start.11) | collective-permute-done | bytes 983072 | tf_op jit(solution)/shard_map/ppermute | solution.py:25
  369.5 5.4 convolution_add_fusion.11
  387.6 4.1 fusion.86
  399.9 22.3 %shard_map.274 = bf16[4,4,160,1536]{3,2,1,0:T(8,128)(2,1)} custom-call(bf16[192,2560]{1,0:T(8,128)(2,1)} %copy-done.18, bf16[192,2560]{1,0:T(8,128)(2,1)} %copy-done.58, bf16[384,1024]{1,0:T(8,128)(2,1)} %pad_maximum_fusion.9.refs_2_, bf16[192,2560]{1,0:T(8,128)(2,1)} %copy-done.46, bf16[192,2560]{1,0:T(8,128)(2,1)} %copy-done.50, ...), custom_call_target="tpu_custom_call" | custom-call | flops 12079595520 | bytes 20447232 | tf_op jit(solution)/shard_map/pallas_call | solution.py:492
  422.9 5.2 convolution_add_fusion.15
  428.2 4.3 fusion.128
  443.7 4.1 fusion.63
  447.9 5.0 convolution_add_fusion.6
  454.2 4.6 convolution_add_fusion.17
  461.5 4.2 fusion.65
  465.6 4.5 convolution_add_fusion.7
  477.8 4.6 fusion.70
  482.6 21.7 %shard_map.277 = bf16[4,4,160,1344]{3,2,1,0:T(8,128)(2,1)} custom-call(bf16[192,2560]{1,0:T(8,128)(2,1)} %copy-done.18, bf16[192,2560]{1,0:T(8,128)(2,1)} %copy-done.58, bf16[384,896]{1,0:T(8,128)(2,1)} %pad_maximum_fusion.13.refs_2_, bf16[192,2560]{1,0:T(8,128)(2,1)} %copy-done.46, bf16[192,2560]{1,0:T(8,128)(2,1)} %copy-done.50, ...), custom_call_target="tpu_custom_call" | custom-call | flops 10569646080 | bytes 18874368 | tf_op jit(solution)/shard_map/pallas_call | solution.py:492
  505.4 5.8 convolution_add_fusion.8
  512.2 3.1 fusion.149
  515.4 3.8 fusion.151
  529.3 18.4 %collective-permute-done.19 = bf16[192,2560]{1,0:T(8,128)(2,1)S(1)} collective-permute-done((bf16[192,2560]{1,0:T(8,128)(2,1)S(1)}, bf16[192,2560]{1,0:T(8,128)(2,1)S(1)}, u32[]{:S(2)}, u32[]{:S(2)}) %collective-permute-start.19) | collective-permute-done | bytes 983072 | tf_op jit(solution)/shard_map/ppermute | solution.py:25
  552.1 23.1 %collective-permute-done.20 = bf16[192,2560]{1,0:T(8,128)(2,1)S(1)} collective-permute-done((bf16[192,2560]{1,0:T(8,128)(2,1)S(1)}, bf16[192,2560]{1,0:T(8,128)(2,1)S(1)}, u32[]{:S(2)}, u32[]{:S(2)}) %collective-permute-start.20) | collective-permute-done | bytes 983072 | tf_op jit(solution)/shard_map/ppermute | solution.py:25
  579.5 22.4 %collective-permute-done.21 = bf16[192,2560]{1,0:T(8,128)(2,1)S(1)} collective-permute-done((bf16[192,2560]{1,0:T(8,128)(2,1)S(1)}, bf16[192,2560]{1,0:T(8,128)(2,1)S(1)}, u32[]{:S(2)}, u32[]{:S(2)}) %collective-permute-start.21) | collective-permute-done | bytes 983072 | tf_op jit(solution)/shard_map/ppermute | solution.py:25
  622.3 8.3 convert_reduce_fusion.2
  630.6 7.2 shard_map.275
  639.3 12.9 %shard_map.276 = f32[1,1280]{1,0:T(1,128)} custom-call(f32[2,1280]{1,0:T(2,128)} %pad_maximum_fusion.19.ends_ref), custom_call_target="tpu_custom_call" | custom-call | tf_op jit(solution)/shard_map/pallas_call | solution.py:204
  653.0 7.2 multiply_reduce_fusion
  670.4 4.0 fusion.56
  677.4 6.1 fusion.36
  683.5 4.1 collective-permute-start.27
  689.8 3.7 convert_element_type.300.refs_2_
  693.4 7.1 convert_reduce_fusion.3
  700.5 8.1 shard_map.278
  711.6 11.2 %shard_map.279 = bf16[4,4,160,2560]{3,2,1,0:T(8,128)(2,1)} custom-call(bf16[384,2560]{1,0:T(8,128)(2,1)} %pad_maximum_fusion.4.refs_0_, bf16[384,1280]{1,0:T(8,128)(2,1)} %copy-done.43, bf16[384,2560]{1,0:T(8,128)(2,1)} %slice.308.refs_0_.refs_2_, bf16[384,1280]{1,0:T(8,128)(2,1)} %get-tuple-element.148.refs_3_), custom_call_target="tpu_custom_call" | custom-call | flops 5033164800 | bytes 17039360 | tf_op jit(solution)/shard_map/pallas_call | solution.py:492
  726.8 5.2 fusion.189
  732.0 5.0 convolution_add_fusion.4
  743.1 4.4 all-to-all-start
  759.6 73.6 %all-to-all-done = bf16[4,160,1536]{2,1,0:T(8,128)(2,1)} async-done(((bf16[4,160,1536]{2,1,0:T(8,128)(2,1)}), bf16[4,160,1536]{2,1,0:T(8,128)(2,1)}, u32[]{:S(2)}, u32[]{:S(2)}) %all-to-all-start) | async-done | bytes 1966112 | tf_op jit(solution)/shard_map/all_to_all | solution.py:576
  833.2 6.5 all-to-all-start.1
  840.0 35.4 %collective-permute-done.30 = bf16[192,2560]{1,0:T(8,128)(2,1)} collective-permute-done((bf16[192,2560]{1,0:T(8,128)(2,1)}, bf16[192,2560]{1,0:T(8,128)(2,1)}, u32[]{:S(2)}, u32[]{:S(2)}) %collective-permute-start.30) | collective-permute-done | bytes 983072 | tf_op jit(solution)/shard_map/ppermute | solution.py:570
  875.4 19.3 %collective-permute-done.32 = bf16[192,2560]{1,0:T(8,128)(2,1)} collective-permute-done((bf16[192,2560]{1,0:T(8,128)(2,1)}, bf16[192,2560]{1,0:T(8,128)(2,1)}, u32[]{:S(2)}, u32[]{:S(2)}) %collective-permute-start.32) | collective-permute-done | bytes 983072 | tf_op jit(solution)/shard_map/ppermute | solution.py:570
  894.7 8.1 add_add_fusion
  904.1 7.5 collective-permute-done.42
  911.6 3.6 collective-permute-start.43
  915.2 3.4 collective-permute-done.43
  919.8 5.1 collective-permute-done.44
  932.5 3.4 reshape.235
  938.4 4.3 reshape.221
  945.1 5.7 copy.116
  950.8 7.4 reshape.234
  963.1 3.7 pad_maximum_fusion
  970.6 4.3 collective-permute-start.35
  979.2 3.1 dynamic-slice_bitcast_fusion.2
  988.5 25.5 %collective-permute-done.35 = bf16[192,1280]{1,0:T(8,128)(2,1)S(1)} collective-permute-done((bf16[192,1280]{1,0:T(8,128)(2,1)}, bf16[192,1280]{1,0:T(8,128)(2,1)S(1)}, u32[]{:S(2)}, u32[]{:S(2)}) %collective-permute-start.35) | collective-permute-done | bytes 491552 | tf_op jit(solution)/shard_map/ppermute | solution.py:595
  1014.8 38.1 %collective-permute-done.36 = bf16[192,1280]{1,0:T(8,128)(2,1)} collective-permute-done((bf16[192,1280]{1,0:T(8,128)(2,1)}, bf16[192,1280]{1,0:T(8,128)(2,1)}, u32[]{:S(2)}, u32[]{:S(2)}) %collective-permute-start.36) | collective-permute-done | bytes 491552 | tf_op jit(solution)/shard_map/ppermute | solution.py:595
  1056.9 9.7 collective-permute-done.37
  1066.7 16.5 %collective-permute-done.38 = bf16[160,2560]{1,0:T(8,128)(2,1)S(1)} collective-permute-done((bf16[160,2560]{1,0:T(8,128)(2,1)}, bf16[160,2560]{1,0:T(8,128)(2,1)S(1)}, u32[]{:S(2)}, u32[]{:S(2)}) %collective-permute-start.38) | collective-permute-done | bytes 819232 | tf_op jit(solution)/shard_map/ppermute | solution.py:595
  1083.1 4.0 collective-permute-done.39
  (527 shorter events, 215.7 us)
Async XLA Ops:
  7.2 240.6 %copy-start = (f32[2,3840]{1,0:T(2,128)S(1)}, f32[2,3840]{1,0:T(2,128)}, u32[]{:S(2)}) copy-start(f32[2,3840]{1,0:T(2,128)} %param.31) | copy-start | bytes 92164
  7.2 362.3 %all-gather.3.cloned.1.call-start = ((), (), s32[]{:S(2)}) async-start(), calls=%async_computation.6 | async-start | bytes 9830400 | tf_op jit(solution)/shard_map/all_gather | solution.py:580
  10.9 263.8 %copy-start.84 = (f32[2560]{0:T(1024)}, f32[2560]{0:T(1024)S(1)}, u32[]{:S(2)}) copy-start(f32[2560]{0:T(1024)S(1)} %get-tuple-element.137) | copy-start | bytes 30724
  187.0 235.9 %all-gather.5.cloned.1.call-start = ((), (), s32[]{:S(2)}) async-start(), calls=%async_computation.7 | async-start | bytes 9011200 | tf_op jit(solution)/shard_map/all_gather | solution.py:580
  189.1 59.4 %copy-start.7 = (bf16[192,2560]{1,0:T(8,128)(2,1)}, bf16[192,2560]{1,0:T(8,128)(2,1)S(1)}, u32[]{:S(2)}) copy-start(bf16[192,2560]{1,0:T(8,128)(2,1)S(1)} %get-tuple-element.78.refs_12_) | copy-start | bytes 2949124
  189.1 40.0 %collective-permute-start = (bf16[192,2560]{1,0:T(8,128)(2,1)S(1)}, bf16[192,2560]{1,0:T(8,128)(2,1)}, u32[]{:S(2)}, u32[]{:S(2)}) collective-permute-start(bf16[192,2560]{1,0:T(8,128)(2,1)S(1)} %get-tuple-element.78.refs_12_), channel_id=1, source_target_pairs={{0,8},{8,16},{16,24},{24,0},{1,9},{9,17},{17,25},{25,1},{2,10},{10... | collective-permute-start | bytes 2949128 | tf_op jit(solution)/shard_map/ppermute | solution.py:25
  246.0 26.0 %collective-permute-start.1 = (f32[192,2560]{1,0:T(8,128)}, f32[192,2560]{1,0:T(8,128)S(1)}, u32[]{:S(2)}, u32[]{:S(2)}) collective-permute-start(f32[192,2560]{1,0:T(8,128)} %constant_dynamic-slice_fusion.1), channel_id=1, source_target_pairs={{0,1},{1,0},{2,3},{3,2},{4,5},{5,4},{6,7},{7,6},{8,9},{9,8},{10,11... | collective-permute-start | bytes 5898248 | tf_op jit(solution)/shard_map/ppermute | solution.py:20
  246.0 24.5 %collective-permute-start.9 = (bf16[192,2560]{1,0:T(8,128)(2,1)}, bf16[192,2560]{1,0:T(8,128)(2,1)}, u32[]{:S(2)}, u32[]{:S(2)}) collective-permute-start(bf16[192,2560]{1,0:T(8,128)(2,1)} %collective-permute-done.refs_15_), channel_id=1, source_target_pairs={{0,8},{8,16},{16,24},{24,0},{1,9},{9,17},{17,25},{25,1},{2,10},{10... | collective-permute-start | bytes 2949128 | tf_op jit(solution)/shard_map/ppermute | solution.py:25
  247.5 29.9 %collective-permute-start.2 = (bf16[192,2560]{1,0:T(8,128)(2,1)S(1)}, bf16[192,2560]{1,0:T(8,128)(2,1)}, u32[]{:S(2)}, u32[]{:S(2)}) collective-permute-start(bf16[192,2560]{1,0:T(8,128)(2,1)S(1)} %get-tuple-element.78.refs_12_), channel_id=1, source_target_pairs={{0,1},{1,0},{2,3},{3,2},{4,5},{5,4},{6,7},{7,6},{8,9},{9,8},{10,11... | collective-permute-start | bytes 2949128 | tf_op jit(solution)/shard_map/ppermute | solution.py:20
  247.7 357.1 %reduce-scatter.5.cloned.1.call-start = ((), (), s32[]{:S(2)}) async-start(), calls=%async_computation.8 | async-start | bytes 9830400 | tf_op jit(solution)/shard_map/reduce_scatter | solution.py:584
  248.6 32.1 %collective-permute-start.6 = (bf16[192,2560]{1,0:T(8,128)(2,1)}, bf16[192,2560]{1,0:T(8,128)(2,1)S(1)}, u32[]{:S(2)}, u32[]{:S(2)}) collective-permute-start(bf16[192,2560]{1,0:T(8,128)(2,1)} %collective-permute-done.refs_15_), channel_id=1, source_target_pairs={{0,1},{1,0},{2,3},{3,2},{4,5},{5,4},{6,7},{7,6},{8,9},{9,8},{10,11... | collective-permute-start | bytes 2949128 | tf_op jit(solution)/shard_map/ppermute | solution.py:20
  270.5 26.1 %collective-permute-start.13 = (bf16[192,2560]{1,0:T(8,128)(2,1)}, bf16[192,2560]{1,0:T(8,128)(2,1)S(1)}, u32[]{:S(2)}, u32[]{:S(2)}) collective-permute-start(bf16[192,2560]{1,0:T(8,128)(2,1)} %collective-permute-done.9.refs_18_), channel_id=1, source_target_pairs={{0,8},{8,16},{16,24},{24,0},{1,9},{9,17},{17,25},{25,1},{2,10},{10... | collective-permute-start | bytes 2949128 | tf_op jit(solution)/shard_map/ppermute | solution.py:25
  275.0 118.6 %copy-start.18 = (bf16[192,2560]{1,0:T(8,128)(2,1)}, bf16[192,2560]{1,0:T(8,128)(2,1)S(1)}, u32[]{:S(2)}) copy-start(bf16[192,2560]{1,0:T(8,128)(2,1)S(1)} %multiply_convert_fusion.1.refs_0_) | copy-start | bytes 2949124
  275.0 41.6 %collective-permute-start.4 = (bf16[192,2560]{1,0:T(8,128)(2,1)S(1)}, bf16[192,2560]{1,0:T(8,128)(2,1)S(1)}, u32[]{:S(2)}, u32[]{:S(2)}) collective-permute-start(bf16[192,2560]{1,0:T(8,128)(2,1)S(1)} %multiply_convert_fusion.1.refs_0_), channel_id=1, source_target_pairs={{0,8},{8,16},{16,24},{24,0},{1,9},{9,17},{17,25},{25,1},{2,10},{10... | collective-permute-start | bytes 2949128 | tf_op jit(solution)/shard_map/ppermute | solution.py:25
  278.7 38.0 %collective-permute-start.10 = (bf16[192,2560]{1,0:T(8,128)(2,1)}, bf16[192,2560]{1,0:T(8,128)(2,1)S(1)}, u32[]{:S(2)}, u32[]{:S(2)}) collective-permute-start(bf16[192,2560]{1,0:T(8,128)(2,1)} %collective-permute-done.9.refs_18_), channel_id=1, source_target_pairs={{0,1},{1,0},{2,3},{3,2},{4,5},{5,4},{6,7},{7,6},{8,9},{9,8},{10,11... | collective-permute-start | bytes 2949128 | tf_op jit(solution)/shard_map/ppermute | solution.py:20
  280.7 36.1 %copy-start.44 = (bf16[192,2560]{1,0:T(8,128)(2,1)}, bf16[192,2560]{1,0:T(8,128)(2,1)S(1)}, u32[]{:S(2)}) copy-start(bf16[192,2560]{1,0:T(8,128)(2,1)S(1)} %collective-permute-done.6.refs_16_) | copy-start | bytes 2949124
  281.8 61.0 %collective-permute-start.3 = (bf16[192,2560]{1,0:T(8,128)(2,1)S(1)}, bf16[192,2560]{1,0:T(8,128)(2,1)S(1)}, u32[]{:S(2)}, u32[]{:S(2)}) collective-permute-start(bf16[192,2560]{1,0:T(8,128)(2,1)S(1)} %multiply_convert_fusion.1.refs_0_), channel_id=1, source_target_pairs={{0,1},{1,0},{2,3},{3,2},{4,5},{5,4},{6,7},{7,6},{8,9},{9,8},{10,11... | collective-permute-start | bytes 2949128 | tf_op jit(solution)/shard_map/ppermute | solution.py:20
  296.6 44.5 %collective-permute-start.14 = (bf16[192,2560]{1,0:T(8,128)(2,1)S(1)}, bf16[192,2560]{1,0:T(8,128)(2,1)S(1)}, u32[]{:S(2)}, u32[]{:S(2)}) collective-permute-start(bf16[192,2560]{1,0:T(8,128)(2,1)S(1)} %collective-permute-done.13.refs_21_), channel_id=1, source_target_pairs={{0,1},{1,0},{2,3},{3,2},{4,5},{5,4},{6,7},{7,6},{8,9},{9,8},{10,11... | collective-permute-start | bytes 2949128 | tf_op jit(solution)/shard_map/ppermute | solution.py:20
  316.6 24.3 %collective-permute-start.7 = (bf16[192,2560]{1,0:T(8,128)(2,1)S(1)}, bf16[192,2560]{1,0:T(8,128)(2,1)S(1)}, u32[]{:S(2)}, u32[]{:S(2)}) collective-permute-start(bf16[192,2560]{1,0:T(8,128)(2,1)S(1)} %collective-permute-done.4.refs_3_), channel_id=1, source_target_pairs={{0,8},{8,16},{16,24},{24,0},{1,9},{9,17},{17,25},{25,1},{2,10},{10... | collective-permute-start | bytes 2949128 | tf_op jit(solution)/shard_map/ppermute | solution.py:25
  316.8 47.6 %collective-permute-start.5 = (bf16[192,2560]{1,0:T(8,128)(2,1)S(1)}, bf16[192,2560]{1,0:T(8,128)(2,1)S(1)}, u32[]{:S(2)}, u32[]{:S(2)}) collective-permute-start(bf16[192,2560]{1,0:T(8,128)(2,1)S(1)} %collective-permute-done.4.refs_3_), channel_id=1, source_target_pairs={{0,1},{1,0},{2,3},{3,2},{4,5},{5,4},{6,7},{7,6},{8,9},{9,8},{10,11... | collective-permute-start | bytes 2949128 | tf_op jit(solution)/shard_map/ppermute | solution.py:20
  340.8 23.6 %collective-permute-start.11 = (bf16[192,2560]{1,0:T(8,128)(2,1)S(1)}, bf16[192,2560]{1,0:T(8,128)(2,1)S(1)}, u32[]{:S(2)}, u32[]{:S(2)}) collective-permute-start(bf16[192,2560]{1,0:T(8,128)(2,1)S(1)} %collective-permute-done.7.refs_6_), channel_id=1, source_target_pairs={{0,8},{8,16},{16,24},{24,0},{1,9},{9,17},{17,25},{25,1},{2,10},{10... | collective-permute-start | bytes 2949128 | tf_op jit(solution)/shard_map/ppermute | solution.py:25
  344.4 21.3 %collective-permute-start.8 = (bf16[192,2560]{1,0:T(8,128)(2,1)S(1)}, bf16[192,2560]{1,0:T(8,128)(2,1)S(1)}, u32[]{:S(2)}, u32[]{:S(2)}) collective-permute-start(bf16[192,2560]{1,0:T(8,128)(2,1)S(1)} %collective-permute-done.7.refs_6_), channel_id=1, source_target_pairs={{0,1},{1,0},{2,3},{3,2},{4,5},{5,4},{6,7},{7,6},{8,9},{9,8},{10,11... | collective-permute-start | bytes 2949128 | tf_op jit(solution)/shard_map/ppermute | solution.py:20
  364.4 2.6 collective-permute-start.12
  377.9 83.6 %copy-start.32 = (bf16[384,512]{1,0:T(8,128)(2,1)}, bf16[384,512]{1,0:T(8,128)(2,1)S(1)}, u32[]{:S(2)}) copy-start(bf16[384,512]{1,0:T(8,128)(2,1)S(1)} %get-tuple-element.174) | copy-start | bytes 1179652
  383.6 60.1 %copy-start.33 = (bf16[384,512]{1,0:T(8,128)(2,1)}, bf16[384,512]{1,0:T(8,128)(2,1)S(1)}, u32[]{:S(2)}) copy-start(bf16[384,512]{1,0:T(8,128)(2,1)S(1)} %get-tuple-element.175) | copy-start | bytes 1179652
  398.2 79.6 %copy-start.40 = (bf16[384,512]{1,0:T(8,128)(2,1)}, bf16[384,512]{1,0:T(8,128)(2,1)S(1)}, u32[]{:S(2)}) copy-start(bf16[384,512]{1,0:T(8,128)(2,1)S(1)} %get-tuple-element.179) | copy-start | bytes 1179652
  422.3 230.7 %reduce-scatter.7.cloned.1.call-start = ((), (), s32[]{:S(2)}) async-start(), calls=%async_computation.9 | async-start | bytes 9011200 | tf_op jit(solution)/shard_map/reduce_scatter | solution.py:584
  437.4 45.0 %collective-permute-start.18 = (bf16[192,2560]{1,0:T(8,128)(2,1)S(1)}, bf16[192,2560]{1,0:T(8,128)(2,1)S(1)}, u32[]{:S(2)}, u32[]{:S(2)}) collective-permute-start(bf16[192,2560]{1,0:T(8,128)(2,1)S(1)} %slice.755), channel_id=1, source_target_pairs={{0,1},{1,0},{2,3},{3,2},{4,5},{5,4},{6,7},{7,6},{8,9},{9,8},{10,11... | collective-permute-start | bytes 2949128 | tf_op jit(solution)/shard_map/ppermute | solution.py:20
  454.1 75.0 %collective-permute-start.17 = (bf16[192,2560]{1,0:T(8,128)(2,1)}, bf16[192,2560]{1,0:T(8,128)(2,1)}, u32[]{:S(2)}, u32[]{:S(2)}) collective-permute-start(bf16[192,2560]{1,0:T(8,128)(2,1)} %slice.756), channel_id=1, source_target_pairs={{0,1},{1,0},{2,3},{3,2},{4,5},{5,4},{6,7},{7,6},{8,9},{9,8},{10,11... | collective-permute-start | bytes 2949128 | tf_op jit(solution)/shard_map/ppermute | solution.py:20
  471.4 80.7 %collective-permute-start.16 = (bf16[192,2560]{1,0:T(8,128)(2,1)}, bf16[192,2560]{1,0:T(8,128)(2,1)}, u32[]{:S(2)}, u32[]{:S(2)}) collective-permute-start(bf16[192,2560]{1,0:T(8,128)(2,1)} %slice.757), channel_id=1, source_target_pairs={{0,1},{1,0},{2,3},{3,2},{4,5},{5,4},{6,7},{7,6},{8,9},{9,8},{10,11... | collective-permute-start | bytes 2949128 | tf_op jit(solution)/shard_map/ppermute | solution.py:20
  504.3 462.5 %reduce-scatter.9.cloned.1.call-start = ((), (), s32[]{:S(2)}) async-start(), calls=%async_computation.10 | async-start | bytes 9830400 | tf_op jit(solution)/shard_map/reduce_scatter | solution.py:584
  512.2 67.3 %collective-permute-start.15 = (bf16[192,2560]{1,0:T(8,128)(2,1)}, bf16[192,2560]{1,0:T(8,128)(2,1)}, u32[]{:S(2)}, u32[]{:S(2)}) collective-permute-start(bf16[192,2560]{1,0:T(8,128)(2,1)} %slice.758), channel_id=1, source_target_pairs={{0,1},{1,0},{2,3},{3,2},{4,5},{5,4},{6,7},{7,6},{8,9},{9,8},{10,11... | collective-permute-start | bytes 2949128 | tf_op jit(solution)/shard_map/ppermute | solution.py:20
  521.7 26.0 %collective-permute-start.19 = (bf16[192,2560]{1,0:T(8,128)(2,1)S(1)}, bf16[192,2560]{1,0:T(8,128)(2,1)S(1)}, u32[]{:S(2)}, u32[]{:S(2)}) collective-permute-start(bf16[192,2560]{1,0:T(8,128)(2,1)S(1)} %slice_add_fusion.4), channel_id=1, source_target_pairs={{0,8},{8,16},{16,24},{24,0},{1,9},{9,17},{17,25},{25,1},{2,10},{10... | collective-permute-start | bytes 2949128 | tf_op jit(solution)/shard_map/ppermute | solution.py:25
  524.1 25.2 %collective-permute-start.25 = (bf16[192,2560]{1,0:T(8,128)(2,1)S(1)}, bf16[192,2560]{1,0:T(8,128)(2,1)S(1)}, u32[]{:S(2)}, u32[]{:S(2)}) collective-permute-start(bf16[192,2560]{1,0:T(8,128)(2,1)S(1)} %slice.751), channel_id=1, source_target_pairs={{0,1},{1,0},{2,3},{3,2},{4,5},{5,4},{6,7},{7,6},{8,9},{9,8},{10,11... | collective-permute-start | bytes 2949128 | tf_op jit(solution)/shard_map/ppermute | solution.py:20
  529.1 21.5 %collective-permute-start.24 = (bf16[192,2560]{1,0:T(8,128)(2,1)S(1)}, bf16[192,2560]{1,0:T(8,128)(2,1)S(1)}, u32[]{:S(2)}, u32[]{:S(2)}) collective-permute-start(bf16[192,2560]{1,0:T(8,128)(2,1)S(1)} %slice.752), channel_id=1, source_target_pairs={{0,1},{1,0},{2,3},{3,2},{4,5},{5,4},{6,7},{7,6},{8,9},{9,8},{10,11... | collective-permute-start | bytes 2949128 | tf_op jit(solution)/shard_map/ppermute | solution.py:20
  547.7 29.2 %collective-permute-start.23 = (bf16[192,2560]{1,0:T(8,128)(2,1)S(1)}, bf16[192,2560]{1,0:T(8,128)(2,1)S(1)}, u32[]{:S(2)}, u32[]{:S(2)}) collective-permute-start(bf16[192,2560]{1,0:T(8,128)(2,1)S(1)} %slice.753), channel_id=1, source_target_pairs={{0,1},{1,0},{2,3},{3,2},{4,5},{5,4},{6,7},{7,6},{8,9},{9,8},{10,11... | collective-permute-start | bytes 2949128 | tf_op jit(solution)/shard_map/ppermute | solution.py:20
  549.3 25.9 %collective-permute-start.20 = (bf16[192,2560]{1,0:T(8,128)(2,1)S(1)}, bf16[192,2560]{1,0:T(8,128)(2,1)S(1)}, u32[]{:S(2)}, u32[]{:S(2)}) collective-permute-start(bf16[192,2560]{1,0:T(8,128)(2,1)S(1)} %fusion.49), channel_id=1, source_target_pairs={{0,8},{8,16},{16,24},{24,0},{1,9},{9,17},{17,25},{25,1},{2,10},{10... | collective-permute-start | bytes 2949128 | tf_op jit(solution)/shard_map/ppermute | solution.py:25
  550.5 27.5 %collective-permute-start.22 = (bf16[192,2560]{1,0:T(8,128)(2,1)S(1)}, bf16[192,2560]{1,0:T(8,128)(2,1)S(1)}, u32[]{:S(2)}, u32[]{:S(2)}) collective-permute-start(bf16[192,2560]{1,0:T(8,128)(2,1)S(1)} %slice.754), channel_id=1, source_target_pairs={{0,1},{1,0},{2,3},{3,2},{4,5},{5,4},{6,7},{7,6},{8,9},{9,8},{10,11... | collective-permute-start | bytes 2949128 | tf_op jit(solution)/shard_map/ppermute | solution.py:20
  576.8 25.2 %collective-permute-start.21 = (bf16[192,2560]{1,0:T(8,128)(2,1)S(1)}, bf16[192,2560]{1,0:T(8,128)(2,1)S(1)}, u32[]{:S(2)}, u32[]{:S(2)}) collective-permute-start(bf16[192,2560]{1,0:T(8,128)(2,1)S(1)} %fusion.51), channel_id=1, source_target_pairs={{0,8},{8,16},{16,24},{24,0},{1,9},{9,17},{17,25},{25,1},{2,10},{10... | collective-permute-start | bytes 2949128 | tf_op jit(solution)/shard_map/ppermute | solution.py:25
  579.5 25.3 %copy-start.99 = (f32[192]{0:T(256)S(1)}, f32[192]{0:T(256)}, u32[]{:S(2)}) copy-start(f32[192]{0:T(256)} %copy-done.98) | copy-start | bytes 2308
  608.9 10.7 collective-permute-start.26
  683.5 9.9 collective-permute-start.27
  708.7 270.5 %reduce-scatter.11.cloned.1.call-start = ((), (), s32[]{:S(2)}) async-start(), calls=%async_computation.11 | async-start | bytes 16384000 | tf_op jit(solution)/shard_map/reduce_scatter | solution.py:584
  740.0 15.1 %collective-permute-start.28 = (bf16[192,2560]{1,0:T(8,128)(2,1)}, bf16[192,2560]{1,0:T(8,128)(2,1)}, u32[]{:S(2)}, u32[]{:S(2)}) collective-permute-start(bf16[192,2560]{1,0:T(8,128)(2,1)} %dynamic-slice_convert_fusion), channel_id=1, source_target_pairs={{0,1},{1,0},{2,3},{3,2},{4,5},{5,4},{6,7},{7,6},{8,9},{9,8},{10,11... | collective-permute-start | bytes 2949128 | tf_op jit(solution)/shard_map/ppermute | solution.py:20
  743.1 90.1 %all-to-all-start = ((bf16[4,160,1536]{2,1,0:T(8,128)(2,1)}), bf16[4,160,1536]{2,1,0:T(8,128)(2,1)}, u32[]{:S(2)}, u32[]{:S(2)}) async-start(bf16[4,160,1536]{2,1,0:T(8,128)(2,1)} %bitcast.174), calls=%async_computation.3 | async-start | bytes 3932160 | tf_op jit(solution)/shard_map/all_to_all | solution.py:576
  750.0 125.4 %collective-permute-start.30 = (bf16[192,2560]{1,0:T(8,128)(2,1)}, bf16[192,2560]{1,0:T(8,128)(2,1)}, u32[]{:S(2)}, u32[]{:S(2)}) collective-permute-start(bf16[192,2560]{1,0:T(8,128)(2,1)} %fusion.47), channel_id=1, source_target_pairs={{0,24},{8,0},{16,8},{24,16},{1,25},{9,1},{17,9},{25,17},{2,26},{10... | collective-permute-start | bytes 2949128 | tf_op jit(solution)/shard_map/ppermute | solution.py:570
  750.1 125.3 %collective-permute-start.31 = (bf16[192,2560]{1,0:T(8,128)(2,1)}, bf16[192,2560]{1,0:T(8,128)(2,1)}, u32[]{:S(2)}, u32[]{:S(2)}) collective-permute-start(bf16[192,2560]{1,0:T(8,128)(2,1)} %fusion.46), channel_id=1, source_target_pairs={{0,16},{8,24},{16,0},{24,8},{1,17},{9,25},{17,1},{25,9},{2,18},{10... | collective-permute-start | bytes 2949128 | tf_op jit(solution)/shard_map/ppermute | solution.py:570
  752.6 142.1 %collective-permute-start.32 = (bf16[192,2560]{1,0:T(8,128)(2,1)}, bf16[192,2560]{1,0:T(8,128)(2,1)}, u32[]{:S(2)}, u32[]{:S(2)}) collective-permute-start(bf16[192,2560]{1,0:T(8,128)(2,1)} %fusion.45), channel_id=1, source_target_pairs={{0,8},{8,16},{16,24},{24,0},{1,9},{9,17},{17,25},{25,1},{2,10},{10... | collective-permute-start | bytes 2949128 | tf_op jit(solution)/shard_map/ppermute | solution.py:570
  758.0 1.3 collective-permute-start.40
  759.4 135.3 %copy-start.88 = (f32[2560]{0:T(1024)S(1)}, f32[2560]{0:T(1024)}, u32[]{:S(2)}) copy-start(f32[2560]{0:T(1024)} %get-tuple-element.134) | copy-start | bytes 30724
  833.2 96.2 %all-to-all-start.1 = ((bf16[4,160,1344]{2,1,0:T(8,128)(2,1)}), bf16[4,160,1344]{2,1,0:T(8,128)(2,1)}, u32[]{:S(2)}, u32[]{:S(2)}) async-start(bf16[4,160,1344]{2,1,0:T(8,128)(2,1)} %bitcast.177), calls=%async_computation.4 | async-start | bytes 3604480 | tf_op jit(solution)/shard_map/all_to_all | solution.py:576
  839.7 63.1 %collective-permute-start.41 = (f32[240,128]{1,0:T(8,128)S(1)}, f32[240,128]{1,0:T(8,128)S(1)}, u32[]{:S(2)}, u32[]{:S(2)}) collective-permute-start(f32[240,128]{1,0:T(8,128)S(1)} %bitcast.181), channel_id=1, source_target_pairs={{0,2},{2,0},{4,6},{6,4},{8,10},{10,8},{12,14},{14,12},{16,18},{18,... | collective-permute-start | bytes 368648 | tf_op jit(solution)/shard_map/ppermute | solution.py:37
  902.8 55.4 %collective-permute-start.33 = (f32[192,2560]{1,0:T(8,128)}, f32[192,2560]{1,0:T(8,128)}, u32[]{:S(2)}, u32[]{:S(2)}) collective-permute-start(f32[192,2560]{1,0:T(8,128)} %get-tuple-element.192), channel_id=1, source_target_pairs={{0,1},{1,0},{2,3},{3,2},{4,5},{5,4},{6,7},{7,6},{8,9},{9,8},{10,11... | collective-permute-start | bytes 5898248 | tf_op jit(solution)/shard_map/ppermute | solution.py:20
  902.8 8.8 collective-permute-start.42
  911.6 7.0 collective-permute-start.43
  918.6 6.3 collective-permute-start.44
  919.8 40.8 %collective-permute-start.29 = (f32[192,2560]{1,0:T(8,128)}, f32[192,2560]{1,0:T(8,128)}, u32[]{:S(2)}, u32[]{:S(2)}) collective-permute-start(f32[192,2560]{1,0:T(8,128)} %get-tuple-element.193), channel_id=1, source_target_pairs={{0,1},{1,0},{2,3},{3,2},{4,5},{5,4},{6,7},{7,6},{8,9},{9,8},{10,11... | collective-permute-start | bytes 5898248 | tf_op jit(solution)/shard_map/ppermute | solution.py:20
  969.2 17.0 %collective-permute-start.34 = (bf16[192,1280]{1,0:T(8,128)(2,1)S(1)}, bf16[192,1280]{1,0:T(8,128)(2,1)S(1)}, u32[]{:S(2)}, u32[]{:S(2)}) collective-permute-start(bf16[192,1280]{1,0:T(8,128)(2,1)S(1)} %get-tuple-element.189), channel_id=1, source_target_pairs={{0,8},{8,16},{16,24},{24,0},{1,9},{9,17},{17,25},{25,1},{2,10},{10... | collective-permute-start | bytes 1474568 | tf_op jit(solution)/shard_map/ppermute | solution.py:595
  970.6 43.4 %collective-permute-start.35 = (bf16[192,1280]{1,0:T(8,128)(2,1)}, bf16[192,1280]{1,0:T(8,128)(2,1)S(1)}, u32[]{:S(2)}, u32[]{:S(2)}) collective-permute-start(bf16[192,1280]{1,0:T(8,128)(2,1)} %get-tuple-element.191), channel_id=1, source_target_pairs={{0,16},{8,24},{16,0},{24,8},{1,17},{9,25},{17,1},{25,9},{2,18},{10... | collective-permute-start | bytes 1474568 | tf_op jit(solution)/shard_map/ppermute | solution.py:595
  974.9 78.0 %collective-permute-start.36 = (bf16[192,1280]{1,0:T(8,128)(2,1)}, bf16[192,1280]{1,0:T(8,128)(2,1)}, u32[]{:S(2)}, u32[]{:S(2)}) collective-permute-start(bf16[192,1280]{1,0:T(8,128)(2,1)} %get-tuple-element.190), channel_id=1, source_target_pairs={{0,24},{8,0},{16,8},{24,16},{1,25},{9,1},{17,9},{25,17},{2,26},{10... | collective-permute-start | bytes 1474568 | tf_op jit(solution)/shard_map/ppermute | solution.py:595
  982.4 84.3 %collective-permute-start.37 = (bf16[160,2560]{1,0:T(8,128)(2,1)}, bf16[160,2560]{1,0:T(8,128)(2,1)S(1)}, u32[]{:S(2)}, u32[]{:S(2)}) collective-permute-start(bf16[160,2560]{1,0:T(8,128)(2,1)} %get-tuple-element.170), channel_id=1, source_target_pairs={{0,8},{8,16},{16,24},{24,0},{1,9},{9,17},{17,25},{25,1},{2,10},{10... | collective-permute-start | bytes 2457608 | tf_op jit(solution)/shard_map/ppermute | solution.py:595
  984.4 98.7 %collective-permute-start.38 = (bf16[160,2560]{1,0:T(8,128)(2,1)}, bf16[160,2560]{1,0:T(8,128)(2,1)S(1)}, u32[]{:S(2)}, u32[]{:S(2)}) collective-permute-start(bf16[160,2560]{1,0:T(8,128)(2,1)} %get-tuple-element.172), channel_id=1, source_target_pairs={{0,16},{8,24},{16,0},{24,8},{1,17},{9,25},{17,1},{25,9},{2,18},{10... | collective-permute-start | bytes 2457608 | tf_op jit(solution)/shard_map/ppermute | solution.py:595
  986.2 27.8 %copy-start.64 = (bf16[192,1280]{1,0:T(8,128)(2,1)}, bf16[192,1280]{1,0:T(8,128)(2,1)S(1)}, u32[]{:S(2)}) copy-start(bf16[192,1280]{1,0:T(8,128)(2,1)S(1)} %collective-permute-done.34) | copy-start | bytes 1474564
  986.2 100.9 %collective-permute-start.39 = (bf16[160,2560]{1,0:T(8,128)(2,1)}, bf16[160,2560]{1,0:T(8,128)(2,1)S(1)}, u32[]{:S(2)}, u32[]{:S(2)}) collective-permute-start(bf16[160,2560]{1,0:T(8,128)(2,1)} %get-tuple-element.171), channel_id=1, source_target_pairs={{0,24},{8,0},{16,8},{24,16},{1,25},{9,1},{17,9},{25,17},{2,26},{10... | collective-permute-start | bytes 2457608 | tf_op jit(solution)/shard_map/ppermute | solution.py:595
  (113 other events, 596.1 us)
Sparse Core Ops, SparseCore 0:
  187.1 88.5 all-gather.2
  277.6 77.6 all-gather.4
  422.4 83.5 reduce-scatter.4
  508.9 77.6 reduce-scatter.6
  708.8 81.6 reduce-scatter.8
  793.5 130.1 reduce-scatter.10

commit v6 on v5

--- a/solution.py
+++ b/solution.py
@@ -555,20 +555,20 @@
     return part[:rows] + swap(part[rows:].astype(BF16)).astype(F32)
 
 
-def reduce_slots(sums):
-    total = sums[0]
-    for part in sums[1:]:
+def ring_sum(parts):
+    total = parts[0].astype(F32)
+    for part in parts[1:]:
         low = total.astype(BF16)
         moved = ring(low)
-        total = part + moved.astype(F32)
+        total = part.astype(F32) + moved.astype(F32)
     return total
 
 
-def send_direct(halves):
-    count = len(halves)
-    return [halves[0]] + [
-        lax.ppermute(halves[k], "o", [(j, (j - k) % count) for j in range(count)])
-        for k in range(1, count)
+def ring_order(parts):
+    count, at = lax.axis_size("o"), lax.axis_index("o")
+    return [
+        lax.dynamic_index_in_dim(parts, lax.rem(at - k + count, count), 0, False)
+        for k in [*range(1, count), 0]
     ]
 
 
@@ -585,15 +585,6 @@
         rows.reshape(-1, rows.shape[-1]), "i", scatter_dimension=0, tiled=True
     )
     return own.reshape(lax.axis_size("o"), -1, rows.shape[-1])
-
-
-def send_parts(parts):
-    count, at = lax.axis_size("o"), lax.axis_index("o")
-    moved = [lax.dynamic_index_in_dim(parts, at, 0, False)]
-    for k in range(1, count):
-        part = lax.dynamic_index_in_dim(parts, lax.rem(at + k, count), 0, False)
-        moved.append(lax.ppermute(part, "o", [(j, (j + k) % count) for j in range(count)]))
-    return moved
 
 
 def cuts_of(size):
@@ -672,9 +663,11 @@
         branch_ext, masks, conv_weight, row_params, gate_weights
     )
     conv_blocks = conv_low.reshape(tok_rows, heads_half, block_size)
+    for k in range(2, min(3, outer)):
+        cot_halves.append(ring(cot_halves[-1]))
     carry_in = entering(ends, False)
     carry_in, cot_halves[-1] = lax.optimization_barrier((carry_in, cot_halves[-1]))
-    for k in range(2, outer):
+    for k in range(3, outer):
         cot_halves.append(ring(cot_halves[-1]))
     states = local_state + cumulative * carry_in
     branch_act, gelu_back = jax.vjp(gelu_tanh, branch_y)
@@ -724,12 +717,12 @@
         )
         rows = grads_rows([list(zip(normed_slots, deltas)), list(zip(cot_slots, hiddens))])
     inner_sums.append(sum_inner(rows))
-    delta_normed_two = reduce_slots(sums)
+    delta_normed_two = ring_sum(sums)
     result_parts = [
         sum(mm_nt(hidden_of[p][k], ffw_parts[p][1]) for p in range(len(cuts))) for k in slots
     ]
     result_parts = [both_cores(part) for part in result_parts]
-    result_parts = [result_parts[0]] + [part.astype(BF16) for part in result_parts[1:]]
+    result_parts = result_parts[1:] + result_parts[:1]
     delta_normed_two, result_parts, inner_sums[0] = lax.optimization_barrier(
         (delta_normed_two, result_parts, inner_sums[0])
     )
@@ -799,7 +792,7 @@
     ).reshape(tok_rows, width_half)
     rim_delta = from_behind(delta_conv[:rim_rows], -1)
     rim_delta, result_parts = lax.optimization_barrier((rim_delta, result_parts))
-    result_moved = send_direct(result_parts)
+    result_sum = ring_sum(result_parts)
     ffw_in_grad = jnp.concatenate(
         [
             grad[:, :, : 2 * size].reshape(outer, part_width, 2, size)
@@ -857,16 +850,14 @@
         grad_decay,
         grad_ffw_bias.reshape(-1),
     ]
-    oy_moved = send_parts(grad_oy_inner)
+    grad_oy_inner, ffw_in_grad, ffw_out_grad = lax.optimization_barrier(
+        (grad_oy_inner, ffw_in_grad, ffw_out_grad)
+    )
+    grad_oy = ring_sum(ring_order(grad_oy_inner))
     small = sum_over_all(jnp.concatenate(flat).reshape(-1, 128))
-    result_half = residual + sum(part.astype(F32) for part in result_moved) + out_bias[1]
+    result_half = residual + result_sum + out_bias[1]
     result = join_halves(result_half, swap(result_half), core)
-    grad_x_inner, input_grad, result, ffw_in_grad, ffw_out_grad = lax.optimization_barrier(
-        (grad_x_inner, input_grad, result, ffw_in_grad, ffw_out_grad)
-    )
-    x_moved = send_parts(grad_x_inner)
-    grad_oy = sum(part.astype(F32) for part in oy_moved)
-    grad_x_gate = sum(part.astype(F32) for part in x_moved)
+    grad_x_gate = ring_sum(ring_order(grad_x_inner))
     grad_branch_x = grad_x_gate[:part_width]
     gate_grad = grad_x_gate[part_width:].reshape(2, heads_half, block_size // count, block_size)
     small = small.reshape(-1)

time: 1110 us -> 1050 us (0.946)
  the two profiles are of different devices: /device:TPU:8 before, /device:TPU:0 now
where the time goes in v6:
time: 1050 us; the launch traced here: 1040 us
  waiting for transfers between devices  357 us (34%)
  Pallas kernels  278 us (26%)
  matrix products  137 us (13%)
  other arithmetic  109 us (10%)
  local copies, waits for them, and re-layouts  100 us (10%)
  starting transfers between devices  45.4 us (4%)
  between operations  16.4 us (2%)
    ppermute x18, waiting for transfers between devices, ring(): lax.ppermute(value, 'o', [(k, (k + 1) % count) for k in range(count)])  306 us
    pallas_call x1, Pallas kernels, gather_weights(): pl.pallas_call(functools.partial(gather_kernel, outer, inner, groups, cut...  175 us
    dot_general x38, matrix products, dot(): lax.dot_general(a, b, ((contract[0], contract[1]), ((), ())), preferred_e...  132 us
    pallas_call x4, Pallas kernels, grads_rows(): pl.pallas_call(functools.partial(grads_kernel, plan, added), grid=(outer,...  63.4 us
    ppermute x4, waiting for transfers between devices, sum_over_all(): lax.ppermute(value, DP, [(k, k ^ bit) for k in range(count)])  31.4 us
    pallas_call x2, Pallas kernels, entering(): pl.pallas_call(functools.partial(enter_kernel, outer, inner, reverse), in...  21.5 us
    ppermute x18, starting transfers between devices, ring(): lax.ppermute(value, 'o', [(k, (k + 1) % count) for k in range(count)])  21.3 us
  transfers between devices with their start and end apart: 53, of which 23 were waited for; matrix products, arithmetic and copies ran while one was open for 27% of the time, Pallas kernels for 9%

profile of v6, /device:TPU:0, one launch (start us, length us, event | category | flops | bytes accessed | tf_op | source)
XLA Modules:
  0.0 1043.0 jit_solution(15890532841528206003)
XLA Ops:
  14.4 175.4 %shard_map.271 = (bf16[4,4,160,1280]{3,2,1,0:T(8,128)(2,1)}, bf16[4,4,160,1280]{3,2,1,0:T(8,128)(2,1)}, bf16[4,4,160,1280]{3,2,1,0:T(8,128)(2,1)}, bf16[4,160,15...) custom-call(bf16[160,1280]{1,0:T(8,128)(2,1)} %get-tuple-element.200, ...), custom_call_target="tpu_custom_call" | custom-call | tf_op jit(solution)/shard_map/pallas_call | solution.py:420
  195.9 17.1 %collective-permute-done.refs_15_ = bf16[192,2560]{1,0:T(8,128)(2,1)} collective-permute-done((bf16[192,2560]{1,0:T(8,128)(2,1)S(1)}, bf16[192,2560]{1,0:T(8,128)(2,1)}, u32[]{:S(2)}, u32[]{:S(2)}) %collective-permute-start) | collective-permute-done | bytes 983072 | tf_op jit(solution)/shard_map/ppermute | solution.py:25
  216.6 7.0 convolution_add_fusion.9.branch_ref
  223.6 10.5 %shard_map.272 = (bf16[384,1280]{1,0:T(8,128)(2,1)}, f32[384,1280]{1,0:T(8,128)}, f32[384,1280]{1,0:T(8,128)}, f32[384,1280]{1,0:T(8,128)}, f32[384,1280]{1,0:T(8,128)}, /*index=5*/f32[2,1280]{1,0:T(2,128)}) custom-call(f32[400,1280]{1,0:T(8,128)} %convolution_add_fusion.9.branch_ref, f32[384,8]{1,0:T(8,128)} %copy.99.mask_ref, f32[4,1280]{1,0:T(4,128)} %taps_ref.1, ...), custom_call_target="tpu_custom_call" | custom-call | flops 503316480 | bytes 10813440 | tf_op jit(solution)/shard_map/pallas_call | solution.py:131
  234.1 12.1 %shard_map.273 = f32[1,1280]{1,0:T(1,128)} custom-call(f32[2,1280]{1,0:T(2,128)} %get-tuple-element.74.ends_ref), custom_call_target="tpu_custom_call" | custom-call | tf_op jit(solution)/shard_map/pallas_call | solution.py:204
  247.0 8.1 multiply_convert_fusion.2
  255.1 5.3 fusion.185
  274.6 18.0 %collective-permute-done.13.refs_21_ = bf16[192,2560]{1,0:T(8,128)(2,1)S(1)} collective-permute-done((bf16[192,2560]{1,0:T(8,128)(2,1)}, bf16[192,2560]{1,0:T(8,128)(2,1)S(1)}, u32[]{:S(2)}, u32[]{:S(2)}) %collective-permute-start.13) | collective-permute-done | bytes 983072 | tf_op jit(solution)/shard_map/ppermute | solution.py:25
  292.7 20.4 %collective-permute-done.5.refs_3_ = bf16[192,2560]{1,0:T(8,128)(2,1)S(1)} collective-permute-done((bf16[192,2560]{1,0:T(8,128)(2,1)S(1)}, bf16[192,2560]{1,0:T(8,128)(2,1)S(1)}, u32[]{:S(2)}, u32[]{:S(2)}) %collective-permute-start.5) | collective-permute-done | bytes 983072 | tf_op jit(solution)/shard_map/ppermute | solution.py:25
  314.0 24.0 %collective-permute-done.8.refs_6_ = bf16[192,2560]{1,0:T(8,128)(2,1)S(1)} collective-permute-done((bf16[192,2560]{1,0:T(8,128)(2,1)S(1)}, bf16[192,2560]{1,0:T(8,128)(2,1)S(1)}, u32[]{:S(2)}, u32[]{:S(2)}) %collective-permute-start.8) | collective-permute-done | bytes 983072 | tf_op jit(solution)/shard_map/ppermute | solution.py:25
  340.0 22.3 %collective-permute-done.11.refs_9_ = bf16[192,2560]{1,0:T(8,128)(2,1)S(1)} collective-permute-done((bf16[192,2560]{1,0:T(8,128)(2,1)S(1)}, bf16[192,2560]{1,0:T(8,128)(2,1)S(1)}, u32[]{:S(2)}, u32[]{:S(2)}) %collective-permute-start.11) | collective-permute-done | bytes 983072 | tf_op jit(solution)/shard_map/ppermute | solution.py:25
  367.5 5.4 convolution_add_fusion.11
  396.2 22.2 %shard_map.274 = bf16[4,4,160,1536]{3,2,1,0:T(8,128)(2,1)} custom-call(bf16[192,2560]{1,0:T(8,128)(2,1)} %copy-done.21, bf16[192,2560]{1,0:T(8,128)(2,1)} %copy-done.63, bf16[384,1024]{1,0:T(8,128)(2,1)} %pad_maximum_fusion.9.refs_2_, bf16[192,2560]{1,0:T(8,128)(2,1)} %copy-done.51, bf16[192,2560]{1,0:T(8,128)(2,1)} %copy-done.55, ...), custom_call_target="tpu_custom_call" | custom-call | flops 12079595520 | bytes 20447232 | tf_op jit(solution)/shard_map/pallas_call | solution.py:492
  419.1 5.2 convolution_add_fusion.15
  425.4 4.2 fusion.125
  440.8 4.1 fusion.60
  444.9 4.6 convolution_add_fusion.6
  450.7 4.2 convolution_add_fusion.17
  457.6 4.1 fusion.62
  461.8 4.7 convolution_add_fusion.7
  474.1 4.1 fusion.67
  478.4 21.8 %shard_map.277 = bf16[4,4,160,1344]{3,2,1,0:T(8,128)(2,1)} custom-call(bf16[192,2560]{1,0:T(8,128)(2,1)} %copy-done.21, bf16[192,2560]{1,0:T(8,128)(2,1)} %copy-done.63, bf16[384,896]{1,0:T(8,128)(2,1)} %pad_maximum_fusion.13.refs_2_, bf16[192,2560]{1,0:T(8,128)(2,1)} %copy-done.51, bf16[192,2560]{1,0:T(8,128)(2,1)} %copy-done.55, ...), custom_call_target="tpu_custom_call" | custom-call | flops 10569646080 | bytes 18874368 | tf_op jit(solution)/shard_map/pallas_call | solution.py:492
  501.3 5.7 convolution_add_fusion.8
  508.1 3.9 fusion.146
  525.8 18.2 %collective-permute-done.19 = bf16[192,2560]{1,0:T(8,128)(2,1)S(1)} collective-permute-done((bf16[192,2560]{1,0:T(8,128)(2,1)S(1)}, bf16[192,2560]{1,0:T(8,128)(2,1)S(1)}, u32[]{:S(2)}, u32[]{:S(2)}) %collective-permute-start.19) | collective-permute-done | bytes 983072 | tf_op jit(solution)/shard_map/ppermute | solution.py:25
  549.0 22.5 %collective-permute-done.20 = bf16[192,2560]{1,0:T(8,128)(2,1)S(1)} collective-permute-done((bf16[192,2560]{1,0:T(8,128)(2,1)S(1)}, bf16[192,2560]{1,0:T(8,128)(2,1)S(1)}, u32[]{:S(2)}, u32[]{:S(2)}) %collective-permute-start.20) | collective-permute-done | bytes 983072 | tf_op jit(solution)/shard_map/ppermute | solution.py:25
  575.8 22.4 %collective-permute-done.21 = bf16[192,2560]{1,0:T(8,128)(2,1)S(1)} collective-permute-done((bf16[192,2560]{1,0:T(8,128)(2,1)S(1)}, bf16[192,2560]{1,0:T(8,128)(2,1)S(1)}, u32[]{:S(2)}, u32[]{:S(2)}) %collective-permute-start.21) | collective-permute-done | bytes 983072 | tf_op jit(solution)/shard_map/ppermute | solution.py:25
  617.4 8.3 convert_reduce_fusion.2
  625.7 7.2 shard_map.275
  634.4 9.3 shard_map.276
  644.5 7.2 multiply_reduce_fusion
  661.9 4.0 fusion.53
  668.9 6.0 fusion.36
  678.4 3.7 convert_element_type.346.refs_2_
  682.1 7.1 convert_reduce_fusion.3
  689.1 8.0 shard_map.278
  700.1 11.3 %shard_map.279 = bf16[4,4,160,2560]{3,2,1,0:T(8,128)(2,1)} custom-call(bf16[384,2560]{1,0:T(8,128)(2,1)} %pad_maximum_fusion.4.refs_0_, bf16[384,1280]{1,0:T(8,128)(2,1)} %copy-done.48, bf16[384,2560]{1,0:T(8,128)(2,1)} %slice.313.refs_0_.refs_2_, bf16[384,1280]{1,0:T(8,128)(2,1)} %get-tuple-element.144.refs_3_), custom_call_target="tpu_custom_call" | custom-call | flops 5033164800 | bytes 17039360 | tf_op jit(solution)/shard_map/pallas_call | solution.py:492
  715.4 5.0 fusion.186
  720.5 5.0 convolution_add_fusion.4
  731.8 5.0 collective-permute-start.28
  737.3 4.5 all-to-all-start
  747.1 13.3 %collective-permute-done.28 = bf16[192,2560]{1,0:T(8,128)(2,1)} collective-permute-done((bf16[192,2560]{1,0:T(8,128)(2,1)}, bf16[192,2560]{1,0:T(8,128)(2,1)}, u32[]{:S(2)}, u32[]{:S(2)}) %collective-permute-start.28) | collective-permute-done | bytes 983072 | tf_op jit(solution)/shard_map/ppermute | solution.py:25
  764.3 48.5 %collective-permute-done.29 = bf16[192,2560]{1,0:T(8,128)(2,1)} collective-permute-done((bf16[192,2560]{1,0:T(8,128)(2,1)}, bf16[192,2560]{1,0:T(8,128)(2,1)}, u32[]{:S(2)}, u32[]{:S(2)}) %collective-permute-start.29) | collective-permute-done | bytes 983072 | tf_op jit(solution)/shard_map/ppermute | solution.py:25
  812.8 3.2 add_convert_fusion
  816.0 10.1 collective-permute-start.30
  826.2 18.0 %all-to-all-done = bf16[4,160,1536]{2,1,0:T(8,128)(2,1)} async-done(((bf16[4,160,1536]{2,1,0:T(8,128)(2,1)}), bf16[4,160,1536]{2,1,0:T(8,128)(2,1)}, u32[]{:S(2)}, u32[]{:S(2)}) %all-to-all-start) | async-done | bytes 1966112 | tf_op jit(solution)/shard_map/all_to_all | solution.py:576
  844.2 4.8 all-to-all-start.1
  849.8 7.1 fusion.13
  859.6 6.8 collective-permute-done.42
  868.1 13.2 %collective-permute-done.43 = f32[240,128]{1,0:T(8,128)S(1)} collective-permute-done((f32[240,128]{1,0:T(8,128)S(1)}, f32[240,128]{1,0:T(8,128)S(1)}, u32[]{:S(2)}, u32[]{:S(2)}) %collective-permute-start.43) | collective-permute-done | bytes 122912 | tf_op jit(solution)/shard_map/ppermute | solution.py:37
  881.4 4.6 collective-permute-start.44
  886.0 10.7 %collective-permute-done.44 = f32[240,128]{1,0:T(8,128)S(1)} collective-permute-done((f32[240,128]{1,0:T(8,128)S(1)}, f32[240,128]{1,0:T(8,128)S(1)}, u32[]{:S(2)}, u32[]{:S(2)}) %collective-permute-start.44) | collective-permute-done | bytes 122912 | tf_op jit(solution)/shard_map/ppermute | solution.py:37
  908.7 3.4 reshape.246
  914.6 4.3 reshape.230
  921.2 5.7 copy.116
  927.0 7.4 reshape.245
  934.4 4.5 broadcast_select_fusion.1
  944.5 4.5 pad_maximum_fusion.1
  949.0 10.1 collective-permute-done.34
  959.3 17.3 %collective-permute-done.37 = bf16[160,2560]{1,0:T(8,128)(2,1)S(1)} collective-permute-done((bf16[160,2560]{1,0:T(8,128)(2,1)S(1)}, bf16[160,2560]{1,0:T(8,128)(2,1)S(1)}, u32[]{:S(2)}, u32[]{:S(2)}) %collective-permute-start.37) | collective-permute-done | bytes 819232 | tf_op jit(solution)/shard_map/ppermute | solution.py:25
  979.1 8.1 collective-permute-done.35
  987.4 17.4 %collective-permute-done.38 = bf16[160,2560]{1,0:T(8,128)(2,1)S(1)} collective-permute-done((bf16[160,2560]{1,0:T(8,128)(2,1)S(1)}, bf16[160,2560]{1,0:T(8,128)(2,1)S(1)}, u32[]{:S(2)}, u32[]{:S(2)}) %collective-permute-start.38) | collective-permute-done | bytes 819232 | tf_op jit(solution)/shard_map/ppermute | solution.py:25
  1005.0 10.3 collective-permute-done.36
  1016.2 16.1 %collective-permute-done.39 = bf16[160,2560]{1,0:T(8,128)(2,1)S(1)} collective-permute-done((bf16[160,2560]{1,0:T(8,128)(2,1)S(1)}, bf16[160,2560]{1,0:T(8,128)(2,1)S(1)}, u32[]{:S(2)}, u32[]{:S(2)}) %collective-permute-start.39) | collective-permute-done | bytes 819232 | tf_op jit(solution)/shard_map/ppermute | solution.py:25
  (544 shorter events, 207.8 us)
Async XLA Ops:
  7.2 256.4 %copy-start = (f32[2,3840]{1,0:T(2,128)S(1)}, f32[2,3840]{1,0:T(2,128)}, u32[]{:S(2)}) copy-start(f32[2,3840]{1,0:T(2,128)} %param.31) | copy-start | bytes 92164
  7.2 360.3 %all-gather.3.cloned.1.call-start = ((), (), s32[]{:S(2)}) async-start(), calls=%async_computation.6 | async-start | bytes 9830400 | tf_op jit(solution)/shard_map/all_gather | solution.py:580
  10.9 259.0 %copy-start.89 = (f32[2560]{0:T(1024)}, f32[2560]{0:T(1024)S(1)}, u32[]{:S(2)}) copy-start(f32[2560]{0:T(1024)S(1)} %get-tuple-element.135) | copy-start | bytes 30724
  189.9 229.2 %all-gather.5.cloned.1.call-start = ((), (), s32[]{:S(2)}) async-start(), calls=%async_computation.7 | async-start | bytes 9011200 | tf_op jit(solution)/shard_map/all_gather | solution.py:580
  192.1 72.2 %copy-start.7 = (bf16[192,2560]{1,0:T(8,128)(2,1)}, bf16[192,2560]{1,0:T(8,128)(2,1)S(1)}, u32[]{:S(2)}) copy-start(bf16[192,2560]{1,0:T(8,128)(2,1)S(1)} %get-tuple-element.75.refs_12_) | copy-start | bytes 2949124
  192.1 20.9 %collective-permute-start = (bf16[192,2560]{1,0:T(8,128)(2,1)S(1)}, bf16[192,2560]{1,0:T(8,128)(2,1)}, u32[]{:S(2)}, u32[]{:S(2)}) collective-permute-start(bf16[192,2560]{1,0:T(8,128)(2,1)S(1)} %get-tuple-element.75.refs_12_), channel_id=1, source_target_pairs={{0,8},{8,16},{16,24},{24,0},{1,9},{9,17},{17,25},{25,1},{2,10},{10... | collective-permute-start | bytes 2949128 | tf_op jit(solution)/shard_map/ppermute | solution.py:25
  213.1 33.9 %collective-permute-start.1 = (bf16[192,2560]{1,0:T(8,128)(2,1)}, bf16[192,2560]{1,0:T(8,128)(2,1)}, u32[]{:S(2)}, u32[]{:S(2)}) collective-permute-start(bf16[192,2560]{1,0:T(8,128)(2,1)} %collective-permute-done.refs_15_), channel_id=1, source_target_pairs={{0,8},{8,16},{16,24},{24,0},{1,9},{9,17},{17,25},{25,1},{2,10},{10... | collective-permute-start | bytes 2949128 | tf_op jit(solution)/shard_map/ppermute | solution.py:25
  263.0 4.2 collective-permute-start.2
  263.0 8.3 collective-permute-start.3
  263.5 336.3 %reduce-scatter.5.cloned.1.call-start = ((), (), s32[]{:S(2)}) async-start(), calls=%async_computation.8 | async-start | bytes 9830400 | tf_op jit(solution)/shard_map/reduce_scatter | solution.py:584
  264.4 28.2 %collective-permute-start.7 = (bf16[192,2560]{1,0:T(8,128)(2,1)}, bf16[192,2560]{1,0:T(8,128)(2,1)S(1)}, u32[]{:S(2)}, u32[]{:S(2)}) collective-permute-start(bf16[192,2560]{1,0:T(8,128)(2,1)} %collective-permute-done.refs_15_), channel_id=1, source_target_pairs={{0,1},{1,0},{2,3},{3,2},{4,5},{5,4},{6,7},{7,6},{8,9},{9,8},{10,11... | collective-permute-start | bytes 2949128 | tf_op jit(solution)/shard_map/ppermute | solution.py:20
  265.9 26.7 %collective-permute-start.13 = (bf16[192,2560]{1,0:T(8,128)(2,1)}, bf16[192,2560]{1,0:T(8,128)(2,1)S(1)}, u32[]{:S(2)}, u32[]{:S(2)}) collective-permute-start(bf16[192,2560]{1,0:T(8,128)(2,1)} %collective-permute-done.1.refs_18_), channel_id=1, source_target_pairs={{0,8},{8,16},{16,24},{24,0},{1,9},{9,17},{17,25},{25,1},{2,10},{10... | collective-permute-start | bytes 2949128 | tf_op jit(solution)/shard_map/ppermute | solution.py:25
  270.2 119.6 %copy-start.21 = (bf16[192,2560]{1,0:T(8,128)(2,1)}, bf16[192,2560]{1,0:T(8,128)(2,1)S(1)}, u32[]{:S(2)}) copy-start(bf16[192,2560]{1,0:T(8,128)(2,1)S(1)} %multiply_convert_fusion.1.refs_0_) | copy-start | bytes 2949124
  270.2 42.8 %collective-permute-start.5 = (bf16[192,2560]{1,0:T(8,128)(2,1)S(1)}, bf16[192,2560]{1,0:T(8,128)(2,1)S(1)}, u32[]{:S(2)}, u32[]{:S(2)}) collective-permute-start(bf16[192,2560]{1,0:T(8,128)(2,1)S(1)} %multiply_convert_fusion.1.refs_0_), channel_id=1, source_target_pairs={{0,8},{8,16},{16,24},{24,0},{1,9},{9,17},{17,25},{25,1},{2,10},{10... | collective-permute-start | bytes 2949128 | tf_op jit(solution)/shard_map/ppermute | solution.py:25
  272.6 40.6 %copy-start.71 = (bf16[384,2560]{1,0:T(8,128)(2,1)}, bf16[384,2560]{1,0:T(8,128)(2,1)S(1)}, u32[]{:S(2)}) copy-start(bf16[384,2560]{1,0:T(8,128)(2,1)S(1)} %constant_dynamic-update-slice_fusion) | copy-start | bytes 5898244
  272.6 40.6 %collective-permute-start.10 = (bf16[192,2560]{1,0:T(8,128)(2,1)}, bf16[192,2560]{1,0:T(8,128)(2,1)S(1)}, u32[]{:S(2)}, u32[]{:S(2)}) collective-permute-start(bf16[192,2560]{1,0:T(8,128)(2,1)} %collective-permute-done.1.refs_18_), channel_id=1, source_target_pairs={{0,1},{1,0},{2,3},{3,2},{4,5},{5,4},{6,7},{7,6},{8,9},{9,8},{10,11... | collective-permute-start | bytes 2949128 | tf_op jit(solution)/shard_map/ppermute | solution.py:20
  292.6 20.8 %collective-permute-start.14 = (bf16[192,2560]{1,0:T(8,128)(2,1)S(1)}, bf16[192,2560]{1,0:T(8,128)(2,1)S(1)}, u32[]{:S(2)}, u32[]{:S(2)}) collective-permute-start(bf16[192,2560]{1,0:T(8,128)(2,1)S(1)} %collective-permute-done.13.refs_21_), channel_id=1, source_target_pairs={{0,1},{1,0},{2,3},{3,2},{4,5},{5,4},{6,7},{7,6},{8,9},{9,8},{10,11... | collective-permute-start | bytes 2949128 | tf_op jit(solution)/shard_map/ppermute | solution.py:20
  313.0 25.0 %collective-permute-start.8 = (bf16[192,2560]{1,0:T(8,128)(2,1)S(1)}, bf16[192,2560]{1,0:T(8,128)(2,1)S(1)}, u32[]{:S(2)}, u32[]{:S(2)}) collective-permute-start(bf16[192,2560]{1,0:T(8,128)(2,1)S(1)} %collective-permute-done.5.refs_3_), channel_id=1, source_target_pairs={{0,8},{8,16},{16,24},{24,0},{1,9},{9,17},{17,25},{25,1},{2,10},{10... | collective-permute-start | bytes 2949128 | tf_op jit(solution)/shard_map/ppermute | solution.py:25
  313.1 25.2 %collective-permute-start.4 = (bf16[192,2560]{1,0:T(8,128)(2,1)S(1)}, bf16[192,2560]{1,0:T(8,128)(2,1)S(1)}, u32[]{:S(2)}, u32[]{:S(2)}) collective-permute-start(bf16[192,2560]{1,0:T(8,128)(2,1)S(1)} %multiply_convert_fusion.1.refs_0_), channel_id=1, source_target_pairs={{0,1},{1,0},{2,3},{3,2},{4,5},{5,4},{6,7},{7,6},{8,9},{9,8},{10,11... | collective-permute-start | bytes 2949128 | tf_op jit(solution)/shard_map/ppermute | solution.py:20
  313.4 48.9 %collective-permute-start.6 = (bf16[192,2560]{1,0:T(8,128)(2,1)S(1)}, bf16[192,2560]{1,0:T(8,128)(2,1)S(1)}, u32[]{:S(2)}, u32[]{:S(2)}) collective-permute-start(bf16[192,2560]{1,0:T(8,128)(2,1)S(1)} %collective-permute-done.5.refs_3_), channel_id=1, source_target_pairs={{0,1},{1,0},{2,3},{3,2},{4,5},{5,4},{6,7},{7,6},{8,9},{9,8},{10,11... | collective-permute-start | bytes 2949128 | tf_op jit(solution)/shard_map/ppermute | solution.py:20
  338.0 24.3 %collective-permute-start.11 = (bf16[192,2560]{1,0:T(8,128)(2,1)S(1)}, bf16[192,2560]{1,0:T(8,128)(2,1)S(1)}, u32[]{:S(2)}, u32[]{:S(2)}) collective-permute-start(bf16[192,2560]{1,0:T(8,128)(2,1)S(1)} %collective-permute-done.8.refs_6_), channel_id=1, source_target_pairs={{0,8},{8,16},{16,24},{24,0},{1,9},{9,17},{17,25},{25,1},{2,10},{10... | collective-permute-start | bytes 2949128 | tf_op jit(solution)/shard_map/ppermute | solution.py:25
  339.9 23.7 %collective-permute-start.9 = (bf16[192,2560]{1,0:T(8,128)(2,1)S(1)}, bf16[192,2560]{1,0:T(8,128)(2,1)S(1)}, u32[]{:S(2)}, u32[]{:S(2)}) collective-permute-start(bf16[192,2560]{1,0:T(8,128)(2,1)S(1)} %collective-permute-done.8.refs_6_), channel_id=1, source_target_pairs={{0,1},{1,0},{2,3},{3,2},{4,5},{5,4},{6,7},{7,6},{8,9},{9,8},{10,11... | collective-permute-start | bytes 2949128 | tf_op jit(solution)/shard_map/ppermute | solution.py:20
  362.3 2.6 collective-permute-start.12
  375.8 81.8 %copy-start.37 = (bf16[384,512]{1,0:T(8,128)(2,1)}, bf16[384,512]{1,0:T(8,128)(2,1)S(1)}, u32[]{:S(2)}) copy-start(bf16[384,512]{1,0:T(8,128)(2,1)S(1)} %get-tuple-element.167) | copy-start | bytes 1179652
  381.5 59.2 %copy-start.38 = (bf16[384,512]{1,0:T(8,128)(2,1)}, bf16[384,512]{1,0:T(8,128)(2,1)S(1)}, u32[]{:S(2)}) copy-start(bf16[384,512]{1,0:T(8,128)(2,1)S(1)} %get-tuple-element.168) | copy-start | bytes 1179652
  394.5 79.6 %copy-start.45 = (bf16[384,512]{1,0:T(8,128)(2,1)}, bf16[384,512]{1,0:T(8,128)(2,1)S(1)}, u32[]{:S(2)}) copy-start(bf16[384,512]{1,0:T(8,128)(2,1)S(1)} %get-tuple-element.172) | copy-start | bytes 1179652
  418.5 226.0 %reduce-scatter.7.cloned.1.call-start = ((), (), s32[]{:S(2)}) async-start(), calls=%async_computation.9 | async-start | bytes 9011200 | tf_op jit(solution)/shard_map/reduce_scatter | solution.py:584
  434.5 43.7 %collective-permute-start.18 = (bf16[192,2560]{1,0:T(8,128)(2,1)S(1)}, bf16[192,2560]{1,0:T(8,128)(2,1)S(1)}, u32[]{:S(2)}, u32[]{:S(2)}) collective-permute-start(bf16[192,2560]{1,0:T(8,128)(2,1)S(1)} %slice.749), channel_id=1, source_target_pairs={{0,1},{1,0},{2,3},{3,2},{4,5},{5,4},{6,7},{7,6},{8,9},{9,8},{10,11... | collective-permute-start | bytes 2949128 | tf_op jit(solution)/shard_map/ppermute | solution.py:20
  450.7 74.6 %collective-permute-start.17 = (bf16[192,2560]{1,0:T(8,128)(2,1)}, bf16[192,2560]{1,0:T(8,128)(2,1)}, u32[]{:S(2)}, u32[]{:S(2)}) collective-permute-start(bf16[192,2560]{1,0:T(8,128)(2,1)} %slice.750), channel_id=1, source_target_pairs={{0,1},{1,0},{2,3},{3,2},{4,5},{5,4},{6,7},{7,6},{8,9},{9,8},{10,11... | collective-permute-start | bytes 2949128 | tf_op jit(solution)/shard_map/ppermute | solution.py:20
  467.7 81.3 %collective-permute-start.16 = (bf16[192,2560]{1,0:T(8,128)(2,1)}, bf16[192,2560]{1,0:T(8,128)(2,1)}, u32[]{:S(2)}, u32[]{:S(2)}) collective-permute-start(bf16[192,2560]{1,0:T(8,128)(2,1)} %slice.751), channel_id=1, source_target_pairs={{0,1},{1,0},{2,3},{3,2},{4,5},{5,4},{6,7},{7,6},{8,9},{9,8},{10,11... | collective-permute-start | bytes 2949128 | tf_op jit(solution)/shard_map/ppermute | solution.py:20
  500.2 441.9 %reduce-scatter.9.cloned.1.call-start = ((), (), s32[]{:S(2)}) async-start(), calls=%async_computation.10 | async-start | bytes 9830400 | tf_op jit(solution)/shard_map/reduce_scatter | solution.py:584
  508.1 67.8 %collective-permute-start.15 = (bf16[192,2560]{1,0:T(8,128)(2,1)}, bf16[192,2560]{1,0:T(8,128)(2,1)S(1)}, u32[]{:S(2)}, u32[]{:S(2)}) collective-permute-start(bf16[192,2560]{1,0:T(8,128)(2,1)} %slice.752), channel_id=1, source_target_pairs={{0,1},{1,0},{2,3},{3,2},{4,5},{5,4},{6,7},{7,6},{8,9},{9,8},{10,11... | collective-permute-start | bytes 2949128 | tf_op jit(solution)/shard_map/ppermute | solution.py:20
  517.7 26.3 %collective-permute-start.19 = (bf16[192,2560]{1,0:T(8,128)(2,1)S(1)}, bf16[192,2560]{1,0:T(8,128)(2,1)S(1)}, u32[]{:S(2)}, u32[]{:S(2)}) collective-permute-start(bf16[192,2560]{1,0:T(8,128)(2,1)S(1)} %slice_add_fusion.4), channel_id=1, source_target_pairs={{0,8},{8,16},{16,24},{24,0},{1,9},{9,17},{17,25},{25,1},{2,10},{10... | collective-permute-start | bytes 2949128 | tf_op jit(solution)/shard_map/ppermute | solution.py:25
  520.4 25.0 %collective-permute-start.25 = (bf16[192,2560]{1,0:T(8,128)(2,1)S(1)}, bf16[192,2560]{1,0:T(8,128)(2,1)S(1)}, u32[]{:S(2)}, u32[]{:S(2)}) collective-permute-start(bf16[192,2560]{1,0:T(8,128)(2,1)S(1)} %slice.745), channel_id=1, source_target_pairs={{0,1},{1,0},{2,3},{3,2},{4,5},{5,4},{6,7},{7,6},{8,9},{9,8},{10,11... | collective-permute-start | bytes 2949128 | tf_op jit(solution)/shard_map/ppermute | solution.py:20
  525.4 21.7 %collective-permute-start.24 = (bf16[192,2560]{1,0:T(8,128)(2,1)S(1)}, bf16[192,2560]{1,0:T(8,128)(2,1)S(1)}, u32[]{:S(2)}, u32[]{:S(2)}) collective-permute-start(bf16[192,2560]{1,0:T(8,128)(2,1)S(1)} %slice.746), channel_id=1, source_target_pairs={{0,1},{1,0},{2,3},{3,2},{4,5},{5,4},{6,7},{7,6},{8,9},{9,8},{10,11... | collective-permute-start | bytes 2949128 | tf_op jit(solution)/shard_map/ppermute | solution.py:20
  544.0 30.4 %collective-permute-start.23 = (bf16[192,2560]{1,0:T(8,128)(2,1)S(1)}, bf16[192,2560]{1,0:T(8,128)(2,1)S(1)}, u32[]{:S(2)}, u32[]{:S(2)}) collective-permute-start(bf16[192,2560]{1,0:T(8,128)(2,1)S(1)} %slice.747), channel_id=1, source_target_pairs={{0,1},{1,0},{2,3},{3,2},{4,5},{5,4},{6,7},{7,6},{8,9},{9,8},{10,11... | collective-permute-start | bytes 2949128 | tf_op jit(solution)/shard_map/ppermute | solution.py:20
  545.5 26.0 %collective-permute-start.20 = (bf16[192,2560]{1,0:T(8,128)(2,1)S(1)}, bf16[192,2560]{1,0:T(8,128)(2,1)S(1)}, u32[]{:S(2)}, u32[]{:S(2)}) collective-permute-start(bf16[192,2560]{1,0:T(8,128)(2,1)S(1)} %fusion.46), channel_id=1, source_target_pairs={{0,8},{8,16},{16,24},{24,0},{1,9},{9,17},{17,25},{25,1},{2,10},{10... | collective-permute-start | bytes 2949128 | tf_op jit(solution)/shard_map/ppermute | solution.py:25
  547.1 26.1 %collective-permute-start.22 = (bf16[192,2560]{1,0:T(8,128)(2,1)S(1)}, bf16[192,2560]{1,0:T(8,128)(2,1)S(1)}, u32[]{:S(2)}, u32[]{:S(2)}) collective-permute-start(bf16[192,2560]{1,0:T(8,128)(2,1)S(1)} %slice.748), channel_id=1, source_target_pairs={{0,1},{1,0},{2,3},{3,2},{4,5},{5,4},{6,7},{7,6},{8,9},{9,8},{10,11... | collective-permute-start | bytes 2949128 | tf_op jit(solution)/shard_map/ppermute | solution.py:20
  573.1 25.2 %collective-permute-start.21 = (bf16[192,2560]{1,0:T(8,128)(2,1)S(1)}, bf16[192,2560]{1,0:T(8,128)(2,1)S(1)}, u32[]{:S(2)}, u32[]{:S(2)}) collective-permute-start(bf16[192,2560]{1,0:T(8,128)(2,1)S(1)} %fusion.48), channel_id=1, source_target_pairs={{0,8},{8,16},{16,24},{24,0},{1,9},{9,17},{17,25},{25,1},{2,10},{10... | collective-permute-start | bytes 2949128 | tf_op jit(solution)/shard_map/ppermute | solution.py:25
  603.9 10.8 %collective-permute-start.26 = (bf16[192,2560]{1,0:T(8,128)(2,1)}, bf16[192,2560]{1,0:T(8,128)(2,1)}, u32[]{:S(2)}, u32[]{:S(2)}) collective-permute-start(bf16[192,2560]{1,0:T(8,128)(2,1)} %get-tuple-element.148), channel_id=1, source_target_pairs={{0,1},{1,0},{2,3},{3,2},{4,5},{5,4},{6,7},{7,6},{8,9},{9,8},{10,11... | collective-permute-start | bytes 2949128 | tf_op jit(solution)/shard_map/ppermute | solution.py:20
  674.9 7.1 collective-permute-start.27
  697.2 246.0 %reduce-scatter.11.cloned.1.call-start = ((), (), s32[]{:S(2)}) async-start(), calls=%async_computation.11 | async-start | bytes 16384000 | tf_op jit(solution)/shard_map/reduce_scatter | solution.py:584
  728.5 15.1 %collective-permute-start.32 = (bf16[192,2560]{1,0:T(8,128)(2,1)}, bf16[192,2560]{1,0:T(8,128)(2,1)}, u32[]{:S(2)}, u32[]{:S(2)}) collective-permute-start(bf16[192,2560]{1,0:T(8,128)(2,1)} %dynamic-slice_convert_fusion), channel_id=1, source_target_pairs={{0,1},{1,0},{2,3},{3,2},{4,5},{5,4},{6,7},{7,6},{8,9},{9,8},{10,11... | collective-permute-start | bytes 2949128 | tf_op jit(solution)/shard_map/ppermute | solution.py:20
  731.8 28.5 %collective-permute-start.28 = (bf16[192,2560]{1,0:T(8,128)(2,1)}, bf16[192,2560]{1,0:T(8,128)(2,1)}, u32[]{:S(2)}, u32[]{:S(2)}) collective-permute-start(bf16[192,2560]{1,0:T(8,128)(2,1)} %slice_add_fusion.3), channel_id=1, source_target_pairs={{0,8},{8,16},{16,24},{24,0},{1,9},{9,17},{17,25},{25,1},{2,10},{10... | collective-permute-start | bytes 2949128 | tf_op jit(solution)/shard_map/ppermute | solution.py:25
  737.3 107.0 %all-to-all-start = ((bf16[4,160,1536]{2,1,0:T(8,128)(2,1)}), bf16[4,160,1536]{2,1,0:T(8,128)(2,1)}, u32[]{:S(2)}, u32[]{:S(2)}) async-start(bf16[4,160,1536]{2,1,0:T(8,128)(2,1)} %bitcast.178), calls=%async_computation.4 | async-start | bytes 3932160 | tf_op jit(solution)/shard_map/all_to_all | solution.py:576
  746.7 17.4 %collective-permute-start.40 = (f32[4,2560]{1,0:T(4,128)S(1)}, f32[4,2560]{1,0:T(4,128)S(1)}, u32[]{:S(2)}, u32[]{:S(2)}) collective-permute-start(f32[4,2560]{1,0:T(4,128)S(1)} %pad_maximum_fusion.18), channel_id=1, source_target_pairs={{0,1},{1,0},{2,3},{3,2},{4,5},{5,4},{6,7},{7,6},{8,9},{9,8},{10,11... | collective-permute-start | bytes 122888 | tf_op jit(solution)/shard_map/ppermute | solution.py:20
  762.7 50.0 %collective-permute-start.29 = (bf16[192,2560]{1,0:T(8,128)(2,1)}, bf16[192,2560]{1,0:T(8,128)(2,1)}, u32[]{:S(2)}, u32[]{:S(2)}) collective-permute-start(bf16[192,2560]{1,0:T(8,128)(2,1)} %add_convert_fusion.1), channel_id=1, source_target_pairs={{0,8},{8,16},{16,24},{24,0},{1,9},{9,17},{17,25},{25,1},{2,10},{10... | collective-permute-start | bytes 2949128 | tf_op jit(solution)/shard_map/ppermute | solution.py:25
  764.2 61.9 %copy-start.96 = (f32[1280]{0:T(1024)S(1)}, f32[1280]{0:T(1024)}, u32[]{:S(2)}) copy-start(f32[1280]{0:T(1024)} %param.29) | copy-start | bytes 15364
  816.0 33.8 %copy-start.93 = (f32[2560]{0:T(1024)S(1)}, f32[2560]{0:T(1024)}, u32[]{:S(2)}) copy-start(f32[2560]{0:T(1024)} %get-tuple-element.136) | copy-start | bytes 30724
  816.0 33.8 %collective-permute-start.30 = (bf16[192,2560]{1,0:T(8,128)(2,1)}, bf16[192,2560]{1,0:T(8,128)(2,1)}, u32[]{:S(2)}, u32[]{:S(2)}) collective-permute-start(bf16[192,2560]{1,0:T(8,128)(2,1)} %add_convert_fusion), channel_id=1, source_target_pairs={{0,8},{8,16},{16,24},{24,0},{1,9},{9,17},{17,25},{25,1},{2,10},{10... | collective-permute-start | bytes 2949128 | tf_op jit(solution)/shard_map/ppermute | solution.py:25
  844.2 61.3 %all-to-all-start.1 = ((bf16[4,160,1344]{2,1,0:T(8,128)(2,1)}), bf16[4,160,1344]{2,1,0:T(8,128)(2,1)}, u32[]{:S(2)}, u32[]{:S(2)}) async-start(bf16[4,160,1344]{2,1,0:T(8,128)(2,1)} %bitcast.185), calls=%async_computation.5 | async-start | bytes 3604480 | tf_op jit(solution)/shard_map/all_to_all | solution.py:576
  849.1 8.6 collective-permute-start.41
  856.9 77.4 %collective-permute-start.33 = (f32[192,2560]{1,0:T(8,128)}, f32[192,2560]{1,0:T(8,128)}, u32[]{:S(2)}, u32[]{:S(2)}) collective-permute-start(f32[192,2560]{1,0:T(8,128)} %get-tuple-element.182), channel_id=1, source_target_pairs={{0,1},{1,0},{2,3},{3,2},{4,5},{5,4},{6,7},{7,6},{8,9},{9,8},{10,11... | collective-permute-start | bytes 5898248 | tf_op jit(solution)/shard_map/ppermute | solution.py:20
  857.7 8.6 collective-permute-start.42
  866.4 15.0 %collective-permute-start.43 = (f32[240,128]{1,0:T(8,128)S(1)}, f32[240,128]{1,0:T(8,128)S(1)}, u32[]{:S(2)}, u32[]{:S(2)}) collective-permute-start(f32[240,128]{1,0:T(8,128)S(1)} %fusion.225), channel_id=1, source_target_pairs={{0,8},{2,10},{4,12},{6,14},{8,0},{10,2},{12,4},{14,6},{16,24},{18,... | collective-permute-start | bytes 368648 | tf_op jit(solution)/shard_map/ppermute | solution.py:37
  881.4 15.3 %collective-permute-start.44 = (f32[240,128]{1,0:T(8,128)S(1)}, f32[240,128]{1,0:T(8,128)S(1)}, u32[]{:S(2)}, u32[]{:S(2)}) collective-permute-start(f32[240,128]{1,0:T(8,128)S(1)} %add.570), channel_id=1, source_target_pairs={{0,16},{2,18},{4,20},{6,22},{8,24},{10,26},{12,28},{14,30},{16,0},... | collective-permute-start | bytes 368648 | tf_op jit(solution)/shard_map/ppermute | solution.py:37
  896.7 42.2 %collective-permute-start.31 = (f32[192,2560]{1,0:T(8,128)}, f32[192,2560]{1,0:T(8,128)}, u32[]{:S(2)}, u32[]{:S(2)}) collective-permute-start(f32[192,2560]{1,0:T(8,128)} %get-tuple-element.183), channel_id=1, source_target_pairs={{0,1},{1,0},{2,3},{3,2},{4,5},{5,4},{6,7},{7,6},{8,9},{9,8},{10,11... | collective-permute-start | bytes 5898248 | tf_op jit(solution)/shard_map/ppermute | solution.py:20
  943.1 15.9 %collective-permute-start.34 = (bf16[192,1280]{1,0:T(8,128)(2,1)S(1)}, bf16[192,1280]{1,0:T(8,128)(2,1)S(1)}, u32[]{:S(2)}, u32[]{:S(2)}) collective-permute-start(bf16[192,1280]{1,0:T(8,128)(2,1)S(1)} %dynamic-slice_bitcast_fusion.1), channel_id=1, source_target_pairs={{0,8},{8,16},{16,24},{24,0},{1,9},{9,17},{17,25},{25,1},{2,10},{10... | collective-permute-start | bytes 1474568 | tf_op jit(solution)/shard_map/ppermute | solution.py:25
  944.4 32.2 %collective-permute-start.37 = (bf16[160,2560]{1,0:T(8,128)(2,1)S(1)}, bf16[160,2560]{1,0:T(8,128)(2,1)S(1)}, u32[]{:S(2)}, u32[]{:S(2)}) collective-permute-start(bf16[160,2560]{1,0:T(8,128)(2,1)S(1)} %dynamic-slice_bitcast_fusion), channel_id=1, source_target_pairs={{0,8},{8,16},{16,24},{24,0},{1,9},{9,17},{17,25},{25,1},{2,10},{10... | collective-permute-start | bytes 2457608 | tf_op jit(solution)/shard_map/ppermute | solution.py:25
  944.5 32.1 %copy-start.24 = (bf16[640,2560]{1,0:T(8,128)(2,1)S(1)}, bf16[640,2560]{1,0:T(8,128)(2,1)}, u32[]{:S(2)}) copy-start(bf16[640,2560]{1,0:T(8,128)(2,1)} %reduce-scatter.11.cloned.1.call-done) | copy-start | bytes 9830404
  959.2 27.9 %collective-permute-start.35 = (bf16[192,1280]{1,0:T(8,128)(2,1)S(1)}, bf16[192,1280]{1,0:T(8,128)(2,1)S(1)}, u32[]{:S(2)}, u32[]{:S(2)}) collective-permute-start(bf16[192,1280]{1,0:T(8,128)(2,1)S(1)} %fusion.55), channel_id=1, source_target_pairs={{0,8},{8,16},{16,24},{24,0},{1,9},{9,17},{17,25},{25,1},{2,10},{10... | collective-permute-start | bytes 1474568 | tf_op jit(solution)/shard_map/ppermute | solution.py:25
  976.8 27.9 %collective-permute-start.38 = (bf16[160,2560]{1,0:T(8,128)(2,1)S(1)}, bf16[160,2560]{1,0:T(8,128)(2,1)S(1)}, u32[]{:S(2)}, u32[]{:S(2)}) collective-permute-start(bf16[160,2560]{1,0:T(8,128)(2,1)S(1)} %fusion.51), channel_id=1, source_target_pairs={{0,8},{8,16},{16,24},{24,0},{1,9},{9,17},{17,25},{25,1},{2,10},{10... | collective-permute-start | bytes 2457608 | tf_op jit(solution)/shard_map/ppermute | solution.py:25
  987.3 28.0 %collective-permute-start.36 = (bf16[192,1280]{1,0:T(8,128)(2,1)S(1)}, bf16[192,1280]{1,0:T(8,128)(2,1)S(1)}, u32[]{:S(2)}, u32[]{:S(2)}) collective-permute-start(bf16[192,1280]{1,0:T(8,128)(2,1)S(1)} %fusion.56), channel_id=1, source_target_pairs={{0,8},{8,16},{16,24},{24,0},{1,9},{9,17},{17,25},{25,1},{2,10},{10... | collective-permute-start | bytes 1474568 | tf_op jit(solution)/shard_map/ppermute | solution.py:25
  1004.9 27.4 %collective-permute-start.39 = (bf16[160,2560]{1,0:T(8,128)(2,1)S(1)}, bf16[160,2560]{1,0:T(8,128)(2,1)S(1)}, u32[]{:S(2)}, u32[]{:S(2)}) collective-permute-start(bf16[160,2560]{1,0:T(8,128)(2,1)S(1)} %fusion.52), channel_id=1, source_target_pairs={{0,8},{8,16},{16,24},{24,0},{1,9},{9,17},{17,25},{25,1},{2,10},{10... | collective-permute-start | bytes 2457608 | tf_op jit(solution)/shard_map/ppermute | solution.py:25
  (118 other events, 899.1 us)
Sparse Core Ops, SparseCore 0:
  190.1 87.4 all-gather.2
  279.4 77.6 all-gather.4
  418.6 80.5 reduce-scatter.4
  502.1 77.6 reduce-scatter.6
  697.3 84.9 reduce-scatter.8
  785.3 127.4 reduce-scatter.10

commit v7 on v6

--- a/solution.py
+++ b/solution.py
@@ -504,6 +504,34 @@
     return result.reshape(inner, -1, size)
 
 
+def unpack_kernel(cuts, *refs):
+    parts, in_ref, out_ref = refs[:-2], refs[-2], refs[-1]
+    outer = parts[0].shape[0]
+    hidden = out_ref.shape[1] // outer
+    for part, (start, size) in zip(parts, cuts):
+        for k in range(outer):
+            at = slice(k * hidden + start, k * hidden + start + size)
+            in_ref[0, :, at] = part[k, :, :size].astype(F32)
+            in_ref[1, :, at] = part[k, :, size : 2 * size].astype(F32)
+            out_ref[:, at] = part[k, :, 2 * size :].astype(F32)
+
+
+def unpack(parts, cuts, hidden):
+    rows = parts[0].shape[1]
+    return pl.pallas_call(
+        functools.partial(unpack_kernel, cuts),
+        in_specs=[VMEM] * len(parts),
+        out_specs=[VMEM] * 2,
+        out_shape=[
+            jax.ShapeDtypeStruct((2, rows, hidden), F32),
+            jax.ShapeDtypeStruct((rows, hidden), F32),
+        ],
+        cost_estimate=pl.CostEstimate(
+            flops=0, bytes_accessed=18 * rows * hidden, transcendentals=0
+        ),
+    )(*parts)
+
+
 def gelu_tanh(values):
     return jax.nn.gelu(values, approximate=True)
 
@@ -561,6 +589,16 @@
         low = total.astype(BF16)
         moved = ring(low)
         total = part.astype(F32) + moved.astype(F32)
+    return total
+
+
+def direct_sum(parts, axis, peer):
+    count, at = lax.axis_size(axis), lax.axis_index(axis)
+    total = lax.dynamic_index_in_dim(parts, at, 0, False).astype(F32)
+    for k in range(1, count):
+        part = lax.dynamic_index_in_dim(parts, peer(at, k), 0, False)
+        moved = lax.ppermute(part, axis, [(j, peer(j, k)) for j in range(count)])
+        total = total + moved.astype(F32)
     return total
 
 
@@ -614,7 +652,6 @@
     count = outer * inner
     core, along = lax.axis_index("tensor"), lax.axis_index("o")
     tok_rows, width = inputs.shape
-    part_width = width // count
     hidden_half = ffw_out.shape[0]
     hidden_part = hidden_half // outer
     taps_count = conv_weight.shape[0]
@@ -783,9 +820,12 @@
     gate_rows = (
         grad_gate_weights.reshape(2, heads_half, count, block_size // count, block_size)
         .transpose(2, 0, 1, 3, 4)
-        .reshape(outer, inner, -1, width_half)
         .astype(BF16)
     )
+    gate_rows = gate_rows.reshape(outer, inner, -1, block_size).transpose(1, 0, 2, 3)
+    gate_part = direct_sum(gate_rows, "i", lambda j, k: j ^ k).astype(BF16)
+    gate_grad = direct_sum(gate_part, "o", lambda j, k: (j + k) % outer)
+    gate_grad = gate_grad.reshape(2, heads_half, block_size // count, block_size)
     grad_gate_bias = jnp.sum(delta_gates, axis=1, dtype=F32)
     delta_conv = delta_conv_direct + jnp.einsum(
         "gthc,ghbc->thb", delta_blocks, gate_weights, preferred_element_type=F32
@@ -793,20 +833,7 @@
     rim_delta = from_behind(delta_conv[:rim_rows], -1)
     rim_delta, result_parts = lax.optimization_barrier((rim_delta, result_parts))
     result_sum = ring_sum(result_parts)
-    ffw_in_grad = jnp.concatenate(
-        [
-            grad[:, :, : 2 * size].reshape(outer, part_width, 2, size)
-            for grad, (_, size) in zip(grads, cuts)
-        ],
-        axis=3,
-    )
-    ffw_in_grad = (
-        ffw_in_grad.transpose(2, 1, 0, 3).reshape(2, part_width, hidden_half).astype(F32)
-    )
-    ffw_out_grad = jnp.concatenate(
-        [grad[:, :, 2 * size :] for grad, (_, size) in zip(grads, cuts)], axis=2
-    )
-    ffw_out_grad = ffw_out_grad.transpose(0, 2, 1).reshape(hidden_half, part_width).astype(F32)
+    ffw_in_grad, ffw_out_grad = unpack(grads, cuts, hidden_half)
     padded_delta = jnp.concatenate([delta_conv, rim_delta], axis=0)
     next_marks = jnp.concatenate([seg_marks, marks_after], axis=0)
     delta_branch_x = jnp.zeros_like(delta_conv)
@@ -821,7 +848,7 @@
         conv_weight_rows.append(jnp.sum(delta_conv * shifted, axis=0))
     grad_conv_bias = jnp.sum(delta_conv, axis=0)
     delta_x_low = delta_branch_x.astype(BF16)
-    x_rows = grads_rows([[([normed_low], delta_x_low)]], gate_rows)
+    x_rows = grads_rows([[([normed_low], delta_x_low)]])
     grad_x_inner = sum_inner(x_rows)
     delta_part = mm_nt(delta_x_low, branch_x_full) + mm_nt(delta_y_low, branch_y_full)
     delta_normed = half_of(delta_part, core) + swap(
@@ -850,16 +877,11 @@
         grad_decay,
         grad_ffw_bias.reshape(-1),
     ]
-    grad_oy_inner, ffw_in_grad, ffw_out_grad = lax.optimization_barrier(
-        (grad_oy_inner, ffw_in_grad, ffw_out_grad)
-    )
     grad_oy = ring_sum(ring_order(grad_oy_inner))
     small = sum_over_all(jnp.concatenate(flat).reshape(-1, 128))
     result_half = residual + result_sum + out_bias[1]
     result = join_halves(result_half, swap(result_half), core)
-    grad_x_gate = ring_sum(ring_order(grad_x_inner))
-    grad_branch_x = grad_x_gate[:part_width]
-    gate_grad = grad_x_gate[part_width:].reshape(2, heads_half, block_size // count, block_size)
+    grad_branch_x = ring_sum(ring_order(grad_x_inner))
     small = small.reshape(-1)
     at = 0
     taken = []
@@ -885,7 +907,7 @@
         jnp.stack([grad_branch_x, grad_oy[:, width_half:]]),
         grad_oy[:, :width_half].T,
         ffw_in_grad,
-        ffw_out_grad,
+        ffw_out_grad.T,
         scales,
         branch_bias_grad,
         taps_grad,

time: 1050 us -> 1010 us (0.962)
  local copies, waits for them, and re-layouts: 100 us -> 62.8 us
  other arithmetic: 109 us -> 97.8 us
    ppermute x4, waiting for transfers between devices: 31.4 us -> 6.85 us  [sum_over_all(): lax.ppermute(value, DP, [(k, k ^ bit) for k in range(count)])]
    ppermute x0 -> x6, waiting for transfers between devices: none -> 24.1 us  [direct_sum(): moved = lax.ppermute(part, axis, [(j, peer(j, k)) for j in range(count)])]
    convert_element_type x4 -> x0, local copies, waits for them, and re-layouts: 18.2 us -> none  [the longest x2 13.1 us: per_device(): ffw_in_grad.transpose(2, 1, 0, 3).reshape(2, part_width, hidden_half)]
    ppermute x0 -> x6, starting transfers between devices: none -> 10.7 us  [direct_sum(): moved = lax.ppermute(part, axis, [(j, peer(j, k)) for j in range(count)])]
  transfers between devices with their start and end apart: 53 -> 59, of which waited for: 23 -> 27; matrix products, arithmetic and copies ran while one was open for 27% -> 24% of each run, Pallas kernels for 9% -> 10%
where the time goes in v7:
time: 1010 us; the launch traced here: 999 us
  waiting for transfers between devices  352 us (35%)
  Pallas kernels  283 us (28%)
  matrix products  139 us (14%)
  other arithmetic  97.8 us (10%)
  local copies, waits for them, and re-layouts  62.8 us (6%)
  starting transfers between devices  48.2 us (5%)
  between operations  16.8 us (2%)
    ppermute x18, waiting for transfers between devices, ring(): lax.ppermute(value, 'o', [(k, (k + 1) % count) for k in range(count)])  299 us
    pallas_call x1, Pallas kernels, gather_weights(): pl.pallas_call(functools.partial(gather_kernel, outer, inner, groups, cut...  175 us
    dot_general x38, matrix products, dot(): lax.dot_general(a, b, ((contract[0], contract[1]), ((), ())), preferred_e...  132 us
    pallas_call x4, Pallas kernels, grads_rows(): pl.pallas_call(functools.partial(grads_kernel, plan, added), grid=(outer,...  62.7 us
    ppermute x6, waiting for transfers between devices, direct_sum(): moved = lax.ppermute(part, axis, [(j, peer(j, k)) for j in range(count)])  24.1 us
    pallas_call x2, Pallas kernels, entering(): pl.pallas_call(functools.partial(enter_kernel, outer, inner, reverse), in...  21.5 us
    unnamed x280, local copies, waits for them, and re-layouts  20.4 us
  transfers between devices with their start and end apart: 59, of which 27 were waited for; matrix products, arithmetic and copies ran while one was open for 24% of the time, Pallas kernels for 10%

profile of v7, /device:TPU:0, one launch (start us, length us, event | category | flops | bytes accessed | tf_op | source)
XLA Modules:
  0.0 999.0 jit_solution(10857456477327897485)
XLA Ops:
  14.4 175.4 %shard_map.271 = (bf16[4,4,160,1280]{3,2,1,0:T(8,128)(2,1)}, bf16[4,4,160,1280]{3,2,1,0:T(8,128)(2,1)}, bf16[4,4,160,1280]{3,2,1,0:T(8,128)(2,1)}, bf16[4,160,15...) custom-call(bf16[160,1280]{1,0:T(8,128)(2,1)} %get-tuple-element.201, ...), custom_call_target="tpu_custom_call" | custom-call | tf_op jit(solution)/shard_map/pallas_call | solution.py:420
  195.9 17.1 %collective-permute-done.refs_15_ = bf16[192,2560]{1,0:T(8,128)(2,1)} collective-permute-done((bf16[192,2560]{1,0:T(8,128)(2,1)S(1)}, bf16[192,2560]{1,0:T(8,128)(2,1)}, u32[]{:S(2)}, u32[]{:S(2)}) %collective-permute-start) | collective-permute-done | bytes 983072 | tf_op jit(solution)/shard_map/ppermute | solution.py:25
  216.6 7.0 convolution_add_fusion.9.branch_ref
  223.6 10.5 %shard_map.272 = (bf16[384,1280]{1,0:T(8,128)(2,1)}, f32[384,1280]{1,0:T(8,128)}, f32[384,1280]{1,0:T(8,128)}, f32[384,1280]{1,0:T(8,128)}, f32[384,1280]{1,0:T(8,128)}, /*index=5*/f32[2,1280]{1,0:T(2,128)}) custom-call(f32[400,1280]{1,0:T(8,128)} %convolution_add_fusion.9.branch_ref, f32[384,8]{1,0:T(8,128)} %copy.68.mask_ref, f32[4,1280]{1,0:T(4,128)} %taps_ref.1, ...), custom_call_target="tpu_custom_call" | custom-call | flops 503316480 | bytes 10813440 | tf_op jit(solution)/shard_map/pallas_call | solution.py:131
  234.1 12.1 %shard_map.273 = f32[1,1280]{1,0:T(1,128)} custom-call(f32[2,1280]{1,0:T(2,128)} %get-tuple-element.73.ends_ref), custom_call_target="tpu_custom_call" | custom-call | tf_op jit(solution)/shard_map/pallas_call | solution.py:204
  247.0 8.1 multiply_convert_fusion.2
  255.1 5.3 fusion.192
  274.5 18.0 %collective-permute-done.13.refs_21_ = bf16[192,2560]{1,0:T(8,128)(2,1)S(1)} collective-permute-done((bf16[192,2560]{1,0:T(8,128)(2,1)}, bf16[192,2560]{1,0:T(8,128)(2,1)S(1)}, u32[]{:S(2)}, u32[]{:S(2)}) %collective-permute-start.13) | collective-permute-done | bytes 983072 | tf_op jit(solution)/shard_map/ppermute | solution.py:25
  292.6 20.4 %collective-permute-done.5.refs_3_ = bf16[192,2560]{1,0:T(8,128)(2,1)S(1)} collective-permute-done((bf16[192,2560]{1,0:T(8,128)(2,1)S(1)}, bf16[192,2560]{1,0:T(8,128)(2,1)S(1)}, u32[]{:S(2)}, u32[]{:S(2)}) %collective-permute-start.5) | collective-permute-done | bytes 983072 | tf_op jit(solution)/shard_map/ppermute | solution.py:25
  314.0 24.0 %collective-permute-done.8.refs_6_ = bf16[192,2560]{1,0:T(8,128)(2,1)S(1)} collective-permute-done((bf16[192,2560]{1,0:T(8,128)(2,1)S(1)}, bf16[192,2560]{1,0:T(8,128)(2,1)S(1)}, u32[]{:S(2)}, u32[]{:S(2)}) %collective-permute-start.8) | collective-permute-done | bytes 983072 | tf_op jit(solution)/shard_map/ppermute | solution.py:25
  340.0 22.3 %collective-permute-done.11.refs_9_ = bf16[192,2560]{1,0:T(8,128)(2,1)S(1)} collective-permute-done((bf16[192,2560]{1,0:T(8,128)(2,1)S(1)}, bf16[192,2560]{1,0:T(8,128)(2,1)S(1)}, u32[]{:S(2)}, u32[]{:S(2)}) %collective-permute-start.11) | collective-permute-done | bytes 983072 | tf_op jit(solution)/shard_map/ppermute | solution.py:25
  367.4 5.4 convolution_add_fusion.11
  396.2 22.3 %shard_map.274 = bf16[4,4,160,1536]{3,2,1,0:T(8,128)(2,1)} custom-call(bf16[192,2560]{1,0:T(8,128)(2,1)} %copy-done.21, bf16[192,2560]{1,0:T(8,128)(2,1)} %copy-done.65, bf16[384,1024]{1,0:T(8,128)(2,1)} %pad_maximum_fusion.9.refs_2_, bf16[192,2560]{1,0:T(8,128)(2,1)} %copy-done.56, bf16[192,2560]{1,0:T(8,128)(2,1)} %copy-done.60, ...), custom_call_target="tpu_custom_call" | custom-call | flops 12079595520 | bytes 20447232 | tf_op jit(solution)/shard_map/pallas_call | solution.py:492
  419.1 5.2 convolution_add_fusion.15
  425.4 4.1 fusion.126
  440.7 4.1 fusion.58
  444.9 4.6 convolution_add_fusion.6
  450.6 4.3 convolution_add_fusion.17
  457.6 4.1 fusion.60
  461.7 4.6 convolution_add_fusion.7
  473.9 4.1 fusion.65
  479.3 21.8 %shard_map.277 = bf16[4,4,160,1344]{3,2,1,0:T(8,128)(2,1)} custom-call(bf16[192,2560]{1,0:T(8,128)(2,1)} %copy-done.21, bf16[192,2560]{1,0:T(8,128)(2,1)} %copy-done.65, bf16[384,896]{1,0:T(8,128)(2,1)} %pad_maximum_fusion.13.refs_2_, bf16[192,2560]{1,0:T(8,128)(2,1)} %copy-done.56, bf16[192,2560]{1,0:T(8,128)(2,1)} %copy-done.60, ...), custom_call_target="tpu_custom_call" | custom-call | flops 10569646080 | bytes 18874368 | tf_op jit(solution)/shard_map/pallas_call | solution.py:492
  502.2 5.7 convolution_add_fusion.8
  509.1 3.3 fusion.150
  512.5 3.1 fusion.152
  526.5 17.6 %collective-permute-done.19 = bf16[192,2560]{1,0:T(8,128)(2,1)S(1)} collective-permute-done((bf16[192,2560]{1,0:T(8,128)(2,1)}, bf16[192,2560]{1,0:T(8,128)(2,1)S(1)}, u32[]{:S(2)}, u32[]{:S(2)}) %collective-permute-start.19) | collective-permute-done | bytes 983072 | tf_op jit(solution)/shard_map/ppermute | solution.py:25
  549.3 22.5 %collective-permute-done.20 = bf16[192,2560]{1,0:T(8,128)(2,1)S(1)} collective-permute-done((bf16[192,2560]{1,0:T(8,128)(2,1)S(1)}, bf16[192,2560]{1,0:T(8,128)(2,1)S(1)}, u32[]{:S(2)}, u32[]{:S(2)}) %collective-permute-start.20) | collective-permute-done | bytes 983072 | tf_op jit(solution)/shard_map/ppermute | solution.py:25
  576.3 22.4 %collective-permute-done.21 = bf16[192,2560]{1,0:T(8,128)(2,1)S(1)} collective-permute-done((bf16[192,2560]{1,0:T(8,128)(2,1)S(1)}, bf16[192,2560]{1,0:T(8,128)(2,1)S(1)}, u32[]{:S(2)}, u32[]{:S(2)}) %collective-permute-start.21) | collective-permute-done | bytes 983072 | tf_op jit(solution)/shard_map/ppermute | solution.py:25
  611.6 8.3 convert_reduce_fusion.2
  619.9 7.1 shard_map.275
  628.4 9.3 shard_map.276
  638.5 7.2 multiply_reduce_fusion
  656.0 4.0 fusion.53
  660.0 2.9 copy.82
  663.0 6.0 fusion.36
  674.7 3.2 convert_reduce_fusion.3
  677.9 7.3 shard_map.278
  685.2 2.9 pad_maximum_fusion.4.refs_0_
  688.1 11.3 %shard_map.279 = bf16[4,4,160,2560]{3,2,1,0:T(8,128)(2,1)} custom-call(bf16[384,2560]{1,0:T(8,128)(2,1)} %pad_maximum_fusion.4.refs_0_, bf16[384,1280]{1,0:T(8,128)(2,1)} %copy-done.53, bf16[384,2560]{1,0:T(8,128)(2,1)} %slice.295.refs_0_.refs_2_, bf16[384,1280]{1,0:T(8,128)(2,1)} %get-tuple-element.142.refs_3_), custom_call_target="tpu_custom_call" | custom-call | flops 5033164800 | bytes 17039360 | tf_op jit(solution)/shard_map/pallas_call | solution.py:492
  705.0 5.7 fusion.193
  710.8 5.1 convolution_add_fusion.4
  722.0 4.4 all-to-all-start
  731.5 3.1 fusion.14
  734.8 11.3 %collective-permute-done.28 = bf16[192,2560]{1,0:T(8,128)(2,1)} collective-permute-done((bf16[192,2560]{1,0:T(8,128)(2,1)}, bf16[192,2560]{1,0:T(8,128)(2,1)}, u32[]{:S(2)}, u32[]{:S(2)}) %collective-permute-start.28) | collective-permute-done | bytes 983072 | tf_op jit(solution)/shard_map/ppermute | solution.py:25
  749.2 47.9 %collective-permute-done.29 = bf16[192,2560]{1,0:T(8,128)(2,1)} collective-permute-done((bf16[192,2560]{1,0:T(8,128)(2,1)}, bf16[192,2560]{1,0:T(8,128)(2,1)}, u32[]{:S(2)}, u32[]{:S(2)}) %collective-permute-start.29) | collective-permute-done | bytes 983072 | tf_op jit(solution)/shard_map/ppermute | solution.py:25
  797.1 2.9 add_convert_fusion
  800.0 9.8 collective-permute-start.30
  810.7 17.8 %all-to-all-done.refs_0_ = bf16[4,160,1536]{2,1,0:T(8,128)(2,1)} async-done(((bf16[4,160,1536]{2,1,0:T(8,128)(2,1)}), bf16[4,160,1536]{2,1,0:T(8,128)(2,1)}, u32[]{:S(2)}, u32[]{:S(2)}) %all-to-all-start) | async-done | bytes 1966112 | tf_op jit(solution)/shard_map/all_to_all | solution.py:614
  828.5 4.7 all-to-all-start.1
  833.2 7.1 fusion.13
  843.0 3.7 collective-permute-start.46
  848.3 3.9 collective-permute-done.45
  852.1 14.1 %collective-permute-done.46 = bf16[4,160,256]{2,1,0:T(8,128)(2,1)S(1)} collective-permute-done((bf16[4,160,256]{2,1,0:T(8,128)(2,1)S(1)}, bf16[4,160,256]{2,1,0:T(8,128)(2,1)S(1)}, u32[]{:S(2)}, u32[]{:S(2)}) %collective-permute-start.46) | collective-permute-done | bytes 327712 | tf_op jit(solution)/shard_map/ppermute | solution.py:600
  866.3 3.8 collective-permute-done.47
  874.0 2.9 collective-permute-start.49
  884.1 5.3 collective-permute-done.44
  893.9 5.8 shard_map.280
  899.7 4.5 broadcast_select_fusion.1
  908.7 10.7 %collective-permute-done.34 = bf16[160,1280]{1,0:T(8,128)(2,1)S(1)} collective-permute-done((bf16[160,1280]{1,0:T(8,128)(2,1)S(1)}, bf16[160,1280]{1,0:T(8,128)(2,1)S(1)}, u32[]{:S(2)}, u32[]{:S(2)}) %collective-permute-start.34) | collective-permute-done | bytes 409632 | tf_op jit(solution)/shard_map/ppermute | solution.py:25
  919.6 17.4 %collective-permute-done.37 = bf16[160,2560]{1,0:T(8,128)(2,1)S(1)} collective-permute-done((bf16[160,2560]{1,0:T(8,128)(2,1)S(1)}, bf16[160,2560]{1,0:T(8,128)(2,1)S(1)}, u32[]{:S(2)}, u32[]{:S(2)}) %collective-permute-start.37) | collective-permute-done | bytes 819232 | tf_op jit(solution)/shard_map/ppermute | solution.py:25
  939.5 6.3 collective-permute-done.35
  946.0 17.4 %collective-permute-done.38 = bf16[160,2560]{1,0:T(8,128)(2,1)S(1)} collective-permute-done((bf16[160,2560]{1,0:T(8,128)(2,1)S(1)}, bf16[160,2560]{1,0:T(8,128)(2,1)S(1)}, u32[]{:S(2)}, u32[]{:S(2)}) %collective-permute-start.38) | collective-permute-done | bytes 819232 | tf_op jit(solution)/shard_map/ppermute | solution.py:25
  965.8 6.3 collective-permute-done.36
  972.2 17.0 %collective-permute-done.39 = bf16[160,2560]{1,0:T(8,128)(2,1)S(1)} collective-permute-done((bf16[160,2560]{1,0:T(8,128)(2,1)S(1)}, bf16[160,2560]{1,0:T(8,128)(2,1)S(1)}, u32[]{:S(2)}, u32[]{:S(2)}) %collective-permute-start.39) | collective-permute-done | bytes 819232 | tf_op jit(solution)/shard_map/ppermute | solution.py:25
  (549 shorter events, 194.1 us)
Async XLA Ops:
  7.2 256.4 %copy-start = (f32[2,3840]{1,0:T(2,128)S(1)}, f32[2,3840]{1,0:T(2,128)}, u32[]{:S(2)}) copy-start(f32[2,3840]{1,0:T(2,128)} %param.31) | copy-start | bytes 92164
  7.2 360.2 %all-gather.3.cloned.1.call-start = ((), (), s32[]{:S(2)}) async-start(), calls=%async_computation.6 | async-start | bytes 9830400 | tf_op jit(solution)/shard_map/all_gather | solution.py:618
  10.9 259.0 %copy-start.91 = (f32[2560]{0:T(1024)}, f32[2560]{0:T(1024)S(1)}, u32[]{:S(2)}) copy-start(f32[2560]{0:T(1024)S(1)} %get-tuple-element.133) | copy-start | bytes 30724
  189.9 229.2 %all-gather.5.cloned.1.call-start = ((), (), s32[]{:S(2)}) async-start(), calls=%async_computation.7 | async-start | bytes 9011200 | tf_op jit(solution)/shard_map/all_gather | solution.py:618
  192.1 20.9 %collective-permute-start = (bf16[192,2560]{1,0:T(8,128)(2,1)S(1)}, bf16[192,2560]{1,0:T(8,128)(2,1)}, u32[]{:S(2)}, u32[]{:S(2)}) collective-permute-start(bf16[192,2560]{1,0:T(8,128)(2,1)S(1)} %get-tuple-element.74.refs_12_), channel_id=1, source_target_pairs={{0,8},{8,16},{16,24},{24,0},{1,9},{9,17},{17,25},{25,1},{2,10},{10... | collective-permute-start | bytes 2949128 | tf_op jit(solution)/shard_map/ppermute | solution.py:25
  213.0 33.9 %collective-permute-start.1 = (bf16[192,2560]{1,0:T(8,128)(2,1)}, bf16[192,2560]{1,0:T(8,128)(2,1)}, u32[]{:S(2)}, u32[]{:S(2)}) collective-permute-start(bf16[192,2560]{1,0:T(8,128)(2,1)} %collective-permute-done.refs_15_), channel_id=1, source_target_pairs={{0,8},{8,16},{16,24},{24,0},{1,9},{9,17},{17,25},{25,1},{2,10},{10... | collective-permute-start | bytes 2949128 | tf_op jit(solution)/shard_map/ppermute | solution.py:25
  263.0 4.2 collective-permute-start.2
  263.0 8.3 collective-permute-start.3
  263.5 336.7 %reduce-scatter.5.cloned.1.call-start = ((), (), s32[]{:S(2)}) async-start(), calls=%async_computation.8 | async-start | bytes 9830400 | tf_op jit(solution)/shard_map/reduce_scatter | solution.py:622
  264.4 28.2 %collective-permute-start.7 = (bf16[192,2560]{1,0:T(8,128)(2,1)}, bf16[192,2560]{1,0:T(8,128)(2,1)S(1)}, u32[]{:S(2)}, u32[]{:S(2)}) collective-permute-start(bf16[192,2560]{1,0:T(8,128)(2,1)} %collective-permute-done.refs_15_), channel_id=1, source_target_pairs={{0,1},{1,0},{2,3},{3,2},{4,5},{5,4},{6,7},{7,6},{8,9},{9,8},{10,11... | collective-permute-start | bytes 2949128 | tf_op jit(solution)/shard_map/ppermute | solution.py:20
  265.8 26.7 %collective-permute-start.13 = (bf16[192,2560]{1,0:T(8,128)(2,1)}, bf16[192,2560]{1,0:T(8,128)(2,1)S(1)}, u32[]{:S(2)}, u32[]{:S(2)}) collective-permute-start(bf16[192,2560]{1,0:T(8,128)(2,1)} %collective-permute-done.1.refs_18_), channel_id=1, source_target_pairs={{0,8},{8,16},{16,24},{24,0},{1,9},{9,17},{17,25},{25,1},{2,10},{10... | collective-permute-start | bytes 2949128 | tf_op jit(solution)/shard_map/ppermute | solution.py:25
  270.2 119.6 %copy-start.21 = (bf16[192,2560]{1,0:T(8,128)(2,1)}, bf16[192,2560]{1,0:T(8,128)(2,1)S(1)}, u32[]{:S(2)}) copy-start(bf16[192,2560]{1,0:T(8,128)(2,1)S(1)} %multiply_convert_fusion.1.refs_0_) | copy-start | bytes 2949124
  270.2 42.8 %collective-permute-start.5 = (bf16[192,2560]{1,0:T(8,128)(2,1)S(1)}, bf16[192,2560]{1,0:T(8,128)(2,1)S(1)}, u32[]{:S(2)}, u32[]{:S(2)}) collective-permute-start(bf16[192,2560]{1,0:T(8,128)(2,1)S(1)} %multiply_convert_fusion.1.refs_0_), channel_id=1, source_target_pairs={{0,8},{8,16},{16,24},{24,0},{1,9},{9,17},{17,25},{25,1},{2,10},{10... | collective-permute-start | bytes 2949128 | tf_op jit(solution)/shard_map/ppermute | solution.py:25
  272.6 40.6 %collective-permute-start.10 = (bf16[192,2560]{1,0:T(8,128)(2,1)}, bf16[192,2560]{1,0:T(8,128)(2,1)S(1)}, u32[]{:S(2)}, u32[]{:S(2)}) collective-permute-start(bf16[192,2560]{1,0:T(8,128)(2,1)} %collective-permute-done.1.refs_18_), channel_id=1, source_target_pairs={{0,1},{1,0},{2,3},{3,2},{4,5},{5,4},{6,7},{7,6},{8,9},{9,8},{10,11... | collective-permute-start | bytes 2949128 | tf_op jit(solution)/shard_map/ppermute | solution.py:20
  292.5 20.8 %collective-permute-start.14 = (bf16[192,2560]{1,0:T(8,128)(2,1)S(1)}, bf16[192,2560]{1,0:T(8,128)(2,1)S(1)}, u32[]{:S(2)}, u32[]{:S(2)}) collective-permute-start(bf16[192,2560]{1,0:T(8,128)(2,1)S(1)} %collective-permute-done.13.refs_21_), channel_id=1, source_target_pairs={{0,1},{1,0},{2,3},{3,2},{4,5},{5,4},{6,7},{7,6},{8,9},{9,8},{10,11... | collective-permute-start | bytes 2949128 | tf_op jit(solution)/shard_map/ppermute | solution.py:20
  313.0 25.0 %collective-permute-start.8 = (bf16[192,2560]{1,0:T(8,128)(2,1)S(1)}, bf16[192,2560]{1,0:T(8,128)(2,1)S(1)}, u32[]{:S(2)}, u32[]{:S(2)}) collective-permute-start(bf16[192,2560]{1,0:T(8,128)(2,1)S(1)} %collective-permute-done.5.refs_3_), channel_id=1, source_target_pairs={{0,8},{8,16},{16,24},{24,0},{1,9},{9,17},{17,25},{25,1},{2,10},{10... | collective-permute-start | bytes 2949128 | tf_op jit(solution)/shard_map/ppermute | solution.py:25
  313.1 25.2 %collective-permute-start.4 = (bf16[192,2560]{1,0:T(8,128)(2,1)S(1)}, bf16[192,2560]{1,0:T(8,128)(2,1)S(1)}, u32[]{:S(2)}, u32[]{:S(2)}) collective-permute-start(bf16[192,2560]{1,0:T(8,128)(2,1)S(1)} %multiply_convert_fusion.1.refs_0_), channel_id=1, source_target_pairs={{0,1},{1,0},{2,3},{3,2},{4,5},{5,4},{6,7},{7,6},{8,9},{9,8},{10,11... | collective-permute-start | bytes 2949128 | tf_op jit(solution)/shard_map/ppermute | solution.py:20
  313.4 48.9 %collective-permute-start.6 = (bf16[192,2560]{1,0:T(8,128)(2,1)S(1)}, bf16[192,2560]{1,0:T(8,128)(2,1)S(1)}, u32[]{:S(2)}, u32[]{:S(2)}) collective-permute-start(bf16[192,2560]{1,0:T(8,128)(2,1)S(1)} %collective-permute-done.5.refs_3_), channel_id=1, source_target_pairs={{0,1},{1,0},{2,3},{3,2},{4,5},{5,4},{6,7},{7,6},{8,9},{9,8},{10,11... | collective-permute-start | bytes 2949128 | tf_op jit(solution)/shard_map/ppermute | solution.py:20
  338.0 24.3 %collective-permute-start.11 = (bf16[192,2560]{1,0:T(8,128)(2,1)S(1)}, bf16[192,2560]{1,0:T(8,128)(2,1)S(1)}, u32[]{:S(2)}, u32[]{:S(2)}) collective-permute-start(bf16[192,2560]{1,0:T(8,128)(2,1)S(1)} %collective-permute-done.8.refs_6_), channel_id=1, source_target_pairs={{0,8},{8,16},{16,24},{24,0},{1,9},{9,17},{17,25},{25,1},{2,10},{10... | collective-permute-start | bytes 2949128 | tf_op jit(solution)/shard_map/ppermute | solution.py:25
  339.9 23.7 %collective-permute-start.9 = (bf16[192,2560]{1,0:T(8,128)(2,1)S(1)}, bf16[192,2560]{1,0:T(8,128)(2,1)S(1)}, u32[]{:S(2)}, u32[]{:S(2)}) collective-permute-start(bf16[192,2560]{1,0:T(8,128)(2,1)S(1)} %collective-permute-done.8.refs_6_), channel_id=1, source_target_pairs={{0,1},{1,0},{2,3},{3,2},{4,5},{5,4},{6,7},{7,6},{8,9},{9,8},{10,11... | collective-permute-start | bytes 2949128 | tf_op jit(solution)/shard_map/ppermute | solution.py:20
  362.3 2.6 collective-permute-start.12
  375.7 81.8 %copy-start.42 = (bf16[384,512]{1,0:T(8,128)(2,1)}, bf16[384,512]{1,0:T(8,128)(2,1)S(1)}, u32[]{:S(2)}) copy-start(bf16[384,512]{1,0:T(8,128)(2,1)S(1)} %get-tuple-element.165) | copy-start | bytes 1179652
  394.5 79.5 %copy-start.50 = (bf16[384,512]{1,0:T(8,128)(2,1)}, bf16[384,512]{1,0:T(8,128)(2,1)S(1)}, u32[]{:S(2)}) copy-start(bf16[384,512]{1,0:T(8,128)(2,1)S(1)} %get-tuple-element.170) | copy-start | bytes 1179652
  418.5 220.0 %reduce-scatter.7.cloned.1.call-start = ((), (), s32[]{:S(2)}) async-start(), calls=%async_computation.9 | async-start | bytes 9011200 | tf_op jit(solution)/shard_map/reduce_scatter | solution.py:622
  434.5 43.6 %collective-permute-start.18 = (bf16[192,2560]{1,0:T(8,128)(2,1)S(1)}, bf16[192,2560]{1,0:T(8,128)(2,1)S(1)}, u32[]{:S(2)}, u32[]{:S(2)}) collective-permute-start(bf16[192,2560]{1,0:T(8,128)(2,1)S(1)} %slice.718), channel_id=1, source_target_pairs={{0,1},{1,0},{2,3},{3,2},{4,5},{5,4},{6,7},{7,6},{8,9},{9,8},{10,11... | collective-permute-start | bytes 2949128 | tf_op jit(solution)/shard_map/ppermute | solution.py:20
  450.6 75.5 %collective-permute-start.17 = (bf16[192,2560]{1,0:T(8,128)(2,1)}, bf16[192,2560]{1,0:T(8,128)(2,1)}, u32[]{:S(2)}, u32[]{:S(2)}) collective-permute-start(bf16[192,2560]{1,0:T(8,128)(2,1)} %slice.719), channel_id=1, source_target_pairs={{0,1},{1,0},{2,3},{3,2},{4,5},{5,4},{6,7},{7,6},{8,9},{9,8},{10,11... | collective-permute-start | bytes 2949128 | tf_op jit(solution)/shard_map/ppermute | solution.py:20
  467.6 81.7 %collective-permute-start.16 = (bf16[192,2560]{1,0:T(8,128)(2,1)}, bf16[192,2560]{1,0:T(8,128)(2,1)}, u32[]{:S(2)}, u32[]{:S(2)}) collective-permute-start(bf16[192,2560]{1,0:T(8,128)(2,1)} %slice.720), channel_id=1, source_target_pairs={{0,1},{1,0},{2,3},{3,2},{4,5},{5,4},{6,7},{7,6},{8,9},{9,8},{10,11... | collective-permute-start | bytes 2949128 | tf_op jit(solution)/shard_map/ppermute | solution.py:20
  501.1 403.1 %reduce-scatter.9.cloned.1.call-start = ((), (), s32[]{:S(2)}) async-start(), calls=%async_computation.10 | async-start | bytes 8192000 | tf_op jit(solution)/shard_map/reduce_scatter | solution.py:622
  509.0 67.3 %collective-permute-start.15 = (bf16[192,2560]{1,0:T(8,128)(2,1)}, bf16[192,2560]{1,0:T(8,128)(2,1)S(1)}, u32[]{:S(2)}, u32[]{:S(2)}) collective-permute-start(bf16[192,2560]{1,0:T(8,128)(2,1)} %slice.721), channel_id=1, source_target_pairs={{0,1},{1,0},{2,3},{3,2},{4,5},{5,4},{6,7},{7,6},{8,9},{9,8},{10,11... | collective-permute-start | bytes 2949128 | tf_op jit(solution)/shard_map/ppermute | solution.py:20
  518.1 26.0 %collective-permute-start.19 = (bf16[192,2560]{1,0:T(8,128)(2,1)}, bf16[192,2560]{1,0:T(8,128)(2,1)S(1)}, u32[]{:S(2)}, u32[]{:S(2)}) collective-permute-start(bf16[192,2560]{1,0:T(8,128)(2,1)} %slice_add_fusion.4), channel_id=1, source_target_pairs={{0,8},{8,16},{16,24},{24,0},{1,9},{9,17},{17,25},{25,1},{2,10},{10... | collective-permute-start | bytes 2949128 | tf_op jit(solution)/shard_map/ppermute | solution.py:25
  521.8 23.9 %collective-permute-start.25 = (bf16[192,2560]{1,0:T(8,128)(2,1)}, bf16[192,2560]{1,0:T(8,128)(2,1)S(1)}, u32[]{:S(2)}, u32[]{:S(2)}) collective-permute-start(bf16[192,2560]{1,0:T(8,128)(2,1)} %slice.714), channel_id=1, source_target_pairs={{0,1},{1,0},{2,3},{3,2},{4,5},{5,4},{6,7},{7,6},{8,9},{9,8},{10,11... | collective-permute-start | bytes 2949128 | tf_op jit(solution)/shard_map/ppermute | solution.py:20
  526.1 21.1 %collective-permute-start.24 = (bf16[192,2560]{1,0:T(8,128)(2,1)S(1)}, bf16[192,2560]{1,0:T(8,128)(2,1)S(1)}, u32[]{:S(2)}, u32[]{:S(2)}) collective-permute-start(bf16[192,2560]{1,0:T(8,128)(2,1)S(1)} %slice.715), channel_id=1, source_target_pairs={{0,1},{1,0},{2,3},{3,2},{4,5},{5,4},{6,7},{7,6},{8,9},{9,8},{10,11... | collective-permute-start | bytes 2949128 | tf_op jit(solution)/shard_map/ppermute | solution.py:20
  544.1 30.7 %collective-permute-start.23 = (bf16[192,2560]{1,0:T(8,128)(2,1)S(1)}, bf16[192,2560]{1,0:T(8,128)(2,1)S(1)}, u32[]{:S(2)}, u32[]{:S(2)}) collective-permute-start(bf16[192,2560]{1,0:T(8,128)(2,1)S(1)} %slice.716), channel_id=1, source_target_pairs={{0,1},{1,0},{2,3},{3,2},{4,5},{5,4},{6,7},{7,6},{8,9},{9,8},{10,11... | collective-permute-start | bytes 2949128 | tf_op jit(solution)/shard_map/ppermute | solution.py:20
  545.7 26.0 %collective-permute-start.20 = (bf16[192,2560]{1,0:T(8,128)(2,1)S(1)}, bf16[192,2560]{1,0:T(8,128)(2,1)S(1)}, u32[]{:S(2)}, u32[]{:S(2)}) collective-permute-start(bf16[192,2560]{1,0:T(8,128)(2,1)S(1)} %fusion.46), channel_id=1, source_target_pairs={{0,8},{8,16},{16,24},{24,0},{1,9},{9,17},{17,25},{25,1},{2,10},{10... | collective-permute-start | bytes 2949128 | tf_op jit(solution)/shard_map/ppermute | solution.py:25
  547.2 26.3 %collective-permute-start.22 = (bf16[192,2560]{1,0:T(8,128)(2,1)S(1)}, bf16[192,2560]{1,0:T(8,128)(2,1)S(1)}, u32[]{:S(2)}, u32[]{:S(2)}) collective-permute-start(bf16[192,2560]{1,0:T(8,128)(2,1)S(1)} %slice.717), channel_id=1, source_target_pairs={{0,1},{1,0},{2,3},{3,2},{4,5},{5,4},{6,7},{7,6},{8,9},{9,8},{10,11... | collective-permute-start | bytes 2949128 | tf_op jit(solution)/shard_map/ppermute | solution.py:20
  573.3 25.3 %collective-permute-start.21 = (bf16[192,2560]{1,0:T(8,128)(2,1)S(1)}, bf16[192,2560]{1,0:T(8,128)(2,1)S(1)}, u32[]{:S(2)}, u32[]{:S(2)}) collective-permute-start(bf16[192,2560]{1,0:T(8,128)(2,1)S(1)} %fusion.48), channel_id=1, source_target_pairs={{0,8},{8,16},{16,24},{24,0},{1,9},{9,17},{17,25},{25,1},{2,10},{10... | collective-permute-start | bytes 2949128 | tf_op jit(solution)/shard_map/ppermute | solution.py:25
  604.3 4.5 collective-permute-start.26
  669.0 5.7 collective-permute-start.27
  685.2 220.2 %reduce-scatter.11.cloned.1.call-start = ((), (), s32[]{:S(2)}) async-start(), calls=%async_computation.11 | async-start | bytes 16384000 | tf_op jit(solution)/shard_map/reduce_scatter | solution.py:622
  716.9 14.5 %collective-permute-start.32 = (bf16[192,2560]{1,0:T(8,128)(2,1)}, bf16[192,2560]{1,0:T(8,128)(2,1)}, u32[]{:S(2)}, u32[]{:S(2)}) collective-permute-start(bf16[192,2560]{1,0:T(8,128)(2,1)} %dynamic-slice_convert_fusion), channel_id=1, source_target_pairs={{0,1},{1,0},{2,3},{3,2},{4,5},{5,4},{6,7},{7,6},{8,9},{9,8},{10,11... | collective-permute-start | bytes 2949128 | tf_op jit(solution)/shard_map/ppermute | solution.py:20
  719.2 26.8 %collective-permute-start.28 = (bf16[192,2560]{1,0:T(8,128)(2,1)}, bf16[192,2560]{1,0:T(8,128)(2,1)}, u32[]{:S(2)}, u32[]{:S(2)}) collective-permute-start(bf16[192,2560]{1,0:T(8,128)(2,1)} %slice_add_fusion.3), channel_id=1, source_target_pairs={{0,8},{8,16},{16,24},{24,0},{1,9},{9,17},{17,25},{25,1},{2,10},{10... | collective-permute-start | bytes 2949128 | tf_op jit(solution)/shard_map/ppermute | solution.py:25
  722.0 106.5 %all-to-all-start = ((bf16[4,160,1536]{2,1,0:T(8,128)(2,1)}), bf16[4,160,1536]{2,1,0:T(8,128)(2,1)}, u32[]{:S(2)}, u32[]{:S(2)}) async-start(bf16[4,160,1536]{2,1,0:T(8,128)(2,1)} %bitcast.191), calls=%async_computation.4 | async-start | bytes 3932160 | tf_op jit(solution)/shard_map/all_to_all | solution.py:614
  734.7 14.3 %collective-permute-start.40 = (f32[4,2560]{1,0:T(4,128)S(1)}, f32[4,2560]{1,0:T(4,128)S(1)}, u32[]{:S(2)}, u32[]{:S(2)}) collective-permute-start(f32[4,2560]{1,0:T(4,128)S(1)} %pad_maximum_fusion.18), channel_id=1, source_target_pairs={{0,1},{1,0},{2,3},{3,2},{4,5},{5,4},{6,7},{7,6},{8,9},{9,8},{10,11... | collective-permute-start | bytes 122888 | tf_op jit(solution)/shard_map/ppermute | solution.py:20
  748.4 48.6 %collective-permute-start.29 = (bf16[192,2560]{1,0:T(8,128)(2,1)}, bf16[192,2560]{1,0:T(8,128)(2,1)}, u32[]{:S(2)}, u32[]{:S(2)}) collective-permute-start(bf16[192,2560]{1,0:T(8,128)(2,1)} %add_convert_fusion.1), channel_id=1, source_target_pairs={{0,8},{8,16},{16,24},{24,0},{1,9},{9,17},{17,25},{25,1},{2,10},{10... | collective-permute-start | bytes 2949128 | tf_op jit(solution)/shard_map/ppermute | solution.py:25
  800.0 33.2 %collective-permute-start.30 = (bf16[192,2560]{1,0:T(8,128)(2,1)}, bf16[192,2560]{1,0:T(8,128)(2,1)}, u32[]{:S(2)}, u32[]{:S(2)}) collective-permute-start(bf16[192,2560]{1,0:T(8,128)(2,1)} %add_convert_fusion), channel_id=1, source_target_pairs={{0,8},{8,16},{16,24},{24,0},{1,9},{9,17},{17,25},{25,1},{2,10},{10... | collective-permute-start | bytes 2949128 | tf_op jit(solution)/shard_map/ppermute | solution.py:25
  809.9 36.8 %collective-permute-start.41 = (f32[240,128]{1,0:T(8,128)S(1)}, f32[240,128]{1,0:T(8,128)S(1)}, u32[]{:S(2)}, u32[]{:S(2)}) collective-permute-start(f32[240,128]{1,0:T(8,128)S(1)} %bitcast.202), channel_id=1, source_target_pairs={{0,2},{2,0},{4,6},{6,4},{8,10},{10,8},{12,14},{14,12},{16,18},{18,... | collective-permute-start | bytes 368648 | tf_op jit(solution)/shard_map/ppermute | solution.py:37
  828.5 65.4 %all-to-all-start.1 = ((bf16[4,160,1344]{2,1,0:T(8,128)(2,1)}), bf16[4,160,1344]{2,1,0:T(8,128)(2,1)}, u32[]{:S(2)}, u32[]{:S(2)}) async-start(bf16[4,160,1344]{2,1,0:T(8,128)(2,1)} %bitcast.194), calls=%async_computation.5 | async-start | bytes 3604480 | tf_op jit(solution)/shard_map/all_to_all | solution.py:614
  840.4 59.3 %collective-permute-start.33 = (f32[192,2560]{1,0:T(8,128)}, f32[192,2560]{1,0:T(8,128)}, u32[]{:S(2)}, u32[]{:S(2)}) collective-permute-start(f32[192,2560]{1,0:T(8,128)} %get-tuple-element.180), channel_id=1, source_target_pairs={{0,1},{1,0},{2,3},{3,2},{4,5},{5,4},{6,7},{7,6},{8,9},{9,8},{10,11... | collective-permute-start | bytes 5898248 | tf_op jit(solution)/shard_map/ppermute | solution.py:20
  841.3 10.8 %collective-permute-start.45 = (bf16[4,160,256]{2,1,0:T(8,128)(2,1)}, bf16[4,160,256]{2,1,0:T(8,128)(2,1)S(1)}, u32[]{:S(2)}, u32[]{:S(2)}) collective-permute-start(bf16[4,160,256]{2,1,0:T(8,128)(2,1)} %get-tuple-element.197), channel_id=1, source_target_pairs={{0,2},{2,0},{4,6},{6,4},{1,3},{3,1},{5,7},{7,5},{8,10},{10,8},{12,... | collective-permute-start | bytes 983048 | tf_op jit(solution)/shard_map/ppermute | solution.py:600
  843.0 23.3 %collective-permute-start.46 = (bf16[4,160,256]{2,1,0:T(8,128)(2,1)S(1)}, bf16[4,160,256]{2,1,0:T(8,128)(2,1)S(1)}, u32[]{:S(2)}, u32[]{:S(2)}) collective-permute-start(bf16[4,160,256]{2,1,0:T(8,128)(2,1)S(1)} %get-tuple-element.199), channel_id=1, source_target_pairs={{0,4},{2,6},{4,0},{6,2},{1,5},{3,7},{5,1},{7,3},{8,12},{10,14},{12... | collective-permute-start | bytes 983048 | tf_op jit(solution)/shard_map/ppermute | solution.py:600
  846.7 23.4 %collective-permute-start.47 = (bf16[4,160,256]{2,1,0:T(8,128)(2,1)S(1)}, bf16[4,160,256]{2,1,0:T(8,128)(2,1)}, u32[]{:S(2)}, u32[]{:S(2)}) collective-permute-start(bf16[4,160,256]{2,1,0:T(8,128)(2,1)S(1)} %get-tuple-element.198), channel_id=1, source_target_pairs={{0,6},{2,4},{4,2},{6,0},{1,7},{3,5},{5,3},{7,1},{8,14},{10,12},{12... | collective-permute-start | bytes 983048 | tf_op jit(solution)/shard_map/ppermute | solution.py:600
  846.7 24.6 %collective-permute-start.42 = (f32[240,128]{1,0:T(8,128)S(1)}, f32[240,128]{1,0:T(8,128)S(1)}, u32[]{:S(2)}, u32[]{:S(2)}) collective-permute-start(f32[240,128]{1,0:T(8,128)S(1)} %bitcast_add_fusion), channel_id=1, source_target_pairs={{0,4},{2,6},{4,0},{6,2},{8,12},{10,14},{12,8},{14,10},{16,20},{18,... | collective-permute-start | bytes 368648 | tf_op jit(solution)/shard_map/ppermute | solution.py:37
  871.3 9.4 collective-permute-start.43
  873.9 8.3 collective-permute-start.48
  874.0 8.2 collective-permute-start.49
  876.9 6.5 collective-permute-start.50
  880.7 8.7 collective-permute-start.44
  889.4 17.3 %collective-permute-start.31 = (f32[192,2560]{1,0:T(8,128)S(1)}, f32[192,2560]{1,0:T(8,128)}, u32[]{:S(2)}, u32[]{:S(2)}) collective-permute-start(f32[192,2560]{1,0:T(8,128)S(1)} %copy-done.15), channel_id=1, source_target_pairs={{0,1},{1,0},{2,3},{3,2},{4,5},{5,4},{6,7},{7,6},{8,9},{9,8},{10,11... | collective-permute-start | bytes 5898248 | tf_op jit(solution)/shard_map/ppermute | solution.py:20
  905.3 14.2 %collective-permute-start.34 = (bf16[160,1280]{1,0:T(8,128)(2,1)S(1)}, bf16[160,1280]{1,0:T(8,128)(2,1)S(1)}, u32[]{:S(2)}, u32[]{:S(2)}) collective-permute-start(bf16[160,1280]{1,0:T(8,128)(2,1)S(1)} %dynamic-slice_bitcast_fusion.1), channel_id=1, source_target_pairs={{0,8},{8,16},{16,24},{24,0},{1,9},{9,17},{17,25},{25,1},{2,10},{10... | collective-permute-start | bytes 1228808 | tf_op jit(solution)/shard_map/ppermute | solution.py:25
  906.6 30.4 %collective-permute-start.37 = (bf16[160,2560]{1,0:T(8,128)(2,1)S(1)}, bf16[160,2560]{1,0:T(8,128)(2,1)S(1)}, u32[]{:S(2)}, u32[]{:S(2)}) collective-permute-start(bf16[160,2560]{1,0:T(8,128)(2,1)S(1)} %dynamic-slice_bitcast_fusion), channel_id=1, source_target_pairs={{0,8},{8,16},{16,24},{24,0},{1,9},{9,17},{17,25},{25,1},{2,10},{10... | collective-permute-start | bytes 2457608 | tf_op jit(solution)/shard_map/ppermute | solution.py:25
  919.6 26.2 %collective-permute-start.35 = (bf16[160,1280]{1,0:T(8,128)(2,1)S(1)}, bf16[160,1280]{1,0:T(8,128)(2,1)S(1)}, u32[]{:S(2)}, u32[]{:S(2)}) collective-permute-start(bf16[160,1280]{1,0:T(8,128)(2,1)S(1)} %fusion.68), channel_id=1, source_target_pairs={{0,8},{8,16},{16,24},{24,0},{1,9},{9,17},{17,25},{25,1},{2,10},{10... | collective-permute-start | bytes 1228808 | tf_op jit(solution)/shard_map/ppermute | solution.py:25
  937.2 26.1 %collective-permute-start.38 = (bf16[160,2560]{1,0:T(8,128)(2,1)S(1)}, bf16[160,2560]{1,0:T(8,128)(2,1)S(1)}, u32[]{:S(2)}, u32[]{:S(2)}) collective-permute-start(bf16[160,2560]{1,0:T(8,128)(2,1)S(1)} %fusion.51), channel_id=1, source_target_pairs={{0,8},{8,16},{16,24},{24,0},{1,9},{9,17},{17,25},{25,1},{2,10},{10... | collective-permute-start | bytes 2457608 | tf_op jit(solution)/shard_map/ppermute | solution.py:25
  945.9 26.2 %collective-permute-start.36 = (bf16[160,1280]{1,0:T(8,128)(2,1)S(1)}, bf16[160,1280]{1,0:T(8,128)(2,1)S(1)}, u32[]{:S(2)}, u32[]{:S(2)}) collective-permute-start(bf16[160,1280]{1,0:T(8,128)(2,1)S(1)} %fusion.69), channel_id=1, source_target_pairs={{0,8},{8,16},{16,24},{24,0},{1,9},{9,17},{17,25},{25,1},{2,10},{10... | collective-permute-start | bytes 1228808 | tf_op jit(solution)/shard_map/ppermute | solution.py:25
  963.5 25.7 %collective-permute-start.39 = (bf16[160,2560]{1,0:T(8,128)(2,1)S(1)}, bf16[160,2560]{1,0:T(8,128)(2,1)S(1)}, u32[]{:S(2)}, u32[]{:S(2)}) collective-permute-start(bf16[160,2560]{1,0:T(8,128)(2,1)S(1)} %fusion.52), channel_id=1, source_target_pairs={{0,8},{8,16},{16,24},{24,0},{1,9},{9,17},{17,25},{25,1},{2,10},{10... | collective-permute-start | bytes 2457608 | tf_op jit(solution)/shard_map/ppermute | solution.py:25
  (126 other events, 1258.3 us)
Sparse Core Ops, SparseCore 0:
  190.0 87.4 all-gather.2
  279.4 77.6 all-gather.4
  418.6 80.5 reduce-scatter.4
  502.1 77.6 reduce-scatter.6
  685.3 73.8 reduce-scatter.8
  762.2 139.1 reduce-scatter.10

commit v8 on v7

--- a/solution.py
+++ b/solution.py
@@ -592,16 +592,6 @@
     return total
 
 
-def direct_sum(parts, axis, peer):
-    count, at = lax.axis_size(axis), lax.axis_index(axis)
-    total = lax.dynamic_index_in_dim(parts, at, 0, False).astype(F32)
-    for k in range(1, count):
-        part = lax.dynamic_index_in_dim(parts, peer(at, k), 0, False)
-        moved = lax.ppermute(part, axis, [(j, peer(j, k)) for j in range(count)])
-        total = total + moved.astype(F32)
-    return total
-
-
 def ring_order(parts):
     count, at = lax.axis_size("o"), lax.axis_index("o")
     return [
@@ -652,6 +642,7 @@
     count = outer * inner
     core, along = lax.axis_index("tensor"), lax.axis_index("o")
     tok_rows, width = inputs.shape
+    part_width = width // count
     hidden_half = ffw_out.shape[0]
     hidden_part = hidden_half // outer
     taps_count = conv_weight.shape[0]
@@ -820,12 +811,9 @@
     gate_rows = (
         grad_gate_weights.reshape(2, heads_half, count, block_size // count, block_size)
         .transpose(2, 0, 1, 3, 4)
+        .reshape(outer, inner, -1, width_half)
         .astype(BF16)
     )
-    gate_rows = gate_rows.reshape(outer, inner, -1, block_size).transpose(1, 0, 2, 3)
-    gate_part = direct_sum(gate_rows, "i", lambda j, k: j ^ k).astype(BF16)
-    gate_grad = direct_sum(gate_part, "o", lambda j, k: (j + k) % outer)
-    gate_grad = gate_grad.reshape(2, heads_half, block_size // count, block_size)
     grad_gate_bias = jnp.sum(delta_gates, axis=1, dtype=F32)
     delta_conv = delta_conv_direct + jnp.einsum(
         "gthc,ghbc->thb", delta_blocks, gate_weights, preferred_element_type=F32
@@ -848,7 +836,7 @@
         conv_weight_rows.append(jnp.sum(delta_conv * shifted, axis=0))
     grad_conv_bias = jnp.sum(delta_conv, axis=0)
     delta_x_low = delta_branch_x.astype(BF16)
-    x_rows = grads_rows([[([normed_low], delta_x_low)]])
+    x_rows = grads_rows([[([normed_low], delta_x_low)]], gate_rows)
     grad_x_inner = sum_inner(x_rows)
     delta_part = mm_nt(delta_x_low, branch_x_full) + mm_nt(delta_y_low, branch_y_full)
     delta_normed = half_of(delta_part, core) + swap(
@@ -881,7 +869,9 @@
     small = sum_over_all(jnp.concatenate(flat).reshape(-1, 128))
     result_half = residual + result_sum + out_bias[1]
     result = join_halves(result_half, swap(result_half), core)
-    grad_branch_x = ring_sum(ring_order(grad_x_inner))
+    grad_x_gate = ring_sum(ring_order(grad_x_inner))
+    grad_branch_x = grad_x_gate[:part_width]
+    gate_grad = grad_x_gate[part_width:].reshape(2, heads_half, block_size // count, block_size)
     small = small.reshape(-1)
     at = 0
     taken = []

time: 1010 us -> 1020 us (level)
    ppermute x4, waiting for transfers between devices: 6.85 us -> 31.8 us  [sum_over_all(): lax.ppermute(value, DP, [(k, k ^ bit) for k in range(count)])]
    ppermute x6 -> x0, waiting for transfers between devices: 24.1 us -> none  [direct_sum(): moved = lax.ppermute(part, axis, [(j, peer(j, k)) for j in range(count)])]
    ppermute x6 -> x0, starting transfers between devices: 10.7 us -> none  [direct_sum(): moved = lax.ppermute(part, axis, [(j, peer(j, k)) for j in range(count)])]
  transfers between devices with their start and end apart: 59 -> 53, of which waited for: 27 -> 25; matrix products, arithmetic and copies ran while one was open for 24% -> 25% of each run, Pallas kernels for 10% -> 10%
where the time goes in v8:
time: 1020 us; the launch traced here: 1010 us
  waiting for transfers between devices  350 us (34%)
  Pallas kernels  284 us (28%)
  matrix products  136 us (13%)
  other arithmetic  107 us (10%)
  local copies, waits for them, and re-layouts  70.9 us (7%)
  starting transfers between devices  47.6 us (5%)
  between operations  16.4 us (2%)
    ppermute x18, waiting for transfers between devices, ring(): lax.ppermute(value, 'o', [(k, (k + 1) % count) for k in range(count)])  298 us
    pallas_call x1, Pallas kernels, gather_weights(): pl.pallas_call(functools.partial(gather_kernel, outer, inner, groups, cut...  175 us
    dot_general x38, matrix products, dot(): lax.dot_general(a, b, ((contract[0], contract[1]), ((), ())), preferred_e...  131 us
    pallas_call x4, Pallas kernels, grads_rows(): pl.pallas_call(functools.partial(grads_kernel, plan, added), grid=(outer,...  63.5 us
    ppermute x4, waiting for transfers between devices, sum_over_all(): lax.ppermute(value, DP, [(k, k ^ bit) for k in range(count)])  31.8 us
    ppermute x18, starting transfers between devices, ring(): lax.ppermute(value, 'o', [(k, (k + 1) % count) for k in range(count)])  25.3 us
    pallas_call x2, Pallas kernels, entering(): pl.pallas_call(functools.partial(enter_kernel, outer, inner, reverse), in...  21.5 us
  transfers between devices with their start and end apart: 53, of which 25 were waited for; matrix products, arithmetic and copies ran while one was open for 25% of the time, Pallas kernels for 10%

profile of v8, /device:TPU:0, one launch (start us, length us, event | category | flops | bytes accessed | tf_op | source)
XLA Modules:
  0.0 1012.3 jit_solution(6545099032452233412)
XLA Ops:
  14.4 175.4 %shard_map.271 = (bf16[4,4,160,1280]{3,2,1,0:T(8,128)(2,1)}, bf16[4,4,160,1280]{3,2,1,0:T(8,128)(2,1)}, bf16[4,4,160,1280]{3,2,1,0:T(8,128)(2,1)}, bf16[4,160,15...) custom-call(bf16[160,1280]{1,0:T(8,128)(2,1)} %get-tuple-element.198, ...), custom_call_target="tpu_custom_call" | custom-call | tf_op jit(solution)/shard_map/pallas_call | solution.py:420
  195.9 17.1 %collective-permute-done.refs_15_ = bf16[192,2560]{1,0:T(8,128)(2,1)} collective-permute-done((bf16[192,2560]{1,0:T(8,128)(2,1)S(1)}, bf16[192,2560]{1,0:T(8,128)(2,1)}, u32[]{:S(2)}, u32[]{:S(2)}) %collective-permute-start) | collective-permute-done | bytes 983072 | tf_op jit(solution)/shard_map/ppermute | solution.py:25
  216.6 7.0 convolution_add_fusion.9.branch_ref
  223.6 10.5 %shard_map.272 = (bf16[384,1280]{1,0:T(8,128)(2,1)}, f32[384,1280]{1,0:T(8,128)}, f32[384,1280]{1,0:T(8,128)}, f32[384,1280]{1,0:T(8,128)}, f32[384,1280]{1,0:T(8,128)}, /*index=5*/f32[2,1280]{1,0:T(2,128)}) custom-call(f32[400,1280]{1,0:T(8,128)} %convolution_add_fusion.9.branch_ref, f32[384,8]{1,0:T(8,128)} %copy.69.mask_ref, f32[4,1280]{1,0:T(4,128)} %taps_ref.1, ...), custom_call_target="tpu_custom_call" | custom-call | flops 503316480 | bytes 10813440 | tf_op jit(solution)/shard_map/pallas_call | solution.py:131
  234.1 12.2 %shard_map.273 = f32[1,1280]{1,0:T(1,128)} custom-call(f32[2,1280]{1,0:T(2,128)} %get-tuple-element.73.ends_ref), custom_call_target="tpu_custom_call" | custom-call | tf_op jit(solution)/shard_map/pallas_call | solution.py:204
  247.0 8.1 multiply_convert_fusion.2
  255.1 5.3 fusion.185
  274.5 18.0 %collective-permute-done.13.refs_21_ = bf16[192,2560]{1,0:T(8,128)(2,1)S(1)} collective-permute-done((bf16[192,2560]{1,0:T(8,128)(2,1)}, bf16[192,2560]{1,0:T(8,128)(2,1)S(1)}, u32[]{:S(2)}, u32[]{:S(2)}) %collective-permute-start.13) | collective-permute-done | bytes 983072 | tf_op jit(solution)/shard_map/ppermute | solution.py:25
  292.6 20.4 %collective-permute-done.5.refs_3_ = bf16[192,2560]{1,0:T(8,128)(2,1)S(1)} collective-permute-done((bf16[192,2560]{1,0:T(8,128)(2,1)S(1)}, bf16[192,2560]{1,0:T(8,128)(2,1)S(1)}, u32[]{:S(2)}, u32[]{:S(2)}) %collective-permute-start.5) | collective-permute-done | bytes 983072 | tf_op jit(solution)/shard_map/ppermute | solution.py:25
  314.0 24.0 %collective-permute-done.8.refs_6_ = bf16[192,2560]{1,0:T(8,128)(2,1)S(1)} collective-permute-done((bf16[192,2560]{1,0:T(8,128)(2,1)S(1)}, bf16[192,2560]{1,0:T(8,128)(2,1)S(1)}, u32[]{:S(2)}, u32[]{:S(2)}) %collective-permute-start.8) | collective-permute-done | bytes 983072 | tf_op jit(solution)/shard_map/ppermute | solution.py:25
  340.3 22.3 %collective-permute-done.11.refs_9_ = bf16[192,2560]{1,0:T(8,128)(2,1)S(1)} collective-permute-done((bf16[192,2560]{1,0:T(8,128)(2,1)S(1)}, bf16[192,2560]{1,0:T(8,128)(2,1)S(1)}, u32[]{:S(2)}, u32[]{:S(2)}) %collective-permute-start.11) | collective-permute-done | bytes 983072 | tf_op jit(solution)/shard_map/ppermute | solution.py:25
  367.7 5.4 convolution_add_fusion.11
  396.6 22.3 %shard_map.274 = bf16[4,4,160,1536]{3,2,1,0:T(8,128)(2,1)} custom-call(bf16[192,2560]{1,0:T(8,128)(2,1)} %copy-done.19, bf16[192,2560]{1,0:T(8,128)(2,1)} %copy-done.61, bf16[384,1024]{1,0:T(8,128)(2,1)} %pad_maximum_fusion.9.refs_2_, bf16[192,2560]{1,0:T(8,128)(2,1)} %copy-done.49, bf16[192,2560]{1,0:T(8,128)(2,1)} %copy-done.53, ...), custom_call_target="tpu_custom_call" | custom-call | flops 12079595520 | bytes 20447232 | tf_op jit(solution)/shard_map/pallas_call | solution.py:492
  419.2 5.2 convolution_add_fusion.15
  425.4 4.2 fusion.125
  440.9 4.1 fusion.60
  445.0 4.6 convolution_add_fusion.6
  450.9 4.2 convolution_add_fusion.17
  457.8 4.2 fusion.62
  461.9 4.6 convolution_add_fusion.7
  474.2 4.1 fusion.67
  479.5 21.9 %shard_map.277 = bf16[4,4,160,1344]{3,2,1,0:T(8,128)(2,1)} custom-call(bf16[192,2560]{1,0:T(8,128)(2,1)} %copy-done.19, bf16[192,2560]{1,0:T(8,128)(2,1)} %copy-done.61, bf16[384,896]{1,0:T(8,128)(2,1)} %pad_maximum_fusion.13.refs_2_, bf16[192,2560]{1,0:T(8,128)(2,1)} %copy-done.49, bf16[192,2560]{1,0:T(8,128)(2,1)} %copy-done.53, ...), custom_call_target="tpu_custom_call" | custom-call | flops 10569646080 | bytes 18874368 | tf_op jit(solution)/shard_map/pallas_call | solution.py:492
  502.5 5.7 convolution_add_fusion.8
  509.4 3.3 fusion.146
  512.8 3.1 fusion.148
  526.8 17.7 %collective-permute-done.19 = bf16[192,2560]{1,0:T(8,128)(2,1)S(1)} collective-permute-done((bf16[192,2560]{1,0:T(8,128)(2,1)}, bf16[192,2560]{1,0:T(8,128)(2,1)S(1)}, u32[]{:S(2)}, u32[]{:S(2)}) %collective-permute-start.19) | collective-permute-done | bytes 983072 | tf_op jit(solution)/shard_map/ppermute | solution.py:25
  549.8 22.5 %collective-permute-done.20 = bf16[192,2560]{1,0:T(8,128)(2,1)S(1)} collective-permute-done((bf16[192,2560]{1,0:T(8,128)(2,1)S(1)}, bf16[192,2560]{1,0:T(8,128)(2,1)S(1)}, u32[]{:S(2)}, u32[]{:S(2)}) %collective-permute-start.20) | collective-permute-done | bytes 983072 | tf_op jit(solution)/shard_map/ppermute | solution.py:25
  576.6 22.4 %collective-permute-done.21 = bf16[192,2560]{1,0:T(8,128)(2,1)S(1)} collective-permute-done((bf16[192,2560]{1,0:T(8,128)(2,1)S(1)}, bf16[192,2560]{1,0:T(8,128)(2,1)S(1)}, u32[]{:S(2)}, u32[]{:S(2)}) %collective-permute-start.21) | collective-permute-done | bytes 983072 | tf_op jit(solution)/shard_map/ppermute | solution.py:25
  604.7 3.1 slice.301.refs_0_.refs_2_
  618.2 8.3 convert_reduce_fusion.2
  626.5 7.1 shard_map.275
  635.0 9.3 shard_map.276
  645.1 7.2 multiply_reduce_fusion
  662.7 4.0 fusion.53
  669.7 6.0 fusion.36
  679.2 3.9 convert_element_type.328.refs_2_
  683.0 7.1 convert_reduce_fusion.3
  690.1 8.1 shard_map.278
  701.1 11.3 %shard_map.279 = bf16[4,4,160,2560]{3,2,1,0:T(8,128)(2,1)} custom-call(bf16[384,2560]{1,0:T(8,128)(2,1)} %pad_maximum_fusion.4.refs_0_, bf16[384,1280]{1,0:T(8,128)(2,1)} %copy-done.46, bf16[384,2560]{1,0:T(8,128)(2,1)} %slice.301.refs_0_.refs_2_, bf16[384,1280]{1,0:T(8,128)(2,1)} %get-tuple-element.142.refs_3_), custom_call_target="tpu_custom_call" | custom-call | flops 5033164800 | bytes 17039360 | tf_op jit(solution)/shard_map/pallas_call | solution.py:492
  716.3 5.1 fusion.186
  721.4 5.1 convolution_add_fusion.4
  729.4 6.2 collective-permute-start.28
  739.2 4.4 all-to-all-start
  748.6 10.0 collective-permute-done.28
  764.5 46.6 %collective-permute-done.29 = bf16[192,2560]{1,0:T(8,128)(2,1)} collective-permute-done((bf16[192,2560]{1,0:T(8,128)(2,1)}, bf16[192,2560]{1,0:T(8,128)(2,1)}, u32[]{:S(2)}, u32[]{:S(2)}) %collective-permute-start.29) | collective-permute-done | bytes 983072 | tf_op jit(solution)/shard_map/ppermute | solution.py:25
  814.0 10.7 %collective-permute-start.30 = (bf16[192,2560]{1,0:T(8,128)(2,1)}, bf16[192,2560]{1,0:T(8,128)(2,1)}, u32[]{:S(2)}, u32[]{:S(2)}) collective-permute-start(bf16[192,2560]{1,0:T(8,128)(2,1)} %add_convert_fusion), channel_id=1, source_target_pairs={{0,8},{8,16},{16,24},{24,0},{1,9},{9,17},{17,25},{25,1},{2,10},{10... | collective-permute-start | bytes 2949128 | tf_op jit(solution)/shard_map/ppermute | solution.py:25
  824.8 17.7 %all-to-all-done.refs_0_ = bf16[4,160,1536]{2,1,0:T(8,128)(2,1)} async-done(((bf16[4,160,1536]{2,1,0:T(8,128)(2,1)}), bf16[4,160,1536]{2,1,0:T(8,128)(2,1)}, u32[]{:S(2)}, u32[]{:S(2)}) %all-to-all-start) | async-done | bytes 1966112 | tf_op jit(solution)/shard_map/all_to_all | solution.py:604
  842.6 4.7 all-to-all-start.1
  847.3 7.4 fusion.13
  854.8 8.7 collective-permute-done.41
  865.0 3.8 collective-permute-done.42
  870.8 8.7 collective-permute-done.43
  879.5 4.6 collective-permute-start.44
  884.1 10.7 %collective-permute-done.44 = f32[240,128]{1,0:T(8,128)S(1)} collective-permute-done((f32[240,128]{1,0:T(8,128)S(1)}, f32[240,128]{1,0:T(8,128)S(1)}, u32[]{:S(2)}, u32[]{:S(2)}) %collective-permute-start.44) | collective-permute-done | bytes 122912 | tf_op jit(solution)/shard_map/ppermute | solution.py:37
  899.1 5.9 shard_map.280
  905.0 3.8 broadcast_select_fusion.1
  908.8 3.8 broadcast_select_fusion.3
  916.6 4.5 pad_maximum_fusion.1
  921.1 8.6 collective-permute-done.34
  929.9 17.3 %collective-permute-done.37 = bf16[160,2560]{1,0:T(8,128)(2,1)S(1)} collective-permute-done((bf16[160,2560]{1,0:T(8,128)(2,1)S(1)}, bf16[160,2560]{1,0:T(8,128)(2,1)S(1)}, u32[]{:S(2)}, u32[]{:S(2)}) %collective-permute-start.37) | collective-permute-done | bytes 819232 | tf_op jit(solution)/shard_map/ppermute | solution.py:25
  949.7 8.1 collective-permute-done.35
  957.9 17.4 %collective-permute-done.38 = bf16[160,2560]{1,0:T(8,128)(2,1)S(1)} collective-permute-done((bf16[160,2560]{1,0:T(8,128)(2,1)S(1)}, bf16[160,2560]{1,0:T(8,128)(2,1)S(1)}, u32[]{:S(2)}, u32[]{:S(2)}) %collective-permute-start.38) | collective-permute-done | bytes 819232 | tf_op jit(solution)/shard_map/ppermute | solution.py:25
  975.6 10.3 %collective-permute-done.36 = bf16[192,1280]{1,0:T(8,128)(2,1)S(1)} collective-permute-done((bf16[192,1280]{1,0:T(8,128)(2,1)S(1)}, bf16[192,1280]{1,0:T(8,128)(2,1)S(1)}, u32[]{:S(2)}, u32[]{:S(2)}) %collective-permute-start.36) | collective-permute-done | bytes 491552 | tf_op jit(solution)/shard_map/ppermute | solution.py:25
  986.7 14.9 %collective-permute-done.39 = bf16[160,2560]{1,0:T(8,128)(2,1)S(1)} collective-permute-done((bf16[160,2560]{1,0:T(8,128)(2,1)S(1)}, bf16[160,2560]{1,0:T(8,128)(2,1)S(1)}, u32[]{:S(2)}, u32[]{:S(2)}) %collective-permute-start.39) | collective-permute-done | bytes 819232 | tf_op jit(solution)/shard_map/ppermute | solution.py:25
  (529 shorter events, 191.9 us)
Async XLA Ops:
  7.2 256.4 %copy-start = (f32[2,3840]{1,0:T(2,128)S(1)}, f32[2,3840]{1,0:T(2,128)}, u32[]{:S(2)}) copy-start(f32[2,3840]{1,0:T(2,128)} %param.31) | copy-start | bytes 92164
  7.2 360.5 %all-gather.3.cloned.1.call-start = ((), (), s32[]{:S(2)}) async-start(), calls=%async_computation.6 | async-start | bytes 9830400 | tf_op jit(solution)/shard_map/all_gather | solution.py:608
  10.9 259.0 %copy-start.87 = (f32[2560]{0:T(1024)}, f32[2560]{0:T(1024)S(1)}, u32[]{:S(2)}) copy-start(f32[2560]{0:T(1024)S(1)} %get-tuple-element.133) | copy-start | bytes 30724
  189.9 229.3 %all-gather.5.cloned.1.call-start = ((), (), s32[]{:S(2)}) async-start(), calls=%async_computation.7 | async-start | bytes 9011200 | tf_op jit(solution)/shard_map/all_gather | solution.py:608
  192.1 72.2 %copy-start.7 = (bf16[192,2560]{1,0:T(8,128)(2,1)}, bf16[192,2560]{1,0:T(8,128)(2,1)S(1)}, u32[]{:S(2)}) copy-start(bf16[192,2560]{1,0:T(8,128)(2,1)S(1)} %get-tuple-element.74.refs_12_) | copy-start | bytes 2949124
  192.1 20.9 %collective-permute-start = (bf16[192,2560]{1,0:T(8,128)(2,1)S(1)}, bf16[192,2560]{1,0:T(8,128)(2,1)}, u32[]{:S(2)}, u32[]{:S(2)}) collective-permute-start(bf16[192,2560]{1,0:T(8,128)(2,1)S(1)} %get-tuple-element.74.refs_12_), channel_id=1, source_target_pairs={{0,8},{8,16},{16,24},{24,0},{1,9},{9,17},{17,25},{25,1},{2,10},{10... | collective-permute-start | bytes 2949128 | tf_op jit(solution)/shard_map/ppermute | solution.py:25
  213.0 33.9 %collective-permute-start.1 = (bf16[192,2560]{1,0:T(8,128)(2,1)}, bf16[192,2560]{1,0:T(8,128)(2,1)}, u32[]{:S(2)}, u32[]{:S(2)}) collective-permute-start(bf16[192,2560]{1,0:T(8,128)(2,1)} %collective-permute-done.refs_15_), channel_id=1, source_target_pairs={{0,8},{8,16},{16,24},{24,0},{1,9},{9,17},{17,25},{25,1},{2,10},{10... | collective-permute-start | bytes 2949128 | tf_op jit(solution)/shard_map/ppermute | solution.py:25
  263.0 4.2 collective-permute-start.2
  263.0 8.3 collective-permute-start.3
  263.5 337.1 %reduce-scatter.5.cloned.1.call-start = ((), (), s32[]{:S(2)}) async-start(), calls=%async_computation.8 | async-start | bytes 9830400 | tf_op jit(solution)/shard_map/reduce_scatter | solution.py:612
  264.4 28.2 %collective-permute-start.7 = (bf16[192,2560]{1,0:T(8,128)(2,1)}, bf16[192,2560]{1,0:T(8,128)(2,1)S(1)}, u32[]{:S(2)}, u32[]{:S(2)}) collective-permute-start(bf16[192,2560]{1,0:T(8,128)(2,1)} %collective-permute-done.refs_15_), channel_id=1, source_target_pairs={{0,1},{1,0},{2,3},{3,2},{4,5},{5,4},{6,7},{7,6},{8,9},{9,8},{10,11... | collective-permute-start | bytes 2949128 | tf_op jit(solution)/shard_map/ppermute | solution.py:20
  265.8 26.7 %collective-permute-start.13 = (bf16[192,2560]{1,0:T(8,128)(2,1)}, bf16[192,2560]{1,0:T(8,128)(2,1)S(1)}, u32[]{:S(2)}, u32[]{:S(2)}) collective-permute-start(bf16[192,2560]{1,0:T(8,128)(2,1)} %collective-permute-done.1.refs_18_), channel_id=1, source_target_pairs={{0,8},{8,16},{16,24},{24,0},{1,9},{9,17},{17,25},{25,1},{2,10},{10... | collective-permute-start | bytes 2949128 | tf_op jit(solution)/shard_map/ppermute | solution.py:25
  270.2 119.9 %copy-start.19 = (bf16[192,2560]{1,0:T(8,128)(2,1)}, bf16[192,2560]{1,0:T(8,128)(2,1)S(1)}, u32[]{:S(2)}) copy-start(bf16[192,2560]{1,0:T(8,128)(2,1)S(1)} %multiply_convert_fusion.1.refs_0_) | copy-start | bytes 2949124
  270.2 42.8 %collective-permute-start.5 = (bf16[192,2560]{1,0:T(8,128)(2,1)S(1)}, bf16[192,2560]{1,0:T(8,128)(2,1)S(1)}, u32[]{:S(2)}, u32[]{:S(2)}) collective-permute-start(bf16[192,2560]{1,0:T(8,128)(2,1)S(1)} %multiply_convert_fusion.1.refs_0_), channel_id=1, source_target_pairs={{0,8},{8,16},{16,24},{24,0},{1,9},{9,17},{17,25},{25,1},{2,10},{10... | collective-permute-start | bytes 2949128 | tf_op jit(solution)/shard_map/ppermute | solution.py:25
  272.5 40.6 %copy-start.69 = (bf16[384,2560]{1,0:T(8,128)(2,1)}, bf16[384,2560]{1,0:T(8,128)(2,1)S(1)}, u32[]{:S(2)}) copy-start(bf16[384,2560]{1,0:T(8,128)(2,1)S(1)} %constant_dynamic-update-slice_fusion) | copy-start | bytes 5898244
  272.5 40.6 %collective-permute-start.10 = (bf16[192,2560]{1,0:T(8,128)(2,1)}, bf16[192,2560]{1,0:T(8,128)(2,1)S(1)}, u32[]{:S(2)}, u32[]{:S(2)}) collective-permute-start(bf16[192,2560]{1,0:T(8,128)(2,1)} %collective-permute-done.1.refs_18_), channel_id=1, source_target_pairs={{0,1},{1,0},{2,3},{3,2},{4,5},{5,4},{6,7},{7,6},{8,9},{9,8},{10,11... | collective-permute-start | bytes 2949128 | tf_op jit(solution)/shard_map/ppermute | solution.py:20
  292.5 20.8 %collective-permute-start.14 = (bf16[192,2560]{1,0:T(8,128)(2,1)S(1)}, bf16[192,2560]{1,0:T(8,128)(2,1)S(1)}, u32[]{:S(2)}, u32[]{:S(2)}) collective-permute-start(bf16[192,2560]{1,0:T(8,128)(2,1)S(1)} %collective-permute-done.13.refs_21_), channel_id=1, source_target_pairs={{0,1},{1,0},{2,3},{3,2},{4,5},{5,4},{6,7},{7,6},{8,9},{9,8},{10,11... | collective-permute-start | bytes 2949128 | tf_op jit(solution)/shard_map/ppermute | solution.py:20
  313.0 25.0 %collective-permute-start.8 = (bf16[192,2560]{1,0:T(8,128)(2,1)S(1)}, bf16[192,2560]{1,0:T(8,128)(2,1)S(1)}, u32[]{:S(2)}, u32[]{:S(2)}) collective-permute-start(bf16[192,2560]{1,0:T(8,128)(2,1)S(1)} %collective-permute-done.5.refs_3_), channel_id=1, source_target_pairs={{0,8},{8,16},{16,24},{24,0},{1,9},{9,17},{17,25},{25,1},{2,10},{10... | collective-permute-start | bytes 2949128 | tf_op jit(solution)/shard_map/ppermute | solution.py:25
  313.1 25.5 %collective-permute-start.4 = (bf16[192,2560]{1,0:T(8,128)(2,1)S(1)}, bf16[192,2560]{1,0:T(8,128)(2,1)S(1)}, u32[]{:S(2)}, u32[]{:S(2)}) collective-permute-start(bf16[192,2560]{1,0:T(8,128)(2,1)S(1)} %multiply_convert_fusion.1.refs_0_), channel_id=1, source_target_pairs={{0,1},{1,0},{2,3},{3,2},{4,5},{5,4},{6,7},{7,6},{8,9},{9,8},{10,11... | collective-permute-start | bytes 2949128 | tf_op jit(solution)/shard_map/ppermute | solution.py:20
  313.3 26.8 %copy-start.51 = (bf16[192,2560]{1,0:T(8,128)(2,1)}, bf16[192,2560]{1,0:T(8,128)(2,1)S(1)}, u32[]{:S(2)}) copy-start(bf16[192,2560]{1,0:T(8,128)(2,1)S(1)} %collective-permute-done.14.refs_22_) | copy-start | bytes 2949124
  313.4 49.2 %collective-permute-start.6 = (bf16[192,2560]{1,0:T(8,128)(2,1)S(1)}, bf16[192,2560]{1,0:T(8,128)(2,1)S(1)}, u32[]{:S(2)}, u32[]{:S(2)}) collective-permute-start(bf16[192,2560]{1,0:T(8,128)(2,1)S(1)} %collective-permute-done.5.refs_3_), channel_id=1, source_target_pairs={{0,1},{1,0},{2,3},{3,2},{4,5},{5,4},{6,7},{7,6},{8,9},{9,8},{10,11... | collective-permute-start | bytes 2949128 | tf_op jit(solution)/shard_map/ppermute | solution.py:20
  338.0 24.6 %collective-permute-start.11 = (bf16[192,2560]{1,0:T(8,128)(2,1)S(1)}, bf16[192,2560]{1,0:T(8,128)(2,1)S(1)}, u32[]{:S(2)}, u32[]{:S(2)}) collective-permute-start(bf16[192,2560]{1,0:T(8,128)(2,1)S(1)} %collective-permute-done.8.refs_6_), channel_id=1, source_target_pairs={{0,8},{8,16},{16,24},{24,0},{1,9},{9,17},{17,25},{25,1},{2,10},{10... | collective-permute-start | bytes 2949128 | tf_op jit(solution)/shard_map/ppermute | solution.py:25
  340.2 23.7 %collective-permute-start.9 = (bf16[192,2560]{1,0:T(8,128)(2,1)S(1)}, bf16[192,2560]{1,0:T(8,128)(2,1)S(1)}, u32[]{:S(2)}, u32[]{:S(2)}) collective-permute-start(bf16[192,2560]{1,0:T(8,128)(2,1)S(1)} %collective-permute-done.8.refs_6_), channel_id=1, source_target_pairs={{0,1},{1,0},{2,3},{3,2},{4,5},{5,4},{6,7},{7,6},{8,9},{9,8},{10,11... | collective-permute-start | bytes 2949128 | tf_op jit(solution)/shard_map/ppermute | solution.py:20
  362.6 2.6 collective-permute-start.12
  376.0 81.7 %copy-start.35 = (bf16[384,512]{1,0:T(8,128)(2,1)}, bf16[384,512]{1,0:T(8,128)(2,1)S(1)}, u32[]{:S(2)}) copy-start(bf16[384,512]{1,0:T(8,128)(2,1)S(1)} %get-tuple-element.165) | copy-start | bytes 1179652
  381.7 59.1 %copy-start.36 = (bf16[384,512]{1,0:T(8,128)(2,1)}, bf16[384,512]{1,0:T(8,128)(2,1)S(1)}, u32[]{:S(2)}) copy-start(bf16[384,512]{1,0:T(8,128)(2,1)S(1)} %get-tuple-element.166) | copy-start | bytes 1179652
  394.8 79.4 %copy-start.43 = (bf16[384,512]{1,0:T(8,128)(2,1)}, bf16[384,512]{1,0:T(8,128)(2,1)S(1)}, u32[]{:S(2)}) copy-start(bf16[384,512]{1,0:T(8,128)(2,1)S(1)} %get-tuple-element.170) | copy-start | bytes 1179652
  418.8 226.2 %reduce-scatter.7.cloned.1.call-start = ((), (), s32[]{:S(2)}) async-start(), calls=%async_computation.9 | async-start | bytes 9011200 | tf_op jit(solution)/shard_map/reduce_scatter | solution.py:612
  434.6 43.8 %collective-permute-start.18 = (bf16[192,2560]{1,0:T(8,128)(2,1)S(1)}, bf16[192,2560]{1,0:T(8,128)(2,1)S(1)}, u32[]{:S(2)}, u32[]{:S(2)}) collective-permute-start(bf16[192,2560]{1,0:T(8,128)(2,1)S(1)} %slice.729), channel_id=1, source_target_pairs={{0,1},{1,0},{2,3},{3,2},{4,5},{5,4},{6,7},{7,6},{8,9},{9,8},{10,11... | collective-permute-start | bytes 2949128 | tf_op jit(solution)/shard_map/ppermute | solution.py:20
  450.8 75.6 %collective-permute-start.17 = (bf16[192,2560]{1,0:T(8,128)(2,1)}, bf16[192,2560]{1,0:T(8,128)(2,1)}, u32[]{:S(2)}, u32[]{:S(2)}) collective-permute-start(bf16[192,2560]{1,0:T(8,128)(2,1)} %slice.730), channel_id=1, source_target_pairs={{0,1},{1,0},{2,3},{3,2},{4,5},{5,4},{6,7},{7,6},{8,9},{9,8},{10,11... | collective-permute-start | bytes 2949128 | tf_op jit(solution)/shard_map/ppermute | solution.py:20
  467.8 82.0 %collective-permute-start.16 = (bf16[192,2560]{1,0:T(8,128)(2,1)}, bf16[192,2560]{1,0:T(8,128)(2,1)}, u32[]{:S(2)}, u32[]{:S(2)}) collective-permute-start(bf16[192,2560]{1,0:T(8,128)(2,1)} %slice.731), channel_id=1, source_target_pairs={{0,1},{1,0},{2,3},{3,2},{4,5},{5,4},{6,7},{7,6},{8,9},{9,8},{10,11... | collective-permute-start | bytes 2949128 | tf_op jit(solution)/shard_map/ppermute | solution.py:20
  501.4 411.2 %reduce-scatter.9.cloned.1.call-start = ((), (), s32[]{:S(2)}) async-start(), calls=%async_computation.10 | async-start | bytes 9830400 | tf_op jit(solution)/shard_map/reduce_scatter | solution.py:612
  509.3 67.3 %collective-permute-start.15 = (bf16[192,2560]{1,0:T(8,128)(2,1)}, bf16[192,2560]{1,0:T(8,128)(2,1)S(1)}, u32[]{:S(2)}, u32[]{:S(2)}) collective-permute-start(bf16[192,2560]{1,0:T(8,128)(2,1)} %slice.732), channel_id=1, source_target_pairs={{0,1},{1,0},{2,3},{3,2},{4,5},{5,4},{6,7},{7,6},{8,9},{9,8},{10,11... | collective-permute-start | bytes 2949128 | tf_op jit(solution)/shard_map/ppermute | solution.py:20
  518.4 26.1 %collective-permute-start.19 = (bf16[192,2560]{1,0:T(8,128)(2,1)}, bf16[192,2560]{1,0:T(8,128)(2,1)S(1)}, u32[]{:S(2)}, u32[]{:S(2)}) collective-permute-start(bf16[192,2560]{1,0:T(8,128)(2,1)} %slice_add_fusion.4), channel_id=1, source_target_pairs={{0,8},{8,16},{16,24},{24,0},{1,9},{9,17},{17,25},{25,1},{2,10},{10... | collective-permute-start | bytes 2949128 | tf_op jit(solution)/shard_map/ppermute | solution.py:25
  522.2 24.0 %collective-permute-start.25 = (bf16[192,2560]{1,0:T(8,128)(2,1)}, bf16[192,2560]{1,0:T(8,128)(2,1)S(1)}, u32[]{:S(2)}, u32[]{:S(2)}) collective-permute-start(bf16[192,2560]{1,0:T(8,128)(2,1)} %slice.725), channel_id=1, source_target_pairs={{0,1},{1,0},{2,3},{3,2},{4,5},{5,4},{6,7},{7,6},{8,9},{9,8},{10,11... | collective-permute-start | bytes 2949128 | tf_op jit(solution)/shard_map/ppermute | solution.py:20
  526.5 21.2 %collective-permute-start.24 = (bf16[192,2560]{1,0:T(8,128)(2,1)S(1)}, bf16[192,2560]{1,0:T(8,128)(2,1)S(1)}, u32[]{:S(2)}, u32[]{:S(2)}) collective-permute-start(bf16[192,2560]{1,0:T(8,128)(2,1)S(1)} %slice.726), channel_id=1, source_target_pairs={{0,1},{1,0},{2,3},{3,2},{4,5},{5,4},{6,7},{7,6},{8,9},{9,8},{10,11... | collective-permute-start | bytes 2949128 | tf_op jit(solution)/shard_map/ppermute | solution.py:20
  544.6 30.5 %collective-permute-start.23 = (bf16[192,2560]{1,0:T(8,128)(2,1)S(1)}, bf16[192,2560]{1,0:T(8,128)(2,1)S(1)}, u32[]{:S(2)}, u32[]{:S(2)}) collective-permute-start(bf16[192,2560]{1,0:T(8,128)(2,1)S(1)} %slice.727), channel_id=1, source_target_pairs={{0,1},{1,0},{2,3},{3,2},{4,5},{5,4},{6,7},{7,6},{8,9},{9,8},{10,11... | collective-permute-start | bytes 2949128 | tf_op jit(solution)/shard_map/ppermute | solution.py:20
  546.2 26.1 %collective-permute-start.20 = (bf16[192,2560]{1,0:T(8,128)(2,1)S(1)}, bf16[192,2560]{1,0:T(8,128)(2,1)S(1)}, u32[]{:S(2)}, u32[]{:S(2)}) collective-permute-start(bf16[192,2560]{1,0:T(8,128)(2,1)S(1)} %fusion.46), channel_id=1, source_target_pairs={{0,8},{8,16},{16,24},{24,0},{1,9},{9,17},{17,25},{25,1},{2,10},{10... | collective-permute-start | bytes 2949128 | tf_op jit(solution)/shard_map/ppermute | solution.py:25
  547.7 26.2 %collective-permute-start.22 = (bf16[192,2560]{1,0:T(8,128)(2,1)S(1)}, bf16[192,2560]{1,0:T(8,128)(2,1)S(1)}, u32[]{:S(2)}, u32[]{:S(2)}) collective-permute-start(bf16[192,2560]{1,0:T(8,128)(2,1)S(1)} %slice.728), channel_id=1, source_target_pairs={{0,1},{1,0},{2,3},{3,2},{4,5},{5,4},{6,7},{7,6},{8,9},{9,8},{10,11... | collective-permute-start | bytes 2949128 | tf_op jit(solution)/shard_map/ppermute | solution.py:20
  573.8 25.2 %collective-permute-start.21 = (bf16[192,2560]{1,0:T(8,128)(2,1)S(1)}, bf16[192,2560]{1,0:T(8,128)(2,1)S(1)}, u32[]{:S(2)}, u32[]{:S(2)}) collective-permute-start(bf16[192,2560]{1,0:T(8,128)(2,1)S(1)} %fusion.48), channel_id=1, source_target_pairs={{0,8},{8,16},{16,24},{24,0},{1,9},{9,17},{17,25},{25,1},{2,10},{10... | collective-permute-start | bytes 2949128 | tf_op jit(solution)/shard_map/ppermute | solution.py:25
  604.7 10.8 %collective-permute-start.26 = (bf16[192,2560]{1,0:T(8,128)(2,1)}, bf16[192,2560]{1,0:T(8,128)(2,1)}, u32[]{:S(2)}, u32[]{:S(2)}) collective-permute-start(bf16[192,2560]{1,0:T(8,128)(2,1)} %get-tuple-element.146), channel_id=1, source_target_pairs={{0,1},{1,0},{2,3},{3,2},{4,5},{5,4},{6,7},{7,6},{8,9},{9,8},{10,11... | collective-permute-start | bytes 2949128 | tf_op jit(solution)/shard_map/ppermute | solution.py:20
  675.7 7.3 collective-permute-start.27
  698.2 215.7 %reduce-scatter.11.cloned.1.call-start = ((), (), s32[]{:S(2)}) async-start(), calls=%async_computation.11 | async-start | bytes 16384000 | tf_op jit(solution)/shard_map/reduce_scatter | solution.py:612
  729.4 16.1 %collective-permute-start.32 = (bf16[192,2560]{1,0:T(8,128)(2,1)}, bf16[192,2560]{1,0:T(8,128)(2,1)}, u32[]{:S(2)}, u32[]{:S(2)}) collective-permute-start(bf16[192,2560]{1,0:T(8,128)(2,1)} %dynamic-slice_convert_fusion), channel_id=1, source_target_pairs={{0,1},{1,0},{2,3},{3,2},{4,5},{5,4},{6,7},{7,6},{8,9},{9,8},{10,11... | collective-permute-start | bytes 2949128 | tf_op jit(solution)/shard_map/ppermute | solution.py:20
  729.4 29.1 %collective-permute-start.28 = (bf16[192,2560]{1,0:T(8,128)(2,1)}, bf16[192,2560]{1,0:T(8,128)(2,1)}, u32[]{:S(2)}, u32[]{:S(2)}) collective-permute-start(bf16[192,2560]{1,0:T(8,128)(2,1)} %slice_add_fusion.3), channel_id=1, source_target_pairs={{0,8},{8,16},{16,24},{24,0},{1,9},{9,17},{17,25},{25,1},{2,10},{10... | collective-permute-start | bytes 2949128 | tf_op jit(solution)/shard_map/ppermute | solution.py:25
  739.2 103.4 %all-to-all-start = ((bf16[4,160,1536]{2,1,0:T(8,128)(2,1)}), bf16[4,160,1536]{2,1,0:T(8,128)(2,1)}, u32[]{:S(2)}, u32[]{:S(2)}) async-start(bf16[4,160,1536]{2,1,0:T(8,128)(2,1)} %bitcast.173), calls=%async_computation.4 | async-start | bytes 3932160 | tf_op jit(solution)/shard_map/all_to_all | solution.py:604
  761.2 50.0 %collective-permute-start.29 = (bf16[192,2560]{1,0:T(8,128)(2,1)}, bf16[192,2560]{1,0:T(8,128)(2,1)}, u32[]{:S(2)}, u32[]{:S(2)}) collective-permute-start(bf16[192,2560]{1,0:T(8,128)(2,1)} %add_convert_fusion.1), channel_id=1, source_target_pairs={{0,8},{8,16},{16,24},{24,0},{1,9},{9,17},{17,25},{25,1},{2,10},{10... | collective-permute-start | bytes 2949128 | tf_op jit(solution)/shard_map/ppermute | solution.py:25
  763.1 1.3 collective-permute-start.40
  814.0 33.2 %copy-start.91 = (f32[2560]{0:T(1024)S(1)}, f32[2560]{0:T(1024)}, u32[]{:S(2)}) copy-start(f32[2560]{0:T(1024)} %get-tuple-element.134) | copy-start | bytes 30724
  814.0 33.2 %collective-permute-start.30 = (bf16[192,2560]{1,0:T(8,128)(2,1)}, bf16[192,2560]{1,0:T(8,128)(2,1)}, u32[]{:S(2)}, u32[]{:S(2)}) collective-permute-start(bf16[192,2560]{1,0:T(8,128)(2,1)} %add_convert_fusion), channel_id=1, source_target_pairs={{0,8},{8,16},{16,24},{24,0},{1,9},{9,17},{17,25},{25,1},{2,10},{10... | collective-permute-start | bytes 2949128 | tf_op jit(solution)/shard_map/ppermute | solution.py:25
  842.6 56.6 %all-to-all-start.1 = ((bf16[4,160,1344]{2,1,0:T(8,128)(2,1)}), bf16[4,160,1344]{2,1,0:T(8,128)(2,1)}, u32[]{:S(2)}, u32[]{:S(2)}) async-start(bf16[4,160,1344]{2,1,0:T(8,128)(2,1)} %bitcast.180), calls=%async_computation.5 | async-start | bytes 3604480 | tf_op jit(solution)/shard_map/all_to_all | solution.py:604
  854.7 50.3 %collective-permute-start.33 = (f32[192,2560]{1,0:T(8,128)}, f32[192,2560]{1,0:T(8,128)S(1)}, u32[]{:S(2)}, u32[]{:S(2)}) collective-permute-start(f32[192,2560]{1,0:T(8,128)} %get-tuple-element.180), channel_id=1, source_target_pairs={{0,1},{1,0},{2,3},{3,2},{4,5},{5,4},{6,7},{7,6},{8,9},{9,8},{10,11... | collective-permute-start | bytes 5898248 | tf_op jit(solution)/shard_map/ppermute | solution.py:20
  854.8 8.8 collective-permute-start.41
  863.6 5.2 collective-permute-start.42
  864.9 43.9 %collective-permute-start.31 = (f32[192,2560]{1,0:T(8,128)}, f32[192,2560]{1,0:T(8,128)}, u32[]{:S(2)}, u32[]{:S(2)}) collective-permute-start(f32[192,2560]{1,0:T(8,128)} %get-tuple-element.181), channel_id=1, source_target_pairs={{0,1},{1,0},{2,3},{3,2},{4,5},{5,4},{6,7},{7,6},{8,9},{9,8},{10,11... | collective-permute-start | bytes 5898248 | tf_op jit(solution)/shard_map/ppermute | solution.py:20
  868.7 10.7 %collective-permute-start.43 = (f32[240,128]{1,0:T(8,128)S(1)}, f32[240,128]{1,0:T(8,128)S(1)}, u32[]{:S(2)}, u32[]{:S(2)}) collective-permute-start(f32[240,128]{1,0:T(8,128)S(1)} %fusion.225), channel_id=1, source_target_pairs={{0,8},{2,10},{4,12},{6,14},{8,0},{10,2},{12,4},{14,6},{16,24},{18,... | collective-permute-start | bytes 368648 | tf_op jit(solution)/shard_map/ppermute | solution.py:37
  879.5 15.3 %collective-permute-start.44 = (f32[240,128]{1,0:T(8,128)S(1)}, f32[240,128]{1,0:T(8,128)S(1)}, u32[]{:S(2)}, u32[]{:S(2)}) collective-permute-start(f32[240,128]{1,0:T(8,128)S(1)} %add.570), channel_id=1, source_target_pairs={{0,16},{2,18},{4,20},{6,22},{8,24},{10,26},{12,28},{14,30},{16,0},... | collective-permute-start | bytes 368648 | tf_op jit(solution)/shard_map/ppermute | solution.py:37
  913.7 15.9 %collective-permute-start.34 = (bf16[192,1280]{1,0:T(8,128)(2,1)S(1)}, bf16[192,1280]{1,0:T(8,128)(2,1)S(1)}, u32[]{:S(2)}, u32[]{:S(2)}) collective-permute-start(bf16[192,1280]{1,0:T(8,128)(2,1)S(1)} %dynamic-slice_bitcast_fusion.1), channel_id=1, source_target_pairs={{0,8},{8,16},{16,24},{24,0},{1,9},{9,17},{17,25},{25,1},{2,10},{10... | collective-permute-start | bytes 1474568 | tf_op jit(solution)/shard_map/ppermute | solution.py:25
  915.1 32.2 %collective-permute-start.37 = (bf16[160,2560]{1,0:T(8,128)(2,1)S(1)}, bf16[160,2560]{1,0:T(8,128)(2,1)S(1)}, u32[]{:S(2)}, u32[]{:S(2)}) collective-permute-start(bf16[160,2560]{1,0:T(8,128)(2,1)S(1)} %dynamic-slice_bitcast_fusion), channel_id=1, source_target_pairs={{0,8},{8,16},{16,24},{24,0},{1,9},{9,17},{17,25},{25,1},{2,10},{10... | collective-permute-start | bytes 2457608 | tf_op jit(solution)/shard_map/ppermute | solution.py:25
  916.6 30.6 %copy-start.22 = (bf16[640,2560]{1,0:T(8,128)(2,1)S(1)}, bf16[640,2560]{1,0:T(8,128)(2,1)}, u32[]{:S(2)}) copy-start(bf16[640,2560]{1,0:T(8,128)(2,1)} %reduce-scatter.11.cloned.1.call-done) | copy-start | bytes 9830404
  929.8 27.9 %collective-permute-start.35 = (bf16[192,1280]{1,0:T(8,128)(2,1)S(1)}, bf16[192,1280]{1,0:T(8,128)(2,1)S(1)}, u32[]{:S(2)}, u32[]{:S(2)}) collective-permute-start(bf16[192,1280]{1,0:T(8,128)(2,1)S(1)} %fusion.55), channel_id=1, source_target_pairs={{0,8},{8,16},{16,24},{24,0},{1,9},{9,17},{17,25},{25,1},{2,10},{10... | collective-permute-start | bytes 1474568 | tf_op jit(solution)/shard_map/ppermute | solution.py:25
  947.4 27.9 %collective-permute-start.38 = (bf16[160,2560]{1,0:T(8,128)(2,1)S(1)}, bf16[160,2560]{1,0:T(8,128)(2,1)S(1)}, u32[]{:S(2)}, u32[]{:S(2)}) collective-permute-start(bf16[160,2560]{1,0:T(8,128)(2,1)S(1)} %fusion.51), channel_id=1, source_target_pairs={{0,8},{8,16},{16,24},{24,0},{1,9},{9,17},{17,25},{25,1},{2,10},{10... | collective-permute-start | bytes 2457608 | tf_op jit(solution)/shard_map/ppermute | solution.py:25
  957.9 28.0 %collective-permute-start.36 = (bf16[192,1280]{1,0:T(8,128)(2,1)S(1)}, bf16[192,1280]{1,0:T(8,128)(2,1)S(1)}, u32[]{:S(2)}, u32[]{:S(2)}) collective-permute-start(bf16[192,1280]{1,0:T(8,128)(2,1)S(1)} %fusion.56), channel_id=1, source_target_pairs={{0,8},{8,16},{16,24},{24,0},{1,9},{9,17},{17,25},{25,1},{2,10},{10... | collective-permute-start | bytes 1474568 | tf_op jit(solution)/shard_map/ppermute | solution.py:25
  975.5 26.1 %collective-permute-start.39 = (bf16[160,2560]{1,0:T(8,128)(2,1)S(1)}, bf16[160,2560]{1,0:T(8,128)(2,1)S(1)}, u32[]{:S(2)}, u32[]{:S(2)}) collective-permute-start(bf16[160,2560]{1,0:T(8,128)(2,1)S(1)} %fusion.52), channel_id=1, source_target_pairs={{0,8},{8,16},{16,24},{24,0},{1,9},{9,17},{17,25},{25,1},{2,10},{10... | collective-permute-start | bytes 2457608 | tf_op jit(solution)/shard_map/ppermute | solution.py:25
  (116 other events, 862.4 us)
Sparse Core Ops, SparseCore 0:
  190.0 87.4 all-gather.2
  279.4 77.6 all-gather.4
  419.0 80.5 reduce-scatter.4
  502.5 77.6 reduce-scatter.6
  698.3 84.9 reduce-scatter.8
  786.3 127.4 reduce-scatter.10

commit v9 on v8

--- a/solution.py
+++ b/solution.py
@@ -808,10 +808,11 @@
     grad_gate_weights = jnp.einsum(
         "thb,gthc->ghbc", conv_blocks, delta_blocks, preferred_element_type=F32
     )
+    split = width_half * 4 // 5
     gate_rows = (
         grad_gate_weights.reshape(2, heads_half, count, block_size // count, block_size)
         .transpose(2, 0, 1, 3, 4)
-        .reshape(outer, inner, -1, width_half)
+        .reshape(outer, inner, -1, split)
         .astype(BF16)
     )
     grad_gate_bias = jnp.sum(delta_gates, axis=1, dtype=F32)
@@ -836,8 +837,10 @@
         conv_weight_rows.append(jnp.sum(delta_conv * shifted, axis=0))
     grad_conv_bias = jnp.sum(delta_conv, axis=0)
     delta_x_low = delta_branch_x.astype(BF16)
-    x_rows = grads_rows([[([normed_low], delta_x_low)]], gate_rows)
+    x_rows = grads_rows([[([normed_low], delta_x_low[:, :split])]], gate_rows)
     grad_x_inner = sum_inner(x_rows)
+    x_rows = grads_rows([[([normed_low], delta_x_low[:, split:])]])
+    grad_z_inner = sum_inner(x_rows)
     delta_part = mm_nt(delta_x_low, branch_x_full) + mm_nt(delta_y_low, branch_y_full)
     delta_normed = half_of(delta_part, core) + swap(
         half_of(delta_part, 1 - core).astype(BF16)
@@ -870,7 +873,8 @@
     result_half = residual + result_sum + out_bias[1]
     result = join_halves(result_half, swap(result_half), core)
     grad_x_gate = ring_sum(ring_order(grad_x_inner))
-    grad_branch_x = grad_x_gate[:part_width]
+    grad_x_rest = ring_sum(ring_order(grad_z_inner))
+    grad_branch_x = jnp.concatenate([grad_x_gate[:part_width], grad_x_rest], axis=1)
     gate_grad = grad_x_gate[part_width:].reshape(2, heads_half, block_size // count, block_size)
     small = small.reshape(-1)
     at = 0

time: 1020 us -> 1040 us (1.020)
    ppermute x18 -> x21, starting transfers between devices: 25.3 us -> 20.8 us  [ring(): lax.ppermute(value, 'o', [(k, (k + 1) % count) for k in range(count)])]
    pallas_call x4 -> x5, Pallas kernels: 63.5 us -> 67 us  [grads_rows(): pl.pallas_call(functools.partial(grads_kernel, plan, added), grid=(outer,...]
    ppermute x18 -> x21, waiting for transfers between devices: 298 us -> 299 us  [ring(): lax.ppermute(value, 'o', [(k, (k + 1) % count) for k in range(count)])]
  transfers between devices with their start and end apart: 53 -> 57, of which waited for: 25 -> 24; matrix products, arithmetic and copies ran while one was open for 25% -> 25% of each run, Pallas kernels for 10% -> 11%
where the time goes in v9:
time: 1040 us; the launch traced here: 1020 us
  waiting for transfers between devices  353 us (34%)
  Pallas kernels  287 us (28%)
  matrix products  138 us (13%)
  other arithmetic  110 us (11%)
  local copies, waits for them, and re-layouts  73.1 us (7%)
  starting transfers between devices  45.4 us (4%)
  between operations  16.8 us (2%)
    ppermute x21, waiting for transfers between devices, ring(): lax.ppermute(value, 'o', [(k, (k + 1) % count) for k in range(count)])  299 us
    pallas_call x1, Pallas kernels, gather_weights(): pl.pallas_call(functools.partial(gather_kernel, outer, inner, groups, cut...  175 us
    dot_general x38, matrix products, dot(): lax.dot_general(a, b, ((contract[0], contract[1]), ((), ())), preferred_e...  131 us
    pallas_call x5, Pallas kernels, grads_rows(): pl.pallas_call(functools.partial(grads_kernel, plan, added), grid=(outer,...  67 us
    ppermute x4, waiting for transfers between devices, sum_over_all(): lax.ppermute(value, DP, [(k, k ^ bit) for k in range(count)])  40.8 us
    pallas_call x2, Pallas kernels, entering(): pl.pallas_call(functools.partial(enter_kernel, outer, inner, reverse), in...  21.4 us
    ppermute x21, starting transfers between devices, ring(): lax.ppermute(value, 'o', [(k, (k + 1) % count) for k in range(count)])  20.8 us
  transfers between devices with their start and end apart: 57, of which 24 were waited for; matrix products, arithmetic and copies ran while one was open for 25% of the time, Pallas kernels for 11%

profile of v9, /device:TPU:0, one launch (start us, length us, event | category | flops | bytes accessed | tf_op | source)
XLA Modules:
  0.0 1023.0 jit_solution(8509229483076933851)
XLA Ops:
  14.4 175.4 %shard_map.271 = (bf16[4,4,160,1280]{3,2,1,0:T(8,128)(2,1)}, bf16[4,4,160,1280]{3,2,1,0:T(8,128)(2,1)}, bf16[4,4,160,1280]{3,2,1,0:T(8,128)(2,1)}, bf16[4,160,15...) custom-call(bf16[160,1280]{1,0:T(8,128)(2,1)} %get-tuple-element.198, ...), custom_call_target="tpu_custom_call" | custom-call | tf_op jit(solution)/shard_map/pallas_call | solution.py:420
  195.9 17.1 %collective-permute-done.refs_15_ = bf16[192,2560]{1,0:T(8,128)(2,1)} collective-permute-done((bf16[192,2560]{1,0:T(8,128)(2,1)S(1)}, bf16[192,2560]{1,0:T(8,128)(2,1)}, u32[]{:S(2)}, u32[]{:S(2)}) %collective-permute-start) | collective-permute-done | bytes 983072 | tf_op jit(solution)/shard_map/ppermute | solution.py:25
  216.6 7.0 convolution_add_fusion.9.branch_ref
  223.6 10.5 %shard_map.272 = (bf16[384,1280]{1,0:T(8,128)(2,1)}, f32[384,1280]{1,0:T(8,128)}, f32[384,1280]{1,0:T(8,128)}, f32[384,1280]{1,0:T(8,128)}, f32[384,1280]{1,0:T(8,128)}, /*index=5*/f32[2,1280]{1,0:T(2,128)}) custom-call(f32[400,1280]{1,0:T(8,128)} %convolution_add_fusion.9.branch_ref, f32[384,8]{1,0:T(8,128)} %copy.69.mask_ref, f32[4,1280]{1,0:T(4,128)} %taps_ref.1, ...), custom_call_target="tpu_custom_call" | custom-call | flops 503316480 | bytes 10813440 | tf_op jit(solution)/shard_map/pallas_call | solution.py:131
  234.1 12.1 %shard_map.273 = f32[1,1280]{1,0:T(1,128)} custom-call(f32[2,1280]{1,0:T(2,128)} %get-tuple-element.73.ends_ref), custom_call_target="tpu_custom_call" | custom-call | tf_op jit(solution)/shard_map/pallas_call | solution.py:204
  247.0 8.1 multiply_convert_fusion.2
  255.1 5.3 fusion.188
  274.6 18.0 %collective-permute-done.13.refs_21_ = bf16[192,2560]{1,0:T(8,128)(2,1)S(1)} collective-permute-done((bf16[192,2560]{1,0:T(8,128)(2,1)}, bf16[192,2560]{1,0:T(8,128)(2,1)S(1)}, u32[]{:S(2)}, u32[]{:S(2)}) %collective-permute-start.13) | collective-permute-done | bytes 983072 | tf_op jit(solution)/shard_map/ppermute | solution.py:25
  292.7 20.4 %collective-permute-done.5.refs_3_ = bf16[192,2560]{1,0:T(8,128)(2,1)S(1)} collective-permute-done((bf16[192,2560]{1,0:T(8,128)(2,1)S(1)}, bf16[192,2560]{1,0:T(8,128)(2,1)S(1)}, u32[]{:S(2)}, u32[]{:S(2)}) %collective-permute-start.5) | collective-permute-done | bytes 983072 | tf_op jit(solution)/shard_map/ppermute | solution.py:25
  314.0 24.0 %collective-permute-done.8.refs_6_ = bf16[192,2560]{1,0:T(8,128)(2,1)S(1)} collective-permute-done((bf16[192,2560]{1,0:T(8,128)(2,1)S(1)}, bf16[192,2560]{1,0:T(8,128)(2,1)S(1)}, u32[]{:S(2)}, u32[]{:S(2)}) %collective-permute-start.8) | collective-permute-done | bytes 983072 | tf_op jit(solution)/shard_map/ppermute | solution.py:25
  340.0 22.3 %collective-permute-done.11.refs_9_ = bf16[192,2560]{1,0:T(8,128)(2,1)S(1)} collective-permute-done((bf16[192,2560]{1,0:T(8,128)(2,1)S(1)}, bf16[192,2560]{1,0:T(8,128)(2,1)S(1)}, u32[]{:S(2)}, u32[]{:S(2)}) %collective-permute-start.11) | collective-permute-done | bytes 983072 | tf_op jit(solution)/shard_map/ppermute | solution.py:25
  367.5 5.4 convolution_add_fusion.11
  396.3 22.3 %shard_map.274 = bf16[4,4,160,1536]{3,2,1,0:T(8,128)(2,1)} custom-call(bf16[192,2560]{1,0:T(8,128)(2,1)} %copy-done.22, bf16[192,2560]{1,0:T(8,128)(2,1)} %copy-done.62, bf16[384,1024]{1,0:T(8,128)(2,1)} %pad_maximum_fusion.9.refs_2_, bf16[192,2560]{1,0:T(8,128)(2,1)} %copy-done.53, bf16[192,2560]{1,0:T(8,128)(2,1)} %copy-done.57, ...), custom_call_target="tpu_custom_call" | custom-call | flops 12079595520 | bytes 20447232 | tf_op jit(solution)/shard_map/pallas_call | solution.py:492
  419.3 5.2 convolution_add_fusion.15
  425.5 4.1 fusion.125
  440.9 4.1 fusion.58
  445.1 4.6 convolution_add_fusion.6
  450.8 4.3 convolution_add_fusion.17
  457.8 4.1 fusion.60
  461.9 4.7 convolution_add_fusion.7
  474.2 4.1 fusion.65
  479.5 21.9 %shard_map.277 = bf16[4,4,160,1344]{3,2,1,0:T(8,128)(2,1)} custom-call(bf16[192,2560]{1,0:T(8,128)(2,1)} %copy-done.22, bf16[192,2560]{1,0:T(8,128)(2,1)} %copy-done.62, bf16[384,896]{1,0:T(8,128)(2,1)} %pad_maximum_fusion.13.refs_2_, bf16[192,2560]{1,0:T(8,128)(2,1)} %copy-done.53, bf16[192,2560]{1,0:T(8,128)(2,1)} %copy-done.57, ...), custom_call_target="tpu_custom_call" | custom-call | flops 10569646080 | bytes 18874368 | tf_op jit(solution)/shard_map/pallas_call | solution.py:492
  502.5 5.7 convolution_add_fusion.8
  509.5 3.2 fusion.146
  512.7 3.1 fusion.148
  526.7 17.7 %collective-permute-done.19 = bf16[192,2560]{1,0:T(8,128)(2,1)S(1)} collective-permute-done((bf16[192,2560]{1,0:T(8,128)(2,1)}, bf16[192,2560]{1,0:T(8,128)(2,1)S(1)}, u32[]{:S(2)}, u32[]{:S(2)}) %collective-permute-start.19) | collective-permute-done | bytes 983072 | tf_op jit(solution)/shard_map/ppermute | solution.py:25
  549.6 22.5 %collective-permute-done.20 = bf16[192,2560]{1,0:T(8,128)(2,1)S(1)} collective-permute-done((bf16[192,2560]{1,0:T(8,128)(2,1)S(1)}, bf16[192,2560]{1,0:T(8,128)(2,1)S(1)}, u32[]{:S(2)}, u32[]{:S(2)}) %collective-permute-start.20) | collective-permute-done | bytes 983072 | tf_op jit(solution)/shard_map/ppermute | solution.py:25
  576.5 22.4 %collective-permute-done.21 = bf16[192,2560]{1,0:T(8,128)(2,1)S(1)} collective-permute-done((bf16[192,2560]{1,0:T(8,128)(2,1)S(1)}, bf16[192,2560]{1,0:T(8,128)(2,1)S(1)}, u32[]{:S(2)}, u32[]{:S(2)}) %collective-permute-start.21) | collective-permute-done | bytes 983072 | tf_op jit(solution)/shard_map/ppermute | solution.py:25
  611.9 8.3 convert_reduce_fusion.2
  620.2 7.1 shard_map.275
  628.8 9.3 shard_map.276
  638.8 7.2 multiply_reduce_fusion
  656.4 4.0 fusion.53
  663.3 6.0 fusion.36
  679.1 4.3 shard_map.279
  683.5 2.9 pad_maximum_fusion.4.refs_0_
  686.4 11.2 %shard_map.280 = bf16[4,4,160,2560]{3,2,1,0:T(8,128)(2,1)} custom-call(bf16[384,2560]{1,0:T(8,128)(2,1)} %pad_maximum_fusion.4.refs_0_, bf16[384,1280]{1,0:T(8,128)(2,1)} %copy-done.50, bf16[384,2560]{1,0:T(8,128)(2,1)} %slice.307.refs_0_.refs_2_, bf16[384,1280]{1,0:T(8,128)(2,1)} %get-tuple-element.142.refs_3_), custom_call_target="tpu_custom_call" | custom-call | flops 5033164800 | bytes 17039360 | tf_op jit(solution)/shard_map/pallas_call | solution.py:492
  703.9 3.4 convert_element_type.363.refs_2_
  709.5 7.2 shard_map.278
  720.0 5.0 fusion.189
  725.0 5.0 convolution_add_fusion.4
  739.3 4.5 all-to-all-start
  745.7 3.1 fusion.14
  749.3 13.6 %collective-permute-done.28 = bf16[192,2560]{1,0:T(8,128)(2,1)} collective-permute-done((bf16[192,2560]{1,0:T(8,128)(2,1)}, bf16[192,2560]{1,0:T(8,128)(2,1)}, u32[]{:S(2)}, u32[]{:S(2)}) %collective-permute-start.28) | collective-permute-done | bytes 983072 | tf_op jit(solution)/shard_map/ppermute | solution.py:25
  766.4 48.9 %collective-permute-done.29 = bf16[192,2560]{1,0:T(8,128)(2,1)} collective-permute-done((bf16[192,2560]{1,0:T(8,128)(2,1)}, bf16[192,2560]{1,0:T(8,128)(2,1)}, u32[]{:S(2)}, u32[]{:S(2)}) %collective-permute-start.29) | collective-permute-done | bytes 983072 | tf_op jit(solution)/shard_map/ppermute | solution.py:25
  815.2 3.3 add_convert_fusion
  818.5 10.1 collective-permute-start.30
  830.0 7.2 collective-permute-done.44
  838.5 8.2 all-to-all-done.refs_0_
  846.7 4.6 all-to-all-start.1
  851.4 7.2 fusion.13
  860.7 22.9 %collective-permute-done.46 = f32[240,128]{1,0:T(8,128)S(1)} collective-permute-done((f32[240,128]{1,0:T(8,128)S(1)}, f32[240,128]{1,0:T(8,128)S(1)}, u32[]{:S(2)}, u32[]{:S(2)}) %collective-permute-start.46) | collective-permute-done | bytes 122912 | tf_op jit(solution)/shard_map/ppermute | solution.py:37
  883.6 4.7 collective-permute-start.47
  888.3 10.6 %collective-permute-done.47 = f32[240,128]{1,0:T(8,128)S(1)} collective-permute-done((f32[240,128]{1,0:T(8,128)S(1)}, f32[240,128]{1,0:T(8,128)S(1)}, u32[]{:S(2)}, u32[]{:S(2)}) %collective-permute-start.47) | collective-permute-done | bytes 122912 | tf_op jit(solution)/shard_map/ppermute | solution.py:37
  899.9 6.2 collective-permute-done.37
  907.2 6.1 collective-permute-done.38
  918.7 5.9 shard_map.281
  925.5 4.6 broadcast_select_fusion.1
  931.4 3.8 broadcast_select_fusion.3
  937.1 17.3 %collective-permute-done.40 = bf16[160,2560]{1,0:T(8,128)(2,1)} collective-permute-done((bf16[160,2560]{1,0:T(8,128)(2,1)S(1)}, bf16[160,2560]{1,0:T(8,128)(2,1)}, u32[]{:S(2)}, u32[]{:S(2)}) %collective-permute-start.40) | collective-permute-done | bytes 819232 | tf_op jit(solution)/shard_map/ppermute | solution.py:25
  956.1 7.0 collective-permute-done.34
  966.6 18.6 %collective-permute-done.35 = bf16[200,1024]{1,0:T(8,128)(2,1)S(1)} collective-permute-done((bf16[200,1024]{1,0:T(8,128)(2,1)S(1)}, bf16[200,1024]{1,0:T(8,128)(2,1)S(1)}, u32[]{:S(2)}, u32[]{:S(2)}) %collective-permute-start.35) | collective-permute-done | bytes 409632 | tf_op jit(solution)/shard_map/ppermute | solution.py:25
  990.6 8.9 collective-permute-done.36
  1004.0 8.1 collective-permute-done.42
  (548 shorter events, 209.9 us)
Async XLA Ops:
  7.2 256.4 %copy-start = (f32[2,3840]{1,0:T(2,128)S(1)}, f32[2,3840]{1,0:T(2,128)}, u32[]{:S(2)}) copy-start(f32[2,3840]{1,0:T(2,128)} %param.31) | copy-start | bytes 92164
  7.2 360.3 %all-gather.3.cloned.1.call-start = ((), (), s32[]{:S(2)}) async-start(), calls=%async_computation.7 | async-start | bytes 9830400 | tf_op jit(solution)/shard_map/all_gather | solution.py:608
  10.9 259.1 %copy-start.88 = (f32[2560]{0:T(1024)}, f32[2560]{0:T(1024)S(1)}, u32[]{:S(2)}) copy-start(f32[2560]{0:T(1024)S(1)} %get-tuple-element.133) | copy-start | bytes 30724
  189.9 229.3 %all-gather.5.cloned.1.call-start = ((), (), s32[]{:S(2)}) async-start(), calls=%async_computation.8 | async-start | bytes 9011200 | tf_op jit(solution)/shard_map/all_gather | solution.py:608
  192.1 72.2 %copy-start.6 = (bf16[192,2560]{1,0:T(8,128)(2,1)}, bf16[192,2560]{1,0:T(8,128)(2,1)S(1)}, u32[]{:S(2)}) copy-start(bf16[192,2560]{1,0:T(8,128)(2,1)S(1)} %get-tuple-element.74.refs_12_) | copy-start | bytes 2949124
  192.1 20.9 %collective-permute-start = (bf16[192,2560]{1,0:T(8,128)(2,1)S(1)}, bf16[192,2560]{1,0:T(8,128)(2,1)}, u32[]{:S(2)}, u32[]{:S(2)}) collective-permute-start(bf16[192,2560]{1,0:T(8,128)(2,1)S(1)} %get-tuple-element.74.refs_12_), channel_id=1, source_target_pairs={{0,8},{8,16},{16,24},{24,0},{1,9},{9,17},{17,25},{25,1},{2,10},{10... | collective-permute-start | bytes 2949128 | tf_op jit(solution)/shard_map/ppermute | solution.py:25
  213.0 33.9 %collective-permute-start.1 = (bf16[192,2560]{1,0:T(8,128)(2,1)}, bf16[192,2560]{1,0:T(8,128)(2,1)}, u32[]{:S(2)}, u32[]{:S(2)}) collective-permute-start(bf16[192,2560]{1,0:T(8,128)(2,1)} %collective-permute-done.refs_15_), channel_id=1, source_target_pairs={{0,8},{8,16},{16,24},{24,0},{1,9},{9,17},{17,25},{25,1},{2,10},{10... | collective-permute-start | bytes 2949128 | tf_op jit(solution)/shard_map/ppermute | solution.py:25
  263.0 4.2 collective-permute-start.2
  263.0 8.3 collective-permute-start.3
  263.6 337.0 %reduce-scatter.6.cloned.1.call-start = ((), (), s32[]{:S(2)}) async-start(), calls=%async_computation.9 | async-start | bytes 9830400 | tf_op jit(solution)/shard_map/reduce_scatter | solution.py:612
  264.4 28.2 %collective-permute-start.7 = (bf16[192,2560]{1,0:T(8,128)(2,1)}, bf16[192,2560]{1,0:T(8,128)(2,1)S(1)}, u32[]{:S(2)}, u32[]{:S(2)}) collective-permute-start(bf16[192,2560]{1,0:T(8,128)(2,1)} %collective-permute-done.refs_15_), channel_id=1, source_target_pairs={{0,1},{1,0},{2,3},{3,2},{4,5},{5,4},{6,7},{7,6},{8,9},{9,8},{10,11... | collective-permute-start | bytes 2949128 | tf_op jit(solution)/shard_map/ppermute | solution.py:20
  265.9 26.7 %collective-permute-start.13 = (bf16[192,2560]{1,0:T(8,128)(2,1)}, bf16[192,2560]{1,0:T(8,128)(2,1)S(1)}, u32[]{:S(2)}, u32[]{:S(2)}) collective-permute-start(bf16[192,2560]{1,0:T(8,128)(2,1)} %collective-permute-done.1.refs_18_), channel_id=1, source_target_pairs={{0,8},{8,16},{16,24},{24,0},{1,9},{9,17},{17,25},{25,1},{2,10},{10... | collective-permute-start | bytes 2949128 | tf_op jit(solution)/shard_map/ppermute | solution.py:25
  270.2 119.7 %copy-start.22 = (bf16[192,2560]{1,0:T(8,128)(2,1)}, bf16[192,2560]{1,0:T(8,128)(2,1)S(1)}, u32[]{:S(2)}) copy-start(bf16[192,2560]{1,0:T(8,128)(2,1)S(1)} %multiply_convert_fusion.1.refs_0_) | copy-start | bytes 2949124
  270.2 42.8 %collective-permute-start.5 = (bf16[192,2560]{1,0:T(8,128)(2,1)S(1)}, bf16[192,2560]{1,0:T(8,128)(2,1)S(1)}, u32[]{:S(2)}, u32[]{:S(2)}) collective-permute-start(bf16[192,2560]{1,0:T(8,128)(2,1)S(1)} %multiply_convert_fusion.1.refs_0_), channel_id=1, source_target_pairs={{0,8},{8,16},{16,24},{24,0},{1,9},{9,17},{17,25},{25,1},{2,10},{10... | collective-permute-start | bytes 2949128 | tf_op jit(solution)/shard_map/ppermute | solution.py:25
  272.6 40.6 %collective-permute-start.10 = (bf16[192,2560]{1,0:T(8,128)(2,1)}, bf16[192,2560]{1,0:T(8,128)(2,1)S(1)}, u32[]{:S(2)}, u32[]{:S(2)}) collective-permute-start(bf16[192,2560]{1,0:T(8,128)(2,1)} %collective-permute-done.1.refs_18_), channel_id=1, source_target_pairs={{0,1},{1,0},{2,3},{3,2},{4,5},{5,4},{6,7},{7,6},{8,9},{9,8},{10,11... | collective-permute-start | bytes 2949128 | tf_op jit(solution)/shard_map/ppermute | solution.py:20
  292.6 20.8 %collective-permute-start.14 = (bf16[192,2560]{1,0:T(8,128)(2,1)S(1)}, bf16[192,2560]{1,0:T(8,128)(2,1)S(1)}, u32[]{:S(2)}, u32[]{:S(2)}) collective-permute-start(bf16[192,2560]{1,0:T(8,128)(2,1)S(1)} %collective-permute-done.13.refs_21_), channel_id=1, source_target_pairs={{0,1},{1,0},{2,3},{3,2},{4,5},{5,4},{6,7},{7,6},{8,9},{9,8},{10,11... | collective-permute-start | bytes 2949128 | tf_op jit(solution)/shard_map/ppermute | solution.py:20
  313.0 25.0 %collective-permute-start.8 = (bf16[192,2560]{1,0:T(8,128)(2,1)S(1)}, bf16[192,2560]{1,0:T(8,128)(2,1)S(1)}, u32[]{:S(2)}, u32[]{:S(2)}) collective-permute-start(bf16[192,2560]{1,0:T(8,128)(2,1)S(1)} %collective-permute-done.5.refs_3_), channel_id=1, source_target_pairs={{0,8},{8,16},{16,24},{24,0},{1,9},{9,17},{17,25},{25,1},{2,10},{10... | collective-permute-start | bytes 2949128 | tf_op jit(solution)/shard_map/ppermute | solution.py:25
  313.1 25.2 %collective-permute-start.4 = (bf16[192,2560]{1,0:T(8,128)(2,1)S(1)}, bf16[192,2560]{1,0:T(8,128)(2,1)S(1)}, u32[]{:S(2)}, u32[]{:S(2)}) collective-permute-start(bf16[192,2560]{1,0:T(8,128)(2,1)S(1)} %multiply_convert_fusion.1.refs_0_), channel_id=1, source_target_pairs={{0,1},{1,0},{2,3},{3,2},{4,5},{5,4},{6,7},{7,6},{8,9},{9,8},{10,11... | collective-permute-start | bytes 2949128 | tf_op jit(solution)/shard_map/ppermute | solution.py:20
  313.4 48.9 %collective-permute-start.6 = (bf16[192,2560]{1,0:T(8,128)(2,1)S(1)}, bf16[192,2560]{1,0:T(8,128)(2,1)S(1)}, u32[]{:S(2)}, u32[]{:S(2)}) collective-permute-start(bf16[192,2560]{1,0:T(8,128)(2,1)S(1)} %collective-permute-done.5.refs_3_), channel_id=1, source_target_pairs={{0,1},{1,0},{2,3},{3,2},{4,5},{5,4},{6,7},{7,6},{8,9},{9,8},{10,11... | collective-permute-start | bytes 2949128 | tf_op jit(solution)/shard_map/ppermute | solution.py:20
  338.0 24.3 %collective-permute-start.11 = (bf16[192,2560]{1,0:T(8,128)(2,1)S(1)}, bf16[192,2560]{1,0:T(8,128)(2,1)S(1)}, u32[]{:S(2)}, u32[]{:S(2)}) collective-permute-start(bf16[192,2560]{1,0:T(8,128)(2,1)S(1)} %collective-permute-done.8.refs_6_), channel_id=1, source_target_pairs={{0,8},{8,16},{16,24},{24,0},{1,9},{9,17},{17,25},{25,1},{2,10},{10... | collective-permute-start | bytes 2949128 | tf_op jit(solution)/shard_map/ppermute | solution.py:25
  339.9 23.7 %collective-permute-start.9 = (bf16[192,2560]{1,0:T(8,128)(2,1)S(1)}, bf16[192,2560]{1,0:T(8,128)(2,1)S(1)}, u32[]{:S(2)}, u32[]{:S(2)}) collective-permute-start(bf16[192,2560]{1,0:T(8,128)(2,1)S(1)} %collective-permute-done.8.refs_6_), channel_id=1, source_target_pairs={{0,1},{1,0},{2,3},{3,2},{4,5},{5,4},{6,7},{7,6},{8,9},{9,8},{10,11... | collective-permute-start | bytes 2949128 | tf_op jit(solution)/shard_map/ppermute | solution.py:20
  362.3 2.6 collective-permute-start.12
  375.8 82.0 %copy-start.39 = (bf16[384,512]{1,0:T(8,128)(2,1)}, bf16[384,512]{1,0:T(8,128)(2,1)S(1)}, u32[]{:S(2)}) copy-start(bf16[384,512]{1,0:T(8,128)(2,1)S(1)} %get-tuple-element.165) | copy-start | bytes 1179652
  394.6 79.6 %copy-start.47 = (bf16[384,512]{1,0:T(8,128)(2,1)}, bf16[384,512]{1,0:T(8,128)(2,1)S(1)}, u32[]{:S(2)}) copy-start(bf16[384,512]{1,0:T(8,128)(2,1)S(1)} %get-tuple-element.170) | copy-start | bytes 1179652
  418.7 220.1 %reduce-scatter.8.cloned.1.call-start = ((), (), s32[]{:S(2)}) async-start(), calls=%async_computation.10 | async-start | bytes 9011200 | tf_op jit(solution)/shard_map/reduce_scatter | solution.py:612
  434.6 43.7 %collective-permute-start.18 = (bf16[192,2560]{1,0:T(8,128)(2,1)S(1)}, bf16[192,2560]{1,0:T(8,128)(2,1)S(1)}, u32[]{:S(2)}, u32[]{:S(2)}) collective-permute-start(bf16[192,2560]{1,0:T(8,128)(2,1)S(1)} %slice.738), channel_id=1, source_target_pairs={{0,1},{1,0},{2,3},{3,2},{4,5},{5,4},{6,7},{7,6},{8,9},{9,8},{10,11... | collective-permute-start | bytes 2949128 | tf_op jit(solution)/shard_map/ppermute | solution.py:20
  450.8 75.6 %collective-permute-start.17 = (bf16[192,2560]{1,0:T(8,128)(2,1)}, bf16[192,2560]{1,0:T(8,128)(2,1)}, u32[]{:S(2)}, u32[]{:S(2)}) collective-permute-start(bf16[192,2560]{1,0:T(8,128)(2,1)} %slice.739), channel_id=1, source_target_pairs={{0,1},{1,0},{2,3},{3,2},{4,5},{5,4},{6,7},{7,6},{8,9},{9,8},{10,11... | collective-permute-start | bytes 2949128 | tf_op jit(solution)/shard_map/ppermute | solution.py:20
  467.8 81.7 %collective-permute-start.16 = (bf16[192,2560]{1,0:T(8,128)(2,1)}, bf16[192,2560]{1,0:T(8,128)(2,1)}, u32[]{:S(2)}, u32[]{:S(2)}) collective-permute-start(bf16[192,2560]{1,0:T(8,128)(2,1)} %slice.740), channel_id=1, source_target_pairs={{0,1},{1,0},{2,3},{3,2},{4,5},{5,4},{6,7},{7,6},{8,9},{9,8},{10,11... | collective-permute-start | bytes 2949128 | tf_op jit(solution)/shard_map/ppermute | solution.py:20
  501.4 397.5 %reduce-scatter.12.cloned.1.call-start = ((), (), s32[]{:S(2)}) async-start(), calls=%async_computation.12 | async-start | bytes 1638400 | tf_op jit(solution)/shard_map/reduce_scatter | solution.py:612
  509.3 67.2 %collective-permute-start.15 = (bf16[192,2560]{1,0:T(8,128)(2,1)}, bf16[192,2560]{1,0:T(8,128)(2,1)S(1)}, u32[]{:S(2)}, u32[]{:S(2)}) collective-permute-start(bf16[192,2560]{1,0:T(8,128)(2,1)} %slice.741), channel_id=1, source_target_pairs={{0,1},{1,0},{2,3},{3,2},{4,5},{5,4},{6,7},{7,6},{8,9},{9,8},{10,11... | collective-permute-start | bytes 2949128 | tf_op jit(solution)/shard_map/ppermute | solution.py:20
  518.3 26.1 %collective-permute-start.19 = (bf16[192,2560]{1,0:T(8,128)(2,1)}, bf16[192,2560]{1,0:T(8,128)(2,1)S(1)}, u32[]{:S(2)}, u32[]{:S(2)}) collective-permute-start(bf16[192,2560]{1,0:T(8,128)(2,1)} %slice_add_fusion.4), channel_id=1, source_target_pairs={{0,8},{8,16},{16,24},{24,0},{1,9},{9,17},{17,25},{25,1},{2,10},{10... | collective-permute-start | bytes 2949128 | tf_op jit(solution)/shard_map/ppermute | solution.py:25
  522.0 23.9 %collective-permute-start.25 = (bf16[192,2560]{1,0:T(8,128)(2,1)}, bf16[192,2560]{1,0:T(8,128)(2,1)S(1)}, u32[]{:S(2)}, u32[]{:S(2)}) collective-permute-start(bf16[192,2560]{1,0:T(8,128)(2,1)} %slice.734), channel_id=1, source_target_pairs={{0,1},{1,0},{2,3},{3,2},{4,5},{5,4},{6,7},{7,6},{8,9},{9,8},{10,11... | collective-permute-start | bytes 2949128 | tf_op jit(solution)/shard_map/ppermute | solution.py:20
  526.4 21.1 %collective-permute-start.24 = (bf16[192,2560]{1,0:T(8,128)(2,1)S(1)}, bf16[192,2560]{1,0:T(8,128)(2,1)S(1)}, u32[]{:S(2)}, u32[]{:S(2)}) collective-permute-start(bf16[192,2560]{1,0:T(8,128)(2,1)S(1)} %slice.735), channel_id=1, source_target_pairs={{0,1},{1,0},{2,3},{3,2},{4,5},{5,4},{6,7},{7,6},{8,9},{9,8},{10,11... | collective-permute-start | bytes 2949128 | tf_op jit(solution)/shard_map/ppermute | solution.py:20
  544.4 30.6 %collective-permute-start.23 = (bf16[192,2560]{1,0:T(8,128)(2,1)S(1)}, bf16[192,2560]{1,0:T(8,128)(2,1)S(1)}, u32[]{:S(2)}, u32[]{:S(2)}) collective-permute-start(bf16[192,2560]{1,0:T(8,128)(2,1)S(1)} %slice.736), channel_id=1, source_target_pairs={{0,1},{1,0},{2,3},{3,2},{4,5},{5,4},{6,7},{7,6},{8,9},{9,8},{10,11... | collective-permute-start | bytes 2949128 | tf_op jit(solution)/shard_map/ppermute | solution.py:20
  546.0 26.0 %collective-permute-start.20 = (bf16[192,2560]{1,0:T(8,128)(2,1)S(1)}, bf16[192,2560]{1,0:T(8,128)(2,1)S(1)}, u32[]{:S(2)}, u32[]{:S(2)}) collective-permute-start(bf16[192,2560]{1,0:T(8,128)(2,1)S(1)} %fusion.46), channel_id=1, source_target_pairs={{0,8},{8,16},{16,24},{24,0},{1,9},{9,17},{17,25},{25,1},{2,10},{10... | collective-permute-start | bytes 2949128 | tf_op jit(solution)/shard_map/ppermute | solution.py:25
  547.5 26.3 %collective-permute-start.22 = (bf16[192,2560]{1,0:T(8,128)(2,1)S(1)}, bf16[192,2560]{1,0:T(8,128)(2,1)S(1)}, u32[]{:S(2)}, u32[]{:S(2)}) collective-permute-start(bf16[192,2560]{1,0:T(8,128)(2,1)S(1)} %slice.737), channel_id=1, source_target_pairs={{0,1},{1,0},{2,3},{3,2},{4,5},{5,4},{6,7},{7,6},{8,9},{9,8},{10,11... | collective-permute-start | bytes 2949128 | tf_op jit(solution)/shard_map/ppermute | solution.py:20
  573.6 25.4 %collective-permute-start.21 = (bf16[192,2560]{1,0:T(8,128)(2,1)S(1)}, bf16[192,2560]{1,0:T(8,128)(2,1)S(1)}, u32[]{:S(2)}, u32[]{:S(2)}) collective-permute-start(bf16[192,2560]{1,0:T(8,128)(2,1)S(1)} %fusion.48), channel_id=1, source_target_pairs={{0,8},{8,16},{16,24},{24,0},{1,9},{9,17},{17,25},{25,1},{2,10},{10... | collective-permute-start | bytes 2949128 | tf_op jit(solution)/shard_map/ppermute | solution.py:25
  604.6 4.6 collective-permute-start.26
  669.3 5.7 collective-permute-start.27
  683.5 246.6 %reduce-scatter.14.cloned.1.call-start = ((), (), s32[]{:S(2)}) async-start(), calls=%async_computation.13 | async-start | bytes 16384000 | tf_op jit(solution)/shard_map/reduce_scatter | solution.py:612
  697.7 237.5 %reduce-scatter.10.cloned.1.call-start = ((), (), s32[]{:S(2)}) async-start(), calls=%async_computation.11 | async-start | bytes 8192000 | tf_op jit(solution)/shard_map/reduce_scatter | solution.py:612
  733.0 12.7 %collective-permute-start.32 = (bf16[192,2560]{1,0:T(8,128)(2,1)}, bf16[192,2560]{1,0:T(8,128)(2,1)}, u32[]{:S(2)}, u32[]{:S(2)}) collective-permute-start(bf16[192,2560]{1,0:T(8,128)(2,1)} %dynamic-slice_convert_fusion), channel_id=1, source_target_pairs={{0,1},{1,0},{2,3},{3,2},{4,5},{5,4},{6,7},{7,6},{8,9},{9,8},{10,11... | collective-permute-start | bytes 2949128 | tf_op jit(solution)/shard_map/ppermute | solution.py:20
  736.1 26.9 %collective-permute-start.28 = (bf16[192,2560]{1,0:T(8,128)(2,1)}, bf16[192,2560]{1,0:T(8,128)(2,1)}, u32[]{:S(2)}, u32[]{:S(2)}) collective-permute-start(bf16[192,2560]{1,0:T(8,128)(2,1)} %slice_add_fusion.3), channel_id=1, source_target_pairs={{0,8},{8,16},{16,24},{24,0},{1,9},{9,17},{17,25},{25,1},{2,10},{10... | collective-permute-start | bytes 2949128 | tf_op jit(solution)/shard_map/ppermute | solution.py:25
  739.3 107.4 %all-to-all-start = ((bf16[4,160,1536]{2,1,0:T(8,128)(2,1)}), bf16[4,160,1536]{2,1,0:T(8,128)(2,1)}, u32[]{:S(2)}, u32[]{:S(2)}) async-start(bf16[4,160,1536]{2,1,0:T(8,128)(2,1)} %bitcast.187), calls=%async_computation.5 | async-start | bytes 3932160 | tf_op jit(solution)/shard_map/all_to_all | solution.py:604
  748.8 17.3 %collective-permute-start.43 = (f32[4,2560]{1,0:T(4,128)S(1)}, f32[4,2560]{1,0:T(4,128)S(1)}, u32[]{:S(2)}, u32[]{:S(2)}) collective-permute-start(f32[4,2560]{1,0:T(4,128)S(1)} %pad_maximum_fusion.18), channel_id=1, source_target_pairs={{0,1},{1,0},{2,3},{3,2},{4,5},{5,4},{6,7},{7,6},{8,9},{9,8},{10,11... | collective-permute-start | bytes 122888 | tf_op jit(solution)/shard_map/ppermute | solution.py:20
  765.5 49.7 %collective-permute-start.29 = (bf16[192,2560]{1,0:T(8,128)(2,1)}, bf16[192,2560]{1,0:T(8,128)(2,1)}, u32[]{:S(2)}, u32[]{:S(2)}) collective-permute-start(bf16[192,2560]{1,0:T(8,128)(2,1)} %add_convert_fusion.1), channel_id=1, source_target_pairs={{0,8},{8,16},{16,24},{24,0},{1,9},{9,17},{17,25},{25,1},{2,10},{10... | collective-permute-start | bytes 2949128 | tf_op jit(solution)/shard_map/ppermute | solution.py:25
  766.4 62.3 %copy-start.95 = (f32[1280]{0:T(1024)S(1)}, f32[1280]{0:T(1024)}, u32[]{:S(2)}) copy-start(f32[1280]{0:T(1024)} %param.29) | copy-start | bytes 15364
  818.5 32.8 %collective-permute-start.30 = (bf16[192,2560]{1,0:T(8,128)(2,1)}, bf16[192,2560]{1,0:T(8,128)(2,1)}, u32[]{:S(2)}, u32[]{:S(2)}) collective-permute-start(bf16[192,2560]{1,0:T(8,128)(2,1)} %add_convert_fusion), channel_id=1, source_target_pairs={{0,8},{8,16},{16,24},{24,0},{1,9},{9,17},{17,25},{25,1},{2,10},{10... | collective-permute-start | bytes 2949128 | tf_op jit(solution)/shard_map/ppermute | solution.py:25
  828.7 8.5 collective-permute-start.44
  837.2 21.3 %collective-permute-start.45 = (f32[240,128]{1,0:T(8,128)S(1)}, f32[240,128]{1,0:T(8,128)S(1)}, u32[]{:S(2)}, u32[]{:S(2)}) collective-permute-start(f32[240,128]{1,0:T(8,128)S(1)} %bitcast_add_fusion), channel_id=1, source_target_pairs={{0,4},{2,6},{4,0},{6,2},{8,12},{10,14},{12,8},{14,10},{16,20},{18,... | collective-permute-start | bytes 368648 | tf_op jit(solution)/shard_map/ppermute | solution.py:37
  846.7 72.0 %all-to-all-start.1 = ((bf16[4,160,1344]{2,1,0:T(8,128)(2,1)}), bf16[4,160,1344]{2,1,0:T(8,128)(2,1)}, u32[]{:S(2)}, u32[]{:S(2)}) async-start(bf16[4,160,1344]{2,1,0:T(8,128)(2,1)} %bitcast.190), calls=%async_computation.6 | async-start | bytes 3604480 | tf_op jit(solution)/shard_map/all_to_all | solution.py:604
  858.5 67.0 %collective-permute-start.33 = (f32[192,2560]{1,0:T(8,128)}, f32[192,2560]{1,0:T(8,128)}, u32[]{:S(2)}, u32[]{:S(2)}) collective-permute-start(f32[192,2560]{1,0:T(8,128)} %get-tuple-element.180), channel_id=1, source_target_pairs={{0,1},{1,0},{2,3},{3,2},{4,5},{5,4},{6,7},{7,6},{8,9},{9,8},{10,11... | collective-permute-start | bytes 5898248 | tf_op jit(solution)/shard_map/ppermute | solution.py:20
  858.6 25.0 %collective-permute-start.46 = (f32[240,128]{1,0:T(8,128)S(1)}, f32[240,128]{1,0:T(8,128)S(1)}, u32[]{:S(2)}, u32[]{:S(2)}) collective-permute-start(f32[240,128]{1,0:T(8,128)S(1)} %fusion.228), channel_id=1, source_target_pairs={{0,8},{2,10},{4,12},{6,14},{8,0},{10,2},{12,4},{14,6},{16,24},{18,... | collective-permute-start | bytes 368648 | tf_op jit(solution)/shard_map/ppermute | solution.py:37
  883.6 15.3 %collective-permute-start.47 = (f32[240,128]{1,0:T(8,128)S(1)}, f32[240,128]{1,0:T(8,128)S(1)}, u32[]{:S(2)}, u32[]{:S(2)}) collective-permute-start(f32[240,128]{1,0:T(8,128)S(1)} %add.593), channel_id=1, source_target_pairs={{0,16},{2,18},{4,20},{6,22},{8,24},{10,26},{12,28},{14,30},{16,0},... | collective-permute-start | bytes 368648 | tf_op jit(solution)/shard_map/ppermute | solution.py:37
  899.9 6.2 collective-permute-start.37
  907.1 6.3 collective-permute-start.38
  907.1 24.2 %collective-permute-start.31 = (f32[192,2560]{1,0:T(8,128)}, f32[192,2560]{1,0:T(8,128)}, u32[]{:S(2)}, u32[]{:S(2)}) collective-permute-start(f32[192,2560]{1,0:T(8,128)} %get-tuple-element.181), channel_id=1, source_target_pairs={{0,1},{1,0},{2,3},{3,2},{4,5},{5,4},{6,7},{7,6},{8,9},{9,8},{10,11... | collective-permute-start | bytes 5898248 | tf_op jit(solution)/shard_map/ppermute | solution.py:20
  914.3 10.3 %collective-permute-start.39 = (bf16[160,256]{1,0:T(8,128)(2,1)S(1)}, bf16[160,256]{1,0:T(8,128)(2,1)S(1)}, u32[]{:S(2)}, u32[]{:S(2)}) collective-permute-start(bf16[160,256]{1,0:T(8,128)(2,1)S(1)} %fusion.163), channel_id=1, source_target_pairs={{0,8},{8,16},{16,24},{24,0},{1,9},{9,17},{17,25},{25,1},{2,10},{10... | collective-permute-start | bytes 245768 | tf_op jit(solution)/shard_map/ppermute | solution.py:25
  931.3 23.1 %collective-permute-start.40 = (bf16[160,2560]{1,0:T(8,128)(2,1)S(1)}, bf16[160,2560]{1,0:T(8,128)(2,1)}, u32[]{:S(2)}, u32[]{:S(2)}) collective-permute-start(bf16[160,2560]{1,0:T(8,128)(2,1)S(1)} %dynamic-slice_bitcast_fusion), channel_id=1, source_target_pairs={{0,8},{8,16},{16,24},{24,0},{1,9},{9,17},{17,25},{25,1},{2,10},{10... | collective-permute-start | bytes 2457608 | tf_op jit(solution)/shard_map/ppermute | solution.py:25
  936.4 26.7 %collective-permute-start.34 = (bf16[200,1024]{1,0:T(8,128)(2,1)S(1)}, bf16[200,1024]{1,0:T(8,128)(2,1)S(1)}, u32[]{:S(2)}, u32[]{:S(2)}) collective-permute-start(bf16[200,1024]{1,0:T(8,128)(2,1)S(1)} %dynamic-slice_bitcast_fusion.1), channel_id=1, source_target_pairs={{0,8},{8,16},{16,24},{24,0},{1,9},{9,17},{17,25},{25,1},{2,10},{10... | collective-permute-start | bytes 1228808 | tf_op jit(solution)/shard_map/ppermute | solution.py:25
  956.0 29.4 %collective-permute-start.41 = (bf16[160,2560]{1,0:T(8,128)(2,1)S(1)}, bf16[160,2560]{1,0:T(8,128)(2,1)S(1)}, u32[]{:S(2)}, u32[]{:S(2)}) collective-permute-start(bf16[160,2560]{1,0:T(8,128)(2,1)S(1)} %fusion.51), channel_id=1, source_target_pairs={{0,8},{8,16},{16,24},{24,0},{1,9},{9,17},{17,25},{25,1},{2,10},{10... | collective-permute-start | bytes 2457608 | tf_op jit(solution)/shard_map/ppermute | solution.py:25
  964.2 21.0 %collective-permute-start.35 = (bf16[200,1024]{1,0:T(8,128)(2,1)S(1)}, bf16[200,1024]{1,0:T(8,128)(2,1)S(1)}, u32[]{:S(2)}, u32[]{:S(2)}) collective-permute-start(bf16[200,1024]{1,0:T(8,128)(2,1)S(1)} %fusion.68), channel_id=1, source_target_pairs={{0,8},{8,16},{16,24},{24,0},{1,9},{9,17},{17,25},{25,1},{2,10},{10... | collective-permute-start | bytes 1228808 | tf_op jit(solution)/shard_map/ppermute | solution.py:25
  985.3 14.2 %collective-permute-start.36 = (bf16[200,1024]{1,0:T(8,128)(2,1)S(1)}, bf16[200,1024]{1,0:T(8,128)(2,1)S(1)}, u32[]{:S(2)}, u32[]{:S(2)}) collective-permute-start(bf16[200,1024]{1,0:T(8,128)(2,1)S(1)} %fusion.69), channel_id=1, source_target_pairs={{0,8},{8,16},{16,24},{24,0},{1,9},{9,17},{17,25},{25,1},{2,10},{10... | collective-permute-start | bytes 1228808 | tf_op jit(solution)/shard_map/ppermute | solution.py:25
  986.5 25.6 %collective-permute-start.42 = (bf16[160,2560]{1,0:T(8,128)(2,1)}, bf16[160,2560]{1,0:T(8,128)(2,1)}, u32[]{:S(2)}, u32[]{:S(2)}) collective-permute-start(bf16[160,2560]{1,0:T(8,128)(2,1)} %fusion.52), channel_id=1, source_target_pairs={{0,8},{8,16},{16,24},{24,0},{1,9},{9,17},{17,25},{25,1},{2,10},{10... | collective-permute-start | bytes 2457608 | tf_op jit(solution)/shard_map/ppermute | solution.py:25
  (121 other events, 1100.3 us)
Sparse Core Ops, SparseCore 0:
  190.0 87.4 all-gather.2
  279.4 77.6 all-gather.4
  418.8 80.5 reduce-scatter.5
  502.3 77.6 reduce-scatter.7
  683.6 31.0 reduce-scatter.11
  717.7 127.4 reduce-scatter.13
  848.2 72.2 reduce-scatter.9
